TPU v7x, 128 devices: a whole 4x4x4 slice. The times are simulated.
128 devices in a mesh: lat: 8 (over x, core), lon: 16 (over z, y).
Axes of the slice: x: 4, y: 4, z: 4, core: 2. Of those that a mesh axis runs over, the one named last changes fastest.
Arguments:
- tracers: bfloat16 [512, 2048, 32, 4], P('lat', 'lon'), may hold values from 0 to 2
- weights: bfloat16 [512, 16, 8, 128, 128], P('lat', 'lon'), may hold values from -1 to 1, as said below
- source_row: int32 [512, 16, 8], P('lat', 'lon'), may hold values from 0 to 511, as said below
- source_block: int32 [512, 16, 8], P('lat', 'lon'), may hold values from 0 to 15, as said below
- slot_count: int32 [512, 16], P('lat', 'lon'), may hold values from 1 to 8, as said below
Outputs:
- advected_fixed: float32 [512, 2048, 32, 4], P('lat', 'lon')
Inputs may be any that keep to these rules, and one draw needn't show every extreme that they name: source_row differs from the target tile's own row by at most 4 and lies within the grid. source_block lies at cyclic distance at most 2 from the target tile's own index along the row, except for target tiles of the first and the last latitude row, where it may reach 3; the allowed distance grows from 1 at the equator towards the poles; in the two outermost rows slot 0 reaches exactly 3 sectors ahead on even tiles and 3 sectors behind on odd tiles. slot_count grows from 1 or 2 at the equator to 8 at the two outermost rows. weights are of either sign; for each target tile the weights of each target cell over the used slots and all source cells sum (before rounding to bfloat16) to one value of that tile between 0.9 and 1.05.
All inputs are finite; a program needn't handle non-finite values.
Results may differ from a plain program's by a relative error of at most 0.0003.
Values may be sent and summed in bfloat16 or wider, within the bound.
No kernel may reach another device: no remote copies, remote signals or barrier semaphores. Data moves between devices by JAX's collectives and lax.ppermute only.
A program may use at most 192 MiB of HBM per device.

v0:
```python
import math

import jax
import jax.numpy as jnp
from jax import lax
from jax.experimental import pallas as pl
from jax.experimental.pallas import tpu as pltpu
from jax.sharding import PartitionSpec as P

ROWS = 64
C = 128
KMAX = 8
R = 4
E = R + 1
MID = ROWS - 2 * E
PAD = ROWS + 2 * R
NLAT, NLON_DEV, NLAT_DEV = 512, 16, 8
TB = 4
FAR = 2 * PAD
NT = (((1,), (1,)), ((), ()))


def ring(by):
    return [(i, (i + by) % NLON_DEV) for i in range(NLON_DEV)]


UP = [(i, i + 1) for i in range(NLAT_DEV - 1)]
DOWN = [(i + 1, i) for i in range(NLAT_DEV - 1)]


def polar(by):
    return [
        (a * NLON_DEV + i, a * NLON_DEV + (i + by) % NLON_DEV)
        for a in (0, NLAT_DEV - 1)
        for i in range(NLON_DEV)
    ]


def near_kernel(idx_ref, w_ref, *refs):
    parts, (out_ref, src, sem) = refs[:-3], refs[-3:]
    step = pl.program_id(0)
    own, le, lm, re, rm, up, dn = parts

    def copies():
        todo = [(own, 0, ROWS, 0 * PAD + R)]
        for n, (e, m) in enumerate(((le, lm), (re, rm))):
            at = (n + 1) * PAD + R
            todo.append((e, 0, E, at))
            todo.append((m, 0, MID, at + E))
            todo.append((e, E, E, at + E + MID))
        for n in range(3):
            todo.append((up, n * R, R, n * PAD))
            todo.append((dn, n * R, R, n * PAD + R + ROWS))
        return [
            pltpu.make_async_copy(ref.at[pl.ds(a, n)], src.at[pl.ds(to, n)], sem.at[i])
            for i, (ref, a, n, to) in enumerate(todo)
        ]

    @pl.when(step == 0)
    def _():
        for copy in copies():
            copy.start()
        src[3 * PAD] = jnp.zeros((C, C), src.dtype)
        for copy in copies():
            copy.wait()

    for j in range(TB):
        t = step * TB + j
        lhs = jnp.concatenate([src[idx_ref[k, t]] for k in range(KMAX)], axis=1)
        rhs = jnp.concatenate([w_ref[j, k] for k in range(KMAX)], axis=1)
        out_ref[j] = lax.dot_general(lhs, rhs, NT, preferred_element_type=jnp.float32)


def near_call(idx, weights, parts):
    n_copies = 7 + 6
    return pl.pallas_call(
        near_kernel,
        grid_spec=pltpu.PrefetchScalarGridSpec(
            num_scalar_prefetch=1,
            grid=(ROWS // TB,),
            in_specs=[pl.BlockSpec((TB, KMAX, C, C), lambda s, i: (s, 0, 0, 0))]
            + [pl.BlockSpec(memory_space=pltpu.HBM)] * len(parts),
            out_specs=pl.BlockSpec((TB, C, C), lambda s, i: (s, 0, 0)),
            scratch_shapes=[
                pltpu.VMEM((3 * PAD + 1, C, C), jnp.bfloat16),
                pltpu.SemaphoreType.DMA((n_copies,)),
            ],
        ),
        out_shape=jax.ShapeDtypeStruct((ROWS, C, C), jnp.float32),
        compiler_params=pltpu.CompilerParams(
            dimension_semantics=("arbitrary",), vmem_limit_bytes=20 << 20
        ),
        cost_estimate=pl.CostEstimate(
            flops=2 * ROWS * KMAX * C**3, bytes_accessed=28 << 20, transcendentals=0
        ),
        name="near",
    )(idx, weights, *parts)


GROUP = 8


def far_kernel(lst_ref, num_ref, area_ref, w_hbm, le, lm, re, rm, up, dn, l3, r3, part_ref, out_ref, mass_ref, src, wbuf, sem, wsem):
    todo = []
    for n, (e, m) in enumerate(((le, lm), (re, rm))):
        at = n * PAD + R
        todo.append((e, 0, E, at))
        todo.append((m, 0, MID, at + E))
        todo.append((e, E, E, at + E + MID))
        todo.append((up, n * R, R, n * PAD))
        todo.append((dn, n * R, R, n * PAD + R + ROWS))
    todo.append((l3, 0, E, FAR))
    todo.append((r3, 0, E, FAR + E))
    copies = [
        pltpu.make_async_copy(ref.at[pl.ds(a, n)], src.at[pl.ds(to, n)], sem.at[i])
        for i, (ref, a, n, to) in enumerate(todo)
    ]
    for copy in copies:
        copy.start()
    groups = num_ref[0]

    def entry(g, j):
        v = lst_ref[g * GROUP + j]
        slot = lax.shift_right_logical(v, 9)
        return lax.shift_right_logical(slot, 3), slot & (KMAX - 1), v & 511

    def weight_copy(g, j):
        t, k, _ = entry(g, j)
        return pltpu.make_async_copy(w_hbm.at[t, k], wbuf.at[g * GROUP + j], wsem.at[g])

    def issue(g, carry):
        for j in range(GROUP):
            weight_copy(g, j).start()
        return carry

    lax.fori_loop(0, groups, issue, 0)
    out_ref[...] = part_ref[...]
    src[FAR + 2 * E] = jnp.zeros((C, C), src.dtype)
    for copy in copies:
        copy.wait()

    def work(g, carry):
        for j in range(GROUP):
            weight_copy(g, j).wait()
        got = []
        for j in range(GROUP):
            t, _, s = entry(g, j)
            got.append(
                (t, lax.dot_general(src[s], wbuf[g * GROUP + j], NT, preferred_element_type=jnp.float32))
            )
        for t, d in got:
            out_ref[t] = out_ref[t] + d
        return carry

    lax.fori_loop(0, groups, work, 0)

    def add_up(t, acc):
        return acc + area_ref[t] * out_ref[t]

    acc = lax.fori_loop(0, ROWS, add_up, jnp.zeros((C, C), jnp.float32), unroll=4)
    mass_ref[...] = lax.dot_general(
        jnp.ones((8, C), jnp.float32), acc, NT,
        precision=lax.Precision.HIGHEST, preferred_element_type=jnp.float32,
    )


def far_call(lst, num, area, weights, parts, partial):
    smem = pl.BlockSpec(memory_space=pltpu.SMEM)
    hbm = pl.BlockSpec(memory_space=pltpu.HBM)
    vmem = pl.BlockSpec(memory_space=pltpu.VMEM)
    return pl.pallas_call(
        far_kernel,
        in_specs=[smem, smem, smem, hbm] + [hbm] * len(parts) + [vmem],
        out_specs=[vmem, vmem],
        out_shape=[
            jax.ShapeDtypeStruct((ROWS, C, C), jnp.float32),
            jax.ShapeDtypeStruct((8, C), jnp.float32),
        ],
        scratch_shapes=[
            pltpu.VMEM((FAR + 2 * E + 1, C, C), jnp.bfloat16),
            pltpu.VMEM((ROWS * KMAX, C, C), jnp.bfloat16),
            pltpu.SemaphoreType.DMA((12,)),
            pltpu.SemaphoreType.DMA((ROWS * KMAX // GROUP,)),
        ],
        compiler_params=pltpu.CompilerParams(vmem_limit_bytes=40 << 20),
        cost_estimate=pl.CostEstimate(
            flops=2 * ROWS * KMAX * C**3 // 2, bytes_accessed=20 << 20, transcendentals=0
        ),
        name="far",
    )(lst, num, area, weights, *parts, partial)


def latitude_area(first_row, count_rows):
    rows_all = jnp.arange(count_rows, dtype=jnp.int32) + first_row
    angle = -0.5 * math.pi + (rows_all.astype(jnp.float32) + 0.5) * (math.pi / NLAT)
    return jnp.cos(angle)


def slots(source_row, source_block, slot_count, lat, lon):
    row = source_row[:, 0, :].T - (lat * ROWS - R)
    row = jnp.clip(row, 0, PAD - 1)
    rel = (source_block[:, 0, :].T - lon + 3) % NLON_DEV - 3
    active = jnp.arange(KMAX, dtype=jnp.int32)[:, None] < slot_count[:, 0][None, :]
    size = jnp.abs(rel)
    side = (rel > 0).astype(jnp.int32)
    is_near = active & (size <= 1)
    near = jnp.where(is_near, jnp.where(rel == 0, 0, side + 1) * PAD + row, 3 * PAD)
    polar_row = jnp.clip(jnp.where(lat == 0, row - R, row - R - (ROWS - E)), 0, E - 1)
    far = jnp.where(size >= 3, FAR + side * E + polar_row, side * PAD + row)
    is_far = active & (size >= 2)
    target = jnp.arange(ROWS, dtype=jnp.int32)[None, :]
    slot = target * KMAX + jnp.arange(KMAX, dtype=jnp.int32)[:, None]
    order = jnp.where(is_far, slot, ROWS * KMAX + slot)
    zero = FAR + 2 * E
    packed = (order * 512 + jnp.where(is_far, far, zero)).reshape(-1)
    packed = jnp.sort(packed) & (ROWS * KMAX * 512 - 1)
    groups = (jnp.sum(is_far.astype(jnp.int32)) + GROUP - 1) // GROUP
    return near.astype(jnp.int32), packed.astype(jnp.int32), groups.reshape(1)


def everywhere(tracers, weights, source_row, source_block, slot_count):
    lat, lon = lax.axis_index("lat"), lax.axis_index("lon")
    q = tracers.transpose(0, 2, 3, 1).reshape(ROWS, C, C)
    qe = jnp.concatenate([q[:E], q[ROWS - E :]], axis=0)
    qm = q[E : ROWS - E]
    le, re = (lax.ppermute(qe, "lon", ring(1)), lax.ppermute(qe, "lon", ring(-1)))
    lm, rm = (lax.ppermute(qm, "lon", ring(1)), lax.ppermute(qm, "lon", ring(-1)))
    near_idx, far_list, far_groups = slots(source_row, source_block, slot_count, lat, lon)
    area = latitude_area(lat * ROWS, ROWS)
    total_area = C * NLON_DEV * jnp.sum(latitude_area(0, NLAT))
    mass_old = jnp.sum(area[:, None, None] * q.astype(jnp.float32), axis=(0, 2))

    up1 = lax.ppermute(jnp.concatenate([v[2 * E - R :] for v in (qe, le, re)], axis=0), "lat", UP)
    dn1 = lax.ppermute(jnp.concatenate([v[:R] for v in (qe, le, re)], axis=0), "lat", DOWN)
    lle, rre = (lax.ppermute(le, "lon", ring(1)), lax.ppermute(re, "lon", ring(-1)))
    llm, rrm = (lax.ppermute(lm, "lon", ring(1)), lax.ppermute(rm, "lon", ring(-1)))
    up2 = lax.ppermute(jnp.concatenate([v[2 * E - R :] for v in (lle, rre)], axis=0), "lat", UP)
    dn2 = lax.ppermute(jnp.concatenate([v[:R] for v in (lle, rre)], axis=0), "lat", DOWN)
    pole = [jnp.where(lat == 0, v[:E], v[E:]) for v in (lle, rre)]
    l3 = lax.ppermute(pole[0], ("lat", "lon"), polar(1))
    r3 = lax.ppermute(pole[1], ("lat", "lon"), polar(-1))

    w = weights[:, 0]
    partial = near_call(near_idx, w, (q, le, lm, re, rm, up1, dn1))
    advected, mass_new = far_call(
        far_list, far_groups, area, w, (lle, llm, rre, rrm, up2, dn2, l3, r3), partial
    )
    change = lax.psum(mass_old - mass_new[0], ("lat", "lon"))
    fixed = advected + (change / total_area)[None, :, None]
    return fixed


TOTAL_AREA = C * NLON_DEV * math.fsum(
    math.cos(-0.5 * math.pi + (j + 0.5) * math.pi / NLAT) for j in range(NLAT)
)
EDGE = 16
S = 2 * EDGE
M = ROWS - S
B = 16
SIDE = S + M + B + R
FAR2 = 2 * SIDE
SECT = 7 * PAD
CHUNKS = 4
PER = ROWS // CHUNKS
POLAR, NEXT = ((0, NLAT_DEV - 1), (1, NLAT_DEV - 2))


def some(by, lats):
    return [
        (a * NLON_DEV + i, a * NLON_DEV + (i + by) % NLON_DEV) for a in lats for i in range(NLON_DEV)
    ]


WC = 16
WT = ROWS // WC


def sums_kernel(idx_ref, area_ref, w_hbm, *refs):
    outs, (wv, acc, sem) = refs[:-3], refs[-3:]

    def copy(c):
        rows = pl.ds(c * WT, WT)
        return pltpu.make_async_copy(w_hbm.at[rows], wv.at[rows], sem.at[c])

    def start(c, carry):
        copy(c).start()
        return carry

    lax.fori_loop(0, WC, start, 0)
    acc[...] = jnp.zeros(acc.shape, acc.dtype)

    def work(c, carry):
        copy(c).wait()
        for j in range(WT):
            t = c * WT + j
            for k in range(KMAX):
                part = jnp.sum(wv[t, k].astype(jnp.float32).reshape(C // 8, 8, C), axis=0)
                at = idx_ref[k, t]
                acc[at] = acc[at] + area_ref[t] * part
        return carry

    lax.fori_loop(0, WC, work, 0)
    for n, out in enumerate(outs):
        out[...] = jnp.sum(acc[n * PAD : (n + 1) * PAD], axis=1)


def sums_call(idx, area, weights):
    smem = pl.BlockSpec(memory_space=pltpu.SMEM)
    vmem = pl.BlockSpec(memory_space=pltpu.VMEM)
    return pl.pallas_call(
        sums_kernel,
        in_specs=[smem, smem, pl.BlockSpec(memory_space=pltpu.HBM)],
        out_specs=[vmem] * 7,
        out_shape=[jax.ShapeDtypeStruct((PAD, C), jnp.float32)] * 7,
        scratch_shapes=[
            pltpu.VMEM(weights.shape, weights.dtype),
            pltpu.VMEM((SECT + 1, 8, C), jnp.float32),
            pltpu.SemaphoreType.DMA((WC,)),
        ],
        compiler_params=pltpu.CompilerParams(vmem_limit_bytes=22 << 20),
        cost_estimate=pl.CostEstimate(
            flops=20_000_000, bytes_accessed=17 << 20, transcendentals=0
        ),
        name="sums",
    )(idx, area, pltpu.with_memory_space_constraint(weights, pltpu.HBM))


def inner_kernel(idx_ref, w_hbm, own, ls, lm, rs, rm, up, dn, out_ref, wv, src, sem):
    def copy(c):
        rows = pl.ds(c * WT, WT)
        return pltpu.make_async_copy(w_hbm.at[rows], wv.at[rows], sem.at[c])

    def start(c, carry):
        copy(c).start()
        return carry

    lax.fori_loop(0, WC, start, 0)
    src[pl.ds(R, ROWS)] = own[...]
    for n, (e, m) in enumerate(((ls, lm), (rs, rm))):
        at = (n + 1) * PAD + R
        src[pl.ds(at, EDGE)] = e[:EDGE]
        src[pl.ds(at + EDGE, M)] = m[...]
        src[pl.ds(at + EDGE + M, EDGE)] = e[EDGE:]
    for n in range(3):
        src[pl.ds(n * PAD, R)] = up[pl.ds(n * R, R)]
        src[pl.ds(n * PAD + R + ROWS, R)] = dn[pl.ds(n * R, R)]
    src[3 * PAD] = jnp.zeros((C, C), src.dtype)

    def body(c, carry):
        copy(c).wait()
        for j in range(WT):
            t = c * WT + j
            lhs = jnp.concatenate([src[idx_ref[k, t]] for k in range(KMAX)], axis=1)
            rhs = jnp.concatenate([wv[t, k] for k in range(KMAX)], axis=1)
            out_ref[t] = lax.dot_general(lhs, rhs, NT, preferred_element_type=jnp.float32)
        return carry

    lax.fori_loop(0, WC, body, 0)


def inner_call(idx, weights, parts):
    vmem = pl.BlockSpec(memory_space=pltpu.VMEM)
    return pl.pallas_call(
        inner_kernel,
        in_specs=[pl.BlockSpec(memory_space=pltpu.SMEM), pl.BlockSpec(memory_space=pltpu.HBM)]
        + [vmem] * len(parts),
        out_specs=[vmem, vmem],
        out_shape=[
            pltpu.VMEM((ROWS, C, C), jnp.float32),
            pltpu.VMEM(weights.shape, weights.dtype),
        ],
        scratch_shapes=[
            pltpu.VMEM((3 * PAD + 1, C, C), jnp.bfloat16),
            pltpu.SemaphoreType.DMA((WC,)),
        ],
        compiler_params=pltpu.CompilerParams(vmem_limit_bytes=10 << 20),
        cost_estimate=pl.CostEstimate(
            flops=2 * ROWS * KMAX * C**3, bytes_accessed=17 << 20, transcendentals=0
        ),
        name="inner",
    )(idx, pltpu.with_memory_space_constraint(weights, pltpu.HBM), *parts)


def outer_kernel(idx_ref, w_ref, corr_ref, ls, lm, lb, rs, rm, rb, halo, l3, r3, part_ref, out_hbm, src, acc, sem):
    for n, (e, m, b) in enumerate(((ls, lm, lb), (rs, rm, rb))):
        at = n * SIDE
        src[pl.ds(at, S)] = e[...]
        src[pl.ds(at + S, M)] = m[...]
        src[pl.ds(at + S + M, B)] = b[...]
        src[pl.ds(at + S + M + B, R)] = halo[pl.ds(n * R, R)]
    src[pl.ds(FAR2, E)] = l3[...]
    src[pl.ds(FAR2 + E, E)] = r3[...]
    src[FAR2 + 2 * E] = jnp.zeros((C, C), src.dtype)

    def out_copy(c):
        rows = pl.ds(c * PER, PER)
        return pltpu.make_async_copy(acc.at[rows], out_hbm.at[rows], sem.at[c])

    for c in range(CHUNKS):

        def body(t, carry):
            lhs = jnp.concatenate([src[idx_ref[k, t]] for k in range(KMAX)], axis=1)
            rhs = jnp.concatenate([w_ref[t, k] for k in range(KMAX)], axis=1)
            got = lax.dot_general(lhs, rhs, NT, preferred_element_type=jnp.float32)
            acc[t] = (got + part_ref[t]) + corr_ref[...]
            return carry

        lax.fori_loop(c * PER, (c + 1) * PER, body, 0, unroll=4)
        out_copy(c).start()
    for c in range(CHUNKS):
        out_copy(c).wait()


def outer_call(idx, weights, corr, parts, partial):
    vmem = pl.BlockSpec(memory_space=pltpu.VMEM)
    return pl.pallas_call(
        outer_kernel,
        in_specs=[pl.BlockSpec(memory_space=pltpu.SMEM)] + [vmem] * (3 + len(parts)),
        out_specs=pl.BlockSpec(memory_space=pltpu.HBM),
        out_shape=jax.ShapeDtypeStruct((ROWS, C, C), jnp.float32),
        scratch_shapes=[
            pltpu.VMEM((FAR2 + 2 * E + 1, C, C), jnp.bfloat16),
            pltpu.VMEM((ROWS, C, C), jnp.float32),
            pltpu.SemaphoreType.DMA((CHUNKS,)),
        ],
        compiler_params=pltpu.CompilerParams(vmem_limit_bytes=14 << 20),
        cost_estimate=pl.CostEstimate(
            flops=2 * ROWS * KMAX * C**3, bytes_accessed=4 << 20, transcendentals=0
        ),
        name="outer",
    )(idx, weights, corr, *parts, partial)


def tables(source_row, source_block, slot_count, lat, lon):
    p = source_row[:, 0, :].T - (lat * ROWS - R)
    p = jnp.clip(p, 0, PAD - 1)
    rel = (source_block[:, 0, :].T - lon + 3) % NLON_DEV - 3
    rel = jnp.clip(rel, -3, 3)
    active = jnp.arange(KMAX, dtype=jnp.int32)[:, None] < slot_count[:, 0][None, :]
    sums_idx = jnp.where(active, (rel + 3) * PAD + p, SECT)
    size = jnp.abs(rel)
    side = (rel > 0).astype(jnp.int32)
    near_idx = jnp.where(
        active & (size <= 1), jnp.where(rel == 0, 0, side + 1) * PAD + p, 3 * PAD
    )
    r = p - R
    is_polar = (lat == 0) | (lat == NLAT_DEV - 1)
    in_band = jnp.where(r < EDGE, r, jnp.where(r < EDGE + M, r - EDGE + S, r - M))
    below = lat == NLAT_DEV - 2
    in_next = S + M + jnp.where(below, r - (ROWS - B), r)
    halo = S + M + B + jnp.where(r < 0, r + R, r - ROWS)
    two = jnp.where((r < 0) | (r >= ROWS), halo, jnp.where(is_polar, in_band, in_next))
    polar_row = jnp.clip(jnp.where(lat == 0, r, r - (ROWS - E)), 0, E - 1)
    far = jnp.where(size >= 3, FAR2 + side * E + polar_row, side * SIDE + two)
    is_far = active & (size >= 2)
    held = is_polar | ((lat == 1) & (r < B)) | (below & (r >= ROWS - B))
    lost = jnp.sum((is_far & ~held).astype(jnp.float32))
    far_idx = jnp.where(is_far & held, far, FAR2 + 2 * E)
    return sums_idx, near_idx, far_idx, lost


def swap(v, axis, size, to):
    return lax.ppermute(v, axis, [(i, to(i)) for i in range(size)])


def local(tracers, weights, source_row, source_block, slot_count):
    args = (tracers, weights, source_row, source_block, slot_count)
    lost, fixed = usual(*args)

    def redo(state):
        return jnp.zeros_like(state[0]), everywhere(*args)

    _, fixed = lax.while_loop(lambda state: state[0] > 0, redo, (lost, fixed))
    return fixed.reshape(ROWS, 32, 4, C).transpose(0, 3, 1, 2)


def usual(tracers, weights, source_row, source_block, slot_count):
    lat, lon = lax.axis_index("lat"), lax.axis_index("lon")
    both = ("lat", "lon")
    w = weights[:, 0]
    q = tracers.transpose(0, 2, 3, 1).reshape(ROWS, C, C)
    qs = jnp.concatenate([q[:EDGE], q[ROWS - EDGE :]], axis=0)
    ls, rs = lax.ppermute(qs, "lon", ring(1)), lax.ppermute(qs, "lon", ring(-1))
    sums_idx, near_idx, far_idx, lost = tables(source_row, source_block, slot_count, lat, lon)
    area = latitude_area(lat * ROWS, ROWS)
    sums = sums_call(sums_idx, area, w)
    got = sums[3]
    for d in (1, -1, 2, -2):
        got = got + lax.ppermute(sums[d + 3], "lon", ring(d))
    for d in (3, -3):
        got = got + lax.ppermute(sums[d + 3], both, some(d, POLAR))
    qm = q[EDGE : ROWS - EDGE]
    lm, rm = lax.ppermute(qm, "lon", ring(1)), lax.ppermute(qm, "lon", ring(-1))
    up1 = lax.ppermute(jnp.concatenate([v[S - R :] for v in (qs, ls, rs)], axis=0), "lat", UP)
    dn1 = lax.ppermute(jnp.concatenate([v[:R] for v in (qs, ls, rs)], axis=0), "lat", DOWN)

    def weigh(field, by):
        return jnp.sum(field.astype(jnp.float32) * by[:, None, :], axis=(0, 2))

    change = (
        weigh(q, area[:, None] - got[R : R + ROWS])
        - weigh(up1[:R], got[:R])
        - weigh(dn1[:R], got[R + ROWS :])
    )
    v = jnp.stack([change, jnp.full((C,), lost)])
    v = v + swap(v, "lat", NLAT_DEV, lambda i: i ^ 1)
    v = v + swap(v, "lat", NLAT_DEV, lambda i: i ^ 2)
    v = v + swap(v, "lat", NLAT_DEV, lambda i: i ^ 4)
    y = [swap(v, "lon", NLON_DEV, lambda i, by=by: i // 4 * 4 + (i + by) % 4) for by in (1, 2, 3)]
    v = v + (y[0] + y[2]) + y[1]
    v = v + swap(v, "lon", NLON_DEV, lambda i: i ^ 4)
    v = v + swap(v, "lon", NLON_DEV, lambda i: i ^ 8)
    corr = jnp.broadcast_to((v[0] * (1.0 / TOTAL_AREA))[:, None], (C, C))

    lls, rrs = (lax.ppermute(x, both, some(d, POLAR)) for x, d in ((ls, 1), (rs, -1)))
    llm, rrm = (lax.ppermute(x, both, some(d, POLAR)) for x, d in ((lm, 1), (rm, -1)))

    def next_rows(e):
        return jnp.where(lat == 1, e[:B], e[S - B :])

    llb = lax.ppermute(next_rows(ls), both, some(1, NEXT))
    rrb = lax.ppermute(next_rows(rs), both, some(-1, NEXT))

    def border(e, b):
        of_polar = jnp.where(lat == 0, e[S - R :], e[:R])
        return jnp.where(
            (lat == 0) | (lat == NLAT_DEV - 1), of_polar, jnp.where(lat == 1, b[:R], b[B - R :])
        )

    pairs = [(a * NLON_DEV + i, b * NLON_DEV + i) for a, b in ((0, 1), (1, 0), (6, 7), (7, 6)) for i in range(NLON_DEV)]
    halo = lax.ppermute(jnp.concatenate([border(lls, llb), border(rrs, rrb)], axis=0), both, pairs)
    pole = [jnp.where(lat == 0, x[:E], x[S - E :]) for x in (lls, rrs)]
    l3 = lax.ppermute(pole[0], both, some(1, POLAR))
    r3 = lax.ppermute(pole[1], both, some(-1, POLAR))

    partial, wv = inner_call(near_idx, w, (q, ls, lm, rs, rm, up1, dn1))
    fixed = outer_call(
        far_idx, pltpu.with_memory_space_constraint(wv, pltpu.VMEM), corr, (lls, llm, llb, rrs, rrm, rrb, halo, l3, r3),
        pltpu.with_memory_space_constraint(partial, pltpu.VMEM),
    )
    return v[1, 0], fixed


def solution(mesh):
    placed = (
        P("lat", "lon", None, None),
        P("lat", "lon", None, None, None),
        P("lat", "lon", None),
        P("lat", "lon", None),
        P("lat", "lon"),
    )
    return jax.shard_map(
        local, mesh=mesh, in_specs=placed, out_specs=P("lat", "lon", None, None), check_vma=False
    )
```

profile of v0, /device:TPU:0, one launch (start us, length us, event | category | flops | bytes accessed | tf_op | source)
XLA Modules:
  0.0 158.7 jit_solution(5655358328778297697)
XLA Ops:
  0.0 1.7 %fusion.48 = (bf16[16,32,4,128]{3,2,1,0:T(4,128)(2,1)S(1)}, bf16[16,32,4,128]{3,2,1,0:T(4,128)(2,1)S(1)}) fusion(bf16[64,32,4,128]{3,2,1,0:T(4,128)(2,1)} %bitcast.167), kind=kLoop, calls=%fused_computation.115 | loop fusion | bytes 2097152 | tf_op jit(solution)/shard_map/slice | solution.py:482
  1.7 1.1 pad_maximum_fusion.5
  2.7 6.6 %collective-permute-start.21 = (bf16[32,128,128]{2,1,0:T(8,128)(2,1)}, bf16[32,128,128]{2,1,0:T(8,128)(2,1)S(1)}, u32[]{:S(2)}, u32[]{:S(2)}) collective-permute-start(bf16[32,128,128]{2,1,0:T(8,128)(2,1)} %pad_maximum_fusion.5), channel_id=1, source_target_pairs={{0,15},{1,0},{2,1},{3,2},{4,3},{5,4},{6,5},{7,6},{8,7},{9,8},{10,9... | collective-permute-start | bytes 3145736 | tf_op jit(solution)/shard_map/ppermute | solution.py:483
  9.4 7.2 %sums.1 = (f32[72,128]{1,0:T(8,128)S(1)}, f32[72,128]{1,0:T(8,128)S(1)}, f32[72,128]{1,0:T(8,128)S(1)}, f32[72,128]{1,0:T(8,128)S(1)}, f32[72,128]{1,0:T(8,128)S...) custom-call(s32[8,64]{1,0:T(8,128)S(1)} %get-tuple-element.118.idx_ref, f32[64]{0:T(128)S(1)} %add_cosine_fusion.1.area_ref, ...), custom_call_target="tpu_custom_call" | custom-call | flops 20000000 | bytes 17825792 | tf_op jit(solution)/shard_map/sums/pallas_call | solution.py:310
  16.7 2.5 %collective-permute-start.19 = (f32[72,128]{1,0:T(8,128)S(1)}, f32[72,128]{1,0:T(8,128)S(1)}, u32[]{:S(2)}, u32[]{:S(2)}) collective-permute-start(f32[72,128]{1,0:T(8,128)S(1)} %get-tuple-element.59), channel_id=1, source_target_pairs={{0,13},{1,14},{2,15},{3,0},{4,1},{5,2},{6,3},{7,4},{8,5},{9,6},{10... | collective-permute-start | bytes 110600 | tf_op jit(solution)/shard_map/ppermute | solution.py:491
  19.2 4.6 %collective-permute-start.18 = (f32[72,128]{1,0:T(8,128)S(1)}, f32[72,128]{1,0:T(8,128)S(1)}, u32[]{:S(2)}, u32[]{:S(2)}) collective-permute-start(f32[72,128]{1,0:T(8,128)S(1)} %get-tuple-element.58), channel_id=1, source_target_pairs={{0,3},{1,4},{2,5},{3,6},{4,7},{5,8},{6,9},{7,10},{8,11},{9,12},{10... | collective-permute-start | bytes 110600 | tf_op jit(solution)/shard_map/ppermute | solution.py:491
  23.8 3.2 %collective-permute-start.17 = (f32[72,128]{1,0:T(8,128)S(1)}, f32[72,128]{1,0:T(8,128)S(1)}, u32[]{:S(2)}, u32[]{:S(2)}) collective-permute-start(f32[72,128]{1,0:T(8,128)S(1)} %get-tuple-element.57), channel_id=1, source_target_pairs={{0,14},{1,15},{2,0},{3,1},{4,2},{5,3},{6,4},{7,5},{8,6},{9,7},{10,... | collective-permute-start | bytes 110600 | tf_op jit(solution)/shard_map/ppermute | solution.py:489
  27.0 7.4 %collective-permute-done.19 = f32[72,128]{1,0:T(8,128)S(1)} collective-permute-done((f32[72,128]{1,0:T(8,128)S(1)}, f32[72,128]{1,0:T(8,128)S(1)}, u32[]{:S(2)}, u32[]{:S(2)}) %collective-permute-start.19) | collective-permute-done | bytes 36896 | tf_op jit(solution)/shard_map/ppermute | solution.py:491
  34.4 4.6 %collective-permute-start.15 = (f32[72,128]{1,0:T(8,128)S(1)}, f32[72,128]{1,0:T(8,128)S(1)}, u32[]{:S(2)}, u32[]{:S(2)}) collective-permute-start(f32[72,128]{1,0:T(8,128)S(1)} %get-tuple-element.55), channel_id=1, source_target_pairs={{0,15},{1,0},{2,1},{3,2},{4,3},{5,4},{6,5},{7,6},{8,7},{9,8},{10,9... | collective-permute-start | bytes 110600 | tf_op jit(solution)/shard_map/ppermute | solution.py:489
  39.0 0.6 convert_reduce_fusion.1
  39.7 1.4 slice.251
  41.1 1.3 collective-permute-done.16
  42.4 4.3 %collective-permute-done.14 = f32[72,128]{1,0:T(8,128)S(1)} collective-permute-done((f32[72,128]{1,0:T(8,128)S(1)}, f32[72,128]{1,0:T(8,128)S(1)}, u32[]{:S(2)}, u32[]{:S(2)}) %collective-permute-start.14) | collective-permute-done | bytes 36896 | tf_op jit(solution)/shard_map/ppermute | solution.py:489
  47.4 0.8 pad_maximum_fusion.7
  48.2 1.3 collective-permute-start.23
  49.5 0.8 pad_maximum_fusion.6
  50.3 3.8 %collective-permute-start.22 = (bf16[12,128,128]{2,1,0:T(8,128)(2,1)}, bf16[12,128,128]{2,1,0:T(8,128)(2,1)}, u32[]{:S(2)}, u32[]{:S(2)}) collective-permute-start(bf16[12,128,128]{2,1,0:T(8,128)(2,1)} %pad_maximum_fusion.6), channel_id=1, source_target_pairs={{0,16},{16,32},{32,48},{48,64},{64,80},{80,96},{96,112},{1,17},{17... | collective-permute-start | bytes 1179656 | tf_op jit(solution)/shard_map/ppermute | solution.py:494
  54.1 1.8 %multiply_reduce_fusion.1 = f32[32,4]{1,0:T(8,128)} fusion(f32[64,128]{1,0:T(8,128)S(1)} %slice_subtract_fusion, bf16[64,128,32,4]{1,3,2,0:T(4,128)(2,1)S(1)} %copy-done.1), kind=kLoop, calls=%fused_computation.39 | loop fusion | flops 3145600 | bytes 2130432 | tf_op jit(solution)/shard_map/reduce_sum | solution.py:498
  55.9 1.4 reduce_sum.72
  57.2 0.8 fusion.51
  58.2 1.0 multiply_reduce_fusion.3
  59.2 0.6 bitcast_subtract_fusion.1
  59.9 0.6 stack.4
  60.7 1.0 collective-permute-start.33
  61.8 0.6 pad_add_fusion
  62.4 2.6 %collective-permute-start.25 = (f32[2,128]{1,0:T(2,128)S(1)}, f32[2,128]{1,0:T(2,128)S(1)}, u32[]{:S(2)}, u32[]{:S(2)}) collective-permute-start(f32[2,128]{1,0:T(2,128)S(1)} %pad_add_fusion), channel_id=1, source_target_pairs={{0,32},{16,48},{32,0},{48,16},{64,96},{80,112},{96,64},{112,80},{1... | collective-permute-start | bytes 3080 | tf_op jit(solution)/shard_map/ppermute | solution.py:463
  65.0 2.9 %collective-permute-start.37 = (bf16[32,128,128]{2,1,0:T(8,128)(2,1)S(1)}, bf16[32,128,128]{2,1,0:T(8,128)(2,1)S(1)}, u32[]{:S(2)}, u32[]{:S(2)}) collective-permute-start(bf16[32,128,128]{2,1,0:T(8,128)(2,1)S(1)} %collective-permute-done.21.rs), channel_id=1, source_target_pairs={{0,15},{1,0},{2,1},{3,2},{4,3},{5,4},{6,5},{7,6},{8,7},{9,8},{10,9... | collective-permute-start | bytes 3145736 | tf_op jit(solution)/shard_map/ppermute | solution.py:515
  67.9 0.6 fusion.52
  68.7 5.1 %collective-permute-done.26 = f32[2,128]{1,0:T(2,128)S(1)} collective-permute-done((f32[2,128]{1,0:T(2,128)S(1)}, f32[2,128]{1,0:T(2,128)S(1)}, u32[]{:S(2)}, u32[]{:S(2)}) %collective-permute-start.26) | collective-permute-done | bytes 1056 | tf_op jit(solution)/shard_map/ppermute | solution.py:463
  73.7 2.0 %collective-permute-start.29 = (f32[2,128]{1,0:T(2,128)S(1)}, f32[2,128]{1,0:T(2,128)S(1)}, u32[]{:S(2)}, u32[]{:S(2)}) collective-permute-start(f32[2,128]{1,0:T(2,128)S(1)} %add.264), channel_id=1, source_target_pairs={{0,2},{1,3},{2,0},{3,1},{4,6},{5,7},{6,4},{7,5},{8,10},{9,11},{10,... | collective-permute-start | bytes 3080 | tf_op jit(solution)/shard_map/ppermute | solution.py:463
  75.7 3.1 %collective-permute-done.29 = f32[2,128]{1,0:T(2,128)S(1)} collective-permute-done((f32[2,128]{1,0:T(2,128)S(1)}, f32[2,128]{1,0:T(2,128)S(1)}, u32[]{:S(2)}, u32[]{:S(2)}) %collective-permute-start.29) | collective-permute-done | bytes 1056 | tf_op jit(solution)/shard_map/ppermute | solution.py:463
  78.8 23.6 %collective-permute-start.34 = (bf16[32,128,128]{2,1,0:T(8,128)(2,1)S(1)}, bf16[32,128,128]{2,1,0:T(8,128)(2,1)S(1)}, u32[]{:S(2)}, u32[]{:S(2)}) collective-permute-start(bf16[32,128,128]{2,1,0:T(8,128)(2,1)S(1)} %collective-permute-done.20.ls), channel_id=1, source_target_pairs={{0,1},{1,2},{2,3},{3,4},{4,5},{5,6},{6,7},{7,8},{8,9},{9,10},{10,1... | collective-permute-start | bytes 3145736 | tf_op jit(solution)/shard_map/ppermute | solution.py:515
  102.4 3.2 %collective-permute-start.28 = (f32[2,128]{1,0:T(2,128)S(1)}, f32[2,128]{1,0:T(2,128)S(1)}, u32[]{:S(2)}, u32[]{:S(2)}) collective-permute-start(f32[2,128]{1,0:T(2,128)S(1)} %add.264), channel_id=1, source_target_pairs={{0,3},{1,0},{2,1},{3,2},{4,7},{5,4},{6,5},{7,6},{8,11},{9,8},{10,9... | collective-permute-start | bytes 3080 | tf_op jit(solution)/shard_map/ppermute | solution.py:463
  105.7 1.2 collective-permute-done.28
  107.0 0.7 collective-permute-start.39
  107.8 3.5 %collective-permute-done.30 = f32[2,128]{1,0:T(2,128)S(1)} collective-permute-done((f32[2,128]{1,0:T(2,128)S(1)}, f32[2,128]{1,0:T(2,128)S(1)}, u32[]{:S(2)}, u32[]{:S(2)}) %collective-permute-start.30) | collective-permute-done | bytes 1056 | tf_op jit(solution)/shard_map/ppermute | solution.py:463
  111.3 0.7 collective-permute-start.36
  112.0 3.4 %collective-permute-start.31 = (f32[2,128]{1,0:T(2,128)S(1)}, f32[2,128]{1,0:T(2,128)S(1)}, u32[]{:S(2)}, u32[]{:S(2)}) collective-permute-start(f32[2,128]{1,0:T(2,128)S(1)} %add.268), channel_id=1, source_target_pairs={{0,8},{1,9},{2,10},{3,11},{4,12},{5,13},{6,14},{7,15},{8,0},{9,1},... | collective-permute-start | bytes 3080 | tf_op jit(solution)/shard_map/ppermute | solution.py:463
  115.5 9.4 %inner.1 = (f32[64,128,128]{2,1,0:T(8,128)S(1)}, bf16[64,8,128,128]{3,2,1,0:T(8,128)(2,1)S(1)}) custom-call(s32[8,64]{1,0:T(8,128)S(1)} %get-tuple-element.116.idx_ref, bf16[64,8,128,128]{3,2,1,0:T(8,128)(2,1)} %bitcast.163, bf16[64,128,128]{2,1,0:T(8,128)(2,1)S(1)} %bitcast.170, bf16[32,128,128]{2,1,0:T(8,128)(2,1)S(1)} %collective-permute-done.20.ls, ...), custom_call_target="tpu_custom_call" | custom-call | flops 2147483648 | bytes 17825792 | tf_op jit(solution)/shard_map/inner/pallas_call | solution.py:363
  125.5 1.9 %collective-permute-start.35 = (bf16[32,128,128]{2,1,0:T(8,128)(2,1)S(1)}, bf16[32,128,128]{2,1,0:T(8,128)(2,1)S(1)}, u32[]{:S(2)}, u32[]{:S(2)}) collective-permute-start(bf16[32,128,128]{2,1,0:T(8,128)(2,1)S(1)} %collective-permute-done.32.lm), channel_id=1, source_target_pairs={{0,1},{1,2},{2,3},{3,4},{4,5},{5,6},{6,7},{7,8},{8,9},{9,10},{10,1... | collective-permute-start | bytes 3145736 | tf_op jit(solution)/shard_map/ppermute | solution.py:516
  127.4 7.2 %collective-permute-start.38 = (bf16[32,128,128]{2,1,0:T(8,128)(2,1)S(1)}, bf16[32,128,128]{2,1,0:T(8,128)(2,1)S(1)}, u32[]{:S(2)}, u32[]{:S(2)}) collective-permute-start(bf16[32,128,128]{2,1,0:T(8,128)(2,1)S(1)} %collective-permute-done.33.rm), channel_id=1, source_target_pairs={{0,15},{1,0},{2,1},{3,2},{4,3},{5,4},{6,5},{7,6},{8,7},{9,8},{10,9... | collective-permute-start | bytes 3145736 | tf_op jit(solution)/shard_map/ppermute | solution.py:516
  134.8 1.9 %collective-permute-start.40 = (bf16[8,128,128]{2,1,0:T(8,128)(2,1)S(1)}, bf16[8,128,128]{2,1,0:T(8,128)(2,1)S(1)}, u32[]{:S(2)}, u32[]{:S(2)}) collective-permute-start(bf16[8,128,128]{2,1,0:T(8,128)(2,1)S(1)} %pad_maximum_fusion.8), channel_id=1, source_target_pairs={{0,16},{1,17},{2,18},{3,19},{4,20},{5,21},{6,22},{7,23},{8,24},{9,... | collective-permute-start | bytes 786440 | tf_op jit(solution)/shard_map/ppermute | solution.py:531
  136.7 1.9 %collective-permute-start.41 = (bf16[5,128,128]{2,1,0:T(8,128)(2,1)S(1)}, bf16[5,128,128]{2,1,0:T(8,128)(2,1)S(1)}, u32[]{:S(2)}, u32[]{:S(2)}) collective-permute-start(bf16[5,128,128]{2,1,0:T(8,128)(2,1)S(1)} %slice_select_fusion.5), channel_id=1, source_target_pairs={{0,1},{1,2},{2,3},{3,4},{4,5},{5,6},{6,7},{7,8},{8,9},{9,10},{10,1... | collective-permute-start | bytes 491528 | tf_op jit(solution)/shard_map/ppermute | solution.py:533
  138.7 7.4 %collective-permute-start.42 = (bf16[5,128,128]{2,1,0:T(8,128)(2,1)S(1)}, bf16[5,128,128]{2,1,0:T(8,128)(2,1)S(1)}, u32[]{:S(2)}, u32[]{:S(2)}) collective-permute-start(bf16[5,128,128]{2,1,0:T(8,128)(2,1)S(1)} %slice_select_fusion.4), channel_id=1, source_target_pairs={{0,15},{1,0},{2,1},{3,2},{4,3},{5,4},{6,5},{7,6},{8,7},{9,8},{10,9... | collective-permute-start | bytes 491528 | tf_op jit(solution)/shard_map/ppermute | solution.py:534
  146.1 0.8 collective-permute-done.38.rm
  147.3 1.5 collective-permute-done.42.r3
  148.8 9.0 %outer.1 = f32[64,128,128]{2,1,0:T(8,128)} custom-call(s32[8,64]{1,0:T(8,128)S(1)} %get-tuple-element.117.idx_ref, bf16[64,8,128,128]{3,2,1,0:T(8,128)(2,1)S(1)} %get-tuple-element.60.w_ref, f32[128,128]{1,0:T(8,128)S(1)} %broadcast_in_dim.40.corr_ref, bf16[32,128,128]{2,1,0:T(8,128)(2,1)S(1)} %collective-permute-done.34.ls, ...), custom_call_target="tpu_custom_call" | custom-call | flops 2147483648 | bytes 4194304 | tf_op jit(solution)/shard_map/outer/pallas_call | solution.py:416
  157.8 0.7 while.9
  (62 shorter events, 2.7 us)
Async XLA Ops:
  0.0 9.3 %copy-start.4 = (s32[64,1,8]{0,2,1:T(8,128)S(1)}, s32[64,1,8]{0,2,1:T(8,128)}, u32[]{:S(2)}) copy-start(s32[64,1,8]{0,2,1:T(8,128)} %param.9) | copy-start | bytes 6148
  0.0 9.3 %copy-start.8 = (s32[64,1]{0,1:T(1,128)S(1)}, s32[64,1]{0,1:T(1,128)}, u32[]{:S(2)}) copy-start(s32[64,1]{0,1:T(1,128)} %param.11) | copy-start | bytes 772
  0.0 9.3 %copy-start.6 = (s32[64,1,8]{0,2,1:T(8,128)S(1)}, s32[64,1,8]{0,2,1:T(8,128)}, u32[]{:S(2)}) copy-start(s32[64,1,8]{0,2,1:T(8,128)} %param.10) | copy-start | bytes 6148
  2.7 44.6 %collective-permute-start.21 = (bf16[32,128,128]{2,1,0:T(8,128)(2,1)}, bf16[32,128,128]{2,1,0:T(8,128)(2,1)S(1)}, u32[]{:S(2)}, u32[]{:S(2)}) collective-permute-start(bf16[32,128,128]{2,1,0:T(8,128)(2,1)} %pad_maximum_fusion.5), channel_id=1, source_target_pairs={{0,15},{1,0},{2,1},{3,2},{4,3},{5,4},{6,5},{7,6},{8,7},{9,8},{10,9... | collective-permute-start | bytes 3145736 | tf_op jit(solution)/shard_map/ppermute | solution.py:483
  9.3 38.0 %collective-permute-start.20 = (bf16[32,128,128]{2,1,0:T(8,128)(2,1)}, bf16[32,128,128]{2,1,0:T(8,128)(2,1)S(1)}, u32[]{:S(2)}, u32[]{:S(2)}) collective-permute-start(bf16[32,128,128]{2,1,0:T(8,128)(2,1)} %pad_maximum_fusion.5), channel_id=1, source_target_pairs={{0,1},{1,2},{2,3},{3,4},{4,5},{5,6},{6,7},{7,8},{8,9},{9,10},{10,1... | collective-permute-start | bytes 3145736 | tf_op jit(solution)/shard_map/ppermute | solution.py:483
  9.4 17.5 %copy-start.1 = (bf16[64,128,32,4]{1,3,2,0:T(4,128)(2,1)S(1)}, bf16[64,128,32,4]{1,3,2,0:T(4,128)(2,1)}, u32[]{:S(2)}) copy-start(bf16[64,128,32,4]{1,3,2,0:T(4,128)(2,1)} %param.7) | copy-start | bytes 6291460
  16.7 17.7 %collective-permute-start.19 = (f32[72,128]{1,0:T(8,128)S(1)}, f32[72,128]{1,0:T(8,128)S(1)}, u32[]{:S(2)}, u32[]{:S(2)}) collective-permute-start(f32[72,128]{1,0:T(8,128)S(1)} %get-tuple-element.59), channel_id=1, source_target_pairs={{0,13},{1,14},{2,15},{3,0},{4,1},{5,2},{6,3},{7,4},{8,5},{9,6},{10... | collective-permute-start | bytes 110600 | tf_op jit(solution)/shard_map/ppermute | solution.py:491
  19.2 15.2 %collective-permute-start.18 = (f32[72,128]{1,0:T(8,128)S(1)}, f32[72,128]{1,0:T(8,128)S(1)}, u32[]{:S(2)}, u32[]{:S(2)}) collective-permute-start(f32[72,128]{1,0:T(8,128)S(1)} %get-tuple-element.58), channel_id=1, source_target_pairs={{0,3},{1,4},{2,5},{3,6},{4,7},{5,8},{6,9},{7,10},{8,11},{9,12},{10... | collective-permute-start | bytes 110600 | tf_op jit(solution)/shard_map/ppermute | solution.py:491
  23.8 15.3 %collective-permute-start.17 = (f32[72,128]{1,0:T(8,128)S(1)}, f32[72,128]{1,0:T(8,128)S(1)}, u32[]{:S(2)}, u32[]{:S(2)}) collective-permute-start(f32[72,128]{1,0:T(8,128)S(1)} %get-tuple-element.57), channel_id=1, source_target_pairs={{0,14},{1,15},{2,0},{3,1},{4,2},{5,3},{6,4},{7,5},{8,6},{9,7},{10,... | collective-permute-start | bytes 110600 | tf_op jit(solution)/shard_map/ppermute | solution.py:489
  34.4 8.0 %collective-permute-start.16 = (f32[72,128]{1,0:T(8,128)S(1)}, f32[72,128]{1,0:T(8,128)S(1)}, u32[]{:S(2)}, u32[]{:S(2)}) collective-permute-start(f32[72,128]{1,0:T(8,128)S(1)} %get-tuple-element.56), channel_id=1, source_target_pairs={{0,2},{1,3},{2,4},{3,5},{4,6},{5,7},{6,8},{7,9},{8,10},{9,11},{10,... | collective-permute-start | bytes 110600 | tf_op jit(solution)/shard_map/ppermute | solution.py:489
  34.4 8.0 %collective-permute-start.15 = (f32[72,128]{1,0:T(8,128)S(1)}, f32[72,128]{1,0:T(8,128)S(1)}, u32[]{:S(2)}, u32[]{:S(2)}) collective-permute-start(f32[72,128]{1,0:T(8,128)S(1)} %get-tuple-element.55), channel_id=1, source_target_pairs={{0,15},{1,0},{2,1},{3,2},{4,3},{5,4},{6,5},{7,6},{8,7},{9,8},{10,9... | collective-permute-start | bytes 110600 | tf_op jit(solution)/shard_map/ppermute | solution.py:489
  39.0 7.7 %collective-permute-start.14 = (f32[72,128]{1,0:T(8,128)S(1)}, f32[72,128]{1,0:T(8,128)S(1)}, u32[]{:S(2)}, u32[]{:S(2)}) collective-permute-start(f32[72,128]{1,0:T(8,128)S(1)} %get-tuple-element.54), channel_id=1, source_target_pairs={{0,1},{1,2},{2,3},{3,4},{4,5},{5,6},{6,7},{7,8},{8,9},{9,10},{10,1... | collective-permute-start | bytes 110600 | tf_op jit(solution)/shard_map/ppermute | solution.py:489
  42.3 65.3 %collective-permute-start.32 = (bf16[32,128,128]{2,1,0:T(8,128)(2,1)}, bf16[32,128,128]{2,1,0:T(8,128)(2,1)S(1)}, u32[]{:S(2)}, u32[]{:S(2)}) collective-permute-start(bf16[32,128,128]{2,1,0:T(8,128)(2,1)} %bitcast.35), channel_id=1, source_target_pairs={{0,1},{1,2},{2,3},{3,4},{4,5},{5,6},{6,7},{7,8},{8,9},{9,10},{10,1... | collective-permute-start | bytes 3145736 | tf_op jit(solution)/shard_map/ppermute | solution.py:493
  46.7 0.6 copy-start.7
  48.2 9.9 %collective-permute-start.23 = (bf16[12,128,128]{2,1,0:T(8,128)(2,1)}, bf16[12,128,128]{2,1,0:T(8,128)(2,1)S(1)}, u32[]{:S(2)}, u32[]{:S(2)}) collective-permute-start(bf16[12,128,128]{2,1,0:T(8,128)(2,1)} %pad_maximum_fusion.7), channel_id=1, source_target_pairs={{16,0},{32,16},{48,32},{64,48},{80,64},{96,80},{112,96},{17,1},{33... | collective-permute-start | bytes 1179656 | tf_op jit(solution)/shard_map/ppermute | solution.py:495
  50.3 7.9 %collective-permute-start.22 = (bf16[12,128,128]{2,1,0:T(8,128)(2,1)}, bf16[12,128,128]{2,1,0:T(8,128)(2,1)}, u32[]{:S(2)}, u32[]{:S(2)}) collective-permute-start(bf16[12,128,128]{2,1,0:T(8,128)(2,1)} %pad_maximum_fusion.6), channel_id=1, source_target_pairs={{0,16},{16,32},{32,48},{48,64},{64,80},{80,96},{96,112},{1,17},{17... | collective-permute-start | bytes 1179656 | tf_op jit(solution)/shard_map/ppermute | solution.py:494
  57.2 58.2 %copy-start.2 = (bf16[64,128,32,4]{1,3,2,0:T(4,128)(2,1)S(1)}, bf16[64,128,32,4]{1,3,2,0:T(4,128)(2,1)}, u32[]{:S(2)}) copy-start(bf16[64,128,32,4]{1,3,2,0:T(4,128)(2,1)} %param.7) | copy-start | bytes 6291460
  60.5 1.2 collective-permute-start.24
  60.7 51.3 %collective-permute-start.33 = (bf16[32,128,128]{2,1,0:T(8,128)(2,1)}, bf16[32,128,128]{2,1,0:T(8,128)(2,1)S(1)}, u32[]{:S(2)}, u32[]{:S(2)}) collective-permute-start(bf16[32,128,128]{2,1,0:T(8,128)(2,1)} %bitcast.35), channel_id=1, source_target_pairs={{0,15},{1,0},{2,1},{3,2},{4,3},{5,4},{6,5},{7,6},{8,7},{9,8},{10,9... | collective-permute-start | bytes 3145736 | tf_op jit(solution)/shard_map/ppermute | solution.py:493
  62.4 5.5 %collective-permute-start.25 = (f32[2,128]{1,0:T(2,128)S(1)}, f32[2,128]{1,0:T(2,128)S(1)}, u32[]{:S(2)}, u32[]{:S(2)}) collective-permute-start(f32[2,128]{1,0:T(2,128)S(1)} %pad_add_fusion), channel_id=1, source_target_pairs={{0,32},{16,48},{32,0},{48,16},{64,96},{80,112},{96,64},{112,80},{1... | collective-permute-start | bytes 3080 | tf_op jit(solution)/shard_map/ppermute | solution.py:463
  65.0 69.6 %collective-permute-start.37 = (bf16[32,128,128]{2,1,0:T(8,128)(2,1)S(1)}, bf16[32,128,128]{2,1,0:T(8,128)(2,1)S(1)}, u32[]{:S(2)}, u32[]{:S(2)}) collective-permute-start(bf16[32,128,128]{2,1,0:T(8,128)(2,1)S(1)} %collective-permute-done.21.rs), channel_id=1, source_target_pairs={{0,15},{1,0},{2,1},{3,2},{4,3},{5,4},{6,5},{7,6},{8,7},{9,8},{10,9... | collective-permute-start | bytes 3145736 | tf_op jit(solution)/shard_map/ppermute | solution.py:515
  68.6 5.2 %collective-permute-start.26 = (f32[2,128]{1,0:T(2,128)S(1)}, f32[2,128]{1,0:T(2,128)S(1)}, u32[]{:S(2)}, u32[]{:S(2)}) collective-permute-start(f32[2,128]{1,0:T(2,128)S(1)} %fusion.52), channel_id=1, source_target_pairs={{0,64},{16,80},{32,96},{48,112},{64,0},{80,16},{96,32},{112,48},{1... | collective-permute-start | bytes 3080 | tf_op jit(solution)/shard_map/ppermute | solution.py:463
  73.7 5.1 %collective-permute-start.29 = (f32[2,128]{1,0:T(2,128)S(1)}, f32[2,128]{1,0:T(2,128)S(1)}, u32[]{:S(2)}, u32[]{:S(2)}) collective-permute-start(f32[2,128]{1,0:T(2,128)S(1)} %add.264), channel_id=1, source_target_pairs={{0,2},{1,3},{2,0},{3,1},{4,6},{5,7},{6,4},{7,5},{8,10},{9,11},{10,... | collective-permute-start | bytes 3080 | tf_op jit(solution)/shard_map/ppermute | solution.py:463
  75.7 26.7 %collective-permute-start.27 = (f32[2,128]{1,0:T(2,128)S(1)}, f32[2,128]{1,0:T(2,128)S(1)}, u32[]{:S(2)}, u32[]{:S(2)}) collective-permute-start(f32[2,128]{1,0:T(2,128)S(1)} %add.264), channel_id=1, source_target_pairs={{0,1},{1,2},{2,3},{3,0},{4,5},{5,6},{6,7},{7,4},{8,9},{9,10},{10,1... | collective-permute-start | bytes 3080 | tf_op jit(solution)/shard_map/ppermute | solution.py:463
  78.8 55.9 %collective-permute-start.34 = (bf16[32,128,128]{2,1,0:T(8,128)(2,1)S(1)}, bf16[32,128,128]{2,1,0:T(8,128)(2,1)S(1)}, u32[]{:S(2)}, u32[]{:S(2)}) collective-permute-start(bf16[32,128,128]{2,1,0:T(8,128)(2,1)S(1)} %collective-permute-done.20.ls), channel_id=1, source_target_pairs={{0,1},{1,2},{2,3},{3,4},{4,5},{5,6},{6,7},{7,8},{8,9},{9,10},{10,1... | collective-permute-start | bytes 3145736 | tf_op jit(solution)/shard_map/ppermute | solution.py:515
  102.4 4.5 %collective-permute-start.28 = (f32[2,128]{1,0:T(2,128)S(1)}, f32[2,128]{1,0:T(2,128)S(1)}, u32[]{:S(2)}, u32[]{:S(2)}) collective-permute-start(f32[2,128]{1,0:T(2,128)S(1)} %add.264), channel_id=1, source_target_pairs={{0,3},{1,0},{2,1},{3,2},{4,7},{5,4},{6,5},{7,6},{8,11},{9,8},{10,9... | collective-permute-start | bytes 3080 | tf_op jit(solution)/shard_map/ppermute | solution.py:463
  107.0 20.4 %collective-permute-start.39 = (bf16[16,128,128]{2,1,0:T(8,128)(2,1)S(1)}, bf16[16,128,128]{2,1,0:T(8,128)(2,1)S(1)}, u32[]{:S(2)}, u32[]{:S(2)}) collective-permute-start(bf16[16,128,128]{2,1,0:T(8,128)(2,1)S(1)} %slice_select_fusion.2), channel_id=1, source_target_pairs={{16,31},{17,16},{18,17},{19,18},{20,19},{21,20},{22,21},{23,22},{2... | collective-permute-start | bytes 1572872 | tf_op jit(solution)/shard_map/ppermute | solution.py:522
  107.7 3.7 %collective-permute-start.30 = (f32[2,128]{1,0:T(2,128)S(1)}, f32[2,128]{1,0:T(2,128)S(1)}, u32[]{:S(2)}, u32[]{:S(2)}) collective-permute-start(f32[2,128]{1,0:T(2,128)S(1)} %add_add_fusion.1), channel_id=1, source_target_pairs={{0,4},{1,5},{2,6},{3,7},{4,0},{5,1},{6,2},{7,3},{8,12},{9,13},{10,... | collective-permute-start | bytes 3080 | tf_op jit(solution)/shard_map/ppermute | solution.py:463
  111.3 23.4 %collective-permute-start.36 = (bf16[16,128,128]{2,1,0:T(8,128)(2,1)S(1)}, bf16[16,128,128]{2,1,0:T(8,128)(2,1)S(1)}, u32[]{:S(2)}, u32[]{:S(2)}) collective-permute-start(bf16[16,128,128]{2,1,0:T(8,128)(2,1)S(1)} %slice_select_fusion.3), channel_id=1, source_target_pairs={{16,17},{17,18},{18,19},{19,20},{20,21},{21,22},{22,23},{23,24},{2... | collective-permute-start | bytes 1572872 | tf_op jit(solution)/shard_map/ppermute | solution.py:521
  112.0 12.8 %collective-permute-start.31 = (f32[2,128]{1,0:T(2,128)S(1)}, f32[2,128]{1,0:T(2,128)S(1)}, u32[]{:S(2)}, u32[]{:S(2)}) collective-permute-start(f32[2,128]{1,0:T(2,128)S(1)} %add.268), channel_id=1, source_target_pairs={{0,8},{1,9},{2,10},{3,11},{4,12},{5,13},{6,14},{7,15},{8,0},{9,1},... | collective-permute-start | bytes 3080 | tf_op jit(solution)/shard_map/ppermute | solution.py:463
  125.5 20.7 %collective-permute-start.35 = (bf16[32,128,128]{2,1,0:T(8,128)(2,1)S(1)}, bf16[32,128,128]{2,1,0:T(8,128)(2,1)S(1)}, u32[]{:S(2)}, u32[]{:S(2)}) collective-permute-start(bf16[32,128,128]{2,1,0:T(8,128)(2,1)S(1)} %collective-permute-done.32.lm), channel_id=1, source_target_pairs={{0,1},{1,2},{2,3},{3,4},{4,5},{5,6},{6,7},{7,8},{8,9},{9,10},{10,1... | collective-permute-start | bytes 3145736 | tf_op jit(solution)/shard_map/ppermute | solution.py:516
  127.4 19.5 %collective-permute-start.38 = (bf16[32,128,128]{2,1,0:T(8,128)(2,1)S(1)}, bf16[32,128,128]{2,1,0:T(8,128)(2,1)S(1)}, u32[]{:S(2)}, u32[]{:S(2)}) collective-permute-start(bf16[32,128,128]{2,1,0:T(8,128)(2,1)S(1)} %collective-permute-done.33.rm), channel_id=1, source_target_pairs={{0,15},{1,0},{2,1},{3,2},{4,3},{5,4},{6,5},{7,6},{8,7},{9,8},{10,9... | collective-permute-start | bytes 3145736 | tf_op jit(solution)/shard_map/ppermute | solution.py:516
  134.8 14.0 %collective-permute-start.40 = (bf16[8,128,128]{2,1,0:T(8,128)(2,1)S(1)}, bf16[8,128,128]{2,1,0:T(8,128)(2,1)S(1)}, u32[]{:S(2)}, u32[]{:S(2)}) collective-permute-start(bf16[8,128,128]{2,1,0:T(8,128)(2,1)S(1)} %pad_maximum_fusion.8), channel_id=1, source_target_pairs={{0,16},{1,17},{2,18},{3,19},{4,20},{5,21},{6,22},{7,23},{8,24},{9,... | collective-permute-start | bytes 786440 | tf_op jit(solution)/shard_map/ppermute | solution.py:531
  136.7 10.5 %collective-permute-start.41 = (bf16[5,128,128]{2,1,0:T(8,128)(2,1)S(1)}, bf16[5,128,128]{2,1,0:T(8,128)(2,1)S(1)}, u32[]{:S(2)}, u32[]{:S(2)}) collective-permute-start(bf16[5,128,128]{2,1,0:T(8,128)(2,1)S(1)} %slice_select_fusion.5), channel_id=1, source_target_pairs={{0,1},{1,2},{2,3},{3,4},{4,5},{5,6},{6,7},{7,8},{8,9},{9,10},{10,1... | collective-permute-start | bytes 491528 | tf_op jit(solution)/shard_map/ppermute | solution.py:533
  138.7 10.1 %collective-permute-start.42 = (bf16[5,128,128]{2,1,0:T(8,128)(2,1)S(1)}, bf16[5,128,128]{2,1,0:T(8,128)(2,1)S(1)}, u32[]{:S(2)}, u32[]{:S(2)}) collective-permute-start(bf16[5,128,128]{2,1,0:T(8,128)(2,1)S(1)} %slice_select_fusion.4), channel_id=1, source_target_pairs={{0,15},{1,0},{2,1},{3,2},{4,3},{5,4},{6,5},{7,6},{8,7},{9,8},{10,9... | collective-permute-start | bytes 491528 | tf_op jit(solution)/shard_map/ppermute | solution.py:534
where the time goes:
time: 159 us
  starting transfers between devices  87.5 us (55%)
  waiting for transfers between devices  28.5 us (18%)
  Pallas kernels  25.6 us (16%)
  other arithmetic  8.59 us (5%)
  local copies, waits for them, and re-layouts  7.24 us (5%)
    ppermute x4, starting transfers between devices, usual(): lax.ppermute(x, both, some(d, POLAR))  35.7 us
    ppermute x8, waiting for transfers between devices, swap(): return lax.ppermute(v, axis, [(i, to(i)) for i in range(size)])  12.9 us
    ppermute x8, starting transfers between devices, swap(): return lax.ppermute(v, axis, [(i, to(i)) for i in range(size)])  11.6 us
    pallas_call x1, Pallas kernels, inner_call(): pl.pallas_call(inner_kernel, in_specs=[pl.BlockSpec(memory_space=pltpu.SM...  9.38 us
    pallas_call x1, Pallas kernels, outer_call(): pl.pallas_call(outer_kernel, in_specs=[pl.BlockSpec(memory_space=pltpu.SM...  9 us
    ppermute x4, starting transfers between devices, usual(): got = got + lax.ppermute(sums[d + 3], 'lon', ring(d))  7.78 us
    ppermute x1, starting transfers between devices, usual(): r3 = lax.ppermute(pole[1], both, some(-1, POLAR))  7.42 us
    ppermute x2, waiting for transfers between devices, usual(): got = got + lax.ppermute(sums[d + 3], both, some(d, POLAR))  7.37 us
  transfers between devices with their start and end apart: 29, of which 10 were waited for; matrix products, arithmetic and copies ran while one was open for 8% of the time, Pallas kernels for 10%

commit v1 on v0

--- a/solution.py
+++ b/solution.py
@@ -325,6 +325,46 @@
     )(idx, area, pltpu.with_memory_space_constraint(weights, pltpu.HBM))
 
 
+def mass_kernel(area_ref, lost_ref, at_ref, c0, c1, c2, c3, c4, s3m, s3p, q, up, dn, l3, r3, out_ref, by):
+    by[...] = -(((c0[...] + c1[...]) + (c2[...] + c3[...])) + c4[...])
+    acc = jnp.zeros((C, C), jnp.float32)
+    for i in range(R):
+        acc = acc + by[i : i + 1] * up[i].astype(jnp.float32)
+        acc = acc + by[R + ROWS + i : R + ROWS + i + 1] * dn[i].astype(jnp.float32)
+    at = at_ref[0]
+    for i in range(E):
+        acc = acc - s3m[pl.ds(at + i, 1)] * l3[i].astype(jnp.float32)
+        acc = acc - s3p[pl.ds(at + i, 1)] * r3[i].astype(jnp.float32)
+
+    def body(r, acc):
+        return acc + (by[pl.ds(r + R, 1)] + area_ref[r]) * q[r].astype(jnp.float32)
+
+    acc = lax.fori_loop(0, ROWS, body, acc, unroll=4)
+    change = lax.dot_general(
+        jnp.ones((8, C), jnp.float32), acc, NT,
+        precision=lax.Precision.HIGHEST, preferred_element_type=jnp.float32,
+    )
+    row = lax.broadcasted_iota(jnp.int32, (8, C), 0)
+    out_ref[...] = jnp.where(row == 0, change, lost_ref[0])
+
+
+def mass_call(area, lost, at, parts):
+    smem = pl.BlockSpec(memory_space=pltpu.SMEM)
+    vmem = pl.BlockSpec(memory_space=pltpu.VMEM)
+    return pl.pallas_call(
+        mass_kernel,
+        in_specs=[smem] * 3 + [vmem] * len(parts),
+        out_specs=vmem,
+        out_shape=jax.ShapeDtypeStruct((8, C), jnp.float32),
+        scratch_shapes=[pltpu.VMEM((PAD, C), jnp.float32)],
+        compiler_params=pltpu.CompilerParams(vmem_limit_bytes=4 << 20),
+        cost_estimate=pl.CostEstimate(
+            flops=4_000_000, bytes_accessed=3 << 20, transcendentals=0
+        ),
+        name="mass",
+    )(area, lost, at, *parts)
+
+
 def inner_kernel(idx_ref, w_hbm, own, ls, lm, rs, rm, up, dn, out_ref, wv, src, sem):
     def copy(c):
         rows = pl.ds(c * WT, WT)
@@ -381,13 +421,13 @@
     )(idx, pltpu.with_memory_space_constraint(weights, pltpu.HBM), *parts)
 
 
-def outer_kernel(idx_ref, w_ref, corr_ref, ls, lm, lb, rs, rm, rb, halo, l3, r3, part_ref, out_hbm, src, acc, sem):
-    for n, (e, m, b) in enumerate(((ls, lm, lb), (rs, rm, rb))):
+def outer_kernel(idx_ref, w_ref, corr_ref, ls, lm, lb, lh, rs, rm, rb, rh, l3, r3, part_ref, out_hbm, src, acc, sem):
+    for n, (e, m, b, h) in enumerate(((ls, lm, lb, lh), (rs, rm, rb, rh))):
         at = n * SIDE
         src[pl.ds(at, S)] = e[...]
         src[pl.ds(at + S, M)] = m[...]
         src[pl.ds(at + S + M, B)] = b[...]
-        src[pl.ds(at + S + M + B, R)] = halo[pl.ds(n * R, R)]
+        src[pl.ds(at + S + M + B, R)] = h[...]
     src[pl.ds(FAR2, E)] = l3[...]
     src[pl.ds(FAR2 + E, E)] = r3[...]
     src[FAR2 + 2 * E] = jnp.zeros((C, C), src.dtype)
@@ -481,35 +521,25 @@
     q = tracers.transpose(0, 2, 3, 1).reshape(ROWS, C, C)
     qs = jnp.concatenate([q[:EDGE], q[ROWS - EDGE :]], axis=0)
     ls, rs = lax.ppermute(qs, "lon", ring(1)), lax.ppermute(qs, "lon", ring(-1))
+    pole = jnp.where(lat == 0, q[:E], q[ROWS - E :])
+    l3 = lax.ppermute(pole, both, some(3, POLAR))
+    r3 = lax.ppermute(pole, both, some(-3, POLAR))
     sums_idx, near_idx, far_idx, lost = tables(source_row, source_block, slot_count, lat, lon)
     area = latitude_area(lat * ROWS, ROWS)
     sums = sums_call(sums_idx, area, w)
-    got = sums[3]
-    for d in (1, -1, 2, -2):
-        got = got + lax.ppermute(sums[d + 3], "lon", ring(d))
-    for d in (3, -3):
-        got = got + lax.ppermute(sums[d + 3], both, some(d, POLAR))
+    got = [lax.ppermute(sums[d + 3], "lon", ring(d)) for d in (1, -1, 2, -2)]
     qm = q[EDGE : ROWS - EDGE]
     lm, rm = lax.ppermute(qm, "lon", ring(1)), lax.ppermute(qm, "lon", ring(-1))
     up1 = lax.ppermute(jnp.concatenate([v[S - R :] for v in (qs, ls, rs)], axis=0), "lat", UP)
     dn1 = lax.ppermute(jnp.concatenate([v[:R] for v in (qs, ls, rs)], axis=0), "lat", DOWN)
-
-    def weigh(field, by):
-        return jnp.sum(field.astype(jnp.float32) * by[:, None, :], axis=(0, 2))
-
-    change = (
-        weigh(q, area[:, None] - got[R : R + ROWS])
-        - weigh(up1[:R], got[:R])
-        - weigh(dn1[:R], got[R + ROWS :])
-    )
-    v = jnp.stack([change, jnp.full((C,), lost)])
-    v = v + swap(v, "lat", NLAT_DEV, lambda i: i ^ 1)
-    v = v + swap(v, "lat", NLAT_DEV, lambda i: i ^ 2)
-    v = v + swap(v, "lat", NLAT_DEV, lambda i: i ^ 4)
+    at = jnp.where(lat == 0, R, R + ROWS - E).reshape(1).astype(jnp.int32)
+    v = mass_call(
+        area, lost.reshape(1), at, (sums[3], *got, sums[0], sums[6], q, up1, dn1, l3, r3)
+    )
+    for axis, size, bit in (("lat", NLAT_DEV, 1), ("lat", NLAT_DEV, 2), ("lat", NLAT_DEV, 4), ("lon", NLON_DEV, 4), ("lon", NLON_DEV, 8)):
+        v = v + swap(v, axis, size, lambda i, bit=bit: i ^ bit)
     y = [swap(v, "lon", NLON_DEV, lambda i, by=by: i // 4 * 4 + (i + by) % 4) for by in (1, 2, 3)]
     v = v + (y[0] + y[2]) + y[1]
-    v = v + swap(v, "lon", NLON_DEV, lambda i: i ^ 4)
-    v = v + swap(v, "lon", NLON_DEV, lambda i: i ^ 8)
     corr = jnp.broadcast_to((v[0] * (1.0 / TOTAL_AREA))[:, None], (C, C))
 
     lls, rrs = (lax.ppermute(x, both, some(d, POLAR)) for x, d in ((ls, 1), (rs, -1)))
@@ -520,22 +550,13 @@
 
     llb = lax.ppermute(next_rows(ls), both, some(1, NEXT))
     rrb = lax.ppermute(next_rows(rs), both, some(-1, NEXT))
-
-    def border(e, b):
-        of_polar = jnp.where(lat == 0, e[S - R :], e[:R])
-        return jnp.where(
-            (lat == 0) | (lat == NLAT_DEV - 1), of_polar, jnp.where(lat == 1, b[:R], b[B - R :])
-        )
-
-    pairs = [(a * NLON_DEV + i, b * NLON_DEV + i) for a, b in ((0, 1), (1, 0), (6, 7), (7, 6)) for i in range(NLON_DEV)]
-    halo = lax.ppermute(jnp.concatenate([border(lls, llb), border(rrs, rrb)], axis=0), both, pairs)
-    pole = [jnp.where(lat == 0, x[:E], x[S - E :]) for x in (lls, rrs)]
-    l3 = lax.ppermute(pole[0], both, some(1, POLAR))
-    r3 = lax.ppermute(pole[1], both, some(-1, POLAR))
+    beyond = jnp.where((lat == 0) | (lat == NLAT_DEV - 2), dn1[R:], up1[R:])
+    llh = lax.ppermute(beyond[:R], both, some(1, POLAR + NEXT))
+    rrh = lax.ppermute(beyond[R:], both, some(-1, POLAR + NEXT))
 
     partial, wv = inner_call(near_idx, w, (q, ls, lm, rs, rm, up1, dn1))
     fixed = outer_call(
-        far_idx, pltpu.with_memory_space_constraint(wv, pltpu.VMEM), corr, (lls, llm, llb, rrs, rrm, rrb, halo, l3, r3),
+        far_idx, pltpu.with_memory_space_constraint(wv, pltpu.VMEM), corr, (lls, llm, llb, llh, rrs, rrm, rrb, rrh, l3, r3),
         pltpu.with_memory_space_constraint(partial, pltpu.VMEM),
     )
     return v[1, 0], fixed

time: 159 us -> 172 us (1.082)
  waiting for transfers between devices: 28.5 us -> 69.5 us
  starting transfers between devices: 87.5 us -> 61.5 us
  Pallas kernels: 25.6 us -> 30.1 us
  other arithmetic: 8.59 us -> 4.43 us
  local copies, waits for them, and re-layouts: 7.24 us -> 4.95 us
    ppermute x9 -> x8, waiting for transfers between devices: 14.8 us -> 46.1 us  [the longest x4 21.9 us: usual(): got = [lax.ppermute(sums[d + 3], 'lon', ring(d)) for d in (1, -1, 2, -2)]]
    ppermute x4, starting transfers between devices: 35.7 us -> 18.3 us  [usual(): lax.ppermute(x, both, some(d, POLAR))]
    ppermute x1, waiting for transfers between devices: 0.01 us -> 7.23 us  [usual(): lax.ppermute(qs, 'lon', ring(-1))]
    ppermute x9 -> x8, starting transfers between devices: 26.1 us -> 19.6 us  [the longest x4 11.6 us: usual(): got = [lax.ppermute(sums[d + 3], 'lon', ring(d)) for d in (1, -1, 2, -2)]]
    ppermute x8, starting transfers between devices: 11.6 us -> 6.74 us  [swap(): return lax.ppermute(v, axis, [(i, to(i)) for i in range(size)])]
    ppermute x1, starting transfers between devices: 1.01 us -> 5.34 us  [usual(): lax.ppermute(qm, 'lon', ring(-1))]
    ppermute x8, waiting for transfers between devices: 12.9 us -> 16.2 us  [swap(): return lax.ppermute(v, axis, [(i, to(i)) for i in range(size)])]
    pallas_call x0 -> x1, Pallas kernels: none -> 3.01 us  [mass_call(): pl.pallas_call(mass_kernel, in_specs=[smem] * 3 + [vmem] * len(parts), ou...]
  transfers between devices with their start and end apart: 29 -> 28, of which waited for: 10 -> 11; matrix products, arithmetic and copies ran while one was open for 8% -> 4% of each run, Pallas kernels for 10% -> 12%
where the time goes in v1:
time: 172 us
  waiting for transfers between devices  69.5 us (40%)
  starting transfers between devices  61.5 us (36%)
  Pallas kernels  30.1 us (18%)
  local copies, waits for them, and re-layouts  4.95 us (3%)
  other arithmetic  4.43 us (3%)
    ppermute x4, waiting for transfers between devices, usual(): got = [lax.ppermute(sums[d + 3], 'lon', ring(d)) for d in (1, -1, 2, -2)]  21.9 us
    ppermute x4, starting transfers between devices, usual(): lax.ppermute(x, both, some(d, POLAR))  18.3 us
    ppermute x8, waiting for transfers between devices, swap(): return lax.ppermute(v, axis, [(i, to(i)) for i in range(size)])  16.2 us
    ppermute x1, waiting for transfers between devices, usual(): llh = lax.ppermute(beyond[:R], both, some(1, POLAR + NEXT))  12.2 us
    ppermute x4, starting transfers between devices, usual(): got = [lax.ppermute(sums[d + 3], 'lon', ring(d)) for d in (1, -1, 2, -2)]  11.6 us
    pallas_call x1, Pallas kernels, inner_call(): pl.pallas_call(inner_kernel, in_specs=[pl.BlockSpec(memory_space=pltpu.SM...  10.1 us
    pallas_call x1, Pallas kernels, outer_call(): pl.pallas_call(outer_kernel, in_specs=[pl.BlockSpec(memory_space=pltpu.SM...  9.86 us
    ppermute x1, waiting for transfers between devices, usual(): r3 = lax.ppermute(pole, both, some(-3, POLAR))  7.38 us
  transfers between devices with their start and end apart: 28, of which 11 were waited for; matrix products, arithmetic and copies ran while one was open for 4% of the time, Pallas kernels for 12%

profile of v1, /device:TPU:0, one launch (start us, length us, event | category | flops | bytes accessed | tf_op | source)
XLA Modules:
  0.0 171.6 jit_solution(4624388726431412538)
XLA Ops:
  0.0 1.8 %fusion.46 = (bf16[16,32,4,128]{3,2,1,0:T(4,128)(2,1)S(1)}, bf16[16,32,4,128]{3,2,1,0:T(4,128)(2,1)S(1)}) fusion(bf16[64,32,4,128]{3,2,1,0:T(4,128)(2,1)} %bitcast.163), kind=kLoop, calls=%fused_computation.100 | loop fusion | bytes 2097152 | tf_op jit(solution)/shard_map/slice | solution.py:522
  1.8 0.1 pad_maximum_fusion.5
  1.9 6.7 %collective-permute-start.19 = (bf16[32,128,128]{2,1,0:T(8,128)(2,1)S(1)}, bf16[32,128,128]{2,1,0:T(8,128)(2,1)S(1)}, u32[]{:S(2)}, u32[]{:S(2)}) collective-permute-start(bf16[32,128,128]{2,1,0:T(8,128)(2,1)S(1)} %pad_maximum_fusion.5), channel_id=1, source_target_pairs={{0,15},{1,0},{2,1},{3,2},{4,3},{5,4},{6,5},{7,6},{8,7},{9,8},{10,9... | collective-permute-start | bytes 3145736 | tf_op jit(solution)/shard_map/ppermute | solution.py:523
  8.6 1.4 slice.206
  10.0 5.3 %collective-permute-start.33 = (bf16[32,128,128]{2,1,0:T(8,128)(2,1)}, bf16[32,128,128]{2,1,0:T(8,128)(2,1)}, u32[]{:S(2)}, u32[]{:S(2)}) collective-permute-start(bf16[32,128,128]{2,1,0:T(8,128)(2,1)} %bitcast.37), channel_id=1, source_target_pairs={{0,15},{1,0},{2,1},{3,2},{4,3},{5,4},{6,5},{7,6},{8,7},{9,8},{10,9... | collective-permute-start | bytes 3145736 | tf_op jit(solution)/shard_map/ppermute | solution.py:532
  15.4 7.2 %sums.1 = (f32[72,128]{1,0:T(8,128)S(1)}, f32[72,128]{1,0:T(8,128)S(1)}, f32[72,128]{1,0:T(8,128)S(1)}, f32[72,128]{1,0:T(8,128)S(1)}, f32[72,128]{1,0:T(8,128)S...) custom-call(s32[8,64]{1,0:T(8,128)S(1)} %get-tuple-element.117.idx_ref, f32[64]{0:T(128)S(1)} %add_cosine_fusion.1.area_ref, ...), custom_call_target="tpu_custom_call" | custom-call | flops 20000000 | bytes 17825792 | tf_op jit(solution)/shard_map/sums/pallas_call | solution.py:310
  22.6 1.1 slice_select_fusion.5
  23.7 1.1 fusion.45
  24.8 0.1 collective-permute-start.14
  24.9 7.2 %collective-permute-done.19.rs = bf16[32,128,128]{2,1,0:T(8,128)(2,1)S(1)} collective-permute-done((bf16[32,128,128]{2,1,0:T(8,128)(2,1)S(1)}, bf16[32,128,128]{2,1,0:T(8,128)(2,1)S(1)}, u32[]{:S(2)}, u32[]{:S(2)}) %collective-permute-start.19) | collective-permute-done | bytes 1048608 | tf_op jit(solution)/shard_map/ppermute | solution.py:523
  32.1 5.9 %collective-permute-start.15 = (f32[72,128]{1,0:T(8,128)S(1)}, f32[72,128]{1,0:T(8,128)S(1)}, u32[]{:S(2)}, u32[]{:S(2)}) collective-permute-start(f32[72,128]{1,0:T(8,128)S(1)} %get-tuple-element.55), channel_id=1, source_target_pairs={{0,15},{1,0},{2,1},{3,2},{4,3},{5,4},{6,5},{7,6},{8,7},{9,8},{10,9... | collective-permute-start | bytes 110600 | tf_op jit(solution)/shard_map/ppermute | solution.py:530
  38.0 1.9 %collective-permute-start.22 = (bf16[5,128,128]{2,1,0:T(8,128)(2,1)S(1)}, bf16[5,128,128]{2,1,0:T(8,128)(2,1)S(1)}, u32[]{:S(2)}, u32[]{:S(2)}) collective-permute-start(bf16[5,128,128]{2,1,0:T(8,128)(2,1)S(1)} %bitcast.181), channel_id=1, source_target_pairs={{0,3},{1,4},{2,5},{3,6},{4,7},{5,8},{6,9},{7,10},{8,11},{9,12},{10... | collective-permute-start | bytes 491528 | tf_op jit(solution)/shard_map/ppermute | solution.py:525
  40.0 0.8 pad_maximum_fusion.6
  40.8 20.8 %collective-permute-done.14.c1 = f32[72,128]{1,0:T(8,128)S(1)} collective-permute-done((f32[72,128]{1,0:T(8,128)S(1)}, f32[72,128]{1,0:T(8,128)S(1)}, u32[]{:S(2)}, u32[]{:S(2)}) %collective-permute-start.14) | collective-permute-done | bytes 36896 | tf_op jit(solution)/shard_map/ppermute | solution.py:530
  61.5 5.6 %collective-permute-start.17 = (f32[72,128]{1,0:T(8,128)S(1)}, f32[72,128]{1,0:T(8,128)S(1)}, u32[]{:S(2)}, u32[]{:S(2)}) collective-permute-start(f32[72,128]{1,0:T(8,128)S(1)} %get-tuple-element.57), channel_id=1, source_target_pairs={{0,14},{1,15},{2,0},{3,1},{4,2},{5,3},{6,4},{7,5},{8,6},{9,7},{10,... | collective-permute-start | bytes 110600 | tf_op jit(solution)/shard_map/ppermute | solution.py:530
  67.2 0.8 pad_maximum_fusion.7
  68.0 1.1 collective-permute-done.16.c3
  69.1 1.3 collective-permute-start.20
  70.4 1.3 collective-permute-start.21
  71.7 1.9 %collective-permute-start.23 = (bf16[5,128,128]{2,1,0:T(8,128)(2,1)S(1)}, bf16[5,128,128]{2,1,0:T(8,128)(2,1)S(1)}, u32[]{:S(2)}, u32[]{:S(2)}) collective-permute-start(bf16[5,128,128]{2,1,0:T(8,128)(2,1)S(1)} %bitcast.182), channel_id=1, source_target_pairs={{0,13},{1,14},{2,15},{3,0},{4,1},{5,2},{6,3},{7,4},{8,5},{9,6},{10... | collective-permute-start | bytes 491528 | tf_op jit(solution)/shard_map/ppermute | solution.py:526
  73.7 0.9 slice_select_fusion.3
  74.5 7.4 %collective-permute-done.23.r3 = bf16[5,128,128]{2,1,0:T(8,128)(2,1)S(1)} collective-permute-done((bf16[5,128,128]{2,1,0:T(8,128)(2,1)S(1)}, bf16[5,128,128]{2,1,0:T(8,128)(2,1)S(1)}, u32[]{:S(2)}, u32[]{:S(2)}) %collective-permute-start.23) | collective-permute-done | bytes 163872 | tf_op jit(solution)/shard_map/ppermute | solution.py:526
  81.9 1.5 collective-permute-start.36
  83.4 0.6 convert_reduce_fusion.1
  84.0 3.0 %mass.1 = f32[8,128]{1,0:T(8,128)S(1)} custom-call(f32[64]{0:T(128)S(1)} %add_cosine_fusion.1.area_ref, f32[1]{0:T(128)} %bitcast.24.lost_ref, s32[1]{0:T(128)} %bitcast.25.at_ref, f32[72,128]{1,0:T(8,128)S(1)} %get-tuple-element.53.c0, f32[72,128]{1,0:T(8,128)S(1)} %collective-permute-done.14.c1, f32[72,128]{1,0:T(8,128)S(1)} %collective-permute-done.15.c2, ...), custom_call_target="tpu_custom_call" | custom-call | flops 4000000 | bytes 3145728 | tf_op jit(solution)/shard_map/mass/pallas_call | solution.py:354
  87.0 1.2 collective-permute-done.24
  88.2 3.6 %collective-permute-done.25 = f32[8,128]{1,0:T(8,128)S(1)} collective-permute-done((f32[8,128]{1,0:T(8,128)S(1)}, f32[8,128]{1,0:T(8,128)S(1)}, u32[]{:S(2)}, u32[]{:S(2)}) %collective-permute-start.25) | collective-permute-done | bytes 4128 | tf_op jit(solution)/shard_map/ppermute | solution.py:503
  91.8 2.5 %collective-permute-start.26 = (f32[8,128]{1,0:T(8,128)S(1)}, f32[8,128]{1,0:T(8,128)S(1)}, u32[]{:S(2)}, u32[]{:S(2)}) collective-permute-start(f32[8,128]{1,0:T(8,128)S(1)} %add.225), channel_id=1, source_target_pairs={{0,64},{16,80},{32,96},{48,112},{64,0},{80,16},{96,32},{112,48},{1... | collective-permute-start | bytes 12296 | tf_op jit(solution)/shard_map/ppermute | solution.py:503
  94.2 2.7 %collective-permute-done.26 = f32[8,128]{1,0:T(8,128)S(1)} collective-permute-done((f32[8,128]{1,0:T(8,128)S(1)}, f32[8,128]{1,0:T(8,128)S(1)}, u32[]{:S(2)}, u32[]{:S(2)}) %collective-permute-start.26) | collective-permute-done | bytes 4128 | tf_op jit(solution)/shard_map/ppermute | solution.py:503
  96.9 3.6 %collective-permute-done.27 = f32[8,128]{1,0:T(8,128)S(1)} collective-permute-done((f32[8,128]{1,0:T(8,128)S(1)}, f32[8,128]{1,0:T(8,128)S(1)}, u32[]{:S(2)}, u32[]{:S(2)}) %collective-permute-start.27) | collective-permute-done | bytes 4128 | tf_op jit(solution)/shard_map/ppermute | solution.py:503
  100.5 5.1 %collective-permute-done.28 = f32[8,128]{1,0:T(8,128)S(1)} collective-permute-done((f32[8,128]{1,0:T(8,128)S(1)}, f32[8,128]{1,0:T(8,128)S(1)}, u32[]{:S(2)}, u32[]{:S(2)}) %collective-permute-start.28) | collective-permute-done | bytes 4128 | tf_op jit(solution)/shard_map/ppermute | solution.py:503
  105.6 1.0 collective-permute-start.31
  106.7 3.2 %collective-permute-start.30 = (f32[8,128]{1,0:T(8,128)S(1)}, f32[8,128]{1,0:T(8,128)S(1)}, u32[]{:S(2)}, u32[]{:S(2)}) collective-permute-start(f32[8,128]{1,0:T(8,128)S(1)} %add.228), channel_id=1, source_target_pairs={{0,3},{1,0},{2,1},{3,2},{4,7},{5,4},{6,5},{7,6},{8,11},{9,8},{10,9... | collective-permute-start | bytes 12296 | tf_op jit(solution)/shard_map/ppermute | solution.py:503
  110.0 1.9 %collective-permute-start.34 = (bf16[32,128,128]{2,1,0:T(8,128)(2,1)S(1)}, bf16[32,128,128]{2,1,0:T(8,128)(2,1)S(1)}, u32[]{:S(2)}, u32[]{:S(2)}) collective-permute-start(bf16[32,128,128]{2,1,0:T(8,128)(2,1)S(1)} %collective-permute-done.18.ls), channel_id=1, source_target_pairs={{0,1},{1,2},{2,3},{3,4},{4,5},{5,6},{6,7},{7,8},{8,9},{9,10},{10,1... | collective-permute-start | bytes 3145736 | tf_op jit(solution)/shard_map/ppermute | solution.py:545
  111.9 7.2 %collective-permute-start.38 = (bf16[32,128,128]{2,1,0:T(8,128)(2,1)S(1)}, bf16[32,128,128]{2,1,0:T(8,128)(2,1)S(1)}, u32[]{:S(2)}, u32[]{:S(2)}) collective-permute-start(bf16[32,128,128]{2,1,0:T(8,128)(2,1)S(1)} %collective-permute-done.19.rs), channel_id=1, source_target_pairs={{0,15},{1,0},{2,1},{3,2},{4,3},{5,4},{6,5},{7,6},{8,7},{9,8},{10,9... | collective-permute-start | bytes 3145736 | tf_op jit(solution)/shard_map/ppermute | solution.py:545
  119.2 1.9 %collective-permute-start.35 = (bf16[32,128,128]{2,1,0:T(8,128)(2,1)}, bf16[32,128,128]{2,1,0:T(8,128)(2,1)S(1)}, u32[]{:S(2)}, u32[]{:S(2)}) collective-permute-start(bf16[32,128,128]{2,1,0:T(8,128)(2,1)} %collective-permute-done.32.lm), channel_id=1, source_target_pairs={{0,1},{1,2},{2,3},{3,4},{4,5},{5,6},{6,7},{7,8},{8,9},{9,10},{10,1... | collective-permute-start | bytes 3145736 | tf_op jit(solution)/shard_map/ppermute | solution.py:546
  121.1 7.2 %collective-permute-start.39 = (bf16[32,128,128]{2,1,0:T(8,128)(2,1)}, bf16[32,128,128]{2,1,0:T(8,128)(2,1)S(1)}, u32[]{:S(2)}, u32[]{:S(2)}) collective-permute-start(bf16[32,128,128]{2,1,0:T(8,128)(2,1)} %collective-permute-done.33.rm), channel_id=1, source_target_pairs={{0,15},{1,0},{2,1},{3,2},{4,3},{5,4},{6,5},{7,6},{8,7},{9,8},{10,9... | collective-permute-start | bytes 3145736 | tf_op jit(solution)/shard_map/ppermute | solution.py:546
  128.4 1.9 %collective-permute-start.37 = (bf16[4,128,128]{2,1,0:T(8,128)(2,1)S(1)}, bf16[4,128,128]{2,1,0:T(8,128)(2,1)S(1)}, u32[]{:S(2)}, u32[]{:S(2)}) collective-permute-start(bf16[4,128,128]{2,1,0:T(8,128)(2,1)S(1)} %get-tuple-element.115), channel_id=1, source_target_pairs={{0,1},{1,2},{2,3},{3,4},{4,5},{5,6},{6,7},{7,8},{8,9},{9,10},{10,1... | collective-permute-start | bytes 393224 | tf_op jit(solution)/shard_map/ppermute | solution.py:554
  130.3 0.1 slice_select_fusion.2
  130.4 12.2 %collective-permute-done.37.lh = bf16[4,128,128]{2,1,0:T(8,128)(2,1)S(1)} collective-permute-done((bf16[4,128,128]{2,1,0:T(8,128)(2,1)S(1)}, bf16[4,128,128]{2,1,0:T(8,128)(2,1)S(1)}, u32[]{:S(2)}, u32[]{:S(2)}) %collective-permute-start.37) | collective-permute-done | bytes 131104 | tf_op jit(solution)/shard_map/ppermute | solution.py:554
  142.6 0.7 collective-permute-start.40
  143.3 10.1 %inner.1 = (f32[64,128,128]{2,1,0:T(8,128)S(1)}, bf16[64,8,128,128]{3,2,1,0:T(8,128)(2,1)S(1)}) custom-call(s32[8,64]{1,0:T(8,128)S(1)} %get-tuple-element.116.idx_ref, bf16[64,8,128,128]{3,2,1,0:T(8,128)(2,1)} %bitcast.159, bf16[64,128,128]{2,1,0:T(8,128)(2,1)S(1)} %bitcast.168, bf16[32,128,128]{2,1,0:T(8,128)(2,1)S(1)} %collective-permute-done.18.ls, ...), custom_call_target="tpu_custom_call" | custom-call | flops 2147483648 | bytes 17825792 | tf_op jit(solution)/shard_map/inner/pallas_call | solution.py:403
  153.4 0.6 slice.167
  154.0 2.3 %collective-permute-start.41 = (bf16[4,128,128]{2,1,0:T(8,128)(2,1)S(1)}, bf16[4,128,128]{2,1,0:T(8,128)(2,1)S(1)}, u32[]{:S(2)}, u32[]{:S(2)}) collective-permute-start(bf16[4,128,128]{2,1,0:T(8,128)(2,1)S(1)} %get-tuple-element.114), channel_id=1, source_target_pairs={{0,15},{1,0},{2,1},{3,2},{4,3},{5,4},{6,5},{7,6},{8,7},{9,8},{10,9... | collective-permute-start | bytes 393224 | tf_op jit(solution)/shard_map/ppermute | solution.py:555
  156.3 4.5 %collective-permute-done.41.rh = bf16[4,128,128]{2,1,0:T(8,128)(2,1)S(1)} collective-permute-done((bf16[4,128,128]{2,1,0:T(8,128)(2,1)S(1)}, bf16[4,128,128]{2,1,0:T(8,128)(2,1)S(1)}, u32[]{:S(2)}, u32[]{:S(2)}) %collective-permute-start.41) | collective-permute-done | bytes 131104 | tf_op jit(solution)/shard_map/ppermute | solution.py:555
  160.8 0.1 broadcast_in_dim.36.corr_ref
  160.9 9.9 %outer.1 = f32[64,128,128]{2,1,0:T(8,128)} custom-call(s32[8,64]{1,0:T(8,128)S(1)} %get-tuple-element.118.idx_ref, bf16[64,8,128,128]{3,2,1,0:T(8,128)(2,1)S(1)} %get-tuple-element.60.w_ref, f32[128,128]{1,0:T(8,128)S(1)} %broadcast_in_dim.36.corr_ref, bf16[32,128,128]{2,1,0:T(8,128)(2,1)S(1)} %collective-permute-done.34.ls, ...), custom_call_target="tpu_custom_call" | custom-call | flops 2147483648 | bytes 4194304 | tf_op jit(solution)/shard_map/outer/pallas_call | solution.py:456
  170.8 0.6 while.9
  (48 shorter events, 0.3 us)
Async XLA Ops:
  0.0 8.6 %copy-start.1 = (bf16[64,128,32,4]{1,3,2,0:T(4,128)(2,1)S(1)}, bf16[64,128,32,4]{1,3,2,0:T(4,128)(2,1)}, u32[]{:S(2)}) copy-start(bf16[64,128,32,4]{1,3,2,0:T(4,128)(2,1)} %param.7) | copy-start | bytes 6291460
  0.0 15.4 %copy-start.8 = (s32[64,1]{0,1:T(1,128)S(1)}, s32[64,1]{0,1:T(1,128)}, u32[]{:S(2)}) copy-start(s32[64,1]{0,1:T(1,128)} %param.11) | copy-start | bytes 772
  0.0 15.4 %copy-start.4 = (s32[64,1,8]{0,2,1:T(8,128)S(1)}, s32[64,1,8]{0,2,1:T(8,128)}, u32[]{:S(2)}) copy-start(s32[64,1,8]{0,2,1:T(8,128)} %param.9) | copy-start | bytes 6148
  0.0 15.4 %copy-start.6 = (s32[64,1,8]{0,2,1:T(8,128)S(1)}, s32[64,1,8]{0,2,1:T(8,128)}, u32[]{:S(2)}) copy-start(s32[64,1,8]{0,2,1:T(8,128)} %param.10) | copy-start | bytes 6148
  1.9 30.2 %collective-permute-start.19 = (bf16[32,128,128]{2,1,0:T(8,128)(2,1)S(1)}, bf16[32,128,128]{2,1,0:T(8,128)(2,1)S(1)}, u32[]{:S(2)}, u32[]{:S(2)}) collective-permute-start(bf16[32,128,128]{2,1,0:T(8,128)(2,1)S(1)} %pad_maximum_fusion.5), channel_id=1, source_target_pairs={{0,15},{1,0},{2,1},{3,2},{4,3},{5,4},{6,5},{7,6},{8,7},{9,8},{10,9... | collective-permute-start | bytes 3145736 | tf_op jit(solution)/shard_map/ppermute | solution.py:523
  8.6 29.4 %collective-permute-start.18 = (bf16[32,128,128]{2,1,0:T(8,128)(2,1)S(1)}, bf16[32,128,128]{2,1,0:T(8,128)(2,1)S(1)}, u32[]{:S(2)}, u32[]{:S(2)}) collective-permute-start(bf16[32,128,128]{2,1,0:T(8,128)(2,1)S(1)} %pad_maximum_fusion.5), channel_id=1, source_target_pairs={{0,1},{1,2},{2,3},{3,4},{4,5},{5,6},{6,7},{7,8},{8,9},{9,10},{10,1... | collective-permute-start | bytes 3145736 | tf_op jit(solution)/shard_map/ppermute | solution.py:523
  10.0 96.7 %collective-permute-start.32 = (bf16[32,128,128]{2,1,0:T(8,128)(2,1)}, bf16[32,128,128]{2,1,0:T(8,128)(2,1)}, u32[]{:S(2)}, u32[]{:S(2)}) collective-permute-start(bf16[32,128,128]{2,1,0:T(8,128)(2,1)} %bitcast.37), channel_id=1, source_target_pairs={{0,1},{1,2},{2,3},{3,4},{4,5},{5,6},{6,7},{7,8},{8,9},{9,10},{10,1... | collective-permute-start | bytes 3145736 | tf_op jit(solution)/shard_map/ppermute | solution.py:532
  10.0 100.0 %collective-permute-start.33 = (bf16[32,128,128]{2,1,0:T(8,128)(2,1)}, bf16[32,128,128]{2,1,0:T(8,128)(2,1)}, u32[]{:S(2)}, u32[]{:S(2)}) collective-permute-start(bf16[32,128,128]{2,1,0:T(8,128)(2,1)} %bitcast.37), channel_id=1, source_target_pairs={{0,15},{1,0},{2,1},{3,2},{4,3},{5,4},{6,5},{7,6},{8,7},{9,8},{10,9... | collective-permute-start | bytes 3145736 | tf_op jit(solution)/shard_map/ppermute | solution.py:532
  24.8 36.7 %collective-permute-start.14 = (f32[72,128]{1,0:T(8,128)S(1)}, f32[72,128]{1,0:T(8,128)S(1)}, u32[]{:S(2)}, u32[]{:S(2)}) collective-permute-start(f32[72,128]{1,0:T(8,128)S(1)} %get-tuple-element.54), channel_id=1, source_target_pairs={{0,1},{1,2},{2,3},{3,4},{4,5},{5,6},{6,7},{7,8},{8,9},{9,10},{10,1... | collective-permute-start | bytes 110600 | tf_op jit(solution)/shard_map/ppermute | solution.py:530
  32.1 29.4 %collective-permute-start.15 = (f32[72,128]{1,0:T(8,128)S(1)}, f32[72,128]{1,0:T(8,128)S(1)}, u32[]{:S(2)}, u32[]{:S(2)}) collective-permute-start(f32[72,128]{1,0:T(8,128)S(1)} %get-tuple-element.55), channel_id=1, source_target_pairs={{0,15},{1,0},{2,1},{3,2},{4,3},{5,4},{6,5},{7,6},{8,7},{9,8},{10,9... | collective-permute-start | bytes 110600 | tf_op jit(solution)/shard_map/ppermute | solution.py:530
  38.0 33.7 %collective-permute-start.22 = (bf16[5,128,128]{2,1,0:T(8,128)(2,1)S(1)}, bf16[5,128,128]{2,1,0:T(8,128)(2,1)S(1)}, u32[]{:S(2)}, u32[]{:S(2)}) collective-permute-start(bf16[5,128,128]{2,1,0:T(8,128)(2,1)S(1)} %bitcast.181), channel_id=1, source_target_pairs={{0,3},{1,4},{2,5},{3,6},{4,7},{5,8},{6,9},{7,10},{8,11},{9,12},{10... | collective-permute-start | bytes 491528 | tf_op jit(solution)/shard_map/ppermute | solution.py:525
  61.5 7.6 %collective-permute-start.16 = (f32[72,128]{1,0:T(8,128)S(1)}, f32[72,128]{1,0:T(8,128)S(1)}, u32[]{:S(2)}, u32[]{:S(2)}) collective-permute-start(f32[72,128]{1,0:T(8,128)S(1)} %get-tuple-element.56), channel_id=1, source_target_pairs={{0,2},{1,3},{2,4},{3,5},{4,6},{5,7},{6,8},{7,9},{8,10},{9,11},{10,... | collective-permute-start | bytes 110600 | tf_op jit(solution)/shard_map/ppermute | solution.py:530
  61.5 8.9 %collective-permute-start.17 = (f32[72,128]{1,0:T(8,128)S(1)}, f32[72,128]{1,0:T(8,128)S(1)}, u32[]{:S(2)}, u32[]{:S(2)}) collective-permute-start(f32[72,128]{1,0:T(8,128)S(1)} %get-tuple-element.57), channel_id=1, source_target_pairs={{0,14},{1,15},{2,0},{3,1},{4,2},{5,3},{6,4},{7,5},{8,6},{9,7},{10,... | collective-permute-start | bytes 110600 | tf_op jit(solution)/shard_map/ppermute | solution.py:530
  69.1 14.9 %collective-permute-start.20 = (bf16[12,128,128]{2,1,0:T(8,128)(2,1)}, bf16[12,128,128]{2,1,0:T(8,128)(2,1)S(1)}, u32[]{:S(2)}, u32[]{:S(2)}) collective-permute-start(bf16[12,128,128]{2,1,0:T(8,128)(2,1)} %pad_maximum_fusion.6), channel_id=1, source_target_pairs={{0,16},{16,32},{32,48},{48,64},{64,80},{80,96},{96,112},{1,17},{17... | collective-permute-start | bytes 1179656 | tf_op jit(solution)/shard_map/ppermute | solution.py:533
  70.4 13.6 %collective-permute-start.21 = (bf16[12,128,128]{2,1,0:T(8,128)(2,1)}, bf16[12,128,128]{2,1,0:T(8,128)(2,1)S(1)}, u32[]{:S(2)}, u32[]{:S(2)}) collective-permute-start(bf16[12,128,128]{2,1,0:T(8,128)(2,1)} %pad_maximum_fusion.7), channel_id=1, source_target_pairs={{16,0},{32,16},{48,32},{64,48},{80,64},{96,80},{112,96},{17,1},{33... | collective-permute-start | bytes 1179656 | tf_op jit(solution)/shard_map/ppermute | solution.py:534
  71.7 10.2 %collective-permute-start.23 = (bf16[5,128,128]{2,1,0:T(8,128)(2,1)S(1)}, bf16[5,128,128]{2,1,0:T(8,128)(2,1)S(1)}, u32[]{:S(2)}, u32[]{:S(2)}) collective-permute-start(bf16[5,128,128]{2,1,0:T(8,128)(2,1)S(1)} %bitcast.182), channel_id=1, source_target_pairs={{0,13},{1,14},{2,15},{3,0},{4,1},{5,2},{6,3},{7,4},{8,5},{9,6},{10... | collective-permute-start | bytes 491528 | tf_op jit(solution)/shard_map/ppermute | solution.py:526
  81.9 46.5 %collective-permute-start.36 = (bf16[16,128,128]{2,1,0:T(8,128)(2,1)}, bf16[16,128,128]{2,1,0:T(8,128)(2,1)}, u32[]{:S(2)}, u32[]{:S(2)}) collective-permute-start(bf16[16,128,128]{2,1,0:T(8,128)(2,1)} %slice_select_fusion.3), channel_id=1, source_target_pairs={{16,17},{17,18},{18,19},{19,20},{20,21},{21,22},{22,23},{23,24},{2... | collective-permute-start | bytes 1572872 | tf_op jit(solution)/shard_map/ppermute | solution.py:551
  87.0 1.2 collective-permute-start.24
  88.2 3.6 %collective-permute-start.25 = (f32[8,128]{1,0:T(8,128)S(1)}, f32[8,128]{1,0:T(8,128)S(1)}, u32[]{:S(2)}, u32[]{:S(2)}) collective-permute-start(f32[8,128]{1,0:T(8,128)S(1)} %add.224), channel_id=1, source_target_pairs={{0,32},{16,48},{32,0},{48,16},{64,96},{80,112},{96,64},{112,80},{1... | collective-permute-start | bytes 12296 | tf_op jit(solution)/shard_map/ppermute | solution.py:503
  91.8 5.1 %collective-permute-start.26 = (f32[8,128]{1,0:T(8,128)S(1)}, f32[8,128]{1,0:T(8,128)S(1)}, u32[]{:S(2)}, u32[]{:S(2)}) collective-permute-start(f32[8,128]{1,0:T(8,128)S(1)} %add.225), channel_id=1, source_target_pairs={{0,64},{16,80},{32,96},{48,112},{64,0},{80,16},{96,32},{112,48},{1... | collective-permute-start | bytes 12296 | tf_op jit(solution)/shard_map/ppermute | solution.py:503
  96.9 3.6 %collective-permute-start.27 = (f32[8,128]{1,0:T(8,128)S(1)}, f32[8,128]{1,0:T(8,128)S(1)}, u32[]{:S(2)}, u32[]{:S(2)}) collective-permute-start(f32[8,128]{1,0:T(8,128)S(1)} %add.226), channel_id=1, source_target_pairs={{0,4},{1,5},{2,6},{3,7},{4,0},{5,1},{6,2},{7,3},{8,12},{9,13},{10,... | collective-permute-start | bytes 12296 | tf_op jit(solution)/shard_map/ppermute | solution.py:503
  100.5 5.1 %collective-permute-start.28 = (f32[8,128]{1,0:T(8,128)S(1)}, f32[8,128]{1,0:T(8,128)S(1)}, u32[]{:S(2)}, u32[]{:S(2)}) collective-permute-start(f32[8,128]{1,0:T(8,128)S(1)} %add.227), channel_id=1, source_target_pairs={{0,8},{1,9},{2,10},{3,11},{4,12},{5,13},{6,14},{7,15},{8,0},{9,1},... | collective-permute-start | bytes 12296 | tf_op jit(solution)/shard_map/ppermute | solution.py:503
  100.5 42.8 %copy-start.2 = (bf16[64,128,32,4]{1,3,2,0:T(4,128)(2,1)S(1)}, bf16[64,128,32,4]{1,3,2,0:T(4,128)(2,1)}, u32[]{:S(2)}) copy-start(bf16[64,128,32,4]{1,3,2,0:T(4,128)(2,1)} %param.7) | copy-start | bytes 6291460
  105.6 6.3 %collective-permute-start.31 = (f32[8,128]{1,0:T(8,128)S(1)}, f32[8,128]{1,0:T(8,128)S(1)}, u32[]{:S(2)}, u32[]{:S(2)}) collective-permute-start(f32[8,128]{1,0:T(8,128)S(1)} %add.228), channel_id=1, source_target_pairs={{0,2},{1,3},{2,0},{3,1},{4,6},{5,7},{6,4},{7,5},{8,10},{9,11},{10,... | collective-permute-start | bytes 12296 | tf_op jit(solution)/shard_map/ppermute | solution.py:503
  106.7 12.5 %collective-permute-start.29 = (f32[8,128]{1,0:T(8,128)S(1)}, f32[8,128]{1,0:T(8,128)S(1)}, u32[]{:S(2)}, u32[]{:S(2)}) collective-permute-start(f32[8,128]{1,0:T(8,128)S(1)} %add.228), channel_id=1, source_target_pairs={{0,1},{1,2},{2,3},{3,0},{4,5},{5,6},{6,7},{7,4},{8,9},{9,10},{10,1... | collective-permute-start | bytes 12296 | tf_op jit(solution)/shard_map/ppermute | solution.py:503
  106.7 14.4 %collective-permute-start.30 = (f32[8,128]{1,0:T(8,128)S(1)}, f32[8,128]{1,0:T(8,128)S(1)}, u32[]{:S(2)}, u32[]{:S(2)}) collective-permute-start(f32[8,128]{1,0:T(8,128)S(1)} %add.228), channel_id=1, source_target_pairs={{0,3},{1,0},{2,1},{3,2},{4,7},{5,4},{6,5},{7,6},{8,11},{9,8},{10,9... | collective-permute-start | bytes 12296 | tf_op jit(solution)/shard_map/ppermute | solution.py:503
  110.0 50.9 %collective-permute-start.34 = (bf16[32,128,128]{2,1,0:T(8,128)(2,1)S(1)}, bf16[32,128,128]{2,1,0:T(8,128)(2,1)S(1)}, u32[]{:S(2)}, u32[]{:S(2)}) collective-permute-start(bf16[32,128,128]{2,1,0:T(8,128)(2,1)S(1)} %collective-permute-done.18.ls), channel_id=1, source_target_pairs={{0,1},{1,2},{2,3},{3,4},{4,5},{5,6},{6,7},{7,8},{8,9},{9,10},{10,1... | collective-permute-start | bytes 3145736 | tf_op jit(solution)/shard_map/ppermute | solution.py:545
  111.9 48.9 %collective-permute-start.38 = (bf16[32,128,128]{2,1,0:T(8,128)(2,1)S(1)}, bf16[32,128,128]{2,1,0:T(8,128)(2,1)S(1)}, u32[]{:S(2)}, u32[]{:S(2)}) collective-permute-start(bf16[32,128,128]{2,1,0:T(8,128)(2,1)S(1)} %collective-permute-done.19.rs), channel_id=1, source_target_pairs={{0,15},{1,0},{2,1},{3,2},{4,3},{5,4},{6,5},{7,6},{8,7},{9,8},{10,9... | collective-permute-start | bytes 3145736 | tf_op jit(solution)/shard_map/ppermute | solution.py:545
  119.2 41.7 %collective-permute-start.35 = (bf16[32,128,128]{2,1,0:T(8,128)(2,1)}, bf16[32,128,128]{2,1,0:T(8,128)(2,1)S(1)}, u32[]{:S(2)}, u32[]{:S(2)}) collective-permute-start(bf16[32,128,128]{2,1,0:T(8,128)(2,1)} %collective-permute-done.32.lm), channel_id=1, source_target_pairs={{0,1},{1,2},{2,3},{3,4},{4,5},{5,6},{6,7},{7,8},{8,9},{9,10},{10,1... | collective-permute-start | bytes 3145736 | tf_op jit(solution)/shard_map/ppermute | solution.py:546
  121.1 39.7 %collective-permute-start.39 = (bf16[32,128,128]{2,1,0:T(8,128)(2,1)}, bf16[32,128,128]{2,1,0:T(8,128)(2,1)S(1)}, u32[]{:S(2)}, u32[]{:S(2)}) collective-permute-start(bf16[32,128,128]{2,1,0:T(8,128)(2,1)} %collective-permute-done.33.rm), channel_id=1, source_target_pairs={{0,15},{1,0},{2,1},{3,2},{4,3},{5,4},{6,5},{7,6},{8,7},{9,8},{10,9... | collective-permute-start | bytes 3145736 | tf_op jit(solution)/shard_map/ppermute | solution.py:546
  128.4 14.2 %collective-permute-start.37 = (bf16[4,128,128]{2,1,0:T(8,128)(2,1)S(1)}, bf16[4,128,128]{2,1,0:T(8,128)(2,1)S(1)}, u32[]{:S(2)}, u32[]{:S(2)}) collective-permute-start(bf16[4,128,128]{2,1,0:T(8,128)(2,1)S(1)} %get-tuple-element.115), channel_id=1, source_target_pairs={{0,1},{1,2},{2,3},{3,4},{4,5},{5,6},{6,7},{7,8},{8,9},{9,10},{10,1... | collective-permute-start | bytes 393224 | tf_op jit(solution)/shard_map/ppermute | solution.py:554
  142.6 11.4 %collective-permute-start.40 = (bf16[16,128,128]{2,1,0:T(8,128)(2,1)S(1)}, bf16[16,128,128]{2,1,0:T(8,128)(2,1)S(1)}, u32[]{:S(2)}, u32[]{:S(2)}) collective-permute-start(bf16[16,128,128]{2,1,0:T(8,128)(2,1)S(1)} %slice_select_fusion.2), channel_id=1, source_target_pairs={{16,31},{17,16},{18,17},{19,18},{20,19},{21,20},{22,21},{23,22},{2... | collective-permute-start | bytes 1572872 | tf_op jit(solution)/shard_map/ppermute | solution.py:552
  154.0 6.9 %collective-permute-start.41 = (bf16[4,128,128]{2,1,0:T(8,128)(2,1)S(1)}, bf16[4,128,128]{2,1,0:T(8,128)(2,1)S(1)}, u32[]{:S(2)}, u32[]{:S(2)}) collective-permute-start(bf16[4,128,128]{2,1,0:T(8,128)(2,1)S(1)} %get-tuple-element.114), channel_id=1, source_target_pairs={{0,15},{1,0},{2,1},{3,2},{4,3},{5,4},{6,5},{7,6},{8,7},{9,8},{10,9... | collective-permute-start | bytes 393224 | tf_op jit(solution)/shard_map/ppermute | solution.py:555

commit v2 on v1

--- a/solution.py
+++ b/solution.py
@@ -1,3 +1,4 @@
+import functools
 import math
 
 import jax
@@ -276,7 +277,7 @@
 
 
 def sums_kernel(idx_ref, area_ref, w_hbm, *refs):
-    outs, (wv, acc, sem) = refs[:-3], refs[-3:]
+    left, right, own, s3m, s3p, wv, acc, sem = refs
 
     def copy(c):
         rows = pl.ds(c * WT, WT)
@@ -300,8 +301,18 @@
         return carry
 
     lax.fori_loop(0, WC, work, 0)
-    for n, out in enumerate(outs):
-        out[...] = jnp.sum(acc[n * PAD : (n + 1) * PAD], axis=1)
+
+    def summed(rel):
+        at = (rel + 3) * PAD
+        return jnp.sum(acc[at : at + PAD], axis=1)
+
+    left[:PAD] = summed(-1)
+    left[PAD:] = summed(-2)
+    right[:PAD] = summed(1)
+    right[PAD:] = summed(2)
+    own[...] = summed(0)
+    s3m[...] = summed(-3)
+    s3p[...] = summed(3)
 
 
 def sums_call(idx, area, weights):
@@ -310,8 +321,8 @@
     return pl.pallas_call(
         sums_kernel,
         in_specs=[smem, smem, pl.BlockSpec(memory_space=pltpu.HBM)],
-        out_specs=[vmem] * 7,
-        out_shape=[jax.ShapeDtypeStruct((PAD, C), jnp.float32)] * 7,
+        out_specs=[vmem] * 5,
+        out_shape=[jax.ShapeDtypeStruct((n * PAD, C), jnp.float32) for n in (2, 2, 1, 1, 1)],
         scratch_shapes=[
             pltpu.VMEM(weights.shape, weights.dtype),
             pltpu.VMEM((SECT + 1, 8, C), jnp.float32),
@@ -325,56 +336,7 @@
     )(idx, area, pltpu.with_memory_space_constraint(weights, pltpu.HBM))
 
 
-def mass_kernel(area_ref, lost_ref, at_ref, c0, c1, c2, c3, c4, s3m, s3p, q, up, dn, l3, r3, out_ref, by):
-    by[...] = -(((c0[...] + c1[...]) + (c2[...] + c3[...])) + c4[...])
-    acc = jnp.zeros((C, C), jnp.float32)
-    for i in range(R):
-        acc = acc + by[i : i + 1] * up[i].astype(jnp.float32)
-        acc = acc + by[R + ROWS + i : R + ROWS + i + 1] * dn[i].astype(jnp.float32)
-    at = at_ref[0]
-    for i in range(E):
-        acc = acc - s3m[pl.ds(at + i, 1)] * l3[i].astype(jnp.float32)
-        acc = acc - s3p[pl.ds(at + i, 1)] * r3[i].astype(jnp.float32)
-
-    def body(r, acc):
-        return acc + (by[pl.ds(r + R, 1)] + area_ref[r]) * q[r].astype(jnp.float32)
-
-    acc = lax.fori_loop(0, ROWS, body, acc, unroll=4)
-    change = lax.dot_general(
-        jnp.ones((8, C), jnp.float32), acc, NT,
-        precision=lax.Precision.HIGHEST, preferred_element_type=jnp.float32,
-    )
-    row = lax.broadcasted_iota(jnp.int32, (8, C), 0)
-    out_ref[...] = jnp.where(row == 0, change, lost_ref[0])
-
-
-def mass_call(area, lost, at, parts):
-    smem = pl.BlockSpec(memory_space=pltpu.SMEM)
-    vmem = pl.BlockSpec(memory_space=pltpu.VMEM)
-    return pl.pallas_call(
-        mass_kernel,
-        in_specs=[smem] * 3 + [vmem] * len(parts),
-        out_specs=vmem,
-        out_shape=jax.ShapeDtypeStruct((8, C), jnp.float32),
-        scratch_shapes=[pltpu.VMEM((PAD, C), jnp.float32)],
-        compiler_params=pltpu.CompilerParams(vmem_limit_bytes=4 << 20),
-        cost_estimate=pl.CostEstimate(
-            flops=4_000_000, bytes_accessed=3 << 20, transcendentals=0
-        ),
-        name="mass",
-    )(area, lost, at, *parts)
-
-
-def inner_kernel(idx_ref, w_hbm, own, ls, lm, rs, rm, up, dn, out_ref, wv, src, sem):
-    def copy(c):
-        rows = pl.ds(c * WT, WT)
-        return pltpu.make_async_copy(w_hbm.at[rows], wv.at[rows], sem.at[c])
-
-    def start(c, carry):
-        copy(c).start()
-        return carry
-
-    lax.fori_loop(0, WC, start, 0)
+def mass_kernel(area_ref, lost_ref, at_ref, c0, cl, cr, s3m, s3p, own, ls, lm, rs, rm, up, dn, l3, r3, out_ref, src, by):
     src[pl.ds(R, ROWS)] = own[...]
     for n, (e, m) in enumerate(((ls, lm), (rs, rm))):
         at = (n + 1) * PAD + R
@@ -385,43 +347,95 @@
         src[pl.ds(n * PAD, R)] = up[pl.ds(n * R, R)]
         src[pl.ds(n * PAD + R + ROWS, R)] = dn[pl.ds(n * R, R)]
     src[3 * PAD] = jnp.zeros((C, C), src.dtype)
+    by[:PAD] = (c0[...] + cl[:PAD]) + cr[:PAD]
+    by[PAD : 2 * PAD] = cl[PAD:]
+    by[2 * PAD :] = cr[PAD:]
+    for r in range(ROWS):
+        by[R + r : R + r + 1] = by[R + r : R + r + 1] - area_ref[r]
+
+    def body(p, acc):
+        return acc + by[pl.ds(p, 1)] * src[p].astype(jnp.float32)
+
+    acc = lax.fori_loop(0, 3 * PAD, body, jnp.zeros((C, C), jnp.float32), unroll=4)
+    at = at_ref[0]
+    for i in range(E):
+        acc = acc + s3m[pl.ds(at + i, 1)] * l3[i].astype(jnp.float32)
+        acc = acc + s3p[pl.ds(at + i, 1)] * r3[i].astype(jnp.float32)
+    change = lax.dot_general(
+        jnp.full((8, C), -1.0, jnp.float32), acc, NT,
+        precision=lax.Precision.HIGHEST, preferred_element_type=jnp.float32,
+    )
+    row = lax.broadcasted_iota(jnp.int32, (8, C), 0)
+    out_ref[...] = jnp.where(row == 0, change, lost_ref[0])
+
+
+def mass_call(area, lost, at, parts):
+    smem = pl.BlockSpec(memory_space=pltpu.SMEM)
+    vmem = pl.BlockSpec(memory_space=pltpu.VMEM)
+    return pl.pallas_call(
+        mass_kernel,
+        in_specs=[smem] * 3 + [vmem] * len(parts),
+        out_specs=[vmem, vmem],
+        out_shape=[
+            jax.ShapeDtypeStruct((8, C), jnp.float32),
+            pltpu.VMEM((3 * PAD + 1, C, C), jnp.bfloat16),
+        ],
+        scratch_shapes=[pltpu.VMEM((3 * PAD, C), jnp.float32)],
+        compiler_params=pltpu.CompilerParams(vmem_limit_bytes=6 << 20),
+        cost_estimate=pl.CostEstimate(
+            flops=9_000_000, bytes_accessed=3 << 20, transcendentals=0
+        ),
+        name="mass",
+    )(area, lost, at, *parts)
+
+
+PARTS = 4
+PT = PER // PARTS
+
+
+def inner_kernel(first, idx_ref, w_hbm, src, out_ref, wv, sem):
+    def copy(c):
+        return pltpu.make_async_copy(
+            w_hbm.at[pl.ds(first + c * PT, PT)], wv.at[pl.ds(c * PT, PT)], sem.at[c]
+        )
+
+    for c in range(PARTS):
+        copy(c).start()
 
     def body(c, carry):
         copy(c).wait()
-        for j in range(WT):
-            t = c * WT + j
-            lhs = jnp.concatenate([src[idx_ref[k, t]] for k in range(KMAX)], axis=1)
-            rhs = jnp.concatenate([wv[t, k] for k in range(KMAX)], axis=1)
-            out_ref[t] = lax.dot_general(lhs, rhs, NT, preferred_element_type=jnp.float32)
+        for i in range(PT):
+            j = c * PT + i
+            lhs = jnp.concatenate([src[idx_ref[k, first + j]] for k in range(KMAX)], axis=1)
+            rhs = jnp.concatenate([wv[j, k] for k in range(KMAX)], axis=1)
+            out_ref[j] = lax.dot_general(lhs, rhs, NT, preferred_element_type=jnp.float32)
         return carry
 
-    lax.fori_loop(0, WC, body, 0)
-
-
-def inner_call(idx, weights, parts):
+    lax.fori_loop(0, PARTS, body, 0)
+
+
+def inner_call(chunk, idx, weights, near):
     vmem = pl.BlockSpec(memory_space=pltpu.VMEM)
     return pl.pallas_call(
-        inner_kernel,
-        in_specs=[pl.BlockSpec(memory_space=pltpu.SMEM), pl.BlockSpec(memory_space=pltpu.HBM)]
-        + [vmem] * len(parts),
+        functools.partial(inner_kernel, chunk * PER),
+        in_specs=[
+            pl.BlockSpec(memory_space=pltpu.SMEM), pl.BlockSpec(memory_space=pltpu.HBM), vmem
+        ],
         out_specs=[vmem, vmem],
         out_shape=[
-            pltpu.VMEM((ROWS, C, C), jnp.float32),
-            pltpu.VMEM(weights.shape, weights.dtype),
-        ],
-        scratch_shapes=[
-            pltpu.VMEM((3 * PAD + 1, C, C), jnp.bfloat16),
-            pltpu.SemaphoreType.DMA((WC,)),
-        ],
-        compiler_params=pltpu.CompilerParams(vmem_limit_bytes=10 << 20),
+            pltpu.VMEM((PER, C, C), jnp.float32),
+            pltpu.VMEM((PER, KMAX, C, C), jnp.bfloat16),
+        ],
+        scratch_shapes=[pltpu.SemaphoreType.DMA((PARTS,))],
+        compiler_params=pltpu.CompilerParams(vmem_limit_bytes=2 << 20),
         cost_estimate=pl.CostEstimate(
-            flops=2 * ROWS * KMAX * C**3, bytes_accessed=17 << 20, transcendentals=0
-        ),
-        name="inner",
-    )(idx, pltpu.with_memory_space_constraint(weights, pltpu.HBM), *parts)
-
-
-def outer_kernel(idx_ref, w_ref, corr_ref, ls, lm, lb, lh, rs, rm, rb, rh, l3, r3, part_ref, out_hbm, src, acc, sem):
+            flops=2 * PER * KMAX * C**3, bytes_accessed=5 << 20, transcendentals=0
+        ),
+    )(idx, pltpu.with_memory_space_constraint(weights, pltpu.HBM), near)
+
+
+def outer_kernel(idx_ref, corr_ref, ls, lm, lb, lh, rs, rm, rb, rh, l3, r3, *refs):
+    partial, wv, (out_hbm, src, acc, sem) = refs[:CHUNKS], refs[CHUNKS : 2 * CHUNKS], refs[2 * CHUNKS :]
     for n, (e, m, b, h) in enumerate(((ls, lm, lb, lh), (rs, rm, rb, rh))):
         at = n * SIDE
         src[pl.ds(at, S)] = e[...]
@@ -440,9 +454,9 @@
 
         def body(t, carry):
             lhs = jnp.concatenate([src[idx_ref[k, t]] for k in range(KMAX)], axis=1)
-            rhs = jnp.concatenate([w_ref[t, k] for k in range(KMAX)], axis=1)
+            rhs = jnp.concatenate([wv[c][t - c * PER, k] for k in range(KMAX)], axis=1)
             got = lax.dot_general(lhs, rhs, NT, preferred_element_type=jnp.float32)
-            acc[t] = (got + part_ref[t]) + corr_ref[...]
+            acc[t] = (got + partial[c][t - c * PER]) + corr_ref[...]
             return carry
 
         lax.fori_loop(c * PER, (c + 1) * PER, body, 0, unroll=4)
@@ -451,11 +465,11 @@
         out_copy(c).wait()
 
 
-def outer_call(idx, weights, corr, parts, partial):
+def outer_call(idx, corr, parts, partial, weights):
     vmem = pl.BlockSpec(memory_space=pltpu.VMEM)
     return pl.pallas_call(
         outer_kernel,
-        in_specs=[pl.BlockSpec(memory_space=pltpu.SMEM)] + [vmem] * (3 + len(parts)),
+        in_specs=[pl.BlockSpec(memory_space=pltpu.SMEM)] + [vmem] * (1 + 2 * CHUNKS + len(parts)),
         out_specs=pl.BlockSpec(memory_space=pltpu.HBM),
         out_shape=jax.ShapeDtypeStruct((ROWS, C, C), jnp.float32),
         scratch_shapes=[
@@ -463,12 +477,12 @@
             pltpu.VMEM((ROWS, C, C), jnp.float32),
             pltpu.SemaphoreType.DMA((CHUNKS,)),
         ],
-        compiler_params=pltpu.CompilerParams(vmem_limit_bytes=14 << 20),
+        compiler_params=pltpu.CompilerParams(vmem_limit_bytes=18 << 20),
         cost_estimate=pl.CostEstimate(
             flops=2 * ROWS * KMAX * C**3, bytes_accessed=4 << 20, transcendentals=0
         ),
         name="outer",
-    )(idx, weights, corr, *parts, partial)
+    )(idx, corr, *parts, *partial, *weights)
 
 
 def tables(source_row, source_block, slot_count, lat, lon):
@@ -521,21 +535,24 @@
     q = tracers.transpose(0, 2, 3, 1).reshape(ROWS, C, C)
     qs = jnp.concatenate([q[:EDGE], q[ROWS - EDGE :]], axis=0)
     ls, rs = lax.ppermute(qs, "lon", ring(1)), lax.ppermute(qs, "lon", ring(-1))
-    pole = jnp.where(lat == 0, q[:E], q[ROWS - E :])
+    qm = q[EDGE : ROWS - EDGE]
+    lm, rm = lax.ppermute(qm, "lon", ring(1)), lax.ppermute(qm, "lon", ring(-1))
+    pole = jnp.where(lat == 0, qs[:E], qs[S - E :])
     l3 = lax.ppermute(pole, both, some(3, POLAR))
     r3 = lax.ppermute(pole, both, some(-3, POLAR))
     sums_idx, near_idx, far_idx, lost = tables(source_row, source_block, slot_count, lat, lon)
     area = latitude_area(lat * ROWS, ROWS)
-    sums = sums_call(sums_idx, area, w)
-    got = [lax.ppermute(sums[d + 3], "lon", ring(d)) for d in (1, -1, 2, -2)]
-    qm = q[EDGE : ROWS - EDGE]
-    lm, rm = lax.ppermute(qm, "lon", ring(1)), lax.ppermute(qm, "lon", ring(-1))
+    to_left, to_right, own_sums, s3m, s3p = sums_call(sums_idx, area, w)
+    cl = lax.ppermute(to_left, "lon", ring(-1))
+    cr = lax.ppermute(to_right, "lon", ring(1))
     up1 = lax.ppermute(jnp.concatenate([v[S - R :] for v in (qs, ls, rs)], axis=0), "lat", UP)
     dn1 = lax.ppermute(jnp.concatenate([v[:R] for v in (qs, ls, rs)], axis=0), "lat", DOWN)
-    at = jnp.where(lat == 0, R, R + ROWS - E).reshape(1).astype(jnp.int32)
-    v = mass_call(
-        area, lost.reshape(1), at, (sums[3], *got, sums[0], sums[6], q, up1, dn1, l3, r3)
-    )
+    at = jnp.where(jnp.arange(NLAT_DEV, dtype=jnp.int32) == lat, R, R + ROWS - E).astype(jnp.int32)
+    v, near = mass_call(
+        area, lost.reshape(1), at,
+        (own_sums, cl, cr, s3m, s3p, q, ls, lm, rs, rm, up1, dn1, l3, r3),
+    )
+    near = pltpu.with_memory_space_constraint(near, pltpu.VMEM)
     for axis, size, bit in (("lat", NLAT_DEV, 1), ("lat", NLAT_DEV, 2), ("lat", NLAT_DEV, 4), ("lon", NLON_DEV, 4), ("lon", NLON_DEV, 8)):
         v = v + swap(v, axis, size, lambda i, bit=bit: i ^ bit)
     y = [swap(v, "lon", NLON_DEV, lambda i, by=by: i // 4 * 4 + (i + by) % 4) for by in (1, 2, 3)]
@@ -554,10 +571,10 @@
     llh = lax.ppermute(beyond[:R], both, some(1, POLAR + NEXT))
     rrh = lax.ppermute(beyond[R:], both, some(-1, POLAR + NEXT))
 
-    partial, wv = inner_call(near_idx, w, (q, ls, lm, rs, rm, up1, dn1))
+    pieces = [inner_call(c, near_idx, w, near) for c in range(CHUNKS)]
+    partial, wv = ([pltpu.with_memory_space_constraint(x, pltpu.VMEM) for x in p] for p in zip(*pieces))
     fixed = outer_call(
-        far_idx, pltpu.with_memory_space_constraint(wv, pltpu.VMEM), corr, (lls, llm, llb, llh, rrs, rrm, rrb, rrh, l3, r3),
-        pltpu.with_memory_space_constraint(partial, pltpu.VMEM),
+        far_idx, corr, (lls, llm, llb, llh, rrs, rrm, rrb, rrh, l3, r3), partial, wv
     )
     return v[1, 0], fixed
 

time: 172 us -> 165 us (0.959)
  waiting for transfers between devices: 69.5 us -> 61.7 us
  starting transfers between devices: 61.5 us -> 55.4 us
  Pallas kernels: 30.1 us -> 36 us
    ppermute x1, waiting for transfers between devices: 12.2 us -> 0.01 us  [usual(): llh = lax.ppermute(beyond[:R], both, some(1, POLAR + NEXT))]
    ppermute x4 -> x2, starting transfers between devices: 11.6 us -> 0.15 us  [the longest x1 0.08 us: usual(): cl = lax.ppermute(to_left, 'lon', ring(-1))]
    ppermute x1, waiting for transfers between devices: 0.01 us -> 8.99 us  [usual(): lax.ppermute(qs, 'lon', ring(1))]
    ppermute x1, waiting for transfers between devices: 7.23 us -> 0.01 us  [usual(): lax.ppermute(qs, 'lon', ring(-1))]
    ppermute x1, starting transfers between devices: 2.28 us -> 7.71 us  [usual(): rrh = lax.ppermute(beyond[R:], both, some(-1, POLAR + NEXT))]
    ppermute x1, waiting for transfers between devices: 0.01 us -> 5.21 us  [usual(): l3 = lax.ppermute(pole, both, some(3, POLAR))]
    ppermute x1, waiting for transfers between devices: 4.55 us -> 0.01 us  [usual(): rrh = lax.ppermute(beyond[R:], both, some(-1, POLAR + NEXT))]
    pallas_call x1 -> x4, Pallas kernels: 10.1 us -> 14.4 us  [inner_call(): pl.pallas_call(functools.partial(inner_kernel, chunk * PER), in_specs=[pl...]
  transfers between devices with their start and end apart: 28 -> 26, of which waited for: 11 -> 11; matrix products, arithmetic and copies ran while one was open for 4% -> 4% of each run, Pallas kernels for 12% -> 13%
where the time goes in v2:
time: 165 us
  waiting for transfers between devices  61.7 us (37%)
  starting transfers between devices  55.4 us (34%)
  Pallas kernels  36 us (22%)
  other arithmetic  5.3 us (3%)
  local copies, waits for them, and re-layouts  4.95 us (3%)
    ppermute x1, waiting for transfers between devices, usual(): cl = lax.ppermute(to_left, 'lon', ring(-1))  19.4 us
    ppermute x8, waiting for transfers between devices, swap(): return lax.ppermute(v, axis, [(i, to(i)) for i in range(size)])  19.1 us
    ppermute x4, starting transfers between devices, usual(): lax.ppermute(x, both, some(d, POLAR))  16.4 us
    pallas_call x4, Pallas kernels, inner_call(): pl.pallas_call(functools.partial(inner_kernel, chunk * PER), in_specs=[pl...  14.4 us
    pallas_call x1, Pallas kernels, outer_call(): pl.pallas_call(outer_kernel, in_specs=[pl.BlockSpec(memory_space=pltpu.SM...  9 us
    ppermute x1, waiting for transfers between devices, usual(): lax.ppermute(qs, 'lon', ring(1))  8.99 us
    ppermute x1, starting transfers between devices, usual(): rrh = lax.ppermute(beyond[R:], both, some(-1, POLAR + NEXT))  7.71 us
    pallas_call x1, Pallas kernels, sums_call(): pl.pallas_call(sums_kernel, in_specs=[smem, smem, pl.BlockSpec(memory_spa...  7.21 us
  transfers between devices with their start and end apart: 26, of which 11 were waited for; matrix products, arithmetic and copies ran while one was open for 4% of the time, Pallas kernels for 13%

profile of v2, /device:TPU:0, one launch (start us, length us, event | category | flops | bytes accessed | tf_op | source)
XLA Modules:
  0.0 164.7 jit_solution(1825328149662839503)
XLA Ops:
  0.0 1.8 %fusion.46 = (bf16[16,32,4,128]{3,2,1,0:T(4,128)(2,1)S(1)}, bf16[16,32,4,128]{3,2,1,0:T(4,128)(2,1)S(1)}) fusion(bf16[64,32,4,128]{3,2,1,0:T(4,128)(2,1)} %bitcast.165), kind=kLoop, calls=%fused_computation.101 | loop fusion | bytes 2097152 | tf_op jit(solution)/shard_map/slice | solution.py:536
  1.8 1.1 pad_maximum_fusion.5
  2.8 1.7 %collective-permute-start.16 = (bf16[32,128,128]{2,1,0:T(8,128)(2,1)}, bf16[32,128,128]{2,1,0:T(8,128)(2,1)S(1)}, u32[]{:S(2)}, u32[]{:S(2)}) collective-permute-start(bf16[32,128,128]{2,1,0:T(8,128)(2,1)} %pad_maximum_fusion.5), channel_id=1, source_target_pairs={{0,1},{1,2},{2,3},{3,4},{4,5},{5,6},{6,7},{7,8},{8,9},{9,10},{10,1... | collective-permute-start | bytes 3145736 | tf_op jit(solution)/shard_map/ppermute | solution.py:537
  4.5 4.9 %collective-permute-start.18 = (bf16[32,128,128]{2,1,0:T(8,128)(2,1)}, bf16[32,128,128]{2,1,0:T(8,128)(2,1)S(1)}, u32[]{:S(2)}, u32[]{:S(2)}) collective-permute-start(bf16[32,128,128]{2,1,0:T(8,128)(2,1)} %pad_maximum_fusion.5), channel_id=1, source_target_pairs={{0,15},{1,0},{2,1},{3,2},{4,3},{5,4},{6,5},{7,6},{8,7},{9,8},{10,9... | collective-permute-start | bytes 3145736 | tf_op jit(solution)/shard_map/ppermute | solution.py:537
  9.5 1.4 slice.200
  10.9 5.3 %collective-permute-start.19 = (bf16[32,128,128]{2,1,0:T(8,128)(2,1)}, bf16[32,128,128]{2,1,0:T(8,128)(2,1)}, u32[]{:S(2)}, u32[]{:S(2)}) collective-permute-start(bf16[32,128,128]{2,1,0:T(8,128)(2,1)} %bitcast.31), channel_id=1, source_target_pairs={{0,15},{1,0},{2,1},{3,2},{4,3},{5,4},{6,5},{7,6},{8,7},{9,8},{10,9... | collective-permute-start | bytes 3145736 | tf_op jit(solution)/shard_map/ppermute | solution.py:539
  16.3 7.2 %sums.1 = (f32[144,128]{1,0:T(8,128)S(1)}, f32[144,128]{1,0:T(8,128)S(1)}, f32[72,128]{1,0:T(8,128)S(1)}, f32[72,128]{1,0:T(8,128)S(1)}, f32[72,128]{1,0:T(8,128)S(1)}) custom-call(s32[8,64]{1,0:T(8,128)S(1)} %get-tuple-element.129.idx_ref, f32[64]{0:T(128)S(1)} %add_cosine_fusion.1.area_ref, bf16[64,8,128,128]{3,2,1,0:T(8,128)(2,1)} %bitcast.157), custom_call_target="tpu_custom_call" | custom-call | flops 20000000 | bytes 17825792 | tf_op jit(solution)/shard_map/sums/pallas_call | solution.py:321
  23.5 1.1 fusion.45
  24.6 0.1 collective-permute-start.14
  24.7 9.0 %collective-permute-done.16.ls = bf16[32,128,128]{2,1,0:T(8,128)(2,1)S(1)} collective-permute-done((bf16[32,128,128]{2,1,0:T(8,128)(2,1)}, bf16[32,128,128]{2,1,0:T(8,128)(2,1)S(1)}, u32[]{:S(2)}, u32[]{:S(2)}) %collective-permute-start.16) | collective-permute-done | bytes 1048608 | tf_op jit(solution)/shard_map/ppermute | solution.py:537
  33.8 0.8 pad_maximum_fusion.6
  34.6 0.8 pad_maximum_fusion.7
  35.4 1.3 collective-permute-start.20
  36.7 19.4 %collective-permute-done.14.cl = f32[144,128]{1,0:T(8,128)S(1)} collective-permute-done((f32[144,128]{1,0:T(8,128)S(1)}, f32[144,128]{1,0:T(8,128)S(1)}, u32[]{:S(2)}, u32[]{:S(2)}) %collective-permute-start.14) | collective-permute-done | bytes 73760 | tf_op jit(solution)/shard_map/ppermute | solution.py:546
  56.1 1.3 collective-permute-start.21
  57.4 1.7 %slice_select_fusion.5 = bf16[5,32,4,128]{3,2,1,0:T(4,128)(2,1)} fusion(bf16[64,32,4,128]{3,2,1,0:T(4,128)(2,1)} %bitcast.167, pred[]{:T(512)S(6)} %eq.39), kind=kLoop, calls=%fused_computation.45 | loop fusion | flops 81920 | bytes 491521 | tf_op jit(solution)/shard_map/jit(_where)/select_n | solution.py:540
  59.2 4.3 %collective-permute-start.22 = (bf16[5,128,128]{2,1,0:T(8,128)(2,1)}, bf16[5,128,128]{2,1,0:T(8,128)(2,1)S(1)}, u32[]{:S(2)}, u32[]{:S(2)}) collective-permute-start(bf16[5,128,128]{2,1,0:T(8,128)(2,1)} %bitcast.34), channel_id=1, source_target_pairs={{0,3},{1,4},{2,5},{3,6},{4,7},{5,8},{6,9},{7,10},{8,11},{9,12},{10... | collective-permute-start | bytes 491528 | tf_op jit(solution)/shard_map/ppermute | solution.py:541
  63.5 5.2 %collective-permute-done.22.l3 = bf16[5,128,128]{2,1,0:T(8,128)(2,1)S(1)} collective-permute-done((bf16[5,128,128]{2,1,0:T(8,128)(2,1)}, bf16[5,128,128]{2,1,0:T(8,128)(2,1)S(1)}, u32[]{:S(2)}, u32[]{:S(2)}) %collective-permute-start.22) | collective-permute-done | bytes 163872 | tf_op jit(solution)/shard_map/ppermute | solution.py:541
  68.7 3.0 %collective-permute-start.23 = (bf16[5,128,128]{2,1,0:T(8,128)(2,1)}, bf16[5,128,128]{2,1,0:T(8,128)(2,1)S(1)}, u32[]{:S(2)}, u32[]{:S(2)}) collective-permute-start(bf16[5,128,128]{2,1,0:T(8,128)(2,1)} %bitcast.34), channel_id=1, source_target_pairs={{0,13},{1,14},{2,15},{3,0},{4,1},{5,2},{6,3},{7,4},{8,5},{9,6},{10... | collective-permute-start | bytes 491528 | tf_op jit(solution)/shard_map/ppermute | solution.py:542
  71.7 0.7 convert_reduce_fusion.1
  72.4 4.9 %collective-permute-done.23.r3 = bf16[5,128,128]{2,1,0:T(8,128)(2,1)S(1)} collective-permute-done((bf16[5,128,128]{2,1,0:T(8,128)(2,1)}, bf16[5,128,128]{2,1,0:T(8,128)(2,1)S(1)}, u32[]{:S(2)}, u32[]{:S(2)}) %collective-permute-start.23) | collective-permute-done | bytes 163872 | tf_op jit(solution)/shard_map/ppermute | solution.py:542
  77.3 5.4 %mass.1 = (f32[8,128]{1,0:T(8,128)S(1)}, bf16[217,128,128]{2,1,0:T(8,128)(2,1)S(1)}) custom-call(f32[64]{0:T(128)S(1)} %add_cosine_fusion.1.area_ref, f32[1]{0:T(128)} %bitcast.24.lost_ref, s32[8]{0:T(128)S(1)} %compare_select_fusion.1.at_ref, f32[72,128]{1,0:T(8,128)S(1)} %get-tuple-element.59.c0, f32[144,128]{1,0:T(8,128)S(1)} %collective-permute-done.14.cl, ...), custom_call_target="tpu_custom_call" | custom-call | flops 9000000 | bytes 3145728 | tf_op jit(solution)/shard_map/mass/pallas_call | solution.py:375
  82.8 1.9 %collective-permute-start.35 = (bf16[4,128,128]{2,1,0:T(8,128)(2,1)S(1)}, bf16[4,128,128]{2,1,0:T(8,128)(2,1)S(1)}, u32[]{:S(2)}, u32[]{:S(2)}) collective-permute-start(bf16[4,128,128]{2,1,0:T(8,128)(2,1)S(1)} %get-tuple-element.127), channel_id=1, source_target_pairs={{0,1},{1,2},{2,3},{3,4},{4,5},{5,6},{6,7},{7,8},{8,9},{9,10},{10,1... | collective-permute-start | bytes 393224 | tf_op jit(solution)/shard_map/ppermute | solution.py:571
  84.7 7.7 %collective-permute-start.39 = (bf16[4,128,128]{2,1,0:T(8,128)(2,1)S(1)}, bf16[4,128,128]{2,1,0:T(8,128)(2,1)S(1)}, u32[]{:S(2)}, u32[]{:S(2)}) collective-permute-start(bf16[4,128,128]{2,1,0:T(8,128)(2,1)S(1)} %get-tuple-element.126), channel_id=1, source_target_pairs={{0,15},{1,0},{2,1},{3,2},{4,3},{5,4},{6,5},{7,6},{8,7},{9,8},{10,9... | collective-permute-start | bytes 393224 | tf_op jit(solution)/shard_map/ppermute | solution.py:572
  92.5 0.7 collective-permute-start.34
  93.3 0.1 collective-permute-start.25
  93.3 3.6 %collective-permute-done.25 = f32[8,128]{1,0:T(8,128)S(1)} collective-permute-done((f32[8,128]{1,0:T(8,128)S(1)}, f32[8,128]{1,0:T(8,128)S(1)}, u32[]{:S(2)}, u32[]{:S(2)}) %collective-permute-start.25) | collective-permute-done | bytes 4128 | tf_op jit(solution)/shard_map/ppermute | solution.py:517
  96.9 2.3 %collective-permute-start.26 = (f32[8,128]{1,0:T(8,128)S(1)}, f32[8,128]{1,0:T(8,128)S(1)}, u32[]{:S(2)}, u32[]{:S(2)}) collective-permute-start(f32[8,128]{1,0:T(8,128)S(1)} %add.225), channel_id=1, source_target_pairs={{0,64},{16,80},{32,96},{48,112},{64,0},{80,16},{96,32},{112,48},{1... | collective-permute-start | bytes 12296 | tf_op jit(solution)/shard_map/ppermute | solution.py:517
  99.2 2.8 %collective-permute-done.26 = f32[8,128]{1,0:T(8,128)S(1)} collective-permute-done((f32[8,128]{1,0:T(8,128)S(1)}, f32[8,128]{1,0:T(8,128)S(1)}, u32[]{:S(2)}, u32[]{:S(2)}) %collective-permute-start.26) | collective-permute-done | bytes 4128 | tf_op jit(solution)/shard_map/ppermute | solution.py:517
  102.1 3.6 %collective-permute-done.27 = f32[8,128]{1,0:T(8,128)S(1)} collective-permute-done((f32[8,128]{1,0:T(8,128)S(1)}, f32[8,128]{1,0:T(8,128)S(1)}, u32[]{:S(2)}, u32[]{:S(2)}) %collective-permute-start.27) | collective-permute-done | bytes 4128 | tf_op jit(solution)/shard_map/ppermute | solution.py:517
  105.7 0.2 collective-permute-start.28
  105.9 4.9 %collective-permute-done.28 = f32[8,128]{1,0:T(8,128)S(1)} collective-permute-done((f32[8,128]{1,0:T(8,128)S(1)}, f32[8,128]{1,0:T(8,128)S(1)}, u32[]{:S(2)}, u32[]{:S(2)}) %collective-permute-start.28) | collective-permute-done | bytes 4128 | tf_op jit(solution)/shard_map/ppermute | solution.py:517
  110.8 3.2 %collective-permute-start.30 = (f32[8,128]{1,0:T(8,128)S(1)}, f32[8,128]{1,0:T(8,128)S(1)}, u32[]{:S(2)}, u32[]{:S(2)}) collective-permute-start(f32[8,128]{1,0:T(8,128)S(1)} %add.228), channel_id=1, source_target_pairs={{0,3},{1,0},{2,1},{3,2},{4,7},{5,4},{6,5},{7,6},{8,11},{9,8},{10,9... | collective-permute-start | bytes 12296 | tf_op jit(solution)/shard_map/ppermute | solution.py:517
  114.0 1.6 collective-permute-done.29
  115.6 2.5 %collective-permute-start.32 = (bf16[32,128,128]{2,1,0:T(8,128)(2,1)S(1)}, bf16[32,128,128]{2,1,0:T(8,128)(2,1)S(1)}, u32[]{:S(2)}, u32[]{:S(2)}) collective-permute-start(bf16[32,128,128]{2,1,0:T(8,128)(2,1)S(1)} %collective-permute-done.16.ls), channel_id=1, source_target_pairs={{0,1},{1,2},{2,3},{3,4},{4,5},{5,6},{6,7},{7,8},{8,9},{9,10},{10,1... | collective-permute-start | bytes 3145736 | tf_op jit(solution)/shard_map/ppermute | solution.py:562
  118.1 2.6 %collective-permute-done.31 = f32[8,128]{1,0:T(8,128)S(1)} collective-permute-done((f32[8,128]{1,0:T(8,128)S(1)}, f32[8,128]{1,0:T(8,128)S(1)}, u32[]{:S(2)}, u32[]{:S(2)}) %collective-permute-start.31) | collective-permute-done | bytes 4128 | tf_op jit(solution)/shard_map/ppermute | solution.py:517
  120.7 4.8 %collective-permute-start.36 = (bf16[32,128,128]{2,1,0:T(8,128)(2,1)S(1)}, bf16[32,128,128]{2,1,0:T(8,128)(2,1)S(1)}, u32[]{:S(2)}, u32[]{:S(2)}) collective-permute-start(bf16[32,128,128]{2,1,0:T(8,128)(2,1)S(1)} %collective-permute-done.18.rs), channel_id=1, source_target_pairs={{0,15},{1,0},{2,1},{3,2},{4,3},{5,4},{6,5},{7,6},{8,7},{9,8},{10,9... | collective-permute-start | bytes 3145736 | tf_op jit(solution)/shard_map/ppermute | solution.py:562
  125.5 1.9 %collective-permute-start.33 = (bf16[32,128,128]{2,1,0:T(8,128)(2,1)}, bf16[32,128,128]{2,1,0:T(8,128)(2,1)S(1)}, u32[]{:S(2)}, u32[]{:S(2)}) collective-permute-start(bf16[32,128,128]{2,1,0:T(8,128)(2,1)} %collective-permute-done.17.lm), channel_id=1, source_target_pairs={{0,1},{1,2},{2,3},{3,4},{4,5},{5,6},{6,7},{7,8},{8,9},{9,10},{10,1... | collective-permute-start | bytes 3145736 | tf_op jit(solution)/shard_map/ppermute | solution.py:563
  127.4 7.2 %collective-permute-start.37 = (bf16[32,128,128]{2,1,0:T(8,128)(2,1)}, bf16[32,128,128]{2,1,0:T(8,128)(2,1)S(1)}, u32[]{:S(2)}, u32[]{:S(2)}) collective-permute-start(bf16[32,128,128]{2,1,0:T(8,128)(2,1)} %collective-permute-done.19.rm), channel_id=1, source_target_pairs={{0,15},{1,0},{2,1},{3,2},{4,3},{5,4},{6,5},{7,6},{8,7},{9,8},{10,9... | collective-permute-start | bytes 3145736 | tf_op jit(solution)/shard_map/ppermute | solution.py:563
  134.8 3.6 %shard_map.55 = (f32[16,128,128]{2,1,0:T(8,128)S(1)}, bf16[16,8,128,128]{3,2,1,0:T(8,128)(2,1)S(1)}) custom-call(s32[8,64]{1,0:T(8,128)S(1)} %get-tuple-element.128.idx_ref, bf16[64,8,128,128]{3,2,1,0:T(8,128)(2,1)} %bitcast.158, bf16[217,128,128]{2,1,0:T(8,128)(2,1)S(1)} %get-tuple-element.65.src), custom_call_target="tpu_custom_call" | custom-call | flops 536870912 | bytes 5242880 | tf_op jit(solution)/shard_map/pallas_call | solution.py:419
  138.4 3.6 %shard_map.56 = (f32[16,128,128]{2,1,0:T(8,128)S(1)}, bf16[16,8,128,128]{3,2,1,0:T(8,128)(2,1)S(1)}) custom-call(s32[8,64]{1,0:T(8,128)S(1)} %get-tuple-element.128.idx_ref, bf16[64,8,128,128]{3,2,1,0:T(8,128)(2,1)} %bitcast.159, bf16[217,128,128]{2,1,0:T(8,128)(2,1)S(1)} %get-tuple-element.65.src), custom_call_target="tpu_custom_call" | custom-call | flops 536870912 | bytes 5242880 | tf_op jit(solution)/shard_map/pallas_call | solution.py:419
  142.0 0.9 collective-permute-start.38
  142.9 3.6 %shard_map.57 = (f32[16,128,128]{2,1,0:T(8,128)S(1)}, bf16[16,8,128,128]{3,2,1,0:T(8,128)(2,1)S(1)}) custom-call(s32[8,64]{1,0:T(8,128)S(1)} %get-tuple-element.128.idx_ref, bf16[64,8,128,128]{3,2,1,0:T(8,128)(2,1)} %bitcast.160, bf16[217,128,128]{2,1,0:T(8,128)(2,1)S(1)} %get-tuple-element.65.src), custom_call_target="tpu_custom_call" | custom-call | flops 536870912 | bytes 5242880 | tf_op jit(solution)/shard_map/pallas_call | solution.py:419
  146.5 3.6 %shard_map.58 = (f32[16,128,128]{2,1,0:T(8,128)S(1)}, bf16[16,8,128,128]{3,2,1,0:T(8,128)(2,1)S(1)}) custom-call(s32[8,64]{1,0:T(8,128)S(1)} %get-tuple-element.128.idx_ref, bf16[64,8,128,128]{3,2,1,0:T(8,128)(2,1)} %bitcast.161, bf16[217,128,128]{2,1,0:T(8,128)(2,1)S(1)} %get-tuple-element.65.src), custom_call_target="tpu_custom_call" | custom-call | flops 536870912 | bytes 5242880 | tf_op jit(solution)/shard_map/pallas_call | solution.py:419
  150.1 0.6 slice.171
  150.7 4.0 %collective-permute-done.37.rm = bf16[32,128,128]{2,1,0:T(8,128)(2,1)S(1)} collective-permute-done((bf16[32,128,128]{2,1,0:T(8,128)(2,1)}, bf16[32,128,128]{2,1,0:T(8,128)(2,1)S(1)}, u32[]{:S(2)}, u32[]{:S(2)}) %collective-permute-start.37) | collective-permute-done | bytes 1048608 | tf_op jit(solution)/shard_map/ppermute | solution.py:563
  154.8 9.0 %outer.1 = f32[64,128,128]{2,1,0:T(8,128)} custom-call(s32[8,64]{1,0:T(8,128)S(1)} %get-tuple-element.130.idx_ref, f32[128,128]{1,0:T(8,128)S(1)} %broadcast_in_dim.45.corr_ref, bf16[32,128,128]{2,1,0:T(8,128)(2,1)S(1)} %collective-permute-done.32.ls, bf16[32,128,128]{2,1,0:T(8,128)(2,1)S(1)} %collective-permute-done.33.lm, ...), custom_call_target="tpu_custom_call" | custom-call | flops 2147483648 | bytes 4194304 | tf_op jit(solution)/shard_map/outer/pallas_call | solution.py:470
  163.8 0.7 while.9
  (46 shorter events, 0.5 us)
Async XLA Ops:
  0.0 9.5 %copy-start.1 = (bf16[64,128,32,4]{1,3,2,0:T(4,128)(2,1)S(1)}, bf16[64,128,32,4]{1,3,2,0:T(4,128)(2,1)}, u32[]{:S(2)}) copy-start(bf16[64,128,32,4]{1,3,2,0:T(4,128)(2,1)} %param.7) | copy-start | bytes 6291460
  0.0 16.3 %copy-start.7 = (s32[64,1]{0,1:T(1,128)S(1)}, s32[64,1]{0,1:T(1,128)}, u32[]{:S(2)}) copy-start(s32[64,1]{0,1:T(1,128)} %param.11) | copy-start | bytes 772
  0.0 16.3 %copy-start.5 = (s32[64,1,8]{0,2,1:T(8,128)S(1)}, s32[64,1,8]{0,2,1:T(8,128)}, u32[]{:S(2)}) copy-start(s32[64,1,8]{0,2,1:T(8,128)} %param.10) | copy-start | bytes 6148
  0.0 16.3 %copy-start.3 = (s32[64,1,8]{0,2,1:T(8,128)S(1)}, s32[64,1,8]{0,2,1:T(8,128)}, u32[]{:S(2)}) copy-start(s32[64,1,8]{0,2,1:T(8,128)} %param.9) | copy-start | bytes 6148
  2.8 30.8 %collective-permute-start.16 = (bf16[32,128,128]{2,1,0:T(8,128)(2,1)}, bf16[32,128,128]{2,1,0:T(8,128)(2,1)S(1)}, u32[]{:S(2)}, u32[]{:S(2)}) collective-permute-start(bf16[32,128,128]{2,1,0:T(8,128)(2,1)} %pad_maximum_fusion.5), channel_id=1, source_target_pairs={{0,1},{1,2},{2,3},{3,4},{4,5},{5,6},{6,7},{7,8},{8,9},{9,10},{10,1... | collective-permute-start | bytes 3145736 | tf_op jit(solution)/shard_map/ppermute | solution.py:537
  4.5 29.2 %collective-permute-start.18 = (bf16[32,128,128]{2,1,0:T(8,128)(2,1)}, bf16[32,128,128]{2,1,0:T(8,128)(2,1)S(1)}, u32[]{:S(2)}, u32[]{:S(2)}) collective-permute-start(bf16[32,128,128]{2,1,0:T(8,128)(2,1)} %pad_maximum_fusion.5), channel_id=1, source_target_pairs={{0,15},{1,0},{2,1},{3,2},{4,3},{5,4},{6,5},{7,6},{8,7},{9,8},{10,9... | collective-permute-start | bytes 3145736 | tf_op jit(solution)/shard_map/ppermute | solution.py:537
  10.9 66.5 %collective-permute-start.17 = (bf16[32,128,128]{2,1,0:T(8,128)(2,1)}, bf16[32,128,128]{2,1,0:T(8,128)(2,1)}, u32[]{:S(2)}, u32[]{:S(2)}) collective-permute-start(bf16[32,128,128]{2,1,0:T(8,128)(2,1)} %bitcast.31), channel_id=1, source_target_pairs={{0,1},{1,2},{2,3},{3,4},{4,5},{5,6},{6,7},{7,8},{8,9},{9,10},{10,1... | collective-permute-start | bytes 3145736 | tf_op jit(solution)/shard_map/ppermute | solution.py:539
  10.9 66.5 %collective-permute-start.19 = (bf16[32,128,128]{2,1,0:T(8,128)(2,1)}, bf16[32,128,128]{2,1,0:T(8,128)(2,1)}, u32[]{:S(2)}, u32[]{:S(2)}) collective-permute-start(bf16[32,128,128]{2,1,0:T(8,128)(2,1)} %bitcast.31), channel_id=1, source_target_pairs={{0,15},{1,0},{2,1},{3,2},{4,3},{5,4},{6,5},{7,6},{8,7},{9,8},{10,9... | collective-permute-start | bytes 3145736 | tf_op jit(solution)/shard_map/ppermute | solution.py:539
  24.6 31.5 %collective-permute-start.14 = (f32[144,128]{1,0:T(8,128)S(1)}, f32[144,128]{1,0:T(8,128)S(1)}, u32[]{:S(2)}, u32[]{:S(2)}) collective-permute-start(f32[144,128]{1,0:T(8,128)S(1)} %get-tuple-element.60), channel_id=1, source_target_pairs={{0,15},{1,0},{2,1},{3,2},{4,3},{5,4},{6,5},{7,6},{8,7},{9,8},{10,9... | collective-permute-start | bytes 221192 | tf_op jit(solution)/shard_map/ppermute | solution.py:546
  33.7 25.5 %collective-permute-start.15 = (f32[144,128]{1,0:T(8,128)S(1)}, f32[144,128]{1,0:T(8,128)S(1)}, u32[]{:S(2)}, u32[]{:S(2)}) collective-permute-start(f32[144,128]{1,0:T(8,128)S(1)} %get-tuple-element.61), channel_id=1, source_target_pairs={{0,1},{1,2},{2,3},{3,4},{4,5},{5,6},{6,7},{7,8},{8,9},{9,10},{10,1... | collective-permute-start | bytes 221192 | tf_op jit(solution)/shard_map/ppermute | solution.py:547
  35.4 41.9 %collective-permute-start.20 = (bf16[12,128,128]{2,1,0:T(8,128)(2,1)}, bf16[12,128,128]{2,1,0:T(8,128)(2,1)S(1)}, u32[]{:S(2)}, u32[]{:S(2)}) collective-permute-start(bf16[12,128,128]{2,1,0:T(8,128)(2,1)} %pad_maximum_fusion.6), channel_id=1, source_target_pairs={{0,16},{16,32},{32,48},{48,64},{64,80},{80,96},{96,112},{1,17},{17... | collective-permute-start | bytes 1179656 | tf_op jit(solution)/shard_map/ppermute | solution.py:548
  56.1 21.2 %collective-permute-start.21 = (bf16[12,128,128]{2,1,0:T(8,128)(2,1)}, bf16[12,128,128]{2,1,0:T(8,128)(2,1)S(1)}, u32[]{:S(2)}, u32[]{:S(2)}) collective-permute-start(bf16[12,128,128]{2,1,0:T(8,128)(2,1)} %pad_maximum_fusion.7), channel_id=1, source_target_pairs={{16,0},{32,16},{48,32},{64,48},{80,64},{96,80},{112,96},{17,1},{33... | collective-permute-start | bytes 1179656 | tf_op jit(solution)/shard_map/ppermute | solution.py:549
  59.2 9.5 %collective-permute-start.22 = (bf16[5,128,128]{2,1,0:T(8,128)(2,1)}, bf16[5,128,128]{2,1,0:T(8,128)(2,1)S(1)}, u32[]{:S(2)}, u32[]{:S(2)}) collective-permute-start(bf16[5,128,128]{2,1,0:T(8,128)(2,1)} %bitcast.34), channel_id=1, source_target_pairs={{0,3},{1,4},{2,5},{3,6},{4,7},{5,8},{6,9},{7,10},{8,11},{9,12},{10... | collective-permute-start | bytes 491528 | tf_op jit(solution)/shard_map/ppermute | solution.py:541
  68.7 8.6 %collective-permute-start.23 = (bf16[5,128,128]{2,1,0:T(8,128)(2,1)}, bf16[5,128,128]{2,1,0:T(8,128)(2,1)S(1)}, u32[]{:S(2)}, u32[]{:S(2)}) collective-permute-start(bf16[5,128,128]{2,1,0:T(8,128)(2,1)} %bitcast.34), channel_id=1, source_target_pairs={{0,13},{1,14},{2,15},{3,0},{4,1},{5,2},{6,3},{7,4},{8,5},{9,6},{10... | collective-permute-start | bytes 491528 | tf_op jit(solution)/shard_map/ppermute | solution.py:542
  82.7 10.5 %collective-permute-start.24 = (f32[8,128]{1,0:T(8,128)S(1)}, f32[8,128]{1,0:T(8,128)S(1)}, u32[]{:S(2)}, u32[]{:S(2)}) collective-permute-start(f32[8,128]{1,0:T(8,128)S(1)} %get-tuple-element.64), channel_id=1, source_target_pairs={{0,16},{16,0},{32,48},{48,32},{64,80},{80,64},{96,112},{112,96},{1... | collective-permute-start | bytes 12296 | tf_op jit(solution)/shard_map/ppermute | solution.py:517
  82.8 42.7 %collective-permute-start.35 = (bf16[4,128,128]{2,1,0:T(8,128)(2,1)S(1)}, bf16[4,128,128]{2,1,0:T(8,128)(2,1)S(1)}, u32[]{:S(2)}, u32[]{:S(2)}) collective-permute-start(bf16[4,128,128]{2,1,0:T(8,128)(2,1)S(1)} %get-tuple-element.127), channel_id=1, source_target_pairs={{0,1},{1,2},{2,3},{3,4},{4,5},{5,6},{6,7},{7,8},{8,9},{9,10},{10,1... | collective-permute-start | bytes 393224 | tf_op jit(solution)/shard_map/ppermute | solution.py:571
  84.7 42.7 %collective-permute-start.39 = (bf16[4,128,128]{2,1,0:T(8,128)(2,1)S(1)}, bf16[4,128,128]{2,1,0:T(8,128)(2,1)S(1)}, u32[]{:S(2)}, u32[]{:S(2)}) collective-permute-start(bf16[4,128,128]{2,1,0:T(8,128)(2,1)S(1)} %get-tuple-element.126), channel_id=1, source_target_pairs={{0,15},{1,0},{2,1},{3,2},{4,3},{5,4},{6,5},{7,6},{8,7},{9,8},{10,9... | collective-permute-start | bytes 393224 | tf_op jit(solution)/shard_map/ppermute | solution.py:572
  92.5 49.5 %collective-permute-start.34 = (bf16[16,128,128]{2,1,0:T(8,128)(2,1)S(1)}, bf16[16,128,128]{2,1,0:T(8,128)(2,1)S(1)}, u32[]{:S(2)}, u32[]{:S(2)}) collective-permute-start(bf16[16,128,128]{2,1,0:T(8,128)(2,1)S(1)} %slice_select_fusion.3), channel_id=1, source_target_pairs={{16,17},{17,18},{18,19},{19,20},{20,21},{21,22},{22,23},{23,24},{2... | collective-permute-start | bytes 1572872 | tf_op jit(solution)/shard_map/ppermute | solution.py:568
  93.3 3.7 %collective-permute-start.25 = (f32[8,128]{1,0:T(8,128)S(1)}, f32[8,128]{1,0:T(8,128)S(1)}, u32[]{:S(2)}, u32[]{:S(2)}) collective-permute-start(f32[8,128]{1,0:T(8,128)S(1)} %add.224), channel_id=1, source_target_pairs={{0,32},{16,48},{32,0},{48,16},{64,96},{80,112},{96,64},{112,80},{1... | collective-permute-start | bytes 12296 | tf_op jit(solution)/shard_map/ppermute | solution.py:517
  96.9 5.1 %collective-permute-start.26 = (f32[8,128]{1,0:T(8,128)S(1)}, f32[8,128]{1,0:T(8,128)S(1)}, u32[]{:S(2)}, u32[]{:S(2)}) collective-permute-start(f32[8,128]{1,0:T(8,128)S(1)} %add.225), channel_id=1, source_target_pairs={{0,64},{16,80},{32,96},{48,112},{64,0},{80,16},{96,32},{112,48},{1... | collective-permute-start | bytes 12296 | tf_op jit(solution)/shard_map/ppermute | solution.py:517
  102.1 3.6 %collective-permute-start.27 = (f32[8,128]{1,0:T(8,128)S(1)}, f32[8,128]{1,0:T(8,128)S(1)}, u32[]{:S(2)}, u32[]{:S(2)}) collective-permute-start(f32[8,128]{1,0:T(8,128)S(1)} %add.226), channel_id=1, source_target_pairs={{0,4},{1,5},{2,6},{3,7},{4,0},{5,1},{6,2},{7,3},{8,12},{9,13},{10,... | collective-permute-start | bytes 12296 | tf_op jit(solution)/shard_map/ppermute | solution.py:517
  105.7 5.1 %collective-permute-start.28 = (f32[8,128]{1,0:T(8,128)S(1)}, f32[8,128]{1,0:T(8,128)S(1)}, u32[]{:S(2)}, u32[]{:S(2)}) collective-permute-start(f32[8,128]{1,0:T(8,128)S(1)} %add.227), channel_id=1, source_target_pairs={{0,8},{1,9},{2,10},{3,11},{4,12},{5,13},{6,14},{7,15},{8,0},{9,1},... | collective-permute-start | bytes 12296 | tf_op jit(solution)/shard_map/ppermute | solution.py:517
  110.8 4.8 %collective-permute-start.29 = (f32[8,128]{1,0:T(8,128)S(1)}, f32[8,128]{1,0:T(8,128)S(1)}, u32[]{:S(2)}, u32[]{:S(2)}) collective-permute-start(f32[8,128]{1,0:T(8,128)S(1)} %add.228), channel_id=1, source_target_pairs={{0,1},{1,2},{2,3},{3,0},{4,5},{5,6},{6,7},{7,4},{8,9},{9,10},{10,1... | collective-permute-start | bytes 12296 | tf_op jit(solution)/shard_map/ppermute | solution.py:517
  110.8 4.8 %collective-permute-start.30 = (f32[8,128]{1,0:T(8,128)S(1)}, f32[8,128]{1,0:T(8,128)S(1)}, u32[]{:S(2)}, u32[]{:S(2)}) collective-permute-start(f32[8,128]{1,0:T(8,128)S(1)} %add.228), channel_id=1, source_target_pairs={{0,3},{1,0},{2,1},{3,2},{4,7},{5,4},{6,5},{7,6},{8,11},{9,8},{10,9... | collective-permute-start | bytes 12296 | tf_op jit(solution)/shard_map/ppermute | solution.py:517
  115.6 5.1 %collective-permute-start.31 = (f32[8,128]{1,0:T(8,128)S(1)}, f32[8,128]{1,0:T(8,128)S(1)}, u32[]{:S(2)}, u32[]{:S(2)}) collective-permute-start(f32[8,128]{1,0:T(8,128)S(1)} %add.228), channel_id=1, source_target_pairs={{0,2},{1,3},{2,0},{3,1},{4,6},{5,7},{6,4},{7,5},{8,10},{9,11},{10,... | collective-permute-start | bytes 12296 | tf_op jit(solution)/shard_map/ppermute | solution.py:517
  115.6 35.1 %collective-permute-start.32 = (bf16[32,128,128]{2,1,0:T(8,128)(2,1)S(1)}, bf16[32,128,128]{2,1,0:T(8,128)(2,1)S(1)}, u32[]{:S(2)}, u32[]{:S(2)}) collective-permute-start(bf16[32,128,128]{2,1,0:T(8,128)(2,1)S(1)} %collective-permute-done.16.ls), channel_id=1, source_target_pairs={{0,1},{1,2},{2,3},{3,4},{4,5},{5,6},{6,7},{7,8},{8,9},{9,10},{10,1... | collective-permute-start | bytes 3145736 | tf_op jit(solution)/shard_map/ppermute | solution.py:562
  120.7 30.0 %collective-permute-start.36 = (bf16[32,128,128]{2,1,0:T(8,128)(2,1)S(1)}, bf16[32,128,128]{2,1,0:T(8,128)(2,1)S(1)}, u32[]{:S(2)}, u32[]{:S(2)}) collective-permute-start(bf16[32,128,128]{2,1,0:T(8,128)(2,1)S(1)} %collective-permute-done.18.rs), channel_id=1, source_target_pairs={{0,15},{1,0},{2,1},{3,2},{4,3},{5,4},{6,5},{7,6},{8,7},{9,8},{10,9... | collective-permute-start | bytes 3145736 | tf_op jit(solution)/shard_map/ppermute | solution.py:562
  125.5 25.2 %collective-permute-start.33 = (bf16[32,128,128]{2,1,0:T(8,128)(2,1)}, bf16[32,128,128]{2,1,0:T(8,128)(2,1)S(1)}, u32[]{:S(2)}, u32[]{:S(2)}) collective-permute-start(bf16[32,128,128]{2,1,0:T(8,128)(2,1)} %collective-permute-done.17.lm), channel_id=1, source_target_pairs={{0,1},{1,2},{2,3},{3,4},{4,5},{5,6},{6,7},{7,8},{8,9},{9,10},{10,1... | collective-permute-start | bytes 3145736 | tf_op jit(solution)/shard_map/ppermute | solution.py:563
  127.4 27.3 %collective-permute-start.37 = (bf16[32,128,128]{2,1,0:T(8,128)(2,1)}, bf16[32,128,128]{2,1,0:T(8,128)(2,1)S(1)}, u32[]{:S(2)}, u32[]{:S(2)}) collective-permute-start(bf16[32,128,128]{2,1,0:T(8,128)(2,1)} %collective-permute-done.19.rm), channel_id=1, source_target_pairs={{0,15},{1,0},{2,1},{3,2},{4,3},{5,4},{6,5},{7,6},{8,7},{9,8},{10,9... | collective-permute-start | bytes 3145736 | tf_op jit(solution)/shard_map/ppermute | solution.py:563
  142.0 8.7 %collective-permute-start.38 = (bf16[16,128,128]{2,1,0:T(8,128)(2,1)S(1)}, bf16[16,128,128]{2,1,0:T(8,128)(2,1)S(1)}, u32[]{:S(2)}, u32[]{:S(2)}) collective-permute-start(bf16[16,128,128]{2,1,0:T(8,128)(2,1)S(1)} %slice_select_fusion.2), channel_id=1, source_target_pairs={{16,31},{17,16},{18,17},{19,18},{20,19},{21,20},{22,21},{23,22},{2... | collective-permute-start | bytes 1572872 | tf_op jit(solution)/shard_map/ppermute | solution.py:569

commit v3 on v2

--- a/solution.py
+++ b/solution.py
@@ -258,7 +258,7 @@
 S = 2 * EDGE
 M = ROWS - S
 B = 16
-SIDE = S + M + B + R
+SIDE = S + R + M + B + R
 FAR2 = 2 * SIDE
 SECT = 7 * PAD
 CHUNKS = 4
@@ -277,7 +277,7 @@
 
 
 def sums_kernel(idx_ref, area_ref, w_hbm, *refs):
-    left, right, own, s3m, s3p, wv, acc, sem = refs
+    left, right, own, wv, acc, sem = refs
 
     def copy(c):
         rows = pl.ds(c * WT, WT)
@@ -310,9 +310,9 @@
     left[PAD:] = summed(-2)
     right[:PAD] = summed(1)
     right[PAD:] = summed(2)
-    own[...] = summed(0)
-    s3m[...] = summed(-3)
-    s3p[...] = summed(3)
+    own[:PAD] = summed(0)
+    own[PAD : 2 * PAD] = summed(-3)
+    own[2 * PAD :] = summed(3)
 
 
 def sums_call(idx, area, weights):
@@ -321,8 +321,8 @@
     return pl.pallas_call(
         sums_kernel,
         in_specs=[smem, smem, pl.BlockSpec(memory_space=pltpu.HBM)],
-        out_specs=[vmem] * 5,
-        out_shape=[jax.ShapeDtypeStruct((n * PAD, C), jnp.float32) for n in (2, 2, 1, 1, 1)],
+        out_specs=[vmem] * 3,
+        out_shape=[jax.ShapeDtypeStruct((n * PAD, C), jnp.float32) for n in (2, 2, 3)],
         scratch_shapes=[
             pltpu.VMEM(weights.shape, weights.dtype),
             pltpu.VMEM((SECT + 1, 8, C), jnp.float32),
@@ -336,7 +336,7 @@
     )(idx, area, pltpu.with_memory_space_constraint(weights, pltpu.HBM))
 
 
-def mass_kernel(area_ref, lost_ref, at_ref, c0, cl, cr, s3m, s3p, own, ls, lm, rs, rm, up, dn, l3, r3, out_ref, src, by):
+def mass_kernel(area_ref, lost_ref, at_ref, c0, cl, cr, own, ls, lm, rs, rm, up, dn, l3, r3, out_ref, src, by):
     src[pl.ds(R, ROWS)] = own[...]
     for n, (e, m) in enumerate(((ls, lm), (rs, rm))):
         at = (n + 1) * PAD + R
@@ -347,7 +347,7 @@
         src[pl.ds(n * PAD, R)] = up[pl.ds(n * R, R)]
         src[pl.ds(n * PAD + R + ROWS, R)] = dn[pl.ds(n * R, R)]
     src[3 * PAD] = jnp.zeros((C, C), src.dtype)
-    by[:PAD] = (c0[...] + cl[:PAD]) + cr[:PAD]
+    by[:PAD] = (c0[:PAD] + cl[:PAD]) + cr[:PAD]
     by[PAD : 2 * PAD] = cl[PAD:]
     by[2 * PAD :] = cr[PAD:]
     for r in range(ROWS):
@@ -359,8 +359,8 @@
     acc = lax.fori_loop(0, 3 * PAD, body, jnp.zeros((C, C), jnp.float32), unroll=4)
     at = at_ref[0]
     for i in range(E):
-        acc = acc + s3m[pl.ds(at + i, 1)] * l3[i].astype(jnp.float32)
-        acc = acc + s3p[pl.ds(at + i, 1)] * r3[i].astype(jnp.float32)
+        acc = acc + c0[pl.ds(PAD + at + i, 1)] * l3[i].astype(jnp.float32)
+        acc = acc + c0[pl.ds(2 * PAD + at + i, 1)] * r3[i].astype(jnp.float32)
     change = lax.dot_general(
         jnp.full((8, C), -1.0, jnp.float32), acc, NT,
         precision=lax.Precision.HIGHEST, preferred_element_type=jnp.float32,
@@ -434,55 +434,96 @@
     )(idx, pltpu.with_memory_space_constraint(weights, pltpu.HBM), near)
 
 
-def outer_kernel(idx_ref, corr_ref, ls, lm, lb, lh, rs, rm, rb, rh, l3, r3, *refs):
-    partial, wv, (out_hbm, src, acc, sem) = refs[:CHUNKS], refs[CHUNKS : 2 * CHUNKS], refs[2 * CHUNKS :]
-    for n, (e, m, b, h) in enumerate(((ls, lm, lb, lh), (rs, rm, rb, rh))):
+HALF = CHUNKS // 2
+
+
+def far_part(first, idx_ref, src, partial, wv, out_ref):
+    for c in range(HALF):
+
+        def body(j, carry):
+            t = first + c * PER + j
+            lhs = jnp.concatenate([src[idx_ref[k, t]] for k in range(KMAX)], axis=1)
+            rhs = jnp.concatenate([wv[c][j, k] for k in range(KMAX)], axis=1)
+            got = lax.dot_general(lhs, rhs, NT, preferred_element_type=jnp.float32)
+            out_ref[c * PER + j] = got + partial[c][j]
+            return carry
+
+        lax.fori_loop(0, PER, body, 0, unroll=4)
+
+
+def outer0_kernel(idx_ref, ls, lm, lb, rs, rm, rb, l3, r3, *refs):
+    partial, wv, (out_ref, src) = refs[:HALF], refs[HALF:CHUNKS], refs[CHUNKS:]
+    for n, (e, m, b) in enumerate(((ls, lm, lb), (rs, rm, rb))):
         at = n * SIDE
-        src[pl.ds(at, S)] = e[...]
-        src[pl.ds(at + S, M)] = m[...]
-        src[pl.ds(at + S + M, B)] = b[...]
-        src[pl.ds(at + S + M + B, R)] = h[...]
+        src[pl.ds(at, S + R)] = e[...]
+        src[pl.ds(at + S + R, M)] = m[...]
+        src[pl.ds(at + S + R + M, B + R)] = b[...]
     src[pl.ds(FAR2, E)] = l3[...]
     src[pl.ds(FAR2 + E, E)] = r3[...]
     src[FAR2 + 2 * E] = jnp.zeros((C, C), src.dtype)
-
-    def out_copy(c):
-        rows = pl.ds(c * PER, PER)
-        return pltpu.make_async_copy(acc.at[rows], out_hbm.at[rows], sem.at[c])
-
-    for c in range(CHUNKS):
-
-        def body(t, carry):
-            lhs = jnp.concatenate([src[idx_ref[k, t]] for k in range(KMAX)], axis=1)
-            rhs = jnp.concatenate([wv[c][t - c * PER, k] for k in range(KMAX)], axis=1)
-            got = lax.dot_general(lhs, rhs, NT, preferred_element_type=jnp.float32)
-            acc[t] = (got + partial[c][t - c * PER]) + corr_ref[...]
-            return carry
-
-        lax.fori_loop(c * PER, (c + 1) * PER, body, 0, unroll=4)
-        out_copy(c).start()
-    for c in range(CHUNKS):
-        out_copy(c).wait()
-
-
-def outer_call(idx, corr, parts, partial, weights):
+    far_part(0, idx_ref, src, partial, wv, out_ref)
+
+
+def outer1_kernel(idx_ref, src, *refs):
+    partial, wv, out_ref = refs[:HALF], refs[HALF:CHUNKS], refs[CHUNKS]
+    far_part(HALF * PER, idx_ref, src, partial, wv, out_ref)
+
+
+def outer_call(half, idx, parts, partial, weights):
+    vmem = pl.BlockSpec(memory_space=pltpu.VMEM)
+    out_shape = [pltpu.VMEM((HALF * PER, C, C), jnp.float32)]
+    if half == 0:
+        out_shape.append(pltpu.VMEM((FAR2 + 2 * E + 1, C, C), jnp.bfloat16))
+    return pl.pallas_call(
+        (outer0_kernel, outer1_kernel)[half],
+        in_specs=[pl.BlockSpec(memory_space=pltpu.SMEM)]
+        + [vmem] * (len(parts) + len(partial) + len(weights)),
+        out_specs=[vmem] * len(out_shape),
+        out_shape=out_shape,
+        compiler_params=pltpu.CompilerParams(vmem_limit_bytes=8 << 20),
+        cost_estimate=pl.CostEstimate(
+            flops=2 * HALF * PER * KMAX * C**3, bytes_accessed=1 << 20, transcendentals=0
+        ),
+    )(idx, *parts, *partial, *weights)
+
+
+WRITES = 8
+
+
+def write_kernel(corr_ref, a_ref, b_ref, out_hbm, buf, sem):
+    rows = ROWS // WRITES
+
+    def copy(c):
+        at = pl.ds(c * rows, rows)
+        return pltpu.make_async_copy(buf.at[at], out_hbm.at[at], sem.at[c])
+
+    for c in range(WRITES):
+        ref = a_ref if c < WRITES // 2 else b_ref
+        for i in range(rows):
+            t = c * rows + i
+            buf[t] = ref[t % (ROWS // 2)] + corr_ref[...]
+        copy(c).start()
+    for c in range(WRITES):
+        copy(c).wait()
+
+
+def write_call(corr, first, second):
     vmem = pl.BlockSpec(memory_space=pltpu.VMEM)
     return pl.pallas_call(
-        outer_kernel,
-        in_specs=[pl.BlockSpec(memory_space=pltpu.SMEM)] + [vmem] * (1 + 2 * CHUNKS + len(parts)),
+        write_kernel,
+        in_specs=[vmem] * 3,
         out_specs=pl.BlockSpec(memory_space=pltpu.HBM),
         out_shape=jax.ShapeDtypeStruct((ROWS, C, C), jnp.float32),
         scratch_shapes=[
-            pltpu.VMEM((FAR2 + 2 * E + 1, C, C), jnp.bfloat16),
             pltpu.VMEM((ROWS, C, C), jnp.float32),
-            pltpu.SemaphoreType.DMA((CHUNKS,)),
+            pltpu.SemaphoreType.DMA((WRITES,)),
         ],
-        compiler_params=pltpu.CompilerParams(vmem_limit_bytes=18 << 20),
+        compiler_params=pltpu.CompilerParams(vmem_limit_bytes=6 << 20),
         cost_estimate=pl.CostEstimate(
-            flops=2 * ROWS * KMAX * C**3, bytes_accessed=4 << 20, transcendentals=0
-        ),
-        name="outer",
-    )(idx, corr, *parts, *partial, *weights)
+            flops=1_000_000, bytes_accessed=4 << 20, transcendentals=0
+        ),
+        name="write",
+    )(corr, first, second)
 
 
 def tables(source_row, source_block, slot_count, lat, lon):
@@ -499,10 +540,10 @@
     )
     r = p - R
     is_polar = (lat == 0) | (lat == NLAT_DEV - 1)
-    in_band = jnp.where(r < EDGE, r, jnp.where(r < EDGE + M, r - EDGE + S, r - M))
+    in_band = jnp.where(r < EDGE, r, jnp.where(r < EDGE + M, r - EDGE + S + R, r - M))
     below = lat == NLAT_DEV - 2
-    in_next = S + M + jnp.where(below, r - (ROWS - B), r)
-    halo = S + M + B + jnp.where(r < 0, r + R, r - ROWS)
+    in_next = S + R + M + jnp.where(below, r - (ROWS - B), r)
+    halo = jnp.where(is_polar, S, S + R + M + B) + jnp.where(r < 0, r + R, r - ROWS)
     two = jnp.where((r < 0) | (r >= ROWS), halo, jnp.where(is_polar, in_band, in_next))
     polar_row = jnp.clip(jnp.where(lat == 0, r, r - (ROWS - E)), 0, E - 1)
     far = jnp.where(size >= 3, FAR2 + side * E + polar_row, side * SIDE + two)
@@ -533,7 +574,7 @@
     both = ("lat", "lon")
     w = weights[:, 0]
     q = tracers.transpose(0, 2, 3, 1).reshape(ROWS, C, C)
-    qs = jnp.concatenate([q[:EDGE], q[ROWS - EDGE :]], axis=0)
+    qs = lax.optimization_barrier(jnp.concatenate([q[:EDGE], q[ROWS - EDGE :]], axis=0))
     ls, rs = lax.ppermute(qs, "lon", ring(1)), lax.ppermute(qs, "lon", ring(-1))
     qm = q[EDGE : ROWS - EDGE]
     lm, rm = lax.ppermute(qm, "lon", ring(1)), lax.ppermute(qm, "lon", ring(-1))
@@ -542,7 +583,7 @@
     r3 = lax.ppermute(pole, both, some(-3, POLAR))
     sums_idx, near_idx, far_idx, lost = tables(source_row, source_block, slot_count, lat, lon)
     area = latitude_area(lat * ROWS, ROWS)
-    to_left, to_right, own_sums, s3m, s3p = sums_call(sums_idx, area, w)
+    to_left, to_right, own_sums = sums_call(sums_idx, area, w)
     cl = lax.ppermute(to_left, "lon", ring(-1))
     cr = lax.ppermute(to_right, "lon", ring(1))
     up1 = lax.ppermute(jnp.concatenate([v[S - R :] for v in (qs, ls, rs)], axis=0), "lat", UP)
@@ -550,7 +591,7 @@
     at = jnp.where(jnp.arange(NLAT_DEV, dtype=jnp.int32) == lat, R, R + ROWS - E).astype(jnp.int32)
     v, near = mass_call(
         area, lost.reshape(1), at,
-        (own_sums, cl, cr, s3m, s3p, q, ls, lm, rs, rm, up1, dn1, l3, r3),
+        (own_sums, cl, cr, q, ls, lm, rs, rm, up1, dn1, l3, r3),
     )
     near = pltpu.with_memory_space_constraint(near, pltpu.VMEM)
     for axis, size, bit in (("lat", NLAT_DEV, 1), ("lat", NLAT_DEV, 2), ("lat", NLAT_DEV, 4), ("lon", NLON_DEV, 4), ("lon", NLON_DEV, 8)):
@@ -559,23 +600,28 @@
     v = v + (y[0] + y[2]) + y[1]
     corr = jnp.broadcast_to((v[0] * (1.0 / TOTAL_AREA))[:, None], (C, C))
 
-    lls, rrs = (lax.ppermute(x, both, some(d, POLAR)) for x, d in ((ls, 1), (rs, -1)))
+    beyond = jnp.where((lat == 0) | (lat == NLAT_DEV - 2), dn1[R:], up1[R:])
+    sides = ((ls, beyond[:R], 1), (rs, beyond[R:], -1))
+    lls, rrs = (
+        lax.ppermute(jnp.concatenate([x, h], axis=0), both, some(d, POLAR)) for x, h, d in sides
+    )
+    llb, rrb = (
+        lax.ppermute(
+            jnp.concatenate([jnp.where(lat == 1, x[:B], x[S - B :]), h], axis=0),
+            both, some(d, NEXT),
+        )
+        for x, h, d in sides
+    )
     llm, rrm = (lax.ppermute(x, both, some(d, POLAR)) for x, d in ((lm, 1), (rm, -1)))
-
-    def next_rows(e):
-        return jnp.where(lat == 1, e[:B], e[S - B :])
-
-    llb = lax.ppermute(next_rows(ls), both, some(1, NEXT))
-    rrb = lax.ppermute(next_rows(rs), both, some(-1, NEXT))
-    beyond = jnp.where((lat == 0) | (lat == NLAT_DEV - 2), dn1[R:], up1[R:])
-    llh = lax.ppermute(beyond[:R], both, some(1, POLAR + NEXT))
-    rrh = lax.ppermute(beyond[R:], both, some(-1, POLAR + NEXT))
 
     pieces = [inner_call(c, near_idx, w, near) for c in range(CHUNKS)]
     partial, wv = ([pltpu.with_memory_space_constraint(x, pltpu.VMEM) for x in p] for p in zip(*pieces))
-    fixed = outer_call(
-        far_idx, corr, (lls, llm, llb, llh, rrs, rrm, rrb, rrh, l3, r3), partial, wv
-    )
+    held = lambda x: pltpu.with_memory_space_constraint(x, pltpu.VMEM)
+    first, src = outer_call(
+        0, far_idx, (lls, llm, llb, rrs, rrm, rrb, l3, r3), partial[:HALF], wv[:HALF]
+    )
+    (second,) = outer_call(1, far_idx, (held(src),), partial[HALF:], wv[HALF:])
+    fixed = write_call(corr, held(first), held(second))
     return v[1, 0], fixed
 
 

time: 165 us -> 142 us (0.86)
  waiting for transfers between devices: 61.7 us -> 46.8 us
  starting transfers between devices: 55.4 us -> 47 us
    ppermute x1, waiting for transfers between devices: 19.4 us -> 0.01 us  [usual(): cl = lax.ppermute(to_left, 'lon', ring(-1))]
    ppermute x4 -> x2, starting transfers between devices: 16.4 us -> 6.52 us  [usual(): lax.ppermute(x, both, some(d, POLAR))]
    ppermute x1, waiting for transfers between devices: 0.01 us -> 7.59 us  [usual(): cr = lax.ppermute(to_right, 'lon', ring(1))]
    ppermute x1, waiting for transfers between devices: 8.99 us -> 15.4 us  [usual(): lax.ppermute(qs, 'lon', ring(1))]
    ppermute x1, starting transfers between devices: 0.08 us -> 5.38 us  [usual(): cl = lax.ppermute(to_left, 'lon', ring(-1))]
    ppermute x1, waiting for transfers between devices: 5.21 us -> 0.01 us  [usual(): l3 = lax.ppermute(pole, both, some(3, POLAR))]
    ppermute x1, waiting for transfers between devices: 4.92 us -> 0.01 us  [usual(): r3 = lax.ppermute(pole, both, some(-3, POLAR))]
    ppermute x4, starting transfers between devices: 11.2 us -> 7.42 us  [the longest x2 5.84 us: usual(): lax.ppermute(jnp.concatenate([x, h], axis=0), both, some(d, POLAR))]
  transfers between devices with their start and end apart: 26 -> 24, of which waited for: 11 -> 10; matrix products, arithmetic and copies ran while one was open for 4% -> 4% of each run, Pallas kernels for 13% -> 19%
where the time goes in v3:
time: 142 us; the launch traced here: 141 us
  starting transfers between devices  47 us (33%)
  waiting for transfers between devices  46.8 us (33%)
  Pallas kernels  37.1 us (26%)
  local copies, waits for them, and re-layouts  4.89 us (3%)
  other arithmetic  4.13 us (3%)
    ppermute x8, waiting for transfers between devices, swap(): return lax.ppermute(v, axis, [(i, to(i)) for i in range(size)])  22.8 us
    ppermute x1, waiting for transfers between devices, usual(): lax.ppermute(qs, 'lon', ring(1))  15.4 us
    pallas_call x4, Pallas kernels, inner_call(): pl.pallas_call(functools.partial(inner_kernel, chunk * PER), in_specs=[pl...  14.4 us
    pallas_call x2, Pallas kernels, outer_call(): pl.pallas_call((outer0_kernel, outer1_kernel)[half], in_specs=[pl.BlockSp...  8.61 us
    ppermute x1, waiting for transfers between devices, usual(): cr = lax.ppermute(to_right, 'lon', ring(1))  7.59 us
    pallas_call x1, Pallas kernels, sums_call(): pl.pallas_call(sums_kernel, in_specs=[smem, smem, pl.BlockSpec(memory_spa...  7.21 us
    ppermute x2, starting transfers between devices, usual(): lax.ppermute(x, both, some(d, POLAR))  6.52 us
    ppermute x1, starting transfers between devices, usual(): r3 = lax.ppermute(pole, both, some(-3, POLAR))  6.16 us
  transfers between devices with their start and end apart: 24, of which 10 were waited for; matrix products, arithmetic and copies ran while one was open for 4% of the time, Pallas kernels for 19%

profile of v3, /device:TPU:0, one launch (start us, length us, event | category | flops | bytes accessed | tf_op | source)
XLA Modules:
  0.0 141.2 jit_solution(15911654309530899954)
XLA Ops:
  0.0 1.8 %fusion.45 = (bf16[16,32,4,128]{3,2,1,0:T(4,128)(2,1)S(1)}, bf16[16,32,4,128]{3,2,1,0:T(4,128)(2,1)S(1)}) fusion(bf16[64,32,4,128]{3,2,1,0:T(4,128)(2,1)} %bitcast.162), kind=kLoop, calls=%fused_computation.104 | loop fusion | bytes 2097152 | tf_op jit(solution)/shard_map/slice | solution.py:577
  1.8 1.1 pad_maximum_fusion.7
  2.9 1.7 %collective-permute-start.16 = (bf16[32,128,128]{2,1,0:T(8,128)(2,1)}, bf16[32,128,128]{2,1,0:T(8,128)(2,1)S(1)}, u32[]{:S(2)}, u32[]{:S(2)}) collective-permute-start(bf16[32,128,128]{2,1,0:T(8,128)(2,1)} %pad_maximum_fusion.7), channel_id=1, source_target_pairs={{0,1},{1,2},{2,3},{3,4},{4,5},{5,6},{6,7},{7,8},{8,9},{9,10},{10,1... | collective-permute-start | bytes 3145736 | tf_op jit(solution)/shard_map/ppermute | solution.py:578
  4.6 4.9 %collective-permute-start.18 = (bf16[32,128,128]{2,1,0:T(8,128)(2,1)}, bf16[32,128,128]{2,1,0:T(8,128)(2,1)S(1)}, u32[]{:S(2)}, u32[]{:S(2)}) collective-permute-start(bf16[32,128,128]{2,1,0:T(8,128)(2,1)} %pad_maximum_fusion.7), channel_id=1, source_target_pairs={{0,15},{1,0},{2,1},{3,2},{4,3},{5,4},{6,5},{7,6},{8,7},{9,8},{10,9... | collective-permute-start | bytes 3145736 | tf_op jit(solution)/shard_map/ppermute | solution.py:578
  9.5 1.4 slice.186
  10.9 5.3 %collective-permute-start.19 = (bf16[32,128,128]{2,1,0:T(8,128)(2,1)}, bf16[32,128,128]{2,1,0:T(8,128)(2,1)}, u32[]{:S(2)}, u32[]{:S(2)}) collective-permute-start(bf16[32,128,128]{2,1,0:T(8,128)(2,1)} %bitcast.31), channel_id=1, source_target_pairs={{0,15},{1,0},{2,1},{3,2},{4,3},{5,4},{6,5},{7,6},{8,7},{9,8},{10,9... | collective-permute-start | bytes 3145736 | tf_op jit(solution)/shard_map/ppermute | solution.py:580
  16.3 1.0 slice_select_fusion.5
  17.3 1.0 fusion.46
  18.3 15.4 %collective-permute-done.16.ls = bf16[32,128,128]{2,1,0:T(8,128)(2,1)S(1)} collective-permute-done((bf16[32,128,128]{2,1,0:T(8,128)(2,1)}, bf16[32,128,128]{2,1,0:T(8,128)(2,1)S(1)}, u32[]{:S(2)}, u32[]{:S(2)}) %collective-permute-start.16) | collective-permute-done | bytes 1048608 | tf_op jit(solution)/shard_map/ppermute | solution.py:578
  33.8 1.3 collective-permute-start.21
  35.1 0.8 pad_maximum_fusion.10
  35.9 3.0 %collective-permute-start.20 = (bf16[12,128,128]{2,1,0:T(8,128)(2,1)}, bf16[12,128,128]{2,1,0:T(8,128)(2,1)S(1)}, u32[]{:S(2)}, u32[]{:S(2)}) collective-permute-start(bf16[12,128,128]{2,1,0:T(8,128)(2,1)} %pad_maximum_fusion.10), channel_id=1, source_target_pairs={{0,16},{16,32},{32,48},{48,64},{64,80},{80,96},{96,112},{1,17},{17... | collective-permute-start | bytes 1179656 | tf_op jit(solution)/shard_map/ppermute | solution.py:589
  39.0 7.2 %sums.1 = (f32[144,128]{1,0:T(8,128)S(1)}, f32[144,128]{1,0:T(8,128)S(1)}, f32[216,128]{1,0:T(8,128)S(1)}) custom-call(s32[8,64]{1,0:T(8,128)S(1)} %get-tuple-element.129.idx_ref, f32[64]{0:T(128)S(1)} %add_cosine_fusion.1.area_ref, bf16[64,8,128,128]{3,2,1,0:T(8,128)(2,1)} %bitcast.154), custom_call_target="tpu_custom_call" | custom-call | flops 20000000 | bytes 17825792 | tf_op jit(solution)/shard_map/sums/pallas_call | solution.py:321
  46.2 0.6 convert_reduce_fusion.1
  46.9 5.4 %collective-permute-start.14 = (f32[144,128]{1,0:T(8,128)S(1)}, f32[144,128]{1,0:T(8,128)S(1)}, u32[]{:S(2)}, u32[]{:S(2)}) collective-permute-start(f32[144,128]{1,0:T(8,128)S(1)} %get-tuple-element.60), channel_id=1, source_target_pairs={{0,15},{1,0},{2,1},{3,2},{4,3},{5,4},{6,5},{7,6},{8,7},{9,8},{10,9... | collective-permute-start | bytes 221192 | tf_op jit(solution)/shard_map/ppermute | solution.py:587
  52.3 1.9 %collective-permute-start.22 = (bf16[5,128,128]{2,1,0:T(8,128)(2,1)S(1)}, bf16[5,128,128]{2,1,0:T(8,128)(2,1)S(1)}, u32[]{:S(2)}, u32[]{:S(2)}) collective-permute-start(bf16[5,128,128]{2,1,0:T(8,128)(2,1)S(1)} %slice_select_fusion.5), channel_id=1, source_target_pairs={{0,3},{1,4},{2,5},{3,6},{4,7},{5,8},{6,9},{7,10},{8,11},{9,12},{10... | collective-permute-start | bytes 491528 | tf_op jit(solution)/shard_map/ppermute | solution.py:582
  54.3 0.1 pad_maximum_fusion.6
  54.4 6.2 %collective-permute-start.23 = (bf16[5,128,128]{2,1,0:T(8,128)(2,1)S(1)}, bf16[5,128,128]{2,1,0:T(8,128)(2,1)S(1)}, u32[]{:S(2)}, u32[]{:S(2)}) collective-permute-start(bf16[5,128,128]{2,1,0:T(8,128)(2,1)S(1)} %slice_select_fusion.5), channel_id=1, source_target_pairs={{0,13},{1,14},{2,15},{3,0},{4,1},{5,2},{6,3},{7,4},{8,5},{9,6},{10... | collective-permute-start | bytes 491528 | tf_op jit(solution)/shard_map/ppermute | solution.py:583
  60.6 0.1 collective-permute-start.15
  60.8 7.6 %collective-permute-done.15.cr = f32[144,128]{1,0:T(8,128)S(1)} collective-permute-done((f32[144,128]{1,0:T(8,128)S(1)}, f32[144,128]{1,0:T(8,128)S(1)}, u32[]{:S(2)}, u32[]{:S(2)}) %collective-permute-start.15) | collective-permute-done | bytes 73760 | tf_op jit(solution)/shard_map/ppermute | solution.py:588
  68.4 0.7 collective-permute-start.37
  69.1 0.1 pad_maximum_fusion.5
  69.2 1.9 %collective-permute-start.35 = (bf16[36,128,128]{2,1,0:T(8,128)(2,1)S(1)}, bf16[36,128,128]{2,1,0:T(8,128)(2,1)S(1)}, u32[]{:S(2)}, u32[]{:S(2)}) collective-permute-start(bf16[36,128,128]{2,1,0:T(8,128)(2,1)S(1)} %pad_maximum_fusion.6), channel_id=1, source_target_pairs={{0,15},{1,0},{2,1},{3,2},{4,3},{5,4},{6,5},{7,6},{8,7},{9,8},{10,9... | collective-permute-start | bytes 3538952 | tf_op jit(solution)/shard_map/ppermute | solution.py:606
  71.1 3.9 %collective-permute-start.32 = (bf16[36,128,128]{2,1,0:T(8,128)(2,1)S(1)}, bf16[36,128,128]{2,1,0:T(8,128)(2,1)S(1)}, u32[]{:S(2)}, u32[]{:S(2)}) collective-permute-start(bf16[36,128,128]{2,1,0:T(8,128)(2,1)S(1)} %pad_maximum_fusion.5), channel_id=1, source_target_pairs={{0,1},{1,2},{2,3},{3,4},{4,5},{5,6},{6,7},{7,8},{8,9},{9,10},{10,1... | collective-permute-start | bytes 3538952 | tf_op jit(solution)/shard_map/ppermute | solution.py:606
  75.1 4.8 %mass.1 = (f32[8,128]{1,0:T(8,128)S(1)}, bf16[217,128,128]{2,1,0:T(8,128)(2,1)S(1)}) custom-call(f32[64]{0:T(128)S(1)} %add_cosine_fusion.1.area_ref, f32[1]{0:T(128)} %bitcast.24.lost_ref, s32[8]{0:T(128)S(1)} %compare_select_fusion.1.at_ref, f32[216,128]{1,0:T(8,128)S(1)} %get-tuple-element.59.c0, f32[144,128]{1,0:T(8,128)S(1)} %collective-permute-done.14.cl, ...), custom_call_target="tpu_custom_call" | custom-call | flops 9000000 | bytes 3145728 | tf_op jit(solution)/shard_map/mass/pallas_call | solution.py:375
  79.9 1.2 collective-permute-done.24
  81.1 3.6 %collective-permute-done.25 = f32[8,128]{1,0:T(8,128)S(1)} collective-permute-done((f32[8,128]{1,0:T(8,128)S(1)}, f32[8,128]{1,0:T(8,128)S(1)}, u32[]{:S(2)}, u32[]{:S(2)}) %collective-permute-start.25) | collective-permute-done | bytes 4128 | tf_op jit(solution)/shard_map/ppermute | solution.py:558
  84.7 5.1 %collective-permute-done.26 = f32[8,128]{1,0:T(8,128)S(1)} collective-permute-done((f32[8,128]{1,0:T(8,128)S(1)}, f32[8,128]{1,0:T(8,128)S(1)}, u32[]{:S(2)}, u32[]{:S(2)}) %collective-permute-start.26) | collective-permute-done | bytes 4128 | tf_op jit(solution)/shard_map/ppermute | solution.py:558
  89.8 3.6 %collective-permute-done.27 = f32[8,128]{1,0:T(8,128)S(1)} collective-permute-done((f32[8,128]{1,0:T(8,128)S(1)}, f32[8,128]{1,0:T(8,128)S(1)}, u32[]{:S(2)}, u32[]{:S(2)}) %collective-permute-start.27) | collective-permute-done | bytes 4128 | tf_op jit(solution)/shard_map/ppermute | solution.py:558
  93.4 5.1 %collective-permute-done.28 = f32[8,128]{1,0:T(8,128)S(1)} collective-permute-done((f32[8,128]{1,0:T(8,128)S(1)}, f32[8,128]{1,0:T(8,128)S(1)}, u32[]{:S(2)}, u32[]{:S(2)}) %collective-permute-start.28) | collective-permute-done | bytes 4128 | tf_op jit(solution)/shard_map/ppermute | solution.py:558
  98.5 3.2 %collective-permute-start.30 = (f32[8,128]{1,0:T(8,128)S(1)}, f32[8,128]{1,0:T(8,128)S(1)}, u32[]{:S(2)}, u32[]{:S(2)}) collective-permute-start(f32[8,128]{1,0:T(8,128)S(1)} %add.232), channel_id=1, source_target_pairs={{0,3},{1,0},{2,1},{3,2},{4,7},{5,4},{6,5},{7,6},{8,11},{9,8},{10,9... | collective-permute-start | bytes 12296 | tf_op jit(solution)/shard_map/ppermute | solution.py:558
  101.7 1.6 %collective-permute-done.29 = f32[8,128]{1,0:T(8,128)S(1)} collective-permute-done((f32[8,128]{1,0:T(8,128)S(1)}, f32[8,128]{1,0:T(8,128)S(1)}, u32[]{:S(2)}, u32[]{:S(2)}) %collective-permute-start.29) | collective-permute-done | bytes 4128 | tf_op jit(solution)/shard_map/ppermute | solution.py:558
  103.3 2.5 %collective-permute-start.33 = (bf16[32,128,128]{2,1,0:T(8,128)(2,1)}, bf16[32,128,128]{2,1,0:T(8,128)(2,1)S(1)}, u32[]{:S(2)}, u32[]{:S(2)}) collective-permute-start(bf16[32,128,128]{2,1,0:T(8,128)(2,1)} %collective-permute-done.17.lm), channel_id=1, source_target_pairs={{0,1},{1,2},{2,3},{3,4},{4,5},{5,6},{6,7},{7,8},{8,9},{9,10},{10,1... | collective-permute-start | bytes 3145736 | tf_op jit(solution)/shard_map/ppermute | solution.py:615
  105.8 2.6 %collective-permute-done.31 = f32[8,128]{1,0:T(8,128)S(1)} collective-permute-done((f32[8,128]{1,0:T(8,128)S(1)}, f32[8,128]{1,0:T(8,128)S(1)}, u32[]{:S(2)}, u32[]{:S(2)}) %collective-permute-start.31) | collective-permute-done | bytes 4128 | tf_op jit(solution)/shard_map/ppermute | solution.py:558
  108.5 4.0 %collective-permute-start.36 = (bf16[32,128,128]{2,1,0:T(8,128)(2,1)}, bf16[32,128,128]{2,1,0:T(8,128)(2,1)S(1)}, u32[]{:S(2)}, u32[]{:S(2)}) collective-permute-start(bf16[32,128,128]{2,1,0:T(8,128)(2,1)} %collective-permute-done.19.rm), channel_id=1, source_target_pairs={{0,15},{1,0},{2,1},{3,2},{4,3},{5,4},{6,5},{7,6},{8,7},{9,8},{10,9... | collective-permute-start | bytes 3145736 | tf_op jit(solution)/shard_map/ppermute | solution.py:615
  112.6 0.1 pad_maximum_fusion.8
  112.7 0.9 collective-permute-start.34
  113.5 3.6 %shard_map.55 = (f32[16,128,128]{2,1,0:T(8,128)S(1)}, bf16[16,8,128,128]{3,2,1,0:T(8,128)(2,1)S(1)}) custom-call(s32[8,64]{1,0:T(8,128)S(1)} %get-tuple-element.128.idx_ref, bf16[64,8,128,128]{3,2,1,0:T(8,128)(2,1)} %bitcast.155, bf16[217,128,128]{2,1,0:T(8,128)(2,1)S(1)} %get-tuple-element.63.src), custom_call_target="tpu_custom_call" | custom-call | flops 536870912 | bytes 5242880 | tf_op jit(solution)/shard_map/pallas_call | solution.py:419
  117.2 3.6 %shard_map.56 = (f32[16,128,128]{2,1,0:T(8,128)S(1)}, bf16[16,8,128,128]{3,2,1,0:T(8,128)(2,1)S(1)}) custom-call(s32[8,64]{1,0:T(8,128)S(1)} %get-tuple-element.128.idx_ref, bf16[64,8,128,128]{3,2,1,0:T(8,128)(2,1)} %bitcast.156, bf16[217,128,128]{2,1,0:T(8,128)(2,1)S(1)} %get-tuple-element.63.src), custom_call_target="tpu_custom_call" | custom-call | flops 536870912 | bytes 5242880 | tf_op jit(solution)/shard_map/pallas_call | solution.py:419
  120.8 3.6 %shard_map.58 = (f32[16,128,128]{2,1,0:T(8,128)S(1)}, bf16[16,8,128,128]{3,2,1,0:T(8,128)(2,1)S(1)}) custom-call(s32[8,64]{1,0:T(8,128)S(1)} %get-tuple-element.128.idx_ref, bf16[64,8,128,128]{3,2,1,0:T(8,128)(2,1)} %bitcast.157, bf16[217,128,128]{2,1,0:T(8,128)(2,1)S(1)} %get-tuple-element.63.src), custom_call_target="tpu_custom_call" | custom-call | flops 536870912 | bytes 5242880 | tf_op jit(solution)/shard_map/pallas_call | solution.py:419
  124.4 3.6 %shard_map.59 = (f32[16,128,128]{2,1,0:T(8,128)S(1)}, bf16[16,8,128,128]{3,2,1,0:T(8,128)(2,1)S(1)}) custom-call(s32[8,64]{1,0:T(8,128)S(1)} %get-tuple-element.128.idx_ref, bf16[64,8,128,128]{3,2,1,0:T(8,128)(2,1)} %bitcast.158, bf16[217,128,128]{2,1,0:T(8,128)(2,1)S(1)} %get-tuple-element.63.src), custom_call_target="tpu_custom_call" | custom-call | flops 536870912 | bytes 5242880 | tf_op jit(solution)/shard_map/pallas_call | solution.py:419
  128.0 0.6 slice.157
  128.6 0.9 collective-permute-done.33.lm
  129.5 4.5 %shard_map.57 = (f32[32,128,128]{2,1,0:T(8,128)S(1)}, bf16[187,128,128]{2,1,0:T(8,128)(2,1)S(1)}) custom-call(s32[8,64]{1,0:T(8,128)S(1)} %get-tuple-element.130.idx_ref, bf16[36,128,128]{2,1,0:T(8,128)(2,1)S(1)} %collective-permute-done.32.ls, bf16[32,128,128]{2,1,0:T(8,128)(2,1)S(1)} %collective-permute-done.33.lm, ...), custom_call_target="tpu_custom_call" | custom-call | flops 1073741824 | bytes 1048576 | tf_op jit(solution)/shard_map/pallas_call | solution.py:477
  134.0 4.1 %shard_map.60.b_ref = f32[32,128,128]{2,1,0:T(8,128)S(1)} custom-call(s32[8,64]{1,0:T(8,128)S(1)} %get-tuple-element.130.idx_ref, bf16[187,128,128]{2,1,0:T(8,128)(2,1)S(1)} %get-tuple-element.69.src, f32[16,128,128]{2,1,0:T(8,128)S(1)} %get-tuple-element.70.refs_0_, f32[16,128,128]{2,1,0:T(8,128)S(1)} %get-tuple-element.71.refs_1_, ...), custom_call_target="tpu_custom_call" | custom-call | flops 1073741824 | bytes 1048576 | tf_op jit(solution)/shard_map/pallas_call | solution.py:477
  138.2 0.1 broadcast_in_dim.44.corr_ref
  138.2 2.1 %write.1 = f32[64,128,128]{2,1,0:T(8,128)} custom-call(f32[128,128]{1,0:T(8,128)S(1)} %broadcast_in_dim.44.corr_ref, f32[32,128,128]{2,1,0:T(8,128)S(1)} %get-tuple-element.68.a_ref, f32[32,128,128]{2,1,0:T(8,128)S(1)} %shard_map.60.b_ref), custom_call_target="tpu_custom_call" | custom-call | flops 1000000 | bytes 4194304 | tf_op jit(solution)/shard_map/write/pallas_call | solution.py:512
  140.4 0.7 while.9
  (50 shorter events, 0.5 us)
Async XLA Ops:
  0.0 9.5 %copy-start.1 = (bf16[64,128,32,4]{1,3,2,0:T(4,128)(2,1)S(1)}, bf16[64,128,32,4]{1,3,2,0:T(4,128)(2,1)}, u32[]{:S(2)}) copy-start(bf16[64,128,32,4]{1,3,2,0:T(4,128)(2,1)} %param.7) | copy-start | bytes 6291460
  1.8 14.5 %copy-start.4 = (s32[64,1,8]{0,2,1:T(8,128)S(1)}, s32[64,1,8]{0,2,1:T(8,128)}, u32[]{:S(2)}) copy-start(s32[64,1,8]{0,2,1:T(8,128)} %param.9) | copy-start | bytes 6148
  1.8 14.4 %copy-start.6 = (s32[64,1,8]{0,2,1:T(8,128)S(1)}, s32[64,1,8]{0,2,1:T(8,128)}, u32[]{:S(2)}) copy-start(s32[64,1,8]{0,2,1:T(8,128)} %param.10) | copy-start | bytes 6148
  1.8 14.4 %copy-start.8 = (s32[64,1]{0,1:T(1,128)S(1)}, s32[64,1]{0,1:T(1,128)}, u32[]{:S(2)}) copy-start(s32[64,1]{0,1:T(1,128)} %param.11) | copy-start | bytes 772
  2.9 30.8 %collective-permute-start.16 = (bf16[32,128,128]{2,1,0:T(8,128)(2,1)}, bf16[32,128,128]{2,1,0:T(8,128)(2,1)S(1)}, u32[]{:S(2)}, u32[]{:S(2)}) collective-permute-start(bf16[32,128,128]{2,1,0:T(8,128)(2,1)} %pad_maximum_fusion.7), channel_id=1, source_target_pairs={{0,1},{1,2},{2,3},{3,4},{4,5},{5,6},{6,7},{7,8},{8,9},{9,10},{10,1... | collective-permute-start | bytes 3145736 | tf_op jit(solution)/shard_map/ppermute | solution.py:578
  4.6 29.2 %collective-permute-start.18 = (bf16[32,128,128]{2,1,0:T(8,128)(2,1)}, bf16[32,128,128]{2,1,0:T(8,128)(2,1)S(1)}, u32[]{:S(2)}, u32[]{:S(2)}) collective-permute-start(bf16[32,128,128]{2,1,0:T(8,128)(2,1)} %pad_maximum_fusion.7), channel_id=1, source_target_pairs={{0,15},{1,0},{2,1},{3,2},{4,3},{5,4},{6,5},{7,6},{8,7},{9,8},{10,9... | collective-permute-start | bytes 3145736 | tf_op jit(solution)/shard_map/ppermute | solution.py:578
  10.9 64.2 %collective-permute-start.17 = (bf16[32,128,128]{2,1,0:T(8,128)(2,1)}, bf16[32,128,128]{2,1,0:T(8,128)(2,1)}, u32[]{:S(2)}, u32[]{:S(2)}) collective-permute-start(bf16[32,128,128]{2,1,0:T(8,128)(2,1)} %bitcast.31), channel_id=1, source_target_pairs={{0,1},{1,2},{2,3},{3,4},{4,5},{5,6},{6,7},{7,8},{8,9},{9,10},{10,1... | collective-permute-start | bytes 3145736 | tf_op jit(solution)/shard_map/ppermute | solution.py:580
  10.9 64.2 %collective-permute-start.19 = (bf16[32,128,128]{2,1,0:T(8,128)(2,1)}, bf16[32,128,128]{2,1,0:T(8,128)(2,1)}, u32[]{:S(2)}, u32[]{:S(2)}) collective-permute-start(bf16[32,128,128]{2,1,0:T(8,128)(2,1)} %bitcast.31), channel_id=1, source_target_pairs={{0,15},{1,0},{2,1},{3,2},{4,3},{5,4},{6,5},{7,6},{8,7},{9,8},{10,9... | collective-permute-start | bytes 3145736 | tf_op jit(solution)/shard_map/ppermute | solution.py:580
  33.8 18.5 %collective-permute-start.21 = (bf16[12,128,128]{2,1,0:T(8,128)(2,1)S(1)}, bf16[12,128,128]{2,1,0:T(8,128)(2,1)S(1)}, u32[]{:S(2)}, u32[]{:S(2)}) collective-permute-start(bf16[12,128,128]{2,1,0:T(8,128)(2,1)S(1)} %pad_maximum_fusion.11), channel_id=1, source_target_pairs={{16,0},{32,16},{48,32},{64,48},{80,64},{96,80},{112,96},{17,1},{33... | collective-permute-start | bytes 1179656 | tf_op jit(solution)/shard_map/ppermute | solution.py:590
  35.9 18.3 %collective-permute-start.20 = (bf16[12,128,128]{2,1,0:T(8,128)(2,1)}, bf16[12,128,128]{2,1,0:T(8,128)(2,1)S(1)}, u32[]{:S(2)}, u32[]{:S(2)}) collective-permute-start(bf16[12,128,128]{2,1,0:T(8,128)(2,1)} %pad_maximum_fusion.10), channel_id=1, source_target_pairs={{0,16},{16,32},{32,48},{48,64},{64,80},{80,96},{96,112},{1,17},{17... | collective-permute-start | bytes 1179656 | tf_op jit(solution)/shard_map/ppermute | solution.py:589
  46.9 13.7 %collective-permute-start.14 = (f32[144,128]{1,0:T(8,128)S(1)}, f32[144,128]{1,0:T(8,128)S(1)}, u32[]{:S(2)}, u32[]{:S(2)}) collective-permute-start(f32[144,128]{1,0:T(8,128)S(1)} %get-tuple-element.60), channel_id=1, source_target_pairs={{0,15},{1,0},{2,1},{3,2},{4,3},{5,4},{6,5},{7,6},{8,7},{9,8},{10,9... | collective-permute-start | bytes 221192 | tf_op jit(solution)/shard_map/ppermute | solution.py:587
  52.3 16.9 %collective-permute-start.22 = (bf16[5,128,128]{2,1,0:T(8,128)(2,1)S(1)}, bf16[5,128,128]{2,1,0:T(8,128)(2,1)S(1)}, u32[]{:S(2)}, u32[]{:S(2)}) collective-permute-start(bf16[5,128,128]{2,1,0:T(8,128)(2,1)S(1)} %slice_select_fusion.5), channel_id=1, source_target_pairs={{0,3},{1,4},{2,5},{3,6},{4,7},{5,8},{6,9},{7,10},{8,11},{9,12},{10... | collective-permute-start | bytes 491528 | tf_op jit(solution)/shard_map/ppermute | solution.py:582
  54.4 20.7 %copy-start.2 = (bf16[64,128,32,4]{1,3,2,0:T(4,128)(2,1)S(1)}, bf16[64,128,32,4]{1,3,2,0:T(4,128)(2,1)}, u32[]{:S(2)}) copy-start(bf16[64,128,32,4]{1,3,2,0:T(4,128)(2,1)} %param.7) | copy-start | bytes 6291460
  54.4 16.7 %collective-permute-start.23 = (bf16[5,128,128]{2,1,0:T(8,128)(2,1)S(1)}, bf16[5,128,128]{2,1,0:T(8,128)(2,1)S(1)}, u32[]{:S(2)}, u32[]{:S(2)}) collective-permute-start(bf16[5,128,128]{2,1,0:T(8,128)(2,1)S(1)} %slice_select_fusion.5), channel_id=1, source_target_pairs={{0,13},{1,14},{2,15},{3,0},{4,1},{5,2},{6,3},{7,4},{8,5},{9,6},{10... | collective-permute-start | bytes 491528 | tf_op jit(solution)/shard_map/ppermute | solution.py:583
  60.6 7.7 %collective-permute-start.15 = (f32[144,128]{1,0:T(8,128)S(1)}, f32[144,128]{1,0:T(8,128)S(1)}, u32[]{:S(2)}, u32[]{:S(2)}) collective-permute-start(f32[144,128]{1,0:T(8,128)S(1)} %get-tuple-element.61), channel_id=1, source_target_pairs={{0,1},{1,2},{2,3},{3,4},{4,5},{5,6},{6,7},{7,8},{8,9},{9,10},{10,1... | collective-permute-start | bytes 221192 | tf_op jit(solution)/shard_map/ppermute | solution.py:588
  68.4 44.3 %collective-permute-start.37 = (bf16[20,128,128]{2,1,0:T(8,128)(2,1)S(1)}, bf16[20,128,128]{2,1,0:T(8,128)(2,1)S(1)}, u32[]{:S(2)}, u32[]{:S(2)}) collective-permute-start(bf16[20,128,128]{2,1,0:T(8,128)(2,1)S(1)} %pad_maximum_fusion.9), channel_id=1, source_target_pairs={{16,31},{17,16},{18,17},{19,18},{20,19},{21,20},{22,21},{23,22},{2... | collective-permute-start | bytes 1966088 | tf_op jit(solution)/shard_map/ppermute | solution.py:609
  69.2 60.4 %collective-permute-start.35 = (bf16[36,128,128]{2,1,0:T(8,128)(2,1)S(1)}, bf16[36,128,128]{2,1,0:T(8,128)(2,1)S(1)}, u32[]{:S(2)}, u32[]{:S(2)}) collective-permute-start(bf16[36,128,128]{2,1,0:T(8,128)(2,1)S(1)} %pad_maximum_fusion.6), channel_id=1, source_target_pairs={{0,15},{1,0},{2,1},{3,2},{4,3},{5,4},{6,5},{7,6},{8,7},{9,8},{10,9... | collective-permute-start | bytes 3538952 | tf_op jit(solution)/shard_map/ppermute | solution.py:606
  71.1 58.4 %collective-permute-start.32 = (bf16[36,128,128]{2,1,0:T(8,128)(2,1)S(1)}, bf16[36,128,128]{2,1,0:T(8,128)(2,1)S(1)}, u32[]{:S(2)}, u32[]{:S(2)}) collective-permute-start(bf16[36,128,128]{2,1,0:T(8,128)(2,1)S(1)} %pad_maximum_fusion.5), channel_id=1, source_target_pairs={{0,1},{1,2},{2,3},{3,4},{4,5},{5,6},{6,7},{7,8},{8,9},{9,10},{10,1... | collective-permute-start | bytes 3538952 | tf_op jit(solution)/shard_map/ppermute | solution.py:606
  79.9 1.2 collective-permute-start.24
  81.1 3.6 %collective-permute-start.25 = (f32[8,128]{1,0:T(8,128)S(1)}, f32[8,128]{1,0:T(8,128)S(1)}, u32[]{:S(2)}, u32[]{:S(2)}) collective-permute-start(f32[8,128]{1,0:T(8,128)S(1)} %add.228), channel_id=1, source_target_pairs={{0,32},{16,48},{32,0},{48,16},{64,96},{80,112},{96,64},{112,80},{1... | collective-permute-start | bytes 12296 | tf_op jit(solution)/shard_map/ppermute | solution.py:558
  84.7 5.1 %collective-permute-start.26 = (f32[8,128]{1,0:T(8,128)S(1)}, f32[8,128]{1,0:T(8,128)S(1)}, u32[]{:S(2)}, u32[]{:S(2)}) collective-permute-start(f32[8,128]{1,0:T(8,128)S(1)} %add.229), channel_id=1, source_target_pairs={{0,64},{16,80},{32,96},{48,112},{64,0},{80,16},{96,32},{112,48},{1... | collective-permute-start | bytes 12296 | tf_op jit(solution)/shard_map/ppermute | solution.py:558
  89.8 3.6 %collective-permute-start.27 = (f32[8,128]{1,0:T(8,128)S(1)}, f32[8,128]{1,0:T(8,128)S(1)}, u32[]{:S(2)}, u32[]{:S(2)}) collective-permute-start(f32[8,128]{1,0:T(8,128)S(1)} %add.230), channel_id=1, source_target_pairs={{0,4},{1,5},{2,6},{3,7},{4,0},{5,1},{6,2},{7,3},{8,12},{9,13},{10,... | collective-permute-start | bytes 12296 | tf_op jit(solution)/shard_map/ppermute | solution.py:558
  93.4 5.1 %collective-permute-start.28 = (f32[8,128]{1,0:T(8,128)S(1)}, f32[8,128]{1,0:T(8,128)S(1)}, u32[]{:S(2)}, u32[]{:S(2)}) collective-permute-start(f32[8,128]{1,0:T(8,128)S(1)} %add.231), channel_id=1, source_target_pairs={{0,8},{1,9},{2,10},{3,11},{4,12},{5,13},{6,14},{7,15},{8,0},{9,1},... | collective-permute-start | bytes 12296 | tf_op jit(solution)/shard_map/ppermute | solution.py:558
  98.5 4.8 %collective-permute-start.29 = (f32[8,128]{1,0:T(8,128)S(1)}, f32[8,128]{1,0:T(8,128)S(1)}, u32[]{:S(2)}, u32[]{:S(2)}) collective-permute-start(f32[8,128]{1,0:T(8,128)S(1)} %add.232), channel_id=1, source_target_pairs={{0,1},{1,2},{2,3},{3,0},{4,5},{5,6},{6,7},{7,4},{8,9},{9,10},{10,1... | collective-permute-start | bytes 12296 | tf_op jit(solution)/shard_map/ppermute | solution.py:558
  98.5 4.8 %collective-permute-start.30 = (f32[8,128]{1,0:T(8,128)S(1)}, f32[8,128]{1,0:T(8,128)S(1)}, u32[]{:S(2)}, u32[]{:S(2)}) collective-permute-start(f32[8,128]{1,0:T(8,128)S(1)} %add.232), channel_id=1, source_target_pairs={{0,3},{1,0},{2,1},{3,2},{4,7},{5,4},{6,5},{7,6},{8,11},{9,8},{10,9... | collective-permute-start | bytes 12296 | tf_op jit(solution)/shard_map/ppermute | solution.py:558
  103.3 5.2 %collective-permute-start.31 = (f32[8,128]{1,0:T(8,128)S(1)}, f32[8,128]{1,0:T(8,128)S(1)}, u32[]{:S(2)}, u32[]{:S(2)}) collective-permute-start(f32[8,128]{1,0:T(8,128)S(1)} %add.232), channel_id=1, source_target_pairs={{0,2},{1,3},{2,0},{3,1},{4,6},{5,7},{6,4},{7,5},{8,10},{9,11},{10,... | collective-permute-start | bytes 12296 | tf_op jit(solution)/shard_map/ppermute | solution.py:558
  103.3 26.2 %collective-permute-start.33 = (bf16[32,128,128]{2,1,0:T(8,128)(2,1)}, bf16[32,128,128]{2,1,0:T(8,128)(2,1)S(1)}, u32[]{:S(2)}, u32[]{:S(2)}) collective-permute-start(bf16[32,128,128]{2,1,0:T(8,128)(2,1)} %collective-permute-done.17.lm), channel_id=1, source_target_pairs={{0,1},{1,2},{2,3},{3,4},{4,5},{5,6},{6,7},{7,8},{8,9},{9,10},{10,1... | collective-permute-start | bytes 3145736 | tf_op jit(solution)/shard_map/ppermute | solution.py:615
  108.5 21.0 %collective-permute-start.36 = (bf16[32,128,128]{2,1,0:T(8,128)(2,1)}, bf16[32,128,128]{2,1,0:T(8,128)(2,1)S(1)}, u32[]{:S(2)}, u32[]{:S(2)}) collective-permute-start(bf16[32,128,128]{2,1,0:T(8,128)(2,1)} %collective-permute-done.19.rm), channel_id=1, source_target_pairs={{0,15},{1,0},{2,1},{3,2},{4,3},{5,4},{6,5},{7,6},{8,7},{9,8},{10,9... | collective-permute-start | bytes 3145736 | tf_op jit(solution)/shard_map/ppermute | solution.py:615
  112.7 16.0 %collective-permute-start.34 = (bf16[20,128,128]{2,1,0:T(8,128)(2,1)S(1)}, bf16[20,128,128]{2,1,0:T(8,128)(2,1)S(1)}, u32[]{:S(2)}, u32[]{:S(2)}) collective-permute-start(bf16[20,128,128]{2,1,0:T(8,128)(2,1)S(1)} %pad_maximum_fusion.8), channel_id=1, source_target_pairs={{16,17},{17,18},{18,19},{19,20},{20,21},{21,22},{22,23},{23,24},{2... | collective-permute-start | bytes 1966088 | tf_op jit(solution)/shard_map/ppermute | solution.py:609

commit v4 on v3

--- a/solution.py
+++ b/solution.py
@@ -336,10 +336,61 @@
     )(idx, area, pltpu.with_memory_space_constraint(weights, pltpu.HBM))
 
 
-def mass_kernel(area_ref, lost_ref, at_ref, c0, cl, cr, own, ls, lm, rs, rm, up, dn, l3, r3, out_ref, src, by):
-    src[pl.ds(R, ROWS)] = own[...]
-    for n, (e, m) in enumerate(((ls, lm), (rs, rm))):
-        at = (n + 1) * PAD + R
+def split_kernel(q_hbm, qs, qm, sem):
+    copies = [
+        pltpu.make_async_copy(q_hbm.at[pl.ds(at, n)], ref.at[pl.ds(to, n)], sem.at[i])
+        for i, (at, n, ref, to) in enumerate(
+            ((0, EDGE, qs, 0), (ROWS - EDGE, EDGE, qs, EDGE), (EDGE, M, qm, 0))
+        )
+    ]
+    for copy in copies:
+        copy.start()
+    for copy in copies:
+        copy.wait()
+
+
+def split_call(q):
+    vmem = pl.BlockSpec(memory_space=pltpu.VMEM)
+    return pl.pallas_call(
+        split_kernel,
+        in_specs=[pl.BlockSpec(memory_space=pltpu.HBM)],
+        out_specs=[vmem, vmem],
+        out_shape=[pltpu.VMEM((n, C, C), jnp.bfloat16) for n in (S, M)],
+        scratch_shapes=[pltpu.SemaphoreType.DMA((3,))],
+        compiler_params=pltpu.CompilerParams(vmem_limit_bytes=1 << 20),
+        cost_estimate=pl.CostEstimate(flops=1000, bytes_accessed=2 << 20, transcendentals=0),
+        name="split",
+    )(pltpu.with_memory_space_constraint(q, pltpu.HBM))
+
+
+def pack_kernel(qs, ls, rs, up, dn):
+    for n, v in enumerate((qs, ls, rs)):
+        up[pl.ds(n * R, R)] = v[S - R :]
+        dn[pl.ds(n * R, R)] = v[:R]
+
+
+def pack_call(parts):
+    vmem = pl.BlockSpec(memory_space=pltpu.VMEM)
+    return pl.pallas_call(
+        pack_kernel,
+        in_specs=[vmem] * 3,
+        out_specs=[vmem, vmem],
+        out_shape=[pltpu.VMEM((3 * R, C, C), jnp.bfloat16)] * 2,
+        compiler_params=pltpu.CompilerParams(vmem_limit_bytes=6 << 20),
+        cost_estimate=pl.CostEstimate(flops=1000, bytes_accessed=1000, transcendentals=0),
+        name="pack",
+    )(*parts)
+
+
+def mass_kernel(area_ref, lost_ref, at_ref, w_hbm, c0, cl, cr, qs, qm, ls, lm, rs, rm, up, dn, l3, r3, out_ref, src, wv, by, sem):
+    def copy(c):
+        rows = pl.ds(c * WT, WT)
+        return pltpu.make_async_copy(w_hbm.at[rows], wv.at[rows], sem.at[c])
+
+    for c in range(WC):
+        copy(c).start()
+    for n, (e, m) in enumerate(((qs, qm), (ls, lm), (rs, rm))):
+        at = n * PAD + R
         src[pl.ds(at, EDGE)] = e[:EDGE]
         src[pl.ds(at + EDGE, M)] = m[...]
         src[pl.ds(at + EDGE + M, EDGE)] = e[EDGE:]
@@ -367,83 +418,69 @@
     )
     row = lax.broadcasted_iota(jnp.int32, (8, C), 0)
     out_ref[...] = jnp.where(row == 0, change, lost_ref[0])
-
-
-def mass_call(area, lost, at, parts):
+    for c in range(WC):
+        copy(c).wait()
+
+
+def mass_call(area, lost, at, weights, parts):
     smem = pl.BlockSpec(memory_space=pltpu.SMEM)
     vmem = pl.BlockSpec(memory_space=pltpu.VMEM)
     return pl.pallas_call(
         mass_kernel,
-        in_specs=[smem] * 3 + [vmem] * len(parts),
-        out_specs=[vmem, vmem],
+        in_specs=[smem] * 3 + [pl.BlockSpec(memory_space=pltpu.HBM)] + [vmem] * len(parts),
+        out_specs=[vmem] * 3,
         out_shape=[
             jax.ShapeDtypeStruct((8, C), jnp.float32),
             pltpu.VMEM((3 * PAD + 1, C, C), jnp.bfloat16),
+            pltpu.VMEM(weights.shape, weights.dtype),
         ],
-        scratch_shapes=[pltpu.VMEM((3 * PAD, C), jnp.float32)],
+        scratch_shapes=[
+            pltpu.VMEM((3 * PAD, C), jnp.float32),
+            pltpu.SemaphoreType.DMA((WC,)),
+        ],
         compiler_params=pltpu.CompilerParams(vmem_limit_bytes=6 << 20),
         cost_estimate=pl.CostEstimate(
             flops=9_000_000, bytes_accessed=3 << 20, transcendentals=0
         ),
         name="mass",
-    )(area, lost, at, *parts)
-
-
-PARTS = 4
-PT = PER // PARTS
-
-
-def inner_kernel(first, idx_ref, w_hbm, src, out_ref, wv, sem):
-    def copy(c):
-        return pltpu.make_async_copy(
-            w_hbm.at[pl.ds(first + c * PT, PT)], wv.at[pl.ds(c * PT, PT)], sem.at[c]
-        )
-
-    for c in range(PARTS):
-        copy(c).start()
-
-    def body(c, carry):
-        copy(c).wait()
-        for i in range(PT):
-            j = c * PT + i
-            lhs = jnp.concatenate([src[idx_ref[k, first + j]] for k in range(KMAX)], axis=1)
-            rhs = jnp.concatenate([wv[j, k] for k in range(KMAX)], axis=1)
-            out_ref[j] = lax.dot_general(lhs, rhs, NT, preferred_element_type=jnp.float32)
+    )(area, lost, at, pltpu.with_memory_space_constraint(weights, pltpu.HBM), *parts)
+
+
+def inner_kernel(first, idx_ref, wv, src, out_ref):
+    def body(j, carry):
+        t = first + j
+        lhs = jnp.concatenate([src[idx_ref[k, t]] for k in range(KMAX)], axis=1)
+        rhs = jnp.concatenate([wv[t, k] for k in range(KMAX)], axis=1)
+        out_ref[j] = lax.dot_general(lhs, rhs, NT, preferred_element_type=jnp.float32)
         return carry
 
-    lax.fori_loop(0, PARTS, body, 0)
-
-
-def inner_call(chunk, idx, weights, near):
+    lax.fori_loop(0, PER, body, 0, unroll=4)
+
+
+def inner_call(chunk, idx, wv, near):
     vmem = pl.BlockSpec(memory_space=pltpu.VMEM)
     return pl.pallas_call(
         functools.partial(inner_kernel, chunk * PER),
-        in_specs=[
-            pl.BlockSpec(memory_space=pltpu.SMEM), pl.BlockSpec(memory_space=pltpu.HBM), vmem
-        ],
-        out_specs=[vmem, vmem],
-        out_shape=[
-            pltpu.VMEM((PER, C, C), jnp.float32),
-            pltpu.VMEM((PER, KMAX, C, C), jnp.bfloat16),
-        ],
-        scratch_shapes=[pltpu.SemaphoreType.DMA((PARTS,))],
+        in_specs=[pl.BlockSpec(memory_space=pltpu.SMEM), vmem, vmem],
+        out_specs=vmem,
+        out_shape=pltpu.VMEM((PER, C, C), jnp.float32),
         compiler_params=pltpu.CompilerParams(vmem_limit_bytes=2 << 20),
         cost_estimate=pl.CostEstimate(
-            flops=2 * PER * KMAX * C**3, bytes_accessed=5 << 20, transcendentals=0
-        ),
-    )(idx, pltpu.with_memory_space_constraint(weights, pltpu.HBM), near)
+            flops=2 * PER * KMAX * C**3, bytes_accessed=1 << 20, transcendentals=0
+        ),
+    )(idx, wv, near)
 
 
 HALF = CHUNKS // 2
 
 
-def far_part(first, idx_ref, src, partial, wv, out_ref):
+def far_part(first, idx_ref, wv, src, partial, out_ref):
     for c in range(HALF):
 
         def body(j, carry):
             t = first + c * PER + j
             lhs = jnp.concatenate([src[idx_ref[k, t]] for k in range(KMAX)], axis=1)
-            rhs = jnp.concatenate([wv[c][j, k] for k in range(KMAX)], axis=1)
+            rhs = jnp.concatenate([wv[t, k] for k in range(KMAX)], axis=1)
             got = lax.dot_general(lhs, rhs, NT, preferred_element_type=jnp.float32)
             out_ref[c * PER + j] = got + partial[c][j]
             return carry
@@ -451,8 +488,8 @@
         lax.fori_loop(0, PER, body, 0, unroll=4)
 
 
-def outer0_kernel(idx_ref, ls, lm, lb, rs, rm, rb, l3, r3, *refs):
-    partial, wv, (out_ref, src) = refs[:HALF], refs[HALF:CHUNKS], refs[CHUNKS:]
+def outer0_kernel(idx_ref, wv, ls, lm, lb, rs, rm, rb, l3, r3, *refs):
+    partial, (out_ref, src) = refs[:HALF], refs[HALF:]
     for n, (e, m, b) in enumerate(((ls, lm, lb), (rs, rm, rb))):
         at = n * SIDE
         src[pl.ds(at, S + R)] = e[...]
@@ -461,15 +498,14 @@
     src[pl.ds(FAR2, E)] = l3[...]
     src[pl.ds(FAR2 + E, E)] = r3[...]
     src[FAR2 + 2 * E] = jnp.zeros((C, C), src.dtype)
-    far_part(0, idx_ref, src, partial, wv, out_ref)
-
-
-def outer1_kernel(idx_ref, src, *refs):
-    partial, wv, out_ref = refs[:HALF], refs[HALF:CHUNKS], refs[CHUNKS]
-    far_part(HALF * PER, idx_ref, src, partial, wv, out_ref)
-
-
-def outer_call(half, idx, parts, partial, weights):
+    far_part(0, idx_ref, wv, src, partial, out_ref)
+
+
+def outer1_kernel(idx_ref, wv, src, *refs):
+    far_part(HALF * PER, idx_ref, wv, src, refs[:HALF], refs[HALF])
+
+
+def outer_call(half, idx, wv, parts, partial):
     vmem = pl.BlockSpec(memory_space=pltpu.VMEM)
     out_shape = [pltpu.VMEM((HALF * PER, C, C), jnp.float32)]
     if half == 0:
@@ -477,14 +513,14 @@
     return pl.pallas_call(
         (outer0_kernel, outer1_kernel)[half],
         in_specs=[pl.BlockSpec(memory_space=pltpu.SMEM)]
-        + [vmem] * (len(parts) + len(partial) + len(weights)),
+        + [vmem] * (1 + len(parts) + len(partial)),
         out_specs=[vmem] * len(out_shape),
         out_shape=out_shape,
         compiler_params=pltpu.CompilerParams(vmem_limit_bytes=8 << 20),
         cost_estimate=pl.CostEstimate(
             flops=2 * HALF * PER * KMAX * C**3, bytes_accessed=1 << 20, transcendentals=0
         ),
-    )(idx, *parts, *partial, *weights)
+    )(idx, wv, *parts, *partial)
 
 
 WRITES = 8
@@ -574,9 +610,8 @@
     both = ("lat", "lon")
     w = weights[:, 0]
     q = tracers.transpose(0, 2, 3, 1).reshape(ROWS, C, C)
-    qs = lax.optimization_barrier(jnp.concatenate([q[:EDGE], q[ROWS - EDGE :]], axis=0))
+    qs, qm = split_call(q)
     ls, rs = lax.ppermute(qs, "lon", ring(1)), lax.ppermute(qs, "lon", ring(-1))
-    qm = q[EDGE : ROWS - EDGE]
     lm, rm = lax.ppermute(qm, "lon", ring(1)), lax.ppermute(qm, "lon", ring(-1))
     pole = jnp.where(lat == 0, qs[:E], qs[S - E :])
     l3 = lax.ppermute(pole, both, some(3, POLAR))
@@ -586,14 +621,15 @@
     to_left, to_right, own_sums = sums_call(sums_idx, area, w)
     cl = lax.ppermute(to_left, "lon", ring(-1))
     cr = lax.ppermute(to_right, "lon", ring(1))
-    up1 = lax.ppermute(jnp.concatenate([v[S - R :] for v in (qs, ls, rs)], axis=0), "lat", UP)
-    dn1 = lax.ppermute(jnp.concatenate([v[:R] for v in (qs, ls, rs)], axis=0), "lat", DOWN)
+    first, last = pack_call((qs, ls, rs))
+    up1, dn1 = lax.ppermute(first, "lat", UP), lax.ppermute(last, "lat", DOWN)
     at = jnp.where(jnp.arange(NLAT_DEV, dtype=jnp.int32) == lat, R, R + ROWS - E).astype(jnp.int32)
-    v, near = mass_call(
-        area, lost.reshape(1), at,
-        (own_sums, cl, cr, q, ls, lm, rs, rm, up1, dn1, l3, r3),
-    )
-    near = pltpu.with_memory_space_constraint(near, pltpu.VMEM)
+    v, near, wv = mass_call(
+        area, lost.reshape(1), at, w,
+        (own_sums, cl, cr, qs, qm, ls, lm, rs, rm, up1, dn1, l3, r3),
+    )
+    held = lambda x: pltpu.with_memory_space_constraint(x, pltpu.VMEM)
+    near, wv = held(near), held(wv)
     for axis, size, bit in (("lat", NLAT_DEV, 1), ("lat", NLAT_DEV, 2), ("lat", NLAT_DEV, 4), ("lon", NLON_DEV, 4), ("lon", NLON_DEV, 8)):
         v = v + swap(v, axis, size, lambda i, bit=bit: i ^ bit)
     y = [swap(v, "lon", NLON_DEV, lambda i, by=by: i // 4 * 4 + (i + by) % 4) for by in (1, 2, 3)]
@@ -614,13 +650,11 @@
     )
     llm, rrm = (lax.ppermute(x, both, some(d, POLAR)) for x, d in ((lm, 1), (rm, -1)))
 
-    pieces = [inner_call(c, near_idx, w, near) for c in range(CHUNKS)]
-    partial, wv = ([pltpu.with_memory_space_constraint(x, pltpu.VMEM) for x in p] for p in zip(*pieces))
-    held = lambda x: pltpu.with_memory_space_constraint(x, pltpu.VMEM)
+    partial = [held(inner_call(c, near_idx, wv, near)) for c in range(CHUNKS)]
     first, src = outer_call(
-        0, far_idx, (lls, llm, llb, rrs, rrm, rrb, l3, r3), partial[:HALF], wv[:HALF]
-    )
-    (second,) = outer_call(1, far_idx, (held(src),), partial[HALF:], wv[HALF:])
+        0, far_idx, wv, (lls, llm, llb, rrs, rrm, rrb, l3, r3), partial[:HALF]
+    )
+    (second,) = outer_call(1, far_idx, wv, (held(src),), partial[HALF:])
     fixed = write_call(corr, held(first), held(second))
     return v[1, 0], fixed
 

time: 142 us -> 144 us (1.014)
  local copies, waits for them, and re-layouts: 4.89 us -> 0.65 us
  starting transfers between devices: 47 us -> 50.4 us
  waiting for transfers between devices: 46.8 us -> 49.1 us
  Pallas kernels: 37.1 us -> 39.4 us
    pallas_call x1 -> x3, Pallas kernels: 4.76 us -> 12.1 us  [the longest x1 8.58 us: mass_call(): pl.pallas_call(mass_kernel, in_specs=[smem] * 3 + [pl.BlockSpec(memory_sp...]
    pallas_call x4, Pallas kernels: 14.4 us -> 9.35 us  [inner_call(): pl.pallas_call(functools.partial(inner_kernel, chunk * PER), in_specs=[pl...]
    slice x5 -> x0, local copies, waits for them, and re-layouts: 4.19 us -> none  [the longest x1 1.77 us: usual(): q[:EDGE]]
    ppermute x2, starting transfers between devices: 5.84 us -> 9.16 us  [usual(): lax.ppermute(jnp.concatenate([x, h], axis=0), both, some(d, POLAR))]
    ppermute x1, waiting for transfers between devices: 15.4 us -> 17.8 us  [usual(): lax.ppermute(qs, 'lon', ring(1))]
    concatenate x3 -> x0, other arithmetic: 1.9 us -> none  [the longest x1 1.06 us: usual(): jnp.concatenate([q[:EDGE], q[ROWS - EDGE:]], axis=0)]
    ppermute x8, starting transfers between devices: 3.25 us -> 5.08 us  [swap(): return lax.ppermute(v, axis, [(i, to(i)) for i in range(size)])]
    ppermute x8, waiting for transfers between devices: 22.8 us -> 21 us  [swap(): return lax.ppermute(v, axis, [(i, to(i)) for i in range(size)])]
  transfers between devices with their start and end apart: 24 -> 24, of which waited for: 10 -> 11; matrix products, arithmetic and copies ran while one was open for 4% -> 2% of each run, Pallas kernels for 19% -> 18%
where the time goes in v4:
time: 144 us
  starting transfers between devices  50.4 us (35%)
  waiting for transfers between devices  49.1 us (34%)
  Pallas kernels  39.4 us (27%)
  other arithmetic  2.93 us (2%)
    ppermute x8, waiting for transfers between devices, swap(): return lax.ppermute(v, axis, [(i, to(i)) for i in range(size)])  21 us
    ppermute x1, waiting for transfers between devices, usual(): lax.ppermute(qs, 'lon', ring(1))  17.8 us
    pallas_call x4, Pallas kernels, inner_call(): pl.pallas_call(functools.partial(inner_kernel, chunk * PER), in_specs=[pl...  9.35 us
    ppermute x2, starting transfers between devices, usual(): lax.ppermute(jnp.concatenate([x, h], axis=0), both, some(d, POLAR))  9.16 us
    pallas_call x2, Pallas kernels, outer_call(): pl.pallas_call((outer0_kernel, outer1_kernel)[half], in_specs=[pl.BlockSp...  8.62 us
    pallas_call x1, Pallas kernels, mass_call(): pl.pallas_call(mass_kernel, in_specs=[smem] * 3 + [pl.BlockSpec(memory_sp...  8.58 us
    ppermute x1, waiting for transfers between devices, usual(): cr = lax.ppermute(to_right, 'lon', ring(1))  7.59 us
    pallas_call x1, Pallas kernels, sums_call(): pl.pallas_call(sums_kernel, in_specs=[smem, smem, pl.BlockSpec(memory_spa...  7.21 us
  transfers between devices with their start and end apart: 24, of which 11 were waited for; matrix products, arithmetic and copies ran while one was open for 2% of the time, Pallas kernels for 18%

profile of v4, /device:TPU:0, one launch (start us, length us, event | category | flops | bytes accessed | tf_op | source)
XLA Modules:
  0.0 143.8 jit_solution(5853083218548621418)
XLA Ops:
  0.0 2.6 %split.1 = (bf16[32,128,128]{2,1,0:T(8,128)(2,1)S(1)}, bf16[32,128,128]{2,1,0:T(8,128)(2,1)}) custom-call(bf16[64,128,128]{2,1,0:T(8,128)(2,1)} %bitcast.156), custom_call_target="tpu_custom_call" | custom-call | flops 1000 | bytes 2097152 | tf_op jit(solution)/shard_map/split/pallas_call | solution.py:354
  2.6 1.8 %collective-permute-start.16 = (bf16[32,128,128]{2,1,0:T(8,128)(2,1)S(1)}, bf16[32,128,128]{2,1,0:T(8,128)(2,1)S(1)}, u32[]{:S(2)}, u32[]{:S(2)}) collective-permute-start(bf16[32,128,128]{2,1,0:T(8,128)(2,1)S(1)} %get-tuple-element.59.qs), channel_id=1, source_target_pairs={{0,1},{1,2},{2,3},{3,4},{4,5},{5,6},{6,7},{7,8},{8,9},{9,10},{10,1... | collective-permute-start | bytes 3145736 | tf_op jit(solution)/shard_map/ppermute | solution.py:614
  4.3 5.0 %collective-permute-start.18 = (bf16[32,128,128]{2,1,0:T(8,128)(2,1)S(1)}, bf16[32,128,128]{2,1,0:T(8,128)(2,1)S(1)}, u32[]{:S(2)}, u32[]{:S(2)}) collective-permute-start(bf16[32,128,128]{2,1,0:T(8,128)(2,1)S(1)} %get-tuple-element.59.qs), channel_id=1, source_target_pairs={{0,15},{1,0},{2,1},{3,2},{4,3},{5,4},{6,5},{7,6},{8,7},{9,8},{10,9... | collective-permute-start | bytes 3145736 | tf_op jit(solution)/shard_map/ppermute | solution.py:614
  9.3 5.3 %collective-permute-start.19 = (bf16[32,128,128]{2,1,0:T(8,128)(2,1)}, bf16[32,128,128]{2,1,0:T(8,128)(2,1)}, u32[]{:S(2)}, u32[]{:S(2)}) collective-permute-start(bf16[32,128,128]{2,1,0:T(8,128)(2,1)} %get-tuple-element.60.qm), channel_id=1, source_target_pairs={{0,15},{1,0},{2,1},{3,2},{4,3},{5,4},{6,5},{7,6},{8,7},{9,8},{10,9... | collective-permute-start | bytes 3145736 | tf_op jit(solution)/shard_map/ppermute | solution.py:615
  14.7 0.7 slice_select_fusion.5
  15.4 17.8 %collective-permute-done.16.ls = bf16[32,128,128]{2,1,0:T(8,128)(2,1)S(1)} collective-permute-done((bf16[32,128,128]{2,1,0:T(8,128)(2,1)S(1)}, bf16[32,128,128]{2,1,0:T(8,128)(2,1)S(1)}, u32[]{:S(2)}, u32[]{:S(2)}) %collective-permute-start.16) | collective-permute-done | bytes 1048608 | tf_op jit(solution)/shard_map/ppermute | solution.py:614
  33.3 0.9 pack.1
  34.2 1.3 collective-permute-start.20
  35.5 1.3 collective-permute-start.21
  36.9 7.2 %sums.1 = (f32[144,128]{1,0:T(8,128)S(1)}, f32[144,128]{1,0:T(8,128)S(1)}, f32[216,128]{1,0:T(8,128)S(1)}) custom-call(s32[8,64]{1,0:T(8,128)S(1)} %get-tuple-element.115.idx_ref, f32[64]{0:T(128)S(1)} %add_cosine_fusion.1.area_ref, bf16[64,8,128,128]{3,2,1,0:T(8,128)(2,1)} %bitcast.151), custom_call_target="tpu_custom_call" | custom-call | flops 20000000 | bytes 17825792 | tf_op jit(solution)/shard_map/sums/pallas_call | solution.py:321
  44.2 0.7 convert_reduce_fusion.1
  44.9 5.5 %collective-permute-start.14 = (f32[144,128]{1,0:T(8,128)S(1)}, f32[144,128]{1,0:T(8,128)S(1)}, u32[]{:S(2)}, u32[]{:S(2)}) collective-permute-start(f32[144,128]{1,0:T(8,128)S(1)} %get-tuple-element.57), channel_id=1, source_target_pairs={{0,15},{1,0},{2,1},{3,2},{4,3},{5,4},{6,5},{7,6},{8,7},{9,8},{10,9... | collective-permute-start | bytes 221192 | tf_op jit(solution)/shard_map/ppermute | solution.py:622
  50.4 1.9 %collective-permute-start.22 = (bf16[5,128,128]{2,1,0:T(8,128)(2,1)S(1)}, bf16[5,128,128]{2,1,0:T(8,128)(2,1)S(1)}, u32[]{:S(2)}, u32[]{:S(2)}) collective-permute-start(bf16[5,128,128]{2,1,0:T(8,128)(2,1)S(1)} %copy-done.8), channel_id=1, source_target_pairs={{0,3},{1,4},{2,5},{3,6},{4,7},{5,8},{6,9},{7,10},{8,11},{9,12},{10... | collective-permute-start | bytes 491528 | tf_op jit(solution)/shard_map/ppermute | solution.py:617
  52.3 1.0 slice_select_fusion.4
  53.4 0.1 pad_maximum_fusion.5
  53.5 6.0 %collective-permute-start.23 = (bf16[5,128,128]{2,1,0:T(8,128)(2,1)S(1)}, bf16[5,128,128]{2,1,0:T(8,128)(2,1)S(1)}, u32[]{:S(2)}, u32[]{:S(2)}) collective-permute-start(bf16[5,128,128]{2,1,0:T(8,128)(2,1)S(1)} %copy-done.8), channel_id=1, source_target_pairs={{0,13},{1,14},{2,15},{3,0},{4,1},{5,2},{6,3},{7,4},{8,5},{9,6},{10... | collective-permute-start | bytes 491528 | tf_op jit(solution)/shard_map/ppermute | solution.py:618
  59.5 0.1 collective-permute-start.15
  59.7 7.6 %collective-permute-done.15.cr = f32[144,128]{1,0:T(8,128)S(1)} collective-permute-done((f32[144,128]{1,0:T(8,128)S(1)}, f32[144,128]{1,0:T(8,128)S(1)}, u32[]{:S(2)}, u32[]{:S(2)}) %collective-permute-start.15) | collective-permute-done | bytes 73760 | tf_op jit(solution)/shard_map/ppermute | solution.py:623
  67.3 0.7 collective-permute-start.34
  68.0 0.1 pad_maximum_fusion.6
  68.1 1.9 %collective-permute-start.32 = (bf16[36,128,128]{2,1,0:T(8,128)(2,1)S(1)}, bf16[36,128,128]{2,1,0:T(8,128)(2,1)S(1)}, u32[]{:S(2)}, u32[]{:S(2)}) collective-permute-start(bf16[36,128,128]{2,1,0:T(8,128)(2,1)S(1)} %pad_maximum_fusion.5), channel_id=1, source_target_pairs={{0,1},{1,2},{2,3},{3,4},{4,5},{5,6},{6,7},{7,8},{8,9},{9,10},{10,1... | collective-permute-start | bytes 3538952 | tf_op jit(solution)/shard_map/ppermute | solution.py:642
  70.0 7.2 %collective-permute-start.35 = (bf16[36,128,128]{2,1,0:T(8,128)(2,1)S(1)}, bf16[36,128,128]{2,1,0:T(8,128)(2,1)S(1)}, u32[]{:S(2)}, u32[]{:S(2)}) collective-permute-start(bf16[36,128,128]{2,1,0:T(8,128)(2,1)S(1)} %pad_maximum_fusion.6), channel_id=1, source_target_pairs={{0,15},{1,0},{2,1},{3,2},{4,3},{5,4},{6,5},{7,6},{8,7},{9,8},{10,9... | collective-permute-start | bytes 3538952 | tf_op jit(solution)/shard_map/ppermute | solution.py:642
  77.3 8.6 %mass.1 = (f32[8,128]{1,0:T(8,128)S(1)}, bf16[217,128,128]{2,1,0:T(8,128)(2,1)S(1)}, bf16[64,8,128,128]{3,2,1,0:T(8,128)(2,1)S(1)}) custom-call(f32[64]{0:T(128)S(1)} %add_cosine_fusion.1.area_ref, f32[1]{0:T(128)} %bitcast.24.lost_ref, s32[8]{0:T(128)S(1)} %compare_select_fusion.1.at_ref, bf16[64,8,128,128]{3,2,1,0:T(8,128)(2,1)} %bitcast.152, ...), custom_call_target="tpu_custom_call" | custom-call | flops 9000000 | bytes 3145728 | tf_op jit(solution)/shard_map/mass/pallas_call | solution.py:428
  85.9 0.1 collective-permute-start.24
  86.0 1.2 collective-permute-done.24
  87.2 3.6 %collective-permute-done.25 = f32[8,128]{1,0:T(8,128)S(1)} collective-permute-done((f32[8,128]{1,0:T(8,128)S(1)}, f32[8,128]{1,0:T(8,128)S(1)}, u32[]{:S(2)}, u32[]{:S(2)}) %collective-permute-start.25) | collective-permute-done | bytes 4128 | tf_op jit(solution)/shard_map/ppermute | solution.py:594
  90.8 1.8 %collective-permute-start.26 = (f32[8,128]{1,0:T(8,128)S(1)}, f32[8,128]{1,0:T(8,128)S(1)}, u32[]{:S(2)}, u32[]{:S(2)}) collective-permute-start(f32[8,128]{1,0:T(8,128)S(1)} %add.229), channel_id=1, source_target_pairs={{0,64},{16,80},{32,96},{48,112},{64,0},{80,16},{96,32},{112,48},{1... | collective-permute-start | bytes 12296 | tf_op jit(solution)/shard_map/ppermute | solution.py:594
  92.5 3.4 %collective-permute-done.26 = f32[8,128]{1,0:T(8,128)S(1)} collective-permute-done((f32[8,128]{1,0:T(8,128)S(1)}, f32[8,128]{1,0:T(8,128)S(1)}, u32[]{:S(2)}, u32[]{:S(2)}) %collective-permute-start.26) | collective-permute-done | bytes 4128 | tf_op jit(solution)/shard_map/ppermute | solution.py:594
  95.9 3.6 %collective-permute-done.27 = f32[8,128]{1,0:T(8,128)S(1)} collective-permute-done((f32[8,128]{1,0:T(8,128)S(1)}, f32[8,128]{1,0:T(8,128)S(1)}, u32[]{:S(2)}, u32[]{:S(2)}) %collective-permute-start.27) | collective-permute-done | bytes 4128 | tf_op jit(solution)/shard_map/ppermute | solution.py:594
  99.5 5.1 %collective-permute-done.28 = f32[8,128]{1,0:T(8,128)S(1)} collective-permute-done((f32[8,128]{1,0:T(8,128)S(1)}, f32[8,128]{1,0:T(8,128)S(1)}, u32[]{:S(2)}, u32[]{:S(2)}) %collective-permute-start.28) | collective-permute-done | bytes 4128 | tf_op jit(solution)/shard_map/ppermute | solution.py:594
  104.6 3.2 %collective-permute-start.30 = (f32[8,128]{1,0:T(8,128)S(1)}, f32[8,128]{1,0:T(8,128)S(1)}, u32[]{:S(2)}, u32[]{:S(2)}) collective-permute-start(f32[8,128]{1,0:T(8,128)S(1)} %add.232), channel_id=1, source_target_pairs={{0,3},{1,0},{2,1},{3,2},{4,7},{5,4},{6,5},{7,6},{8,11},{9,8},{10,9... | collective-permute-start | bytes 12296 | tf_op jit(solution)/shard_map/ppermute | solution.py:594
  107.9 1.6 %collective-permute-done.29 = f32[8,128]{1,0:T(8,128)S(1)} collective-permute-done((f32[8,128]{1,0:T(8,128)S(1)}, f32[8,128]{1,0:T(8,128)S(1)}, u32[]{:S(2)}, u32[]{:S(2)}) %collective-permute-start.29) | collective-permute-done | bytes 4128 | tf_op jit(solution)/shard_map/ppermute | solution.py:594
  109.4 2.5 %collective-permute-start.33 = (bf16[32,128,128]{2,1,0:T(8,128)(2,1)}, bf16[32,128,128]{2,1,0:T(8,128)(2,1)S(1)}, u32[]{:S(2)}, u32[]{:S(2)}) collective-permute-start(bf16[32,128,128]{2,1,0:T(8,128)(2,1)} %collective-permute-done.17.lm), channel_id=1, source_target_pairs={{0,1},{1,2},{2,3},{3,4},{4,5},{5,6},{6,7},{7,8},{8,9},{9,10},{10,1... | collective-permute-start | bytes 3145736 | tf_op jit(solution)/shard_map/ppermute | solution.py:651
  111.9 2.6 %collective-permute-done.31 = f32[8,128]{1,0:T(8,128)S(1)} collective-permute-done((f32[8,128]{1,0:T(8,128)S(1)}, f32[8,128]{1,0:T(8,128)S(1)}, u32[]{:S(2)}, u32[]{:S(2)}) %collective-permute-start.31) | collective-permute-done | bytes 4128 | tf_op jit(solution)/shard_map/ppermute | solution.py:594
  114.5 4.1 %collective-permute-start.36 = (bf16[32,128,128]{2,1,0:T(8,128)(2,1)}, bf16[32,128,128]{2,1,0:T(8,128)(2,1)S(1)}, u32[]{:S(2)}, u32[]{:S(2)}) collective-permute-start(bf16[32,128,128]{2,1,0:T(8,128)(2,1)} %collective-permute-done.19.rm), channel_id=1, source_target_pairs={{0,15},{1,0},{2,1},{3,2},{4,3},{5,4},{6,5},{7,6},{8,7},{9,8},{10,9... | collective-permute-start | bytes 3145736 | tf_op jit(solution)/shard_map/ppermute | solution.py:651
  118.8 0.7 collective-permute-start.37
  119.5 2.3 %shard_map.59.refs_1_ = f32[16,128,128]{2,1,0:T(8,128)S(1)} custom-call(s32[8,64]{1,0:T(8,128)S(1)} %get-tuple-element.114.idx_ref, bf16[64,8,128,128]{3,2,1,0:T(8,128)(2,1)S(1)} %get-tuple-element.64.wv, bf16[217,128,128]{2,1,0:T(8,128)(2,1)S(1)} %get-tuple-element.65.src), custom_call_target="tpu_custom_call" | custom-call | flops 536870912 | bytes 1048576 | tf_op jit(solution)/shard_map/pallas_call | solution.py:462
  121.8 2.3 %shard_map.58.refs_0_ = f32[16,128,128]{2,1,0:T(8,128)S(1)} custom-call(s32[8,64]{1,0:T(8,128)S(1)} %get-tuple-element.114.idx_ref, bf16[64,8,128,128]{3,2,1,0:T(8,128)(2,1)S(1)} %get-tuple-element.64.wv, bf16[217,128,128]{2,1,0:T(8,128)(2,1)S(1)} %get-tuple-element.65.src), custom_call_target="tpu_custom_call" | custom-call | flops 536870912 | bytes 1048576 | tf_op jit(solution)/shard_map/pallas_call | solution.py:462
  124.1 2.3 %shard_map.56.refs_1_ = f32[16,128,128]{2,1,0:T(8,128)S(1)} custom-call(s32[8,64]{1,0:T(8,128)S(1)} %get-tuple-element.114.idx_ref, bf16[64,8,128,128]{3,2,1,0:T(8,128)(2,1)S(1)} %get-tuple-element.64.wv, bf16[217,128,128]{2,1,0:T(8,128)(2,1)S(1)} %get-tuple-element.65.src), custom_call_target="tpu_custom_call" | custom-call | flops 536870912 | bytes 1048576 | tf_op jit(solution)/shard_map/pallas_call | solution.py:462
  126.5 2.3 %shard_map.55.refs_0_ = f32[16,128,128]{2,1,0:T(8,128)S(1)} custom-call(s32[8,64]{1,0:T(8,128)S(1)} %get-tuple-element.114.idx_ref, bf16[64,8,128,128]{3,2,1,0:T(8,128)(2,1)S(1)} %get-tuple-element.64.wv, bf16[217,128,128]{2,1,0:T(8,128)(2,1)S(1)} %get-tuple-element.65.src), custom_call_target="tpu_custom_call" | custom-call | flops 536870912 | bytes 1048576 | tf_op jit(solution)/shard_map/pallas_call | solution.py:462
  128.9 0.5 slice.109
  129.4 0.3 collective-permute-done.33.lm
  129.7 2.4 %collective-permute-done.36.rm = bf16[32,128,128]{2,1,0:T(8,128)(2,1)S(1)} collective-permute-done((bf16[32,128,128]{2,1,0:T(8,128)(2,1)}, bf16[32,128,128]{2,1,0:T(8,128)(2,1)S(1)}, u32[]{:S(2)}, u32[]{:S(2)}) %collective-permute-start.36) | collective-permute-done | bytes 1048608 | tf_op jit(solution)/shard_map/ppermute | solution.py:651
  132.0 4.5 %shard_map.57 = (f32[32,128,128]{2,1,0:T(8,128)S(1)}, bf16[187,128,128]{2,1,0:T(8,128)(2,1)S(1)}) custom-call(s32[8,64]{1,0:T(8,128)S(1)} %get-tuple-element.116.idx_ref, bf16[64,8,128,128]{3,2,1,0:T(8,128)(2,1)S(1)} %get-tuple-element.64.wv, bf16[36,128,128]{2,1,0:T(8,128)(2,1)S(1)} %collective-permute-done.32.ls, ...), custom_call_target="tpu_custom_call" | custom-call | flops 1073741824 | bytes 1048576 | tf_op jit(solution)/shard_map/pallas_call | solution.py:513
  136.5 4.1 %shard_map.60.b_ref = f32[32,128,128]{2,1,0:T(8,128)S(1)} custom-call(s32[8,64]{1,0:T(8,128)S(1)} %get-tuple-element.116.idx_ref, bf16[64,8,128,128]{3,2,1,0:T(8,128)(2,1)S(1)} %get-tuple-element.64.wv, bf16[187,128,128]{2,1,0:T(8,128)(2,1)S(1)} %get-tuple-element.67.src, f32[16,128,128]{2,1,0:T(8,128)S(1)} %shard_map.58.refs_0_, ...), custom_call_target="tpu_custom_call" | custom-call | flops 1073741824 | bytes 1048576 | tf_op jit(solution)/shard_map/pallas_call | solution.py:513
  140.7 0.1 broadcast_in_dim.44.corr_ref
  140.7 2.1 %write.1 = f32[64,128,128]{2,1,0:T(8,128)} custom-call(f32[128,128]{1,0:T(8,128)S(1)} %broadcast_in_dim.44.corr_ref, f32[32,128,128]{2,1,0:T(8,128)S(1)} %get-tuple-element.66.a_ref, f32[32,128,128]{2,1,0:T(8,128)S(1)} %shard_map.60.b_ref), custom_call_target="tpu_custom_call" | custom-call | flops 1000000 | bytes 4194304 | tf_op jit(solution)/shard_map/write/pallas_call | solution.py:548
  142.9 0.8 while.9
  (50 shorter events, 0.4 us)
Async XLA Ops:
  0.0 14.7 %copy-start.9 = (s32[64,1]{0,1:T(1,128)S(1)}, s32[64,1]{0,1:T(1,128)}, u32[]{:S(2)}) copy-start(s32[64,1]{0,1:T(1,128)} %param.11) | copy-start | bytes 772
  0.0 14.7 %copy-start.6 = (s32[64,1,8]{0,2,1:T(8,128)S(1)}, s32[64,1,8]{0,2,1:T(8,128)}, u32[]{:S(2)}) copy-start(s32[64,1,8]{0,2,1:T(8,128)} %param.10) | copy-start | bytes 6148
  0.0 14.7 %copy-start.2 = (s32[64,1,8]{0,2,1:T(8,128)S(1)}, s32[64,1,8]{0,2,1:T(8,128)}, u32[]{:S(2)}) copy-start(s32[64,1,8]{0,2,1:T(8,128)} %param.9) | copy-start | bytes 6148
  2.6 30.7 %collective-permute-start.16 = (bf16[32,128,128]{2,1,0:T(8,128)(2,1)S(1)}, bf16[32,128,128]{2,1,0:T(8,128)(2,1)S(1)}, u32[]{:S(2)}, u32[]{:S(2)}) collective-permute-start(bf16[32,128,128]{2,1,0:T(8,128)(2,1)S(1)} %get-tuple-element.59.qs), channel_id=1, source_target_pairs={{0,1},{1,2},{2,3},{3,4},{4,5},{5,6},{6,7},{7,8},{8,9},{9,10},{10,1... | collective-permute-start | bytes 3145736 | tf_op jit(solution)/shard_map/ppermute | solution.py:614
  4.3 28.9 %collective-permute-start.18 = (bf16[32,128,128]{2,1,0:T(8,128)(2,1)S(1)}, bf16[32,128,128]{2,1,0:T(8,128)(2,1)S(1)}, u32[]{:S(2)}, u32[]{:S(2)}) collective-permute-start(bf16[32,128,128]{2,1,0:T(8,128)(2,1)S(1)} %get-tuple-element.59.qs), channel_id=1, source_target_pairs={{0,15},{1,0},{2,1},{3,2},{4,3},{5,4},{6,5},{7,6},{8,7},{9,8},{10,9... | collective-permute-start | bytes 3145736 | tf_op jit(solution)/shard_map/ppermute | solution.py:614
  9.3 68.0 %collective-permute-start.17 = (bf16[32,128,128]{2,1,0:T(8,128)(2,1)}, bf16[32,128,128]{2,1,0:T(8,128)(2,1)}, u32[]{:S(2)}, u32[]{:S(2)}) collective-permute-start(bf16[32,128,128]{2,1,0:T(8,128)(2,1)} %get-tuple-element.60.qm), channel_id=1, source_target_pairs={{0,1},{1,2},{2,3},{3,4},{4,5},{5,6},{6,7},{7,8},{8,9},{9,10},{10,1... | collective-permute-start | bytes 3145736 | tf_op jit(solution)/shard_map/ppermute | solution.py:615
  9.3 68.0 %collective-permute-start.19 = (bf16[32,128,128]{2,1,0:T(8,128)(2,1)}, bf16[32,128,128]{2,1,0:T(8,128)(2,1)}, u32[]{:S(2)}, u32[]{:S(2)}) collective-permute-start(bf16[32,128,128]{2,1,0:T(8,128)(2,1)} %get-tuple-element.60.qm), channel_id=1, source_target_pairs={{0,15},{1,0},{2,1},{3,2},{4,3},{5,4},{6,5},{7,6},{8,7},{9,8},{10,9... | collective-permute-start | bytes 3145736 | tf_op jit(solution)/shard_map/ppermute | solution.py:615
  34.2 16.2 %collective-permute-start.20 = (bf16[12,128,128]{2,1,0:T(8,128)(2,1)}, bf16[12,128,128]{2,1,0:T(8,128)(2,1)S(1)}, u32[]{:S(2)}, u32[]{:S(2)}) collective-permute-start(bf16[12,128,128]{2,1,0:T(8,128)(2,1)} %get-tuple-element.61), channel_id=1, source_target_pairs={{0,16},{16,32},{32,48},{48,64},{64,80},{80,96},{96,112},{1,17},{17... | collective-permute-start | bytes 1179656 | tf_op jit(solution)/shard_map/ppermute | solution.py:625
  35.5 16.8 %collective-permute-start.21 = (bf16[12,128,128]{2,1,0:T(8,128)(2,1)}, bf16[12,128,128]{2,1,0:T(8,128)(2,1)}, u32[]{:S(2)}, u32[]{:S(2)}) collective-permute-start(bf16[12,128,128]{2,1,0:T(8,128)(2,1)} %get-tuple-element.62), channel_id=1, source_target_pairs={{16,0},{32,16},{48,32},{64,48},{80,64},{96,80},{112,96},{17,1},{33... | collective-permute-start | bytes 1179656 | tf_op jit(solution)/shard_map/ppermute | solution.py:625
  36.9 7.3 %copy-start.3 = (s32[64,1,8]{0,2,1:T(8,128)S(1)}, s32[64,1,8]{0,2,1:T(8,128)}, u32[]{:S(2)}) copy-start(s32[64,1,8]{0,2,1:T(8,128)} %param.9) | copy-start | bytes 6148
  36.9 7.3 %copy-start.7 = (s32[64,1,8]{0,2,1:T(8,128)S(1)}, s32[64,1,8]{0,2,1:T(8,128)}, u32[]{:S(2)}) copy-start(s32[64,1,8]{0,2,1:T(8,128)} %param.10) | copy-start | bytes 6148
  36.9 7.3 %copy-start.10 = (s32[64,1]{0,1:T(1,128)S(1)}, s32[64,1]{0,1:T(1,128)}, u32[]{:S(2)}) copy-start(s32[64,1]{0,1:T(1,128)} %param.11) | copy-start | bytes 772
  36.9 13.5 %copy-start.8 = (bf16[5,128,128]{2,1,0:T(8,128)(2,1)S(1)}, bf16[5,128,128]{2,1,0:T(8,128)(2,1)}, u32[]{:S(2)}) copy-start(bf16[5,128,128]{2,1,0:T(8,128)(2,1)} %slice_select_fusion.5) | copy-start | bytes 491524
  44.9 14.6 %collective-permute-start.14 = (f32[144,128]{1,0:T(8,128)S(1)}, f32[144,128]{1,0:T(8,128)S(1)}, u32[]{:S(2)}, u32[]{:S(2)}) collective-permute-start(f32[144,128]{1,0:T(8,128)S(1)} %get-tuple-element.57), channel_id=1, source_target_pairs={{0,15},{1,0},{2,1},{3,2},{4,3},{5,4},{6,5},{7,6},{8,7},{9,8},{10,9... | collective-permute-start | bytes 221192 | tf_op jit(solution)/shard_map/ppermute | solution.py:622
  50.4 17.7 %collective-permute-start.22 = (bf16[5,128,128]{2,1,0:T(8,128)(2,1)S(1)}, bf16[5,128,128]{2,1,0:T(8,128)(2,1)S(1)}, u32[]{:S(2)}, u32[]{:S(2)}) collective-permute-start(bf16[5,128,128]{2,1,0:T(8,128)(2,1)S(1)} %copy-done.8), channel_id=1, source_target_pairs={{0,3},{1,4},{2,5},{3,6},{4,7},{5,8},{6,9},{7,10},{8,11},{9,12},{10... | collective-permute-start | bytes 491528 | tf_op jit(solution)/shard_map/ppermute | solution.py:617
  53.5 16.5 %collective-permute-start.23 = (bf16[5,128,128]{2,1,0:T(8,128)(2,1)S(1)}, bf16[5,128,128]{2,1,0:T(8,128)(2,1)S(1)}, u32[]{:S(2)}, u32[]{:S(2)}) collective-permute-start(bf16[5,128,128]{2,1,0:T(8,128)(2,1)S(1)} %copy-done.8), channel_id=1, source_target_pairs={{0,13},{1,14},{2,15},{3,0},{4,1},{5,2},{6,3},{7,4},{8,5},{9,6},{10... | collective-permute-start | bytes 491528 | tf_op jit(solution)/shard_map/ppermute | solution.py:618
  59.5 7.7 %collective-permute-start.15 = (f32[144,128]{1,0:T(8,128)S(1)}, f32[144,128]{1,0:T(8,128)S(1)}, u32[]{:S(2)}, u32[]{:S(2)}) collective-permute-start(f32[144,128]{1,0:T(8,128)S(1)} %get-tuple-element.58), channel_id=1, source_target_pairs={{0,1},{1,2},{2,3},{3,4},{4,5},{5,6},{6,7},{7,8},{8,9},{9,10},{10,1... | collective-permute-start | bytes 221192 | tf_op jit(solution)/shard_map/ppermute | solution.py:623
  67.3 51.5 %collective-permute-start.34 = (bf16[20,128,128]{2,1,0:T(8,128)(2,1)S(1)}, bf16[20,128,128]{2,1,0:T(8,128)(2,1)S(1)}, u32[]{:S(2)}, u32[]{:S(2)}) collective-permute-start(bf16[20,128,128]{2,1,0:T(8,128)(2,1)S(1)} %pad_maximum_fusion.7), channel_id=1, source_target_pairs={{16,17},{17,18},{18,19},{19,20},{20,21},{21,22},{22,23},{23,24},{2... | collective-permute-start | bytes 1966088 | tf_op jit(solution)/shard_map/ppermute | solution.py:645
  68.1 63.9 %collective-permute-start.32 = (bf16[36,128,128]{2,1,0:T(8,128)(2,1)S(1)}, bf16[36,128,128]{2,1,0:T(8,128)(2,1)S(1)}, u32[]{:S(2)}, u32[]{:S(2)}) collective-permute-start(bf16[36,128,128]{2,1,0:T(8,128)(2,1)S(1)} %pad_maximum_fusion.5), channel_id=1, source_target_pairs={{0,1},{1,2},{2,3},{3,4},{4,5},{5,6},{6,7},{7,8},{8,9},{9,10},{10,1... | collective-permute-start | bytes 3538952 | tf_op jit(solution)/shard_map/ppermute | solution.py:642
  70.0 62.0 %collective-permute-start.35 = (bf16[36,128,128]{2,1,0:T(8,128)(2,1)S(1)}, bf16[36,128,128]{2,1,0:T(8,128)(2,1)S(1)}, u32[]{:S(2)}, u32[]{:S(2)}) collective-permute-start(bf16[36,128,128]{2,1,0:T(8,128)(2,1)S(1)} %pad_maximum_fusion.6), channel_id=1, source_target_pairs={{0,15},{1,0},{2,1},{3,2},{4,3},{5,4},{6,5},{7,6},{8,7},{9,8},{10,9... | collective-permute-start | bytes 3538952 | tf_op jit(solution)/shard_map/ppermute | solution.py:642
  85.9 1.2 collective-permute-start.24
  87.2 3.6 %collective-permute-start.25 = (f32[8,128]{1,0:T(8,128)S(1)}, f32[8,128]{1,0:T(8,128)S(1)}, u32[]{:S(2)}, u32[]{:S(2)}) collective-permute-start(f32[8,128]{1,0:T(8,128)S(1)} %add.228), channel_id=1, source_target_pairs={{0,32},{16,48},{32,0},{48,16},{64,96},{80,112},{96,64},{112,80},{1... | collective-permute-start | bytes 12296 | tf_op jit(solution)/shard_map/ppermute | solution.py:594
  90.8 5.1 %collective-permute-start.26 = (f32[8,128]{1,0:T(8,128)S(1)}, f32[8,128]{1,0:T(8,128)S(1)}, u32[]{:S(2)}, u32[]{:S(2)}) collective-permute-start(f32[8,128]{1,0:T(8,128)S(1)} %add.229), channel_id=1, source_target_pairs={{0,64},{16,80},{32,96},{48,112},{64,0},{80,16},{96,32},{112,48},{1... | collective-permute-start | bytes 12296 | tf_op jit(solution)/shard_map/ppermute | solution.py:594
  95.9 3.6 %collective-permute-start.27 = (f32[8,128]{1,0:T(8,128)S(1)}, f32[8,128]{1,0:T(8,128)S(1)}, u32[]{:S(2)}, u32[]{:S(2)}) collective-permute-start(f32[8,128]{1,0:T(8,128)S(1)} %add.230), channel_id=1, source_target_pairs={{0,4},{1,5},{2,6},{3,7},{4,0},{5,1},{6,2},{7,3},{8,12},{9,13},{10,... | collective-permute-start | bytes 12296 | tf_op jit(solution)/shard_map/ppermute | solution.py:594
  99.5 5.1 %collective-permute-start.28 = (f32[8,128]{1,0:T(8,128)S(1)}, f32[8,128]{1,0:T(8,128)S(1)}, u32[]{:S(2)}, u32[]{:S(2)}) collective-permute-start(f32[8,128]{1,0:T(8,128)S(1)} %add.231), channel_id=1, source_target_pairs={{0,8},{1,9},{2,10},{3,11},{4,12},{5,13},{6,14},{7,15},{8,0},{9,1},... | collective-permute-start | bytes 12296 | tf_op jit(solution)/shard_map/ppermute | solution.py:594
  104.6 4.8 %collective-permute-start.29 = (f32[8,128]{1,0:T(8,128)S(1)}, f32[8,128]{1,0:T(8,128)S(1)}, u32[]{:S(2)}, u32[]{:S(2)}) collective-permute-start(f32[8,128]{1,0:T(8,128)S(1)} %add.232), channel_id=1, source_target_pairs={{0,1},{1,2},{2,3},{3,0},{4,5},{5,6},{6,7},{7,4},{8,9},{9,10},{10,1... | collective-permute-start | bytes 12296 | tf_op jit(solution)/shard_map/ppermute | solution.py:594
  104.6 4.8 %collective-permute-start.30 = (f32[8,128]{1,0:T(8,128)S(1)}, f32[8,128]{1,0:T(8,128)S(1)}, u32[]{:S(2)}, u32[]{:S(2)}) collective-permute-start(f32[8,128]{1,0:T(8,128)S(1)} %add.232), channel_id=1, source_target_pairs={{0,3},{1,0},{2,1},{3,2},{4,7},{5,4},{6,5},{7,6},{8,11},{9,8},{10,9... | collective-permute-start | bytes 12296 | tf_op jit(solution)/shard_map/ppermute | solution.py:594
  109.4 5.1 %collective-permute-start.31 = (f32[8,128]{1,0:T(8,128)S(1)}, f32[8,128]{1,0:T(8,128)S(1)}, u32[]{:S(2)}, u32[]{:S(2)}) collective-permute-start(f32[8,128]{1,0:T(8,128)S(1)} %add.232), channel_id=1, source_target_pairs={{0,2},{1,3},{2,0},{3,1},{4,6},{5,7},{6,4},{7,5},{8,10},{9,11},{10,... | collective-permute-start | bytes 12296 | tf_op jit(solution)/shard_map/ppermute | solution.py:594
  109.4 20.2 %collective-permute-start.33 = (bf16[32,128,128]{2,1,0:T(8,128)(2,1)}, bf16[32,128,128]{2,1,0:T(8,128)(2,1)S(1)}, u32[]{:S(2)}, u32[]{:S(2)}) collective-permute-start(bf16[32,128,128]{2,1,0:T(8,128)(2,1)} %collective-permute-done.17.lm), channel_id=1, source_target_pairs={{0,1},{1,2},{2,3},{3,4},{4,5},{5,6},{6,7},{7,8},{8,9},{9,10},{10,1... | collective-permute-start | bytes 3145736 | tf_op jit(solution)/shard_map/ppermute | solution.py:651
  114.5 17.5 %collective-permute-start.36 = (bf16[32,128,128]{2,1,0:T(8,128)(2,1)}, bf16[32,128,128]{2,1,0:T(8,128)(2,1)S(1)}, u32[]{:S(2)}, u32[]{:S(2)}) collective-permute-start(bf16[32,128,128]{2,1,0:T(8,128)(2,1)} %collective-permute-done.19.rm), channel_id=1, source_target_pairs={{0,15},{1,0},{2,1},{3,2},{4,3},{5,4},{6,5},{7,6},{8,7},{9,8},{10,9... | collective-permute-start | bytes 3145736 | tf_op jit(solution)/shard_map/ppermute | solution.py:651
  118.8 10.6 %collective-permute-start.37 = (bf16[20,128,128]{2,1,0:T(8,128)(2,1)S(1)}, bf16[20,128,128]{2,1,0:T(8,128)(2,1)S(1)}, u32[]{:S(2)}, u32[]{:S(2)}) collective-permute-start(bf16[20,128,128]{2,1,0:T(8,128)(2,1)S(1)} %pad_maximum_fusion.8), channel_id=1, source_target_pairs={{16,31},{17,16},{18,17},{19,18},{20,19},{21,20},{22,21},{23,22},{2... | collective-permute-start | bytes 1966088 | tf_op jit(solution)/shard_map/ppermute | solution.py:645
  140.7 2.1 %copy-start.4 = (s32[64,1,8]{0,2,1:T(8,128)S(1)}, s32[64,1,8]{0,2,1:T(8,128)}, u32[]{:S(2)}) copy-start(s32[64,1,8]{0,2,1:T(8,128)} %param.9) | copy-start | bytes 6148

commit v5 on v4

--- a/solution.py
+++ b/solution.py
@@ -277,7 +277,7 @@
 
 
 def sums_kernel(idx_ref, area_ref, w_hbm, *refs):
-    left, right, own, wv, acc, sem = refs
+    wv, left, right, own, acc, sem = refs
 
     def copy(c):
         rows = pl.ds(c * WT, WT)
@@ -321,14 +321,14 @@
     return pl.pallas_call(
         sums_kernel,
         in_specs=[smem, smem, pl.BlockSpec(memory_space=pltpu.HBM)],
-        out_specs=[vmem] * 3,
-        out_shape=[jax.ShapeDtypeStruct((n * PAD, C), jnp.float32) for n in (2, 2, 3)],
+        out_specs=[vmem] * 4,
+        out_shape=[pltpu.VMEM(weights.shape, weights.dtype)]
+        + [jax.ShapeDtypeStruct((n * PAD, C), jnp.float32) for n in (2, 2, 3)],
         scratch_shapes=[
-            pltpu.VMEM(weights.shape, weights.dtype),
             pltpu.VMEM((SECT + 1, 8, C), jnp.float32),
             pltpu.SemaphoreType.DMA((WC,)),
         ],
-        compiler_params=pltpu.CompilerParams(vmem_limit_bytes=22 << 20),
+        compiler_params=pltpu.CompilerParams(vmem_limit_bytes=6 << 20),
         cost_estimate=pl.CostEstimate(
             flops=20_000_000, bytes_accessed=17 << 20, transcendentals=0
         ),
@@ -382,13 +382,7 @@
     )(*parts)
 
 
-def mass_kernel(area_ref, lost_ref, at_ref, w_hbm, c0, cl, cr, qs, qm, ls, lm, rs, rm, up, dn, l3, r3, out_ref, src, wv, by, sem):
-    def copy(c):
-        rows = pl.ds(c * WT, WT)
-        return pltpu.make_async_copy(w_hbm.at[rows], wv.at[rows], sem.at[c])
-
-    for c in range(WC):
-        copy(c).start()
+def mass_kernel(area_ref, lost_ref, at_ref, c0, cl, cr, qs, qm, ls, lm, rs, rm, up, dn, l3, r3, out_ref, src, by):
     for n, (e, m) in enumerate(((qs, qm), (ls, lm), (rs, rm))):
         at = n * PAD + R
         src[pl.ds(at, EDGE)] = e[:EDGE]
@@ -418,32 +412,28 @@
     )
     row = lax.broadcasted_iota(jnp.int32, (8, C), 0)
     out_ref[...] = jnp.where(row == 0, change, lost_ref[0])
-    for c in range(WC):
-        copy(c).wait()
-
-
-def mass_call(area, lost, at, weights, parts):
+
+
+def mass_call(area, lost, at, parts):
     smem = pl.BlockSpec(memory_space=pltpu.SMEM)
     vmem = pl.BlockSpec(memory_space=pltpu.VMEM)
     return pl.pallas_call(
         mass_kernel,
-        in_specs=[smem] * 3 + [pl.BlockSpec(memory_space=pltpu.HBM)] + [vmem] * len(parts),
-        out_specs=[vmem] * 3,
+        in_specs=[smem] * 3 + [vmem] * len(parts),
+        out_specs=[vmem] * 2,
         out_shape=[
             jax.ShapeDtypeStruct((8, C), jnp.float32),
             pltpu.VMEM((3 * PAD + 1, C, C), jnp.bfloat16),
-            pltpu.VMEM(weights.shape, weights.dtype),
         ],
         scratch_shapes=[
             pltpu.VMEM((3 * PAD, C), jnp.float32),
-            pltpu.SemaphoreType.DMA((WC,)),
         ],
         compiler_params=pltpu.CompilerParams(vmem_limit_bytes=6 << 20),
         cost_estimate=pl.CostEstimate(
             flops=9_000_000, bytes_accessed=3 << 20, transcendentals=0
         ),
         name="mass",
-    )(area, lost, at, pltpu.with_memory_space_constraint(weights, pltpu.HBM), *parts)
+    )(area, lost, at, *parts)
 
 
 def inner_kernel(first, idx_ref, wv, src, out_ref):
@@ -471,25 +461,8 @@
     )(idx, wv, near)
 
 
-HALF = CHUNKS // 2
-
-
-def far_part(first, idx_ref, wv, src, partial, out_ref):
-    for c in range(HALF):
-
-        def body(j, carry):
-            t = first + c * PER + j
-            lhs = jnp.concatenate([src[idx_ref[k, t]] for k in range(KMAX)], axis=1)
-            rhs = jnp.concatenate([wv[t, k] for k in range(KMAX)], axis=1)
-            got = lax.dot_general(lhs, rhs, NT, preferred_element_type=jnp.float32)
-            out_ref[c * PER + j] = got + partial[c][j]
-            return carry
-
-        lax.fori_loop(0, PER, body, 0, unroll=4)
-
-
-def outer0_kernel(idx_ref, wv, ls, lm, lb, rs, rm, rb, l3, r3, *refs):
-    partial, (out_ref, src) = refs[:HALF], refs[HALF:]
+def outer_kernel(idx_ref, wv, ls, lm, lb, rs, rm, rb, l3, r3, *refs):
+    partial, (out_ref, src) = refs[:CHUNKS], refs[CHUNKS:]
     for n, (e, m, b) in enumerate(((ls, lm, lb), (rs, rm, rb))):
         at = n * SIDE
         src[pl.ds(at, S + R)] = e[...]
@@ -498,35 +471,40 @@
     src[pl.ds(FAR2, E)] = l3[...]
     src[pl.ds(FAR2 + E, E)] = r3[...]
     src[FAR2 + 2 * E] = jnp.zeros((C, C), src.dtype)
-    far_part(0, idx_ref, wv, src, partial, out_ref)
-
-
-def outer1_kernel(idx_ref, wv, src, *refs):
-    far_part(HALF * PER, idx_ref, wv, src, refs[:HALF], refs[HALF])
-
-
-def outer_call(half, idx, wv, parts, partial):
-    vmem = pl.BlockSpec(memory_space=pltpu.VMEM)
-    out_shape = [pltpu.VMEM((HALF * PER, C, C), jnp.float32)]
-    if half == 0:
-        out_shape.append(pltpu.VMEM((FAR2 + 2 * E + 1, C, C), jnp.bfloat16))
-    return pl.pallas_call(
-        (outer0_kernel, outer1_kernel)[half],
+    for c in range(CHUNKS):
+
+        def body(j, carry):
+            t = c * PER + j
+            lhs = jnp.concatenate([src[idx_ref[k, t]] for k in range(KMAX)], axis=1)
+            rhs = jnp.concatenate([wv[t, k] for k in range(KMAX)], axis=1)
+            got = lax.dot_general(lhs, rhs, NT, preferred_element_type=jnp.float32)
+            out_ref[t] = got + partial[c][j]
+            return carry
+
+        lax.fori_loop(0, PER, body, 0, unroll=4)
+
+
+def outer_call(idx, wv, parts, partial):
+    vmem = pl.BlockSpec(memory_space=pltpu.VMEM)
+    return pl.pallas_call(
+        outer_kernel,
         in_specs=[pl.BlockSpec(memory_space=pltpu.SMEM)]
         + [vmem] * (1 + len(parts) + len(partial)),
-        out_specs=[vmem] * len(out_shape),
-        out_shape=out_shape,
+        out_specs=vmem,
+        out_shape=pltpu.VMEM((ROWS, C, C), jnp.float32),
+        scratch_shapes=[pltpu.VMEM((FAR2 + 2 * E + 1, C, C), jnp.bfloat16)],
         compiler_params=pltpu.CompilerParams(vmem_limit_bytes=8 << 20),
         cost_estimate=pl.CostEstimate(
-            flops=2 * HALF * PER * KMAX * C**3, bytes_accessed=1 << 20, transcendentals=0
-        ),
+            flops=2 * ROWS * KMAX * C**3, bytes_accessed=1 << 20, transcendentals=0
+        ),
+        name="outer",
     )(idx, wv, *parts, *partial)
 
 
 WRITES = 8
 
 
-def write_kernel(corr_ref, a_ref, b_ref, out_hbm, buf, sem):
+def write_kernel(corr_ref, in_ref, out_hbm, buf, sem):
     rows = ROWS // WRITES
 
     def copy(c):
@@ -534,20 +512,19 @@
         return pltpu.make_async_copy(buf.at[at], out_hbm.at[at], sem.at[c])
 
     for c in range(WRITES):
-        ref = a_ref if c < WRITES // 2 else b_ref
         for i in range(rows):
             t = c * rows + i
-            buf[t] = ref[t % (ROWS // 2)] + corr_ref[...]
+            buf[t] = in_ref[t] + corr_ref[...]
         copy(c).start()
     for c in range(WRITES):
         copy(c).wait()
 
 
-def write_call(corr, first, second):
+def write_call(corr, advected):
     vmem = pl.BlockSpec(memory_space=pltpu.VMEM)
     return pl.pallas_call(
         write_kernel,
-        in_specs=[vmem] * 3,
+        in_specs=[vmem] * 2,
         out_specs=pl.BlockSpec(memory_space=pltpu.HBM),
         out_shape=jax.ShapeDtypeStruct((ROWS, C, C), jnp.float32),
         scratch_shapes=[
@@ -559,7 +536,7 @@
             flops=1_000_000, bytes_accessed=4 << 20, transcendentals=0
         ),
         name="write",
-    )(corr, first, second)
+    )(corr, advected)
 
 
 def tables(source_row, source_block, slot_count, lat, lon):
@@ -594,6 +571,11 @@
     return lax.ppermute(v, axis, [(i, to(i)) for i in range(size)])
 
 
+def three(v, axis, size, to):
+    got = [swap(v, axis, size, functools.partial(to, by=by)) for by in (1, 2, 3)]
+    return (got[0] + got[2]) + got[1]
+
+
 def local(tracers, weights, source_row, source_block, slot_count):
     args = (tracers, weights, source_row, source_block, slot_count)
     lost, fixed = usual(*args)
@@ -618,25 +600,25 @@
     r3 = lax.ppermute(pole, both, some(-3, POLAR))
     sums_idx, near_idx, far_idx, lost = tables(source_row, source_block, slot_count, lat, lon)
     area = latitude_area(lat * ROWS, ROWS)
-    to_left, to_right, own_sums = sums_call(sums_idx, area, w)
+    wv, to_left, to_right, own_sums = sums_call(sums_idx, area, w)
     cl = lax.ppermute(to_left, "lon", ring(-1))
     cr = lax.ppermute(to_right, "lon", ring(1))
     first, last = pack_call((qs, ls, rs))
     up1, dn1 = lax.ppermute(first, "lat", UP), lax.ppermute(last, "lat", DOWN)
     at = jnp.where(jnp.arange(NLAT_DEV, dtype=jnp.int32) == lat, R, R + ROWS - E).astype(jnp.int32)
-    v, near, wv = mass_call(
-        area, lost.reshape(1), at, w,
+    v, near = mass_call(
+        area, lost.reshape(1), at,
         (own_sums, cl, cr, qs, qm, ls, lm, rs, rm, up1, dn1, l3, r3),
     )
     held = lambda x: pltpu.with_memory_space_constraint(x, pltpu.VMEM)
     near, wv = held(near), held(wv)
-    for axis, size, bit in (("lat", NLAT_DEV, 1), ("lat", NLAT_DEV, 2), ("lat", NLAT_DEV, 4), ("lon", NLON_DEV, 4), ("lon", NLON_DEV, 8)):
-        v = v + swap(v, axis, size, lambda i, bit=bit: i ^ bit)
-    y = [swap(v, "lon", NLON_DEV, lambda i, by=by: i // 4 * 4 + (i + by) % 4) for by in (1, 2, 3)]
-    v = v + (y[0] + y[2]) + y[1]
+    v = v + swap(v, "lat", NLAT_DEV, lambda i: i ^ 1)
+    v = v + three(v, "lat", NLAT_DEV, lambda i, by: (i + 2 * by) % NLAT_DEV)
+    v = v + three(v, "lon", NLON_DEV, lambda i, by: (i + 4 * by) % NLON_DEV)
+    v = v + three(v, "lon", NLON_DEV, lambda i, by: i // 4 * 4 + (i + by) % 4)
     corr = jnp.broadcast_to((v[0] * (1.0 / TOTAL_AREA))[:, None], (C, C))
 
-    beyond = jnp.where((lat == 0) | (lat == NLAT_DEV - 2), dn1[R:], up1[R:])
+    beyond = jnp.where(lat == 0, dn1[R:], jnp.where(lat == NLAT_DEV - 2, dn1[R:], up1[R:]))
     sides = ((ls, beyond[:R], 1), (rs, beyond[R:], -1))
     lls, rrs = (
         lax.ppermute(jnp.concatenate([x, h], axis=0), both, some(d, POLAR)) for x, h, d in sides
@@ -651,11 +633,8 @@
     llm, rrm = (lax.ppermute(x, both, some(d, POLAR)) for x, d in ((lm, 1), (rm, -1)))
 
     partial = [held(inner_call(c, near_idx, wv, near)) for c in range(CHUNKS)]
-    first, src = outer_call(
-        0, far_idx, wv, (lls, llm, llb, rrs, rrm, rrb, l3, r3), partial[:HALF]
-    )
-    (second,) = outer_call(1, far_idx, wv, (held(src),), partial[HALF:])
-    fixed = write_call(corr, held(first), held(second))
+    advected = outer_call(far_idx, wv, (lls, llm, llb, rrs, rrm, rrb, l3, r3), partial)
+    fixed = write_call(corr, held(advected))
     return v[1, 0], fixed
 
 

time: 144 us -> 148 us (1.028)
  starting transfers between devices: 50.4 us -> 60.9 us
  Pallas kernels: 39.4 us -> 34.5 us
  other arithmetic: 2.93 us -> 1.25 us
    ppermute x8 -> x10, starting transfers between devices: 5.08 us -> 12.8 us  [swap(): return lax.ppermute(v, axis, [(i, to(i)) for i in range(size)])]
    pallas_call x4 -> x3, Pallas kernels: 19.3 us -> 15.3 us  [the longest x1 8.17 us: outer_call(): pl.pallas_call(outer_kernel, in_specs=[pl.BlockSpec(memory_space=pltpu.SM...]
    ppermute x2, starting transfers between devices: 6.56 us -> 9.15 us  [usual(): lax.ppermute(x, both, some(d, POLAR))]
    ppermute x8 -> x10, waiting for transfers between devices: 21 us -> 20.5 us  [swap(): return lax.ppermute(v, axis, [(i, to(i)) for i in range(size)])]
  transfers between devices with their start and end apart: 24 -> 26, of which waited for: 11 -> 8; matrix products, arithmetic and copies ran while one was open for 2% -> 1% of each run, Pallas kernels for 18% -> 11%
where the time goes in v5:
time: 148 us; the launch traced here: 147 us
  starting transfers between devices  60.9 us (41%)
  waiting for transfers between devices  48.9 us (33%)
  Pallas kernels  34.5 us (23%)
    ppermute x10, waiting for transfers between devices, swap(): return lax.ppermute(v, axis, [(i, to(i)) for i in range(size)])  20.5 us
    ppermute x1, waiting for transfers between devices, usual(): lax.ppermute(qs, 'lon', ring(1))  18.5 us
    ppermute x10, starting transfers between devices, swap(): return lax.ppermute(v, axis, [(i, to(i)) for i in range(size)])  12.8 us
    pallas_call x4, Pallas kernels, inner_call(): pl.pallas_call(functools.partial(inner_kernel, chunk * PER), in_specs=[pl...  9.35 us
    ppermute x2, starting transfers between devices, usual(): lax.ppermute(jnp.concatenate([x, h], axis=0), both, some(d, POLAR))  9.16 us
    ppermute x2, starting transfers between devices, usual(): lax.ppermute(x, both, some(d, POLAR))  9.15 us
    ppermute x1, waiting for transfers between devices, usual(): cr = lax.ppermute(to_right, 'lon', ring(1))  8.21 us
    pallas_call x1, Pallas kernels, outer_call(): pl.pallas_call(outer_kernel, in_specs=[pl.BlockSpec(memory_space=pltpu.SM...  8.17 us
  transfers between devices with their start and end apart: 26, of which 8 were waited for; matrix products, arithmetic and copies ran while one was open for 1% of the time, Pallas kernels for 11%

profile of v5, /device:TPU:0, one launch (start us, length us, event | category | flops | bytes accessed | tf_op | source)
XLA Modules:
  0.0 147.2 jit_solution(12827671400316481697)
XLA Ops:
  0.0 2.6 %split.1 = (bf16[32,128,128]{2,1,0:T(8,128)(2,1)S(1)}, bf16[32,128,128]{2,1,0:T(8,128)(2,1)}) custom-call(bf16[64,128,128]{2,1,0:T(8,128)(2,1)} %bitcast.155), custom_call_target="tpu_custom_call" | custom-call | flops 1000 | bytes 2097152 | tf_op jit(solution)/shard_map/split/pallas_call | solution.py:354
  2.6 1.8 %collective-permute-start.16 = (bf16[32,128,128]{2,1,0:T(8,128)(2,1)S(1)}, bf16[32,128,128]{2,1,0:T(8,128)(2,1)S(1)}, u32[]{:S(2)}, u32[]{:S(2)}) collective-permute-start(bf16[32,128,128]{2,1,0:T(8,128)(2,1)S(1)} %get-tuple-element.57.qs), channel_id=1, source_target_pairs={{0,1},{1,2},{2,3},{3,4},{4,5},{5,6},{6,7},{7,8},{8,9},{9,10},{10,1... | collective-permute-start | bytes 3145736 | tf_op jit(solution)/shard_map/ppermute | solution.py:596
  4.3 5.0 %collective-permute-start.18 = (bf16[32,128,128]{2,1,0:T(8,128)(2,1)S(1)}, bf16[32,128,128]{2,1,0:T(8,128)(2,1)S(1)}, u32[]{:S(2)}, u32[]{:S(2)}) collective-permute-start(bf16[32,128,128]{2,1,0:T(8,128)(2,1)S(1)} %get-tuple-element.57.qs), channel_id=1, source_target_pairs={{0,15},{1,0},{2,1},{3,2},{4,3},{5,4},{6,5},{7,6},{8,7},{9,8},{10,9... | collective-permute-start | bytes 3145736 | tf_op jit(solution)/shard_map/ppermute | solution.py:596
  9.3 5.3 %collective-permute-start.19 = (bf16[32,128,128]{2,1,0:T(8,128)(2,1)}, bf16[32,128,128]{2,1,0:T(8,128)(2,1)}, u32[]{:S(2)}, u32[]{:S(2)}) collective-permute-start(bf16[32,128,128]{2,1,0:T(8,128)(2,1)} %get-tuple-element.58.qm), channel_id=1, source_target_pairs={{0,15},{1,0},{2,1},{3,2},{4,3},{5,4},{6,5},{7,6},{8,7},{9,8},{10,9... | collective-permute-start | bytes 3145736 | tf_op jit(solution)/shard_map/ppermute | solution.py:597
  14.8 18.5 %collective-permute-done.16.ls = bf16[32,128,128]{2,1,0:T(8,128)(2,1)S(1)} collective-permute-done((bf16[32,128,128]{2,1,0:T(8,128)(2,1)S(1)}, bf16[32,128,128]{2,1,0:T(8,128)(2,1)S(1)}, u32[]{:S(2)}, u32[]{:S(2)}) %collective-permute-start.16) | collective-permute-done | bytes 1048608 | tf_op jit(solution)/shard_map/ppermute | solution.py:596
  33.3 1.3 collective-permute-start.20
  34.6 1.3 collective-permute-start.21
  36.0 7.2 %sums.1 = (bf16[64,8,128,128]{3,2,1,0:T(8,128)(2,1)S(1)}, f32[144,128]{1,0:T(8,128)S(1)}, f32[144,128]{1,0:T(8,128)S(1)}, f32[216,128]{1,0:T(8,128)S(1)}) custom-call(s32[8,64]{1,0:T(8,128)S(1)} %get-tuple-element.111.idx_ref, f32[64]{0:T(128)S(1)} %add_cosine_fusion.1.area_ref, bf16[64,8,128,128]{3,2,1,0:T(8,128)(2,1)} %bitcast.151), custom_call_target="tpu_custom_call" | custom-call | flops 20000000 | bytes 17825792 | tf_op jit(solution)/shard_map/sums/pallas_call | solution.py:321
  43.2 0.6 convert_reduce_fusion.1
  43.8 0.1 slice_select_fusion.3
  43.9 5.5 %collective-permute-start.14 = (f32[144,128]{1,0:T(8,128)S(1)}, f32[144,128]{1,0:T(8,128)S(1)}, u32[]{:S(2)}, u32[]{:S(2)}) collective-permute-start(f32[144,128]{1,0:T(8,128)S(1)} %get-tuple-element.55), channel_id=1, source_target_pairs={{0,15},{1,0},{2,1},{3,2},{4,3},{5,4},{6,5},{7,6},{8,7},{9,8},{10,9... | collective-permute-start | bytes 221192 | tf_op jit(solution)/shard_map/ppermute | solution.py:604
  49.4 1.9 %collective-permute-start.22 = (bf16[5,128,128]{2,1,0:T(8,128)(2,1)S(1)}, bf16[5,128,128]{2,1,0:T(8,128)(2,1)S(1)}, u32[]{:S(2)}, u32[]{:S(2)}) collective-permute-start(bf16[5,128,128]{2,1,0:T(8,128)(2,1)S(1)} %slice_select_fusion.4), channel_id=1, source_target_pairs={{0,3},{1,4},{2,5},{3,6},{4,7},{5,8},{6,9},{7,10},{8,11},{9,12},{10... | collective-permute-start | bytes 491528 | tf_op jit(solution)/shard_map/ppermute | solution.py:599
  51.3 6.0 %collective-permute-start.23 = (bf16[5,128,128]{2,1,0:T(8,128)(2,1)S(1)}, bf16[5,128,128]{2,1,0:T(8,128)(2,1)S(1)}, u32[]{:S(2)}, u32[]{:S(2)}) collective-permute-start(bf16[5,128,128]{2,1,0:T(8,128)(2,1)S(1)} %slice_select_fusion.4), channel_id=1, source_target_pairs={{0,13},{1,14},{2,15},{3,0},{4,1},{5,2},{6,3},{7,4},{8,5},{9,6},{10... | collective-permute-start | bytes 491528 | tf_op jit(solution)/shard_map/ppermute | solution.py:600
  57.4 0.1 collective-permute-start.15
  57.5 8.2 %collective-permute-done.15.cr = f32[144,128]{1,0:T(8,128)S(1)} collective-permute-done((f32[144,128]{1,0:T(8,128)S(1)}, f32[144,128]{1,0:T(8,128)S(1)}, u32[]{:S(2)}, u32[]{:S(2)}) %collective-permute-start.15) | collective-permute-done | bytes 73760 | tf_op jit(solution)/shard_map/ppermute | solution.py:605
  65.7 5.0 %mass.1 = (f32[8,128]{1,0:T(8,128)S(1)}, bf16[217,128,128]{2,1,0:T(8,128)(2,1)S(1)}) custom-call(f32[64]{0:T(128)S(1)} %add_cosine_fusion.1.area_ref, f32[1]{0:T(128)} %bitcast.24.lost_ref, s32[8]{0:T(128)S(1)} %compare_select_fusion.1.at_ref, f32[216,128]{1,0:T(8,128)S(1)} %get-tuple-element.54.c0, f32[144,128]{1,0:T(8,128)S(1)} %collective-permute-done.14.cl, ...), custom_call_target="tpu_custom_call" | custom-call | flops 9000000 | bytes 3145728 | tf_op jit(solution)/shard_map/mass/pallas_call | solution.py:420
  70.7 0.1 pad_maximum_fusion.7
  70.8 0.7 collective-permute-start.36
  71.5 0.4 collective-permute-done.24
  71.9 3.9 %collective-permute-start.26 = (f32[8,128]{1,0:T(8,128)S(1)}, f32[8,128]{1,0:T(8,128)S(1)}, u32[]{:S(2)}, u32[]{:S(2)}) collective-permute-start(f32[8,128]{1,0:T(8,128)S(1)} %add.234), channel_id=1, source_target_pairs={{0,96},{16,112},{32,0},{48,16},{64,32},{80,48},{96,64},{112,80},{1... | collective-permute-start | bytes 12296 | tf_op jit(solution)/shard_map/ppermute | solution.py:571
  75.8 1.4 collective-permute-start.27
  77.2 0.1 pad_maximum_fusion.5
  77.3 3.6 %collective-permute-done.27 = f32[8,128]{1,0:T(8,128)S(1)} collective-permute-done((f32[8,128]{1,0:T(8,128)S(1)}, f32[8,128]{1,0:T(8,128)S(1)}, u32[]{:S(2)}, u32[]{:S(2)}) %collective-permute-start.27) | collective-permute-done | bytes 4128 | tf_op jit(solution)/shard_map/ppermute | solution.py:571
  81.0 3.2 %collective-permute-start.29 = (f32[8,128]{1,0:T(8,128)S(1)}, f32[8,128]{1,0:T(8,128)S(1)}, u32[]{:S(2)}, u32[]{:S(2)}) collective-permute-start(f32[8,128]{1,0:T(8,128)S(1)} %add_add_fusion.2), channel_id=1, source_target_pairs={{0,12},{1,13},{2,14},{3,15},{4,0},{5,1},{6,2},{7,3},{8,4},{9,5},{1... | collective-permute-start | bytes 12296 | tf_op jit(solution)/shard_map/ppermute | solution.py:571
  84.2 0.1 pad_maximum_fusion.6
  84.3 1.9 %collective-permute-start.34 = (bf16[36,128,128]{2,1,0:T(8,128)(2,1)S(1)}, bf16[36,128,128]{2,1,0:T(8,128)(2,1)S(1)}, u32[]{:S(2)}, u32[]{:S(2)}) collective-permute-start(bf16[36,128,128]{2,1,0:T(8,128)(2,1)S(1)} %pad_maximum_fusion.5), channel_id=1, source_target_pairs={{0,1},{1,2},{2,3},{3,4},{4,5},{5,6},{6,7},{7,8},{8,9},{9,10},{10,1... | collective-permute-start | bytes 3538952 | tf_op jit(solution)/shard_map/ppermute | solution.py:624
  86.2 7.2 %collective-permute-start.37 = (bf16[36,128,128]{2,1,0:T(8,128)(2,1)S(1)}, bf16[36,128,128]{2,1,0:T(8,128)(2,1)S(1)}, u32[]{:S(2)}, u32[]{:S(2)}) collective-permute-start(bf16[36,128,128]{2,1,0:T(8,128)(2,1)S(1)} %pad_maximum_fusion.6), channel_id=1, source_target_pairs={{0,15},{1,0},{2,1},{3,2},{4,3},{5,4},{6,5},{7,6},{8,7},{9,8},{10,9... | collective-permute-start | bytes 3538952 | tf_op jit(solution)/shard_map/ppermute | solution.py:624
  93.5 0.1 collective-permute-start.31
  93.6 3.2 %collective-permute-start.32 = (f32[8,128]{1,0:T(8,128)S(1)}, f32[8,128]{1,0:T(8,128)S(1)}, u32[]{:S(2)}, u32[]{:S(2)}) collective-permute-start(f32[8,128]{1,0:T(8,128)S(1)} %add_add_fusion.1), channel_id=1, source_target_pairs={{0,3},{1,0},{2,1},{3,2},{4,7},{5,4},{6,5},{7,6},{8,11},{9,8},{10,9... | collective-permute-start | bytes 12296 | tf_op jit(solution)/shard_map/ppermute | solution.py:571
  96.8 7.8 %collective-permute-done.31 = f32[8,128]{1,0:T(8,128)S(1)} collective-permute-done((f32[8,128]{1,0:T(8,128)S(1)}, f32[8,128]{1,0:T(8,128)S(1)}, u32[]{:S(2)}, u32[]{:S(2)}) %collective-permute-start.31) | collective-permute-done | bytes 4128 | tf_op jit(solution)/shard_map/ppermute | solution.py:571
  104.6 1.0 collective-permute-start.33
  105.6 8.7 %collective-permute-done.32 = f32[8,128]{1,0:T(8,128)S(1)} collective-permute-done((f32[8,128]{1,0:T(8,128)S(1)}, f32[8,128]{1,0:T(8,128)S(1)}, u32[]{:S(2)}, u32[]{:S(2)}) %collective-permute-start.32) | collective-permute-done | bytes 4128 | tf_op jit(solution)/shard_map/ppermute | solution.py:571
  114.3 2.5 %collective-permute-start.35 = (bf16[32,128,128]{2,1,0:T(8,128)(2,1)}, bf16[32,128,128]{2,1,0:T(8,128)(2,1)S(1)}, u32[]{:S(2)}, u32[]{:S(2)}) collective-permute-start(bf16[32,128,128]{2,1,0:T(8,128)(2,1)} %collective-permute-done.17.lm), channel_id=1, source_target_pairs={{0,1},{1,2},{2,3},{3,4},{4,5},{5,6},{6,7},{7,8},{8,9},{9,10},{10,1... | collective-permute-start | bytes 3145736 | tf_op jit(solution)/shard_map/ppermute | solution.py:633
  116.8 6.7 %collective-permute-start.38 = (bf16[32,128,128]{2,1,0:T(8,128)(2,1)}, bf16[32,128,128]{2,1,0:T(8,128)(2,1)S(1)}, u32[]{:S(2)}, u32[]{:S(2)}) collective-permute-start(bf16[32,128,128]{2,1,0:T(8,128)(2,1)} %collective-permute-done.19.rm), channel_id=1, source_target_pairs={{0,15},{1,0},{2,1},{3,2},{4,3},{5,4},{6,5},{7,6},{8,7},{9,8},{10,9... | collective-permute-start | bytes 3145736 | tf_op jit(solution)/shard_map/ppermute | solution.py:633
  123.5 0.1 slice_select_fusion.2
  123.6 0.1 pad_maximum_fusion.8
  123.6 0.9 collective-permute-start.39
  124.5 2.3 %shard_map.58.refs_3_ = f32[16,128,128]{2,1,0:T(8,128)S(1)} custom-call(s32[8,64]{1,0:T(8,128)S(1)} %get-tuple-element.110.idx_ref, bf16[64,8,128,128]{3,2,1,0:T(8,128)(2,1)S(1)} %get-tuple-element.62.wv, bf16[217,128,128]{2,1,0:T(8,128)(2,1)S(1)} %get-tuple-element.63.src), custom_call_target="tpu_custom_call" | custom-call | flops 536870912 | bytes 1048576 | tf_op jit(solution)/shard_map/pallas_call | solution.py:452
  126.9 2.3 %shard_map.57.refs_2_ = f32[16,128,128]{2,1,0:T(8,128)S(1)} custom-call(s32[8,64]{1,0:T(8,128)S(1)} %get-tuple-element.110.idx_ref, bf16[64,8,128,128]{3,2,1,0:T(8,128)(2,1)S(1)} %get-tuple-element.62.wv, bf16[217,128,128]{2,1,0:T(8,128)(2,1)S(1)} %get-tuple-element.63.src), custom_call_target="tpu_custom_call" | custom-call | flops 536870912 | bytes 1048576 | tf_op jit(solution)/shard_map/pallas_call | solution.py:452
  129.2 2.3 %shard_map.56.refs_1_ = f32[16,128,128]{2,1,0:T(8,128)S(1)} custom-call(s32[8,64]{1,0:T(8,128)S(1)} %get-tuple-element.110.idx_ref, bf16[64,8,128,128]{3,2,1,0:T(8,128)(2,1)S(1)} %get-tuple-element.62.wv, bf16[217,128,128]{2,1,0:T(8,128)(2,1)S(1)} %get-tuple-element.63.src), custom_call_target="tpu_custom_call" | custom-call | flops 536870912 | bytes 1048576 | tf_op jit(solution)/shard_map/pallas_call | solution.py:452
  131.6 2.3 %shard_map.55.refs_0_ = f32[16,128,128]{2,1,0:T(8,128)S(1)} custom-call(s32[8,64]{1,0:T(8,128)S(1)} %get-tuple-element.110.idx_ref, bf16[64,8,128,128]{3,2,1,0:T(8,128)(2,1)S(1)} %get-tuple-element.62.wv, bf16[217,128,128]{2,1,0:T(8,128)(2,1)S(1)} %get-tuple-element.63.src), custom_call_target="tpu_custom_call" | custom-call | flops 536870912 | bytes 1048576 | tf_op jit(solution)/shard_map/pallas_call | solution.py:452
  133.9 0.5 slice.110
  134.5 0.1 collective-permute-done.35.lm
  134.5 1.6 %collective-permute-done.38.rm = bf16[32,128,128]{2,1,0:T(8,128)(2,1)S(1)} collective-permute-done((bf16[32,128,128]{2,1,0:T(8,128)(2,1)}, bf16[32,128,128]{2,1,0:T(8,128)(2,1)S(1)}, u32[]{:S(2)}, u32[]{:S(2)}) %collective-permute-start.38) | collective-permute-done | bytes 1048608 | tf_op jit(solution)/shard_map/ppermute | solution.py:633
  136.1 8.2 %outer.1.in_ref = f32[64,128,128]{2,1,0:T(8,128)S(1)} custom-call(s32[8,64]{1,0:T(8,128)S(1)} %get-tuple-element.112.idx_ref, bf16[64,8,128,128]{3,2,1,0:T(8,128)(2,1)S(1)} %get-tuple-element.62.wv, bf16[36,128,128]{2,1,0:T(8,128)(2,1)S(1)} %collective-permute-done.34.ls, bf16[32,128,128]{2,1,0:T(8,128)(2,1)S(1)} %collective-permute-done.35.lm, ...), custom_call_target="tpu_custom_call" | custom-call | flops 2147483648 | bytes 1048576 | tf_op jit(solution)/shard_map/outer/pallas_call | solution.py:489
  144.3 0.1 broadcast_in_dim.44.corr_ref
  144.4 2.1 %write.1 = f32[64,128,128]{2,1,0:T(8,128)} custom-call(f32[128,128]{1,0:T(8,128)S(1)} %broadcast_in_dim.44.corr_ref, f32[64,128,128]{2,1,0:T(8,128)S(1)} %outer.1.in_ref), custom_call_target="tpu_custom_call" | custom-call | flops 1000000 | bytes 4194304 | tf_op jit(solution)/shard_map/write/pallas_call | solution.py:525
  146.5 0.6 while.9
  (41 shorter events, 0.3 us)
Async XLA Ops:
  0.0 14.7 %copy-start.6 = (s32[64,1]{0,1:T(1,128)S(1)}, s32[64,1]{0,1:T(1,128)}, u32[]{:S(2)}) copy-start(s32[64,1]{0,1:T(1,128)} %param.11) | copy-start | bytes 772
  0.0 14.7 %copy-start.4 = (s32[64,1,8]{0,2,1:T(8,128)S(1)}, s32[64,1,8]{0,2,1:T(8,128)}, u32[]{:S(2)}) copy-start(s32[64,1,8]{0,2,1:T(8,128)} %param.10) | copy-start | bytes 6148
  0.0 14.7 %copy-start.2 = (s32[64,1,8]{0,2,1:T(8,128)S(1)}, s32[64,1,8]{0,2,1:T(8,128)}, u32[]{:S(2)}) copy-start(s32[64,1,8]{0,2,1:T(8,128)} %param.9) | copy-start | bytes 6148
  2.6 30.7 %collective-permute-start.16 = (bf16[32,128,128]{2,1,0:T(8,128)(2,1)S(1)}, bf16[32,128,128]{2,1,0:T(8,128)(2,1)S(1)}, u32[]{:S(2)}, u32[]{:S(2)}) collective-permute-start(bf16[32,128,128]{2,1,0:T(8,128)(2,1)S(1)} %get-tuple-element.57.qs), channel_id=1, source_target_pairs={{0,1},{1,2},{2,3},{3,4},{4,5},{5,6},{6,7},{7,8},{8,9},{9,10},{10,1... | collective-permute-start | bytes 3145736 | tf_op jit(solution)/shard_map/ppermute | solution.py:596
  4.3 28.9 %collective-permute-start.18 = (bf16[32,128,128]{2,1,0:T(8,128)(2,1)S(1)}, bf16[32,128,128]{2,1,0:T(8,128)(2,1)S(1)}, u32[]{:S(2)}, u32[]{:S(2)}) collective-permute-start(bf16[32,128,128]{2,1,0:T(8,128)(2,1)S(1)} %get-tuple-element.57.qs), channel_id=1, source_target_pairs={{0,15},{1,0},{2,1},{3,2},{4,3},{5,4},{6,5},{7,6},{8,7},{9,8},{10,9... | collective-permute-start | bytes 3145736 | tf_op jit(solution)/shard_map/ppermute | solution.py:596
  9.3 56.4 %collective-permute-start.17 = (bf16[32,128,128]{2,1,0:T(8,128)(2,1)}, bf16[32,128,128]{2,1,0:T(8,128)(2,1)}, u32[]{:S(2)}, u32[]{:S(2)}) collective-permute-start(bf16[32,128,128]{2,1,0:T(8,128)(2,1)} %get-tuple-element.58.qm), channel_id=1, source_target_pairs={{0,1},{1,2},{2,3},{3,4},{4,5},{5,6},{6,7},{7,8},{8,9},{9,10},{10,1... | collective-permute-start | bytes 3145736 | tf_op jit(solution)/shard_map/ppermute | solution.py:597
  9.3 56.4 %collective-permute-start.19 = (bf16[32,128,128]{2,1,0:T(8,128)(2,1)}, bf16[32,128,128]{2,1,0:T(8,128)(2,1)}, u32[]{:S(2)}, u32[]{:S(2)}) collective-permute-start(bf16[32,128,128]{2,1,0:T(8,128)(2,1)} %get-tuple-element.58.qm), channel_id=1, source_target_pairs={{0,15},{1,0},{2,1},{3,2},{4,3},{5,4},{6,5},{7,6},{8,7},{9,8},{10,9... | collective-permute-start | bytes 3145736 | tf_op jit(solution)/shard_map/ppermute | solution.py:597
  33.3 16.0 %collective-permute-start.20 = (bf16[12,128,128]{2,1,0:T(8,128)(2,1)S(1)}, bf16[12,128,128]{2,1,0:T(8,128)(2,1)S(1)}, u32[]{:S(2)}, u32[]{:S(2)}) collective-permute-start(bf16[12,128,128]{2,1,0:T(8,128)(2,1)S(1)} %get-tuple-element.59), channel_id=1, source_target_pairs={{0,16},{16,32},{32,48},{48,64},{64,80},{80,96},{96,112},{1,17},{17... | collective-permute-start | bytes 1179656 | tf_op jit(solution)/shard_map/ppermute | solution.py:607
  34.6 16.6 %collective-permute-start.21 = (bf16[12,128,128]{2,1,0:T(8,128)(2,1)S(1)}, bf16[12,128,128]{2,1,0:T(8,128)(2,1)S(1)}, u32[]{:S(2)}, u32[]{:S(2)}) collective-permute-start(bf16[12,128,128]{2,1,0:T(8,128)(2,1)S(1)} %get-tuple-element.60), channel_id=1, source_target_pairs={{16,0},{32,16},{48,32},{64,48},{80,64},{96,80},{112,96},{17,1},{33... | collective-permute-start | bytes 1179656 | tf_op jit(solution)/shard_map/ppermute | solution.py:607
  43.9 13.5 %collective-permute-start.14 = (f32[144,128]{1,0:T(8,128)S(1)}, f32[144,128]{1,0:T(8,128)S(1)}, u32[]{:S(2)}, u32[]{:S(2)}) collective-permute-start(f32[144,128]{1,0:T(8,128)S(1)} %get-tuple-element.55), channel_id=1, source_target_pairs={{0,15},{1,0},{2,1},{3,2},{4,3},{5,4},{6,5},{7,6},{8,7},{9,8},{10,9... | collective-permute-start | bytes 221192 | tf_op jit(solution)/shard_map/ppermute | solution.py:604
  49.4 16.3 %collective-permute-start.22 = (bf16[5,128,128]{2,1,0:T(8,128)(2,1)S(1)}, bf16[5,128,128]{2,1,0:T(8,128)(2,1)S(1)}, u32[]{:S(2)}, u32[]{:S(2)}) collective-permute-start(bf16[5,128,128]{2,1,0:T(8,128)(2,1)S(1)} %slice_select_fusion.4), channel_id=1, source_target_pairs={{0,3},{1,4},{2,5},{3,6},{4,7},{5,8},{6,9},{7,10},{8,11},{9,12},{10... | collective-permute-start | bytes 491528 | tf_op jit(solution)/shard_map/ppermute | solution.py:599
  51.3 14.4 %collective-permute-start.23 = (bf16[5,128,128]{2,1,0:T(8,128)(2,1)S(1)}, bf16[5,128,128]{2,1,0:T(8,128)(2,1)S(1)}, u32[]{:S(2)}, u32[]{:S(2)}) collective-permute-start(bf16[5,128,128]{2,1,0:T(8,128)(2,1)S(1)} %slice_select_fusion.4), channel_id=1, source_target_pairs={{0,13},{1,14},{2,15},{3,0},{4,1},{5,2},{6,3},{7,4},{8,5},{9,6},{10... | collective-permute-start | bytes 491528 | tf_op jit(solution)/shard_map/ppermute | solution.py:600
  57.4 8.3 %collective-permute-start.15 = (f32[144,128]{1,0:T(8,128)S(1)}, f32[144,128]{1,0:T(8,128)S(1)}, u32[]{:S(2)}, u32[]{:S(2)}) collective-permute-start(f32[144,128]{1,0:T(8,128)S(1)} %get-tuple-element.56), channel_id=1, source_target_pairs={{0,1},{1,2},{2,3},{3,4},{4,5},{5,6},{6,7},{7,8},{8,9},{9,10},{10,1... | collective-permute-start | bytes 221192 | tf_op jit(solution)/shard_map/ppermute | solution.py:605
  70.7 1.2 collective-permute-start.24
  70.8 52.8 %collective-permute-start.36 = (bf16[20,128,128]{2,1,0:T(8,128)(2,1)S(1)}, bf16[20,128,128]{2,1,0:T(8,128)(2,1)S(1)}, u32[]{:S(2)}, u32[]{:S(2)}) collective-permute-start(bf16[20,128,128]{2,1,0:T(8,128)(2,1)S(1)} %pad_maximum_fusion.7), channel_id=1, source_target_pairs={{16,17},{17,18},{18,19},{19,20},{20,21},{21,22},{22,23},{23,24},{2... | collective-permute-start | bytes 1966088 | tf_op jit(solution)/shard_map/ppermute | solution.py:627
  71.9 5.4 %collective-permute-start.25 = (f32[8,128]{1,0:T(8,128)S(1)}, f32[8,128]{1,0:T(8,128)S(1)}, u32[]{:S(2)}, u32[]{:S(2)}) collective-permute-start(f32[8,128]{1,0:T(8,128)S(1)} %add.234), channel_id=1, source_target_pairs={{0,32},{16,48},{32,64},{48,80},{64,96},{80,112},{96,0},{112,16},{1... | collective-permute-start | bytes 12296 | tf_op jit(solution)/shard_map/ppermute | solution.py:571
  71.9 5.4 %collective-permute-start.26 = (f32[8,128]{1,0:T(8,128)S(1)}, f32[8,128]{1,0:T(8,128)S(1)}, u32[]{:S(2)}, u32[]{:S(2)}) collective-permute-start(f32[8,128]{1,0:T(8,128)S(1)} %add.234), channel_id=1, source_target_pairs={{0,96},{16,112},{32,0},{48,16},{64,32},{80,48},{96,64},{112,80},{1... | collective-permute-start | bytes 12296 | tf_op jit(solution)/shard_map/ppermute | solution.py:571
  75.8 5.1 %collective-permute-start.27 = (f32[8,128]{1,0:T(8,128)S(1)}, f32[8,128]{1,0:T(8,128)S(1)}, u32[]{:S(2)}, u32[]{:S(2)}) collective-permute-start(f32[8,128]{1,0:T(8,128)S(1)} %add.234), channel_id=1, source_target_pairs={{0,64},{16,80},{32,96},{48,112},{64,0},{80,16},{96,32},{112,48},{1... | collective-permute-start | bytes 12296 | tf_op jit(solution)/shard_map/ppermute | solution.py:571
  80.9 5.3 %collective-permute-start.28 = (f32[8,128]{1,0:T(8,128)S(1)}, f32[8,128]{1,0:T(8,128)S(1)}, u32[]{:S(2)}, u32[]{:S(2)}) collective-permute-start(f32[8,128]{1,0:T(8,128)S(1)} %add_add_fusion.2), channel_id=1, source_target_pairs={{0,4},{1,5},{2,6},{3,7},{4,8},{5,9},{6,10},{7,11},{8,12},{9,13},{1... | collective-permute-start | bytes 12296 | tf_op jit(solution)/shard_map/ppermute | solution.py:571
  81.0 12.5 %collective-permute-start.29 = (f32[8,128]{1,0:T(8,128)S(1)}, f32[8,128]{1,0:T(8,128)S(1)}, u32[]{:S(2)}, u32[]{:S(2)}) collective-permute-start(f32[8,128]{1,0:T(8,128)S(1)} %add_add_fusion.2), channel_id=1, source_target_pairs={{0,12},{1,13},{2,14},{3,15},{4,0},{5,1},{6,2},{7,3},{8,4},{9,5},{1... | collective-permute-start | bytes 12296 | tf_op jit(solution)/shard_map/ppermute | solution.py:571
  84.2 9.3 %collective-permute-start.30 = (f32[8,128]{1,0:T(8,128)S(1)}, f32[8,128]{1,0:T(8,128)S(1)}, u32[]{:S(2)}, u32[]{:S(2)}) collective-permute-start(f32[8,128]{1,0:T(8,128)S(1)} %add_add_fusion.2), channel_id=1, source_target_pairs={{0,8},{1,9},{2,10},{3,11},{4,12},{5,13},{6,14},{7,15},{8,0},{9,1},... | collective-permute-start | bytes 12296 | tf_op jit(solution)/shard_map/ppermute | solution.py:571
  84.3 51.8 %collective-permute-start.34 = (bf16[36,128,128]{2,1,0:T(8,128)(2,1)S(1)}, bf16[36,128,128]{2,1,0:T(8,128)(2,1)S(1)}, u32[]{:S(2)}, u32[]{:S(2)}) collective-permute-start(bf16[36,128,128]{2,1,0:T(8,128)(2,1)S(1)} %pad_maximum_fusion.5), channel_id=1, source_target_pairs={{0,1},{1,2},{2,3},{3,4},{4,5},{5,6},{6,7},{7,8},{8,9},{9,10},{10,1... | collective-permute-start | bytes 3538952 | tf_op jit(solution)/shard_map/ppermute | solution.py:624
  86.2 49.9 %collective-permute-start.37 = (bf16[36,128,128]{2,1,0:T(8,128)(2,1)S(1)}, bf16[36,128,128]{2,1,0:T(8,128)(2,1)S(1)}, u32[]{:S(2)}, u32[]{:S(2)}) collective-permute-start(bf16[36,128,128]{2,1,0:T(8,128)(2,1)S(1)} %pad_maximum_fusion.6), channel_id=1, source_target_pairs={{0,15},{1,0},{2,1},{3,2},{4,3},{5,4},{6,5},{7,6},{8,7},{9,8},{10,9... | collective-permute-start | bytes 3538952 | tf_op jit(solution)/shard_map/ppermute | solution.py:624
  93.5 11.1 %collective-permute-start.31 = (f32[8,128]{1,0:T(8,128)S(1)}, f32[8,128]{1,0:T(8,128)S(1)}, u32[]{:S(2)}, u32[]{:S(2)}) collective-permute-start(f32[8,128]{1,0:T(8,128)S(1)} %add_add_fusion.1), channel_id=1, source_target_pairs={{0,1},{1,2},{2,3},{3,0},{4,5},{5,6},{6,7},{7,4},{8,9},{9,10},{10,1... | collective-permute-start | bytes 12296 | tf_op jit(solution)/shard_map/ppermute | solution.py:571
  93.6 20.7 %collective-permute-start.32 = (f32[8,128]{1,0:T(8,128)S(1)}, f32[8,128]{1,0:T(8,128)S(1)}, u32[]{:S(2)}, u32[]{:S(2)}) collective-permute-start(f32[8,128]{1,0:T(8,128)S(1)} %add_add_fusion.1), channel_id=1, source_target_pairs={{0,3},{1,0},{2,1},{3,2},{4,7},{5,4},{6,5},{7,6},{8,11},{9,8},{10,9... | collective-permute-start | bytes 12296 | tf_op jit(solution)/shard_map/ppermute | solution.py:571
  104.6 12.2 %collective-permute-start.33 = (f32[8,128]{1,0:T(8,128)S(1)}, f32[8,128]{1,0:T(8,128)S(1)}, u32[]{:S(2)}, u32[]{:S(2)}) collective-permute-start(f32[8,128]{1,0:T(8,128)S(1)} %add_add_fusion.1), channel_id=1, source_target_pairs={{0,2},{1,3},{2,0},{3,1},{4,6},{5,7},{6,4},{7,5},{8,10},{9,11},{10,... | collective-permute-start | bytes 12296 | tf_op jit(solution)/shard_map/ppermute | solution.py:571
  114.3 20.2 %collective-permute-start.35 = (bf16[32,128,128]{2,1,0:T(8,128)(2,1)}, bf16[32,128,128]{2,1,0:T(8,128)(2,1)S(1)}, u32[]{:S(2)}, u32[]{:S(2)}) collective-permute-start(bf16[32,128,128]{2,1,0:T(8,128)(2,1)} %collective-permute-done.17.lm), channel_id=1, source_target_pairs={{0,1},{1,2},{2,3},{3,4},{4,5},{5,6},{6,7},{7,8},{8,9},{9,10},{10,1... | collective-permute-start | bytes 3145736 | tf_op jit(solution)/shard_map/ppermute | solution.py:633
  116.8 19.3 %collective-permute-start.38 = (bf16[32,128,128]{2,1,0:T(8,128)(2,1)}, bf16[32,128,128]{2,1,0:T(8,128)(2,1)S(1)}, u32[]{:S(2)}, u32[]{:S(2)}) collective-permute-start(bf16[32,128,128]{2,1,0:T(8,128)(2,1)} %collective-permute-done.19.rm), channel_id=1, source_target_pairs={{0,15},{1,0},{2,1},{3,2},{4,3},{5,4},{6,5},{7,6},{8,7},{9,8},{10,9... | collective-permute-start | bytes 3145736 | tf_op jit(solution)/shard_map/ppermute | solution.py:633
  123.6 10.8 %collective-permute-start.39 = (bf16[20,128,128]{2,1,0:T(8,128)(2,1)S(1)}, bf16[20,128,128]{2,1,0:T(8,128)(2,1)S(1)}, u32[]{:S(2)}, u32[]{:S(2)}) collective-permute-start(bf16[20,128,128]{2,1,0:T(8,128)(2,1)S(1)} %pad_maximum_fusion.8), channel_id=1, source_target_pairs={{16,31},{17,16},{18,17},{19,18},{20,19},{21,20},{22,21},{23,22},{2... | collective-permute-start | bytes 1966088 | tf_op jit(solution)/shard_map/ppermute | solution.py:627

commit v6 on v4

--- a/solution.py
+++ b/solution.py
@@ -276,8 +276,8 @@
 WT = ROWS // WC
 
 
-def sums_kernel(idx_ref, area_ref, w_hbm, *refs):
-    left, right, own, wv, acc, sem = refs
+def sums_kernel(idx_ref, area_ref, lost_ref, w_hbm, *refs):
+    wv, left, right, own, acc, sem = refs
 
     def copy(c):
         rows = pl.ds(c * WT, WT)
@@ -312,36 +312,35 @@
     right[PAD:] = summed(2)
     own[:PAD] = summed(0)
     own[PAD : 2 * PAD] = summed(-3)
-    own[2 * PAD :] = summed(3)
-
-
-def sums_call(idx, area, weights):
+    own[2 * PAD : 3 * PAD] = summed(3)
+    own[3 * PAD :] = jnp.full((8, C), lost_ref[0])
+
+
+def sums_call(idx, area, lost, weights):
     smem = pl.BlockSpec(memory_space=pltpu.SMEM)
     vmem = pl.BlockSpec(memory_space=pltpu.VMEM)
     return pl.pallas_call(
         sums_kernel,
-        in_specs=[smem, smem, pl.BlockSpec(memory_space=pltpu.HBM)],
-        out_specs=[vmem] * 3,
-        out_shape=[jax.ShapeDtypeStruct((n * PAD, C), jnp.float32) for n in (2, 2, 3)],
+        in_specs=[smem, smem, smem, pl.BlockSpec(memory_space=pltpu.HBM)],
+        out_specs=[vmem] * 4,
+        out_shape=[pltpu.VMEM(weights.shape, weights.dtype)]
+        + [jax.ShapeDtypeStruct((n, C), jnp.float32) for n in (2 * PAD, 2 * PAD, 3 * PAD + 8)],
         scratch_shapes=[
-            pltpu.VMEM(weights.shape, weights.dtype),
             pltpu.VMEM((SECT + 1, 8, C), jnp.float32),
             pltpu.SemaphoreType.DMA((WC,)),
         ],
-        compiler_params=pltpu.CompilerParams(vmem_limit_bytes=22 << 20),
+        compiler_params=pltpu.CompilerParams(vmem_limit_bytes=6 << 20),
         cost_estimate=pl.CostEstimate(
             flops=20_000_000, bytes_accessed=17 << 20, transcendentals=0
         ),
         name="sums",
-    )(idx, area, pltpu.with_memory_space_constraint(weights, pltpu.HBM))
-
-
-def split_kernel(q_hbm, qs, qm, sem):
+    )(idx, area, lost, pltpu.with_memory_space_constraint(weights, pltpu.HBM))
+
+
+def rows_kernel(ranges, q_hbm, out, sem):
     copies = [
-        pltpu.make_async_copy(q_hbm.at[pl.ds(at, n)], ref.at[pl.ds(to, n)], sem.at[i])
-        for i, (at, n, ref, to) in enumerate(
-            ((0, EDGE, qs, 0), (ROWS - EDGE, EDGE, qs, EDGE), (EDGE, M, qm, 0))
-        )
+        pltpu.make_async_copy(q_hbm.at[pl.ds(at, n)], out.at[pl.ds(to, n)], sem.at[i])
+        for i, (at, n, to) in enumerate(ranges)
     ]
     for copy in copies:
         copy.start()
@@ -349,17 +348,16 @@
         copy.wait()
 
 
-def split_call(q):
-    vmem = pl.BlockSpec(memory_space=pltpu.VMEM)
-    return pl.pallas_call(
-        split_kernel,
+def rows_call(ranges, q):
+    count = sum(n for _, n, _ in ranges)
+    return pl.pallas_call(
+        functools.partial(rows_kernel, ranges),
         in_specs=[pl.BlockSpec(memory_space=pltpu.HBM)],
-        out_specs=[vmem, vmem],
-        out_shape=[pltpu.VMEM((n, C, C), jnp.bfloat16) for n in (S, M)],
-        scratch_shapes=[pltpu.SemaphoreType.DMA((3,))],
+        out_specs=pl.BlockSpec(memory_space=pltpu.VMEM),
+        out_shape=pltpu.VMEM((count, C, C), jnp.bfloat16),
+        scratch_shapes=[pltpu.SemaphoreType.DMA((len(ranges),))],
         compiler_params=pltpu.CompilerParams(vmem_limit_bytes=1 << 20),
-        cost_estimate=pl.CostEstimate(flops=1000, bytes_accessed=2 << 20, transcendentals=0),
-        name="split",
+        cost_estimate=pl.CostEstimate(flops=1000, bytes_accessed=1 << 20, transcendentals=0),
     )(pltpu.with_memory_space_constraint(q, pltpu.HBM))
 
 
@@ -382,13 +380,7 @@
     )(*parts)
 
 
-def mass_kernel(area_ref, lost_ref, at_ref, w_hbm, c0, cl, cr, qs, qm, ls, lm, rs, rm, up, dn, l3, r3, out_ref, src, wv, by, sem):
-    def copy(c):
-        rows = pl.ds(c * WT, WT)
-        return pltpu.make_async_copy(w_hbm.at[rows], wv.at[rows], sem.at[c])
-
-    for c in range(WC):
-        copy(c).start()
+def mass_kernel(area_ref, at_ref, c0, cl, cr, qs, qm, ls, lm, rs, rm, up, dn, l3, r3, out_ref, src, by):
     for n, (e, m) in enumerate(((qs, qm), (ls, lm), (rs, rm))):
         at = n * PAD + R
         src[pl.ds(at, EDGE)] = e[:EDGE]
@@ -407,7 +399,7 @@
     def body(p, acc):
         return acc + by[pl.ds(p, 1)] * src[p].astype(jnp.float32)
 
-    acc = lax.fori_loop(0, 3 * PAD, body, jnp.zeros((C, C), jnp.float32), unroll=4)
+    acc = lax.fori_loop(0, 3 * PAD, body, jnp.zeros((C, C), jnp.float32), unroll=8)
     at = at_ref[0]
     for i in range(E):
         acc = acc + c0[pl.ds(PAD + at + i, 1)] * l3[i].astype(jnp.float32)
@@ -417,33 +409,29 @@
         precision=lax.Precision.HIGHEST, preferred_element_type=jnp.float32,
     )
     row = lax.broadcasted_iota(jnp.int32, (8, C), 0)
-    out_ref[...] = jnp.where(row == 0, change, lost_ref[0])
-    for c in range(WC):
-        copy(c).wait()
-
-
-def mass_call(area, lost, at, weights, parts):
+    out_ref[...] = jnp.where(row == 0, change, c0[3 * PAD :])
+
+
+def mass_call(area, at, parts):
     smem = pl.BlockSpec(memory_space=pltpu.SMEM)
     vmem = pl.BlockSpec(memory_space=pltpu.VMEM)
     return pl.pallas_call(
         mass_kernel,
-        in_specs=[smem] * 3 + [pl.BlockSpec(memory_space=pltpu.HBM)] + [vmem] * len(parts),
-        out_specs=[vmem] * 3,
+        in_specs=[smem] * 2 + [vmem] * len(parts),
+        out_specs=[vmem] * 2,
         out_shape=[
             jax.ShapeDtypeStruct((8, C), jnp.float32),
             pltpu.VMEM((3 * PAD + 1, C, C), jnp.bfloat16),
-            pltpu.VMEM(weights.shape, weights.dtype),
         ],
         scratch_shapes=[
             pltpu.VMEM((3 * PAD, C), jnp.float32),
-            pltpu.SemaphoreType.DMA((WC,)),
         ],
         compiler_params=pltpu.CompilerParams(vmem_limit_bytes=6 << 20),
         cost_estimate=pl.CostEstimate(
             flops=9_000_000, bytes_accessed=3 << 20, transcendentals=0
         ),
         name="mass",
-    )(area, lost, at, pltpu.with_memory_space_constraint(weights, pltpu.HBM), *parts)
+    )(area, at, *parts)
 
 
 def inner_kernel(first, idx_ref, wv, src, out_ref):
@@ -454,7 +442,7 @@
         out_ref[j] = lax.dot_general(lhs, rhs, NT, preferred_element_type=jnp.float32)
         return carry
 
-    lax.fori_loop(0, PER, body, 0, unroll=4)
+    lax.fori_loop(0, PER, body, 0, unroll=8)
 
 
 def inner_call(chunk, idx, wv, near):
@@ -474,18 +462,18 @@
 HALF = CHUNKS // 2
 
 
-def far_part(first, idx_ref, wv, src, partial, out_ref):
+def far_part(half, idx_ref, wv, src, partial, out_ref):
     for c in range(HALF):
 
         def body(j, carry):
-            t = first + c * PER + j
+            t = (half * HALF + c) * PER + j
             lhs = jnp.concatenate([src[idx_ref[k, t]] for k in range(KMAX)], axis=1)
             rhs = jnp.concatenate([wv[t, k] for k in range(KMAX)], axis=1)
             got = lax.dot_general(lhs, rhs, NT, preferred_element_type=jnp.float32)
             out_ref[c * PER + j] = got + partial[c][j]
             return carry
 
-        lax.fori_loop(0, PER, body, 0, unroll=4)
+        lax.fori_loop(0, PER, body, 0, unroll=8)
 
 
 def outer0_kernel(idx_ref, wv, ls, lm, lb, rs, rm, rb, l3, r3, *refs):
@@ -502,7 +490,7 @@
 
 
 def outer1_kernel(idx_ref, wv, src, *refs):
-    far_part(HALF * PER, idx_ref, wv, src, refs[:HALF], refs[HALF])
+    far_part(1, idx_ref, wv, src, refs[:HALF], refs[HALF])
 
 
 def outer_call(half, idx, wv, parts, partial):
@@ -594,6 +582,11 @@
     return lax.ppermute(v, axis, [(i, to(i)) for i in range(size)])
 
 
+def three(v, axis, size, to):
+    got = [swap(v, axis, size, functools.partial(to, by=by)) for by in (1, 2, 3)]
+    return (got[0] + got[2]) + got[1]
+
+
 def local(tracers, weights, source_row, source_block, slot_count):
     args = (tracers, weights, source_row, source_block, slot_count)
     lost, fixed = usual(*args)
@@ -610,7 +603,8 @@
     both = ("lat", "lon")
     w = weights[:, 0]
     q = tracers.transpose(0, 2, 3, 1).reshape(ROWS, C, C)
-    qs, qm = split_call(q)
+    qs = rows_call(((0, EDGE, 0), (ROWS - EDGE, EDGE, EDGE)), q)
+    qm = rows_call(((EDGE, M, 0),), q)
     ls, rs = lax.ppermute(qs, "lon", ring(1)), lax.ppermute(qs, "lon", ring(-1))
     lm, rm = lax.ppermute(qm, "lon", ring(1)), lax.ppermute(qm, "lon", ring(-1))
     pole = jnp.where(lat == 0, qs[:E], qs[S - E :])
@@ -618,25 +612,25 @@
     r3 = lax.ppermute(pole, both, some(-3, POLAR))
     sums_idx, near_idx, far_idx, lost = tables(source_row, source_block, slot_count, lat, lon)
     area = latitude_area(lat * ROWS, ROWS)
-    to_left, to_right, own_sums = sums_call(sums_idx, area, w)
+    wv, to_left, to_right, own_sums = sums_call(sums_idx, area, lost.reshape(1), w)
     cl = lax.ppermute(to_left, "lon", ring(-1))
     cr = lax.ppermute(to_right, "lon", ring(1))
     first, last = pack_call((qs, ls, rs))
     up1, dn1 = lax.ppermute(first, "lat", UP), lax.ppermute(last, "lat", DOWN)
     at = jnp.where(jnp.arange(NLAT_DEV, dtype=jnp.int32) == lat, R, R + ROWS - E).astype(jnp.int32)
-    v, near, wv = mass_call(
-        area, lost.reshape(1), at, w,
+    v, near = mass_call(
+        area, at,
         (own_sums, cl, cr, qs, qm, ls, lm, rs, rm, up1, dn1, l3, r3),
     )
     held = lambda x: pltpu.with_memory_space_constraint(x, pltpu.VMEM)
     near, wv = held(near), held(wv)
-    for axis, size, bit in (("lat", NLAT_DEV, 1), ("lat", NLAT_DEV, 2), ("lat", NLAT_DEV, 4), ("lon", NLON_DEV, 4), ("lon", NLON_DEV, 8)):
-        v = v + swap(v, axis, size, lambda i, bit=bit: i ^ bit)
-    y = [swap(v, "lon", NLON_DEV, lambda i, by=by: i // 4 * 4 + (i + by) % 4) for by in (1, 2, 3)]
-    v = v + (y[0] + y[2]) + y[1]
+    v = v + swap(v, "lat", NLAT_DEV, lambda i: i ^ 1)
+    v = v + three(v, "lat", NLAT_DEV, lambda i, by: (i + 2 * by) % NLAT_DEV)
+    v = v + three(v, "lon", NLON_DEV, lambda i, by: (i + 4 * by) % NLON_DEV)
+    v = v + three(v, "lon", NLON_DEV, lambda i, by: i // 4 * 4 + (i + by) % 4)
     corr = jnp.broadcast_to((v[0] * (1.0 / TOTAL_AREA))[:, None], (C, C))
 
-    beyond = jnp.where((lat == 0) | (lat == NLAT_DEV - 2), dn1[R:], up1[R:])
+    beyond = jnp.where(lat == 0, dn1[R:], jnp.where(lat == NLAT_DEV - 2, dn1[R:], up1[R:]))
     sides = ((ls, beyond[:R], 1), (rs, beyond[R:], -1))
     lls, rrs = (
         lax.ppermute(jnp.concatenate([x, h], axis=0), both, some(d, POLAR)) for x, h, d in sides

time: 144 us -> 154 us (1.069)
  waiting for transfers between devices: 49.1 us -> 70 us
  Pallas kernels: 39.4 us -> 33 us
  starting transfers between devices: 50.4 us -> 47.9 us
  other arithmetic: 2.93 us -> 1.23 us
    ppermute x8 -> x10, waiting for transfers between devices: 21 us -> 40.8 us  [swap(): return lax.ppermute(v, axis, [(i, to(i)) for i in range(size)])]
    ppermute x1, waiting for transfers between devices: 0.01 us -> 16.6 us  [usual(): cl = lax.ppermute(to_left, 'lon', ring(-1))]
    ppermute x1, waiting for transfers between devices: 17.8 us -> 5.78 us  [usual(): lax.ppermute(qs, 'lon', ring(1))]
    ppermute x1, waiting for transfers between devices: 7.59 us -> 2.74 us  [usual(): cr = lax.ppermute(to_right, 'lon', ring(1))]
    ppermute x1, starting transfers between devices: 6.03 us -> 1.91 us  [usual(): r3 = lax.ppermute(pole, both, some(-3, POLAR))]
    pallas_call x3 -> x4, Pallas kernels: 18.4 us -> 15.4 us  [the longest x1 7.78 us: sums_call(): pl.pallas_call(sums_kernel, in_specs=[smem, smem, smem, pl.BlockSpec(memo...]
    ppermute x2, waiting for transfers between devices: 2.62 us -> 0.01 us  [usual(): lax.ppermute(x, both, some(d, POLAR))]
    ppermute x1, waiting for transfers between devices: 0.01 us -> 2.03 us  [usual(): l3 = lax.ppermute(pole, both, some(3, POLAR))]
  transfers between devices with their start and end apart: 24 -> 26, of which waited for: 11 -> 13; matrix products, arithmetic and copies ran while one was open for 2% -> 1% of each run, Pallas kernels for 18% -> 14%
where the time goes in v6:
time: 154 us
  waiting for transfers between devices  70 us (45%)
  starting transfers between devices  47.9 us (31%)
  Pallas kernels  33 us (21%)
    ppermute x10, waiting for transfers between devices, swap(): return lax.ppermute(v, axis, [(i, to(i)) for i in range(size)])  40.8 us
    ppermute x1, waiting for transfers between devices, usual(): cl = lax.ppermute(to_left, 'lon', ring(-1))  16.6 us
    ppermute x2, starting transfers between devices, usual(): lax.ppermute(jnp.concatenate([x, h], axis=0), both, some(d, POLAR))  8.2 us
    pallas_call x4, Pallas kernels, inner_call(): pl.pallas_call(functools.partial(inner_kernel, chunk * PER), in_specs=[pl...  8.1 us
    pallas_call x1, Pallas kernels, sums_call(): pl.pallas_call(sums_kernel, in_specs=[smem, smem, smem, pl.BlockSpec(memo...  7.78 us
    pallas_call x2, Pallas kernels, outer_call(): pl.pallas_call((outer0_kernel, outer1_kernel)[half], in_specs=[pl.BlockSp...  7.36 us
    ppermute x2, starting transfers between devices, usual(): lax.ppermute(x, both, some(d, POLAR))  7.2 us
    ppermute x10, starting transfers between devices, swap(): return lax.ppermute(v, axis, [(i, to(i)) for i in range(size)])  7.04 us
  transfers between devices with their start and end apart: 26, of which 13 were waited for; matrix products, arithmetic and copies ran while one was open for 1% of the time, Pallas kernels for 14%

profile of v6, /device:TPU:0, one launch (start us, length us, event | category | flops | bytes accessed | tf_op | source)
XLA Modules:
  0.0 154.0 jit_solution(14131738016342237587)
XLA Ops:
  0.0 1.2 shard_map.55.qs
  1.3 6.7 %collective-permute-start.18 = (bf16[32,128,128]{2,1,0:T(8,128)(2,1)S(1)}, bf16[32,128,128]{2,1,0:T(8,128)(2,1)S(1)}, u32[]{:S(2)}, u32[]{:S(2)}) collective-permute-start(bf16[32,128,128]{2,1,0:T(8,128)(2,1)S(1)} %shard_map.55.qs), channel_id=1, source_target_pairs={{0,15},{1,0},{2,1},{3,2},{4,3},{5,4},{6,5},{7,6},{8,7},{9,8},{10,9... | collective-permute-start | bytes 3145736 | tf_op jit(solution)/shard_map/ppermute | solution.py:608
  7.9 2.2 %shard_map.56.qm = bf16[32,128,128]{2,1,0:T(8,128)(2,1)} custom-call(bf16[64,128,128]{2,1,0:T(8,128)(2,1)} %bitcast.156), custom_call_target="tpu_custom_call" | custom-call | flops 1000 | bytes 1048576 | tf_op jit(solution)/shard_map/pallas_call | solution.py:353
  10.1 5.4 %collective-permute-start.19 = (bf16[32,128,128]{2,1,0:T(8,128)(2,1)}, bf16[32,128,128]{2,1,0:T(8,128)(2,1)}, u32[]{:S(2)}, u32[]{:S(2)}) collective-permute-start(bf16[32,128,128]{2,1,0:T(8,128)(2,1)} %shard_map.56.qm), channel_id=1, source_target_pairs={{0,15},{1,0},{2,1},{3,2},{4,3},{5,4},{6,5},{7,6},{8,7},{9,8},{10,9... | collective-permute-start | bytes 3145736 | tf_op jit(solution)/shard_map/ppermute | solution.py:609
  15.6 0.6 convert_reduce_fusion.1
  16.3 7.8 %sums.1 = (bf16[64,8,128,128]{3,2,1,0:T(8,128)(2,1)S(1)}, f32[144,128]{1,0:T(8,128)S(1)}, f32[144,128]{1,0:T(8,128)S(1)}, f32[224,128]{1,0:T(8,128)S(1)}) custom-call(s32[8,64]{1,0:T(8,128)S(1)} %get-tuple-element.112.idx_ref, f32[64]{0:T(128)S(1)} %add_cosine_fusion.1.area_ref, f32[1]{0:T(128)} %bitcast.25.lost_ref, bf16[64,8,128,128]{3,2,1,0:T(8,128)(2,1)} %bitcast.151), custom_call_target="tpu_custom_call" | custom-call | flops 20000000 | bytes 17825792 | tf_op jit(solution)/shard_map/sums/pallas_call | solution.py:322
  24.1 5.4 %collective-permute-start.14 = (f32[144,128]{1,0:T(8,128)S(1)}, f32[144,128]{1,0:T(8,128)S(1)}, u32[]{:S(2)}, u32[]{:S(2)}) collective-permute-start(f32[144,128]{1,0:T(8,128)S(1)} %get-tuple-element.55), channel_id=1, source_target_pairs={{0,15},{1,0},{2,1},{3,2},{4,3},{5,4},{6,5},{7,6},{8,7},{9,8},{10,9... | collective-permute-start | bytes 221192 | tf_op jit(solution)/shard_map/ppermute | solution.py:616
  29.5 2.0 %collective-permute-done.18.rs = bf16[32,128,128]{2,1,0:T(8,128)(2,1)S(1)} collective-permute-done((bf16[32,128,128]{2,1,0:T(8,128)(2,1)S(1)}, bf16[32,128,128]{2,1,0:T(8,128)(2,1)S(1)}, u32[]{:S(2)}, u32[]{:S(2)}) %collective-permute-start.18) | collective-permute-done | bytes 1048608 | tf_op jit(solution)/shard_map/ppermute | solution.py:608
  31.5 5.8 %collective-permute-done.16.ls = bf16[32,128,128]{2,1,0:T(8,128)(2,1)S(1)} collective-permute-done((bf16[32,128,128]{2,1,0:T(8,128)(2,1)S(1)}, bf16[32,128,128]{2,1,0:T(8,128)(2,1)S(1)}, u32[]{:S(2)}, u32[]{:S(2)}) %collective-permute-start.16) | collective-permute-done | bytes 1048608 | tf_op jit(solution)/shard_map/ppermute | solution.py:608
  37.3 1.9 %collective-permute-start.23 = (bf16[5,128,128]{2,1,0:T(8,128)(2,1)S(1)}, bf16[5,128,128]{2,1,0:T(8,128)(2,1)S(1)}, u32[]{:S(2)}, u32[]{:S(2)}) collective-permute-start(bf16[5,128,128]{2,1,0:T(8,128)(2,1)S(1)} %slice_select_fusion.4), channel_id=1, source_target_pairs={{0,13},{1,14},{2,15},{3,0},{4,1},{5,2},{6,3},{7,4},{8,5},{9,6},{10... | collective-permute-start | bytes 491528 | tf_op jit(solution)/shard_map/ppermute | solution.py:612
  39.3 16.6 %collective-permute-done.14.cl = f32[144,128]{1,0:T(8,128)S(1)} collective-permute-done((f32[144,128]{1,0:T(8,128)S(1)}, f32[144,128]{1,0:T(8,128)S(1)}, u32[]{:S(2)}, u32[]{:S(2)}) %collective-permute-start.14) | collective-permute-done | bytes 73760 | tf_op jit(solution)/shard_map/ppermute | solution.py:616
  55.9 1.3 collective-permute-start.20
  57.2 2.7 %collective-permute-done.15.cr = f32[144,128]{1,0:T(8,128)S(1)} collective-permute-done((f32[144,128]{1,0:T(8,128)S(1)}, f32[144,128]{1,0:T(8,128)S(1)}, u32[]{:S(2)}, u32[]{:S(2)}) %collective-permute-start.15) | collective-permute-done | bytes 73760 | tf_op jit(solution)/shard_map/ppermute | solution.py:617
  59.9 1.3 collective-permute-start.21
  61.2 1.9 %collective-permute-start.22 = (bf16[5,128,128]{2,1,0:T(8,128)(2,1)S(1)}, bf16[5,128,128]{2,1,0:T(8,128)(2,1)S(1)}, u32[]{:S(2)}, u32[]{:S(2)}) collective-permute-start(bf16[5,128,128]{2,1,0:T(8,128)(2,1)S(1)} %slice_select_fusion.4), channel_id=1, source_target_pairs={{0,3},{1,4},{2,5},{3,6},{4,7},{5,8},{6,9},{7,10},{8,11},{9,12},{10... | collective-permute-start | bytes 491528 | tf_op jit(solution)/shard_map/ppermute | solution.py:611
  63.2 5.3 %collective-permute-start.38 = (bf16[32,128,128]{2,1,0:T(8,128)(2,1)}, bf16[32,128,128]{2,1,0:T(8,128)(2,1)S(1)}, u32[]{:S(2)}, u32[]{:S(2)}) collective-permute-start(bf16[32,128,128]{2,1,0:T(8,128)(2,1)} %collective-permute-done.19.rm), channel_id=1, source_target_pairs={{0,15},{1,0},{2,1},{3,2},{4,3},{5,4},{6,5},{7,6},{8,7},{9,8},{10,9... | collective-permute-start | bytes 3145736 | tf_op jit(solution)/shard_map/ppermute | solution.py:645
  68.5 2.0 %collective-permute-done.22.l3 = bf16[5,128,128]{2,1,0:T(8,128)(2,1)S(1)} collective-permute-done((bf16[5,128,128]{2,1,0:T(8,128)(2,1)S(1)}, bf16[5,128,128]{2,1,0:T(8,128)(2,1)S(1)}, u32[]{:S(2)}, u32[]{:S(2)}) %collective-permute-start.22) | collective-permute-done | bytes 163872 | tf_op jit(solution)/shard_map/ppermute | solution.py:611
  70.6 4.2 %mass.1 = (f32[8,128]{1,0:T(8,128)S(1)}, bf16[217,128,128]{2,1,0:T(8,128)(2,1)S(1)}) custom-call(f32[64]{0:T(128)S(1)} %add_cosine_fusion.1.area_ref, s32[8]{0:T(128)S(1)} %compare_select_fusion.1.at_ref, f32[224,128]{1,0:T(8,128)S(1)} %get-tuple-element.54.c0, f32[144,128]{1,0:T(8,128)S(1)} %collective-permute-done.14.cl, ...), custom_call_target="tpu_custom_call" | custom-call | flops 9000000 | bytes 3145728 | tf_op jit(solution)/shard_map/mass/pallas_call | solution.py:418
  74.8 1.1 collective-permute-done.24
  76.0 2.1 %collective-permute-start.27 = (f32[8,128]{1,0:T(8,128)S(1)}, f32[8,128]{1,0:T(8,128)S(1)}, u32[]{:S(2)}, u32[]{:S(2)}) collective-permute-start(f32[8,128]{1,0:T(8,128)S(1)} %add.234), channel_id=1, source_target_pairs={{0,64},{16,80},{32,96},{48,112},{64,0},{80,16},{96,32},{112,48},{1... | collective-permute-start | bytes 12296 | tf_op jit(solution)/shard_map/ppermute | solution.py:582
  78.1 1.7 %collective-permute-start.26 = (f32[8,128]{1,0:T(8,128)S(1)}, f32[8,128]{1,0:T(8,128)S(1)}, u32[]{:S(2)}, u32[]{:S(2)}) collective-permute-start(f32[8,128]{1,0:T(8,128)S(1)} %add.234), channel_id=1, source_target_pairs={{0,96},{16,112},{32,0},{48,16},{64,32},{80,48},{96,64},{112,80},{1... | collective-permute-start | bytes 12296 | tf_op jit(solution)/shard_map/ppermute | solution.py:582
  79.8 0.9 collective-permute-start.25
  80.6 0.1 pad_maximum_fusion.5
  80.7 0.3 collective-permute-done.27
  81.1 1.2 collective-permute-done.26
  82.3 2.3 %collective-permute-done.25 = f32[8,128]{1,0:T(8,128)S(1)} collective-permute-done((f32[8,128]{1,0:T(8,128)S(1)}, f32[8,128]{1,0:T(8,128)S(1)}, u32[]{:S(2)}, u32[]{:S(2)}) %collective-permute-start.25) | collective-permute-done | bytes 4128 | tf_op jit(solution)/shard_map/ppermute | solution.py:582
  84.6 0.1 collective-permute-start.29
  84.7 2.0 %collective-permute-start.28 = (f32[8,128]{1,0:T(8,128)S(1)}, f32[8,128]{1,0:T(8,128)S(1)}, u32[]{:S(2)}, u32[]{:S(2)}) collective-permute-start(f32[8,128]{1,0:T(8,128)S(1)} %add_add_fusion.2), channel_id=1, source_target_pairs={{0,4},{1,5},{2,6},{3,7},{4,8},{5,9},{6,10},{7,11},{8,12},{9,13},{1... | collective-permute-start | bytes 12296 | tf_op jit(solution)/shard_map/ppermute | solution.py:582
  86.7 0.1 pad_maximum_fusion.6
  86.8 1.9 %collective-permute-start.35 = (bf16[32,128,128]{2,1,0:T(8,128)(2,1)}, bf16[32,128,128]{2,1,0:T(8,128)(2,1)S(1)}, u32[]{:S(2)}, u32[]{:S(2)}) collective-permute-start(bf16[32,128,128]{2,1,0:T(8,128)(2,1)} %collective-permute-done.17.lm), channel_id=1, source_target_pairs={{0,1},{1,2},{2,3},{3,4},{4,5},{5,6},{6,7},{7,8},{8,9},{9,10},{10,1... | collective-permute-start | bytes 3145736 | tf_op jit(solution)/shard_map/ppermute | solution.py:645
  88.7 1.0 collective-permute-done.30
  89.7 6.3 %collective-permute-start.37 = (bf16[36,128,128]{2,1,0:T(8,128)(2,1)S(1)}, bf16[36,128,128]{2,1,0:T(8,128)(2,1)S(1)}, u32[]{:S(2)}, u32[]{:S(2)}) collective-permute-start(bf16[36,128,128]{2,1,0:T(8,128)(2,1)S(1)} %pad_maximum_fusion.6), channel_id=1, source_target_pairs={{0,15},{1,0},{2,1},{3,2},{4,3},{5,4},{6,5},{7,6},{8,7},{9,8},{10,9... | collective-permute-start | bytes 3538952 | tf_op jit(solution)/shard_map/ppermute | solution.py:636
  96.0 1.9 %collective-permute-start.34 = (bf16[36,128,128]{2,1,0:T(8,128)(2,1)S(1)}, bf16[36,128,128]{2,1,0:T(8,128)(2,1)S(1)}, u32[]{:S(2)}, u32[]{:S(2)}) collective-permute-start(bf16[36,128,128]{2,1,0:T(8,128)(2,1)S(1)} %pad_maximum_fusion.5), channel_id=1, source_target_pairs={{0,1},{1,2},{2,3},{3,4},{4,5},{5,6},{6,7},{7,8},{8,9},{9,10},{10,1... | collective-permute-start | bytes 3538952 | tf_op jit(solution)/shard_map/ppermute | solution.py:636
  98.0 0.3 collective-permute-start.33
  98.3 26.6 %collective-permute-done.33 = f32[8,128]{1,0:T(8,128)S(1)} collective-permute-done((f32[8,128]{1,0:T(8,128)S(1)}, f32[8,128]{1,0:T(8,128)S(1)}, u32[]{:S(2)}, u32[]{:S(2)}) %collective-permute-start.33) | collective-permute-done | bytes 4128 | tf_op jit(solution)/shard_map/ppermute | solution.py:582
  125.0 3.5 %collective-permute-done.32 = f32[8,128]{1,0:T(8,128)S(1)} collective-permute-done((f32[8,128]{1,0:T(8,128)S(1)}, f32[8,128]{1,0:T(8,128)S(1)}, u32[]{:S(2)}, u32[]{:S(2)}) %collective-permute-start.32) | collective-permute-done | bytes 4128 | tf_op jit(solution)/shard_map/ppermute | solution.py:582
  128.6 4.8 %collective-permute-done.31 = f32[8,128]{1,0:T(8,128)S(1)} collective-permute-done((f32[8,128]{1,0:T(8,128)S(1)}, f32[8,128]{1,0:T(8,128)S(1)}, u32[]{:S(2)}, u32[]{:S(2)}) %collective-permute-start.31) | collective-permute-done | bytes 4128 | tf_op jit(solution)/shard_map/ppermute | solution.py:582
  133.3 0.7 collective-permute-start.36
  134.0 0.9 collective-permute-start.39
  134.9 2.0 %shard_map.61.refs_1_ = f32[16,128,128]{2,1,0:T(8,128)S(1)} custom-call(s32[8,64]{1,0:T(8,128)S(1)} %get-tuple-element.110.idx_ref, bf16[64,8,128,128]{3,2,1,0:T(8,128)(2,1)S(1)} %get-tuple-element.60.wv, bf16[217,128,128]{2,1,0:T(8,128)(2,1)S(1)} %get-tuple-element.61.src), custom_call_target="tpu_custom_call" | custom-call | flops 536870912 | bytes 1048576 | tf_op jit(solution)/shard_map/pallas_call | solution.py:450
  137.0 2.0 %shard_map.60.refs_0_ = f32[16,128,128]{2,1,0:T(8,128)S(1)} custom-call(s32[8,64]{1,0:T(8,128)S(1)} %get-tuple-element.110.idx_ref, bf16[64,8,128,128]{3,2,1,0:T(8,128)(2,1)S(1)} %get-tuple-element.60.wv, bf16[217,128,128]{2,1,0:T(8,128)(2,1)S(1)} %get-tuple-element.61.src), custom_call_target="tpu_custom_call" | custom-call | flops 536870912 | bytes 1048576 | tf_op jit(solution)/shard_map/pallas_call | solution.py:450
  139.0 2.0 %shard_map.58.refs_1_ = f32[16,128,128]{2,1,0:T(8,128)S(1)} custom-call(s32[8,64]{1,0:T(8,128)S(1)} %get-tuple-element.110.idx_ref, bf16[64,8,128,128]{3,2,1,0:T(8,128)(2,1)S(1)} %get-tuple-element.60.wv, bf16[217,128,128]{2,1,0:T(8,128)(2,1)S(1)} %get-tuple-element.61.src), custom_call_target="tpu_custom_call" | custom-call | flops 536870912 | bytes 1048576 | tf_op jit(solution)/shard_map/pallas_call | solution.py:450
  141.0 2.0 %shard_map.57.refs_0_ = f32[16,128,128]{2,1,0:T(8,128)S(1)} custom-call(s32[8,64]{1,0:T(8,128)S(1)} %get-tuple-element.110.idx_ref, bf16[64,8,128,128]{3,2,1,0:T(8,128)(2,1)S(1)} %get-tuple-element.60.wv, bf16[217,128,128]{2,1,0:T(8,128)(2,1)S(1)} %get-tuple-element.61.src), custom_call_target="tpu_custom_call" | custom-call | flops 536870912 | bytes 1048576 | tf_op jit(solution)/shard_map/pallas_call | solution.py:450
  143.1 0.5 slice.110
  143.6 3.9 %shard_map.59 = (f32[32,128,128]{2,1,0:T(8,128)S(1)}, bf16[187,128,128]{2,1,0:T(8,128)(2,1)S(1)}) custom-call(s32[8,64]{1,0:T(8,128)S(1)} %get-tuple-element.111.idx_ref, bf16[64,8,128,128]{3,2,1,0:T(8,128)(2,1)S(1)} %get-tuple-element.60.wv, bf16[36,128,128]{2,1,0:T(8,128)(2,1)S(1)} %collective-permute-done.34.ls, ...), custom_call_target="tpu_custom_call" | custom-call | flops 1073741824 | bytes 1048576 | tf_op jit(solution)/shard_map/pallas_call | solution.py:501
  147.5 3.5 %shard_map.62.b_ref = f32[32,128,128]{2,1,0:T(8,128)S(1)} custom-call(s32[8,64]{1,0:T(8,128)S(1)} %get-tuple-element.111.idx_ref, bf16[64,8,128,128]{3,2,1,0:T(8,128)(2,1)S(1)} %get-tuple-element.60.wv, bf16[187,128,128]{2,1,0:T(8,128)(2,1)S(1)} %get-tuple-element.63.src, f32[16,128,128]{2,1,0:T(8,128)S(1)} %shard_map.60.refs_0_, ...), custom_call_target="tpu_custom_call" | custom-call | flops 1073741824 | bytes 1048576 | tf_op jit(solution)/shard_map/pallas_call | solution.py:501
  151.1 2.1 %write.1 = f32[64,128,128]{2,1,0:T(8,128)} custom-call(f32[128,128]{1,0:T(8,128)S(1)} %broadcast_in_dim.44.corr_ref, f32[32,128,128]{2,1,0:T(8,128)S(1)} %get-tuple-element.62.a_ref, f32[32,128,128]{2,1,0:T(8,128)S(1)} %shard_map.62.b_ref), custom_call_target="tpu_custom_call" | custom-call | flops 1000000 | bytes 4194304 | tf_op jit(solution)/shard_map/write/pallas_call | solution.py:536
  153.2 0.6 while.9
  (43 shorter events, 0.6 us)
Async XLA Ops:
  1.2 14.4 %copy-start.2 = (s32[64,1,8]{0,2,1:T(8,128)S(1)}, s32[64,1,8]{0,2,1:T(8,128)}, u32[]{:S(2)}) copy-start(s32[64,1,8]{0,2,1:T(8,128)} %param.9) | copy-start | bytes 6148
  1.2 14.4 %copy-start.4 = (s32[64,1,8]{0,2,1:T(8,128)S(1)}, s32[64,1,8]{0,2,1:T(8,128)}, u32[]{:S(2)}) copy-start(s32[64,1,8]{0,2,1:T(8,128)} %param.10) | copy-start | bytes 6148
  1.2 14.4 %copy-start.6 = (s32[64,1]{0,1:T(1,128)S(1)}, s32[64,1]{0,1:T(1,128)}, u32[]{:S(2)}) copy-start(s32[64,1]{0,1:T(1,128)} %param.11) | copy-start | bytes 772
  1.3 30.2 %collective-permute-start.18 = (bf16[32,128,128]{2,1,0:T(8,128)(2,1)S(1)}, bf16[32,128,128]{2,1,0:T(8,128)(2,1)S(1)}, u32[]{:S(2)}, u32[]{:S(2)}) collective-permute-start(bf16[32,128,128]{2,1,0:T(8,128)(2,1)S(1)} %shard_map.55.qs), channel_id=1, source_target_pairs={{0,15},{1,0},{2,1},{3,2},{4,3},{5,4},{6,5},{7,6},{8,7},{9,8},{10,9... | collective-permute-start | bytes 3145736 | tf_op jit(solution)/shard_map/ppermute | solution.py:608
  7.9 29.3 %collective-permute-start.16 = (bf16[32,128,128]{2,1,0:T(8,128)(2,1)S(1)}, bf16[32,128,128]{2,1,0:T(8,128)(2,1)S(1)}, u32[]{:S(2)}, u32[]{:S(2)}) collective-permute-start(bf16[32,128,128]{2,1,0:T(8,128)(2,1)S(1)} %shard_map.55.qs), channel_id=1, source_target_pairs={{0,1},{1,2},{2,3},{3,4},{4,5},{5,6},{6,7},{7,8},{8,9},{9,10},{10,1... | collective-permute-start | bytes 3145736 | tf_op jit(solution)/shard_map/ppermute | solution.py:608
  10.1 53.1 %collective-permute-start.19 = (bf16[32,128,128]{2,1,0:T(8,128)(2,1)}, bf16[32,128,128]{2,1,0:T(8,128)(2,1)}, u32[]{:S(2)}, u32[]{:S(2)}) collective-permute-start(bf16[32,128,128]{2,1,0:T(8,128)(2,1)} %shard_map.56.qm), channel_id=1, source_target_pairs={{0,15},{1,0},{2,1},{3,2},{4,3},{5,4},{6,5},{7,6},{8,7},{9,8},{10,9... | collective-permute-start | bytes 3145736 | tf_op jit(solution)/shard_map/ppermute | solution.py:609
  15.6 55.0 %collective-permute-start.17 = (bf16[32,128,128]{2,1,0:T(8,128)(2,1)}, bf16[32,128,128]{2,1,0:T(8,128)(2,1)}, u32[]{:S(2)}, u32[]{:S(2)}) collective-permute-start(bf16[32,128,128]{2,1,0:T(8,128)(2,1)} %shard_map.56.qm), channel_id=1, source_target_pairs={{0,1},{1,2},{2,3},{3,4},{4,5},{5,6},{6,7},{7,8},{8,9},{9,10},{10,1... | collective-permute-start | bytes 3145736 | tf_op jit(solution)/shard_map/ppermute | solution.py:609
  24.1 31.8 %collective-permute-start.14 = (f32[144,128]{1,0:T(8,128)S(1)}, f32[144,128]{1,0:T(8,128)S(1)}, u32[]{:S(2)}, u32[]{:S(2)}) collective-permute-start(f32[144,128]{1,0:T(8,128)S(1)} %get-tuple-element.55), channel_id=1, source_target_pairs={{0,15},{1,0},{2,1},{3,2},{4,3},{5,4},{6,5},{7,6},{8,7},{9,8},{10,9... | collective-permute-start | bytes 221192 | tf_op jit(solution)/shard_map/ppermute | solution.py:616
  31.5 28.4 %collective-permute-start.15 = (f32[144,128]{1,0:T(8,128)S(1)}, f32[144,128]{1,0:T(8,128)S(1)}, u32[]{:S(2)}, u32[]{:S(2)}) collective-permute-start(f32[144,128]{1,0:T(8,128)S(1)} %get-tuple-element.56), channel_id=1, source_target_pairs={{0,1},{1,2},{2,3},{3,4},{4,5},{5,6},{6,7},{7,8},{8,9},{9,10},{10,1... | collective-permute-start | bytes 221192 | tf_op jit(solution)/shard_map/ppermute | solution.py:617
  37.3 23.9 %collective-permute-start.23 = (bf16[5,128,128]{2,1,0:T(8,128)(2,1)S(1)}, bf16[5,128,128]{2,1,0:T(8,128)(2,1)S(1)}, u32[]{:S(2)}, u32[]{:S(2)}) collective-permute-start(bf16[5,128,128]{2,1,0:T(8,128)(2,1)S(1)} %slice_select_fusion.4), channel_id=1, source_target_pairs={{0,13},{1,14},{2,15},{3,0},{4,1},{5,2},{6,3},{7,4},{8,5},{9,6},{10... | collective-permute-start | bytes 491528 | tf_op jit(solution)/shard_map/ppermute | solution.py:612
  55.9 14.7 %collective-permute-start.20 = (bf16[12,128,128]{2,1,0:T(8,128)(2,1)S(1)}, bf16[12,128,128]{2,1,0:T(8,128)(2,1)S(1)}, u32[]{:S(2)}, u32[]{:S(2)}) collective-permute-start(bf16[12,128,128]{2,1,0:T(8,128)(2,1)S(1)} %get-tuple-element.57), channel_id=1, source_target_pairs={{0,16},{16,32},{32,48},{48,64},{64,80},{80,96},{96,112},{1,17},{17... | collective-permute-start | bytes 1179656 | tf_op jit(solution)/shard_map/ppermute | solution.py:619
  59.9 10.6 %collective-permute-start.21 = (bf16[12,128,128]{2,1,0:T(8,128)(2,1)S(1)}, bf16[12,128,128]{2,1,0:T(8,128)(2,1)S(1)}, u32[]{:S(2)}, u32[]{:S(2)}) collective-permute-start(bf16[12,128,128]{2,1,0:T(8,128)(2,1)S(1)} %get-tuple-element.58), channel_id=1, source_target_pairs={{16,0},{32,16},{48,32},{64,48},{80,64},{96,80},{112,96},{17,1},{33... | collective-permute-start | bytes 1179656 | tf_op jit(solution)/shard_map/ppermute | solution.py:619
  61.2 9.3 %collective-permute-start.22 = (bf16[5,128,128]{2,1,0:T(8,128)(2,1)S(1)}, bf16[5,128,128]{2,1,0:T(8,128)(2,1)S(1)}, u32[]{:S(2)}, u32[]{:S(2)}) collective-permute-start(bf16[5,128,128]{2,1,0:T(8,128)(2,1)S(1)} %slice_select_fusion.4), channel_id=1, source_target_pairs={{0,3},{1,4},{2,5},{3,6},{4,7},{5,8},{6,9},{7,10},{8,11},{9,12},{10... | collective-permute-start | bytes 491528 | tf_op jit(solution)/shard_map/ppermute | solution.py:611
  63.2 70.8 %collective-permute-start.38 = (bf16[32,128,128]{2,1,0:T(8,128)(2,1)}, bf16[32,128,128]{2,1,0:T(8,128)(2,1)S(1)}, u32[]{:S(2)}, u32[]{:S(2)}) collective-permute-start(bf16[32,128,128]{2,1,0:T(8,128)(2,1)} %collective-permute-done.19.rm), channel_id=1, source_target_pairs={{0,15},{1,0},{2,1},{3,2},{4,3},{5,4},{6,5},{7,6},{8,7},{9,8},{10,9... | collective-permute-start | bytes 3145736 | tf_op jit(solution)/shard_map/ppermute | solution.py:645
  74.8 1.2 collective-permute-start.24
  76.0 5.1 %collective-permute-start.27 = (f32[8,128]{1,0:T(8,128)S(1)}, f32[8,128]{1,0:T(8,128)S(1)}, u32[]{:S(2)}, u32[]{:S(2)}) collective-permute-start(f32[8,128]{1,0:T(8,128)S(1)} %add.234), channel_id=1, source_target_pairs={{0,64},{16,80},{32,96},{48,112},{64,0},{80,16},{96,32},{112,48},{1... | collective-permute-start | bytes 12296 | tf_op jit(solution)/shard_map/ppermute | solution.py:582
  78.1 4.2 %collective-permute-start.26 = (f32[8,128]{1,0:T(8,128)S(1)}, f32[8,128]{1,0:T(8,128)S(1)}, u32[]{:S(2)}, u32[]{:S(2)}) collective-permute-start(f32[8,128]{1,0:T(8,128)S(1)} %add.234), channel_id=1, source_target_pairs={{0,96},{16,112},{32,0},{48,16},{64,32},{80,48},{96,64},{112,80},{1... | collective-permute-start | bytes 12296 | tf_op jit(solution)/shard_map/ppermute | solution.py:582
  79.8 4.8 %collective-permute-start.25 = (f32[8,128]{1,0:T(8,128)S(1)}, f32[8,128]{1,0:T(8,128)S(1)}, u32[]{:S(2)}, u32[]{:S(2)}) collective-permute-start(f32[8,128]{1,0:T(8,128)S(1)} %add.234), channel_id=1, source_target_pairs={{0,32},{16,48},{32,64},{48,80},{64,96},{80,112},{96,0},{112,16},{1... | collective-permute-start | bytes 12296 | tf_op jit(solution)/shard_map/ppermute | solution.py:582
  84.6 5.1 %collective-permute-start.30 = (f32[8,128]{1,0:T(8,128)S(1)}, f32[8,128]{1,0:T(8,128)S(1)}, u32[]{:S(2)}, u32[]{:S(2)}) collective-permute-start(f32[8,128]{1,0:T(8,128)S(1)} %add_add_fusion.2), channel_id=1, source_target_pairs={{0,8},{1,9},{2,10},{3,11},{4,12},{5,13},{6,14},{7,15},{8,0},{9,1},... | collective-permute-start | bytes 12296 | tf_op jit(solution)/shard_map/ppermute | solution.py:582
  84.6 11.4 %collective-permute-start.29 = (f32[8,128]{1,0:T(8,128)S(1)}, f32[8,128]{1,0:T(8,128)S(1)}, u32[]{:S(2)}, u32[]{:S(2)}) collective-permute-start(f32[8,128]{1,0:T(8,128)S(1)} %add_add_fusion.2), channel_id=1, source_target_pairs={{0,12},{1,13},{2,14},{3,15},{4,0},{5,1},{6,2},{7,3},{8,4},{9,5},{1... | collective-permute-start | bytes 12296 | tf_op jit(solution)/shard_map/ppermute | solution.py:582
  84.7 13.2 %collective-permute-start.28 = (f32[8,128]{1,0:T(8,128)S(1)}, f32[8,128]{1,0:T(8,128)S(1)}, u32[]{:S(2)}, u32[]{:S(2)}) collective-permute-start(f32[8,128]{1,0:T(8,128)S(1)} %add_add_fusion.2), channel_id=1, source_target_pairs={{0,4},{1,5},{2,6},{3,7},{4,8},{5,9},{6,10},{7,11},{8,12},{9,13},{1... | collective-permute-start | bytes 12296 | tf_op jit(solution)/shard_map/ppermute | solution.py:582
  86.8 56.8 %collective-permute-start.35 = (bf16[32,128,128]{2,1,0:T(8,128)(2,1)}, bf16[32,128,128]{2,1,0:T(8,128)(2,1)S(1)}, u32[]{:S(2)}, u32[]{:S(2)}) collective-permute-start(bf16[32,128,128]{2,1,0:T(8,128)(2,1)} %collective-permute-done.17.lm), channel_id=1, source_target_pairs={{0,1},{1,2},{2,3},{3,4},{4,5},{5,6},{6,7},{7,8},{8,9},{9,10},{10,1... | collective-permute-start | bytes 3145736 | tf_op jit(solution)/shard_map/ppermute | solution.py:645
  89.7 53.9 %collective-permute-start.37 = (bf16[36,128,128]{2,1,0:T(8,128)(2,1)S(1)}, bf16[36,128,128]{2,1,0:T(8,128)(2,1)S(1)}, u32[]{:S(2)}, u32[]{:S(2)}) collective-permute-start(bf16[36,128,128]{2,1,0:T(8,128)(2,1)S(1)} %pad_maximum_fusion.6), channel_id=1, source_target_pairs={{0,15},{1,0},{2,1},{3,2},{4,3},{5,4},{6,5},{7,6},{8,7},{9,8},{10,9... | collective-permute-start | bytes 3538952 | tf_op jit(solution)/shard_map/ppermute | solution.py:636
  96.0 47.6 %collective-permute-start.34 = (bf16[36,128,128]{2,1,0:T(8,128)(2,1)S(1)}, bf16[36,128,128]{2,1,0:T(8,128)(2,1)S(1)}, u32[]{:S(2)}, u32[]{:S(2)}) collective-permute-start(bf16[36,128,128]{2,1,0:T(8,128)(2,1)S(1)} %pad_maximum_fusion.5), channel_id=1, source_target_pairs={{0,1},{1,2},{2,3},{3,4},{4,5},{5,6},{6,7},{7,8},{8,9},{9,10},{10,1... | collective-permute-start | bytes 3538952 | tf_op jit(solution)/shard_map/ppermute | solution.py:636
  98.0 26.9 %collective-permute-start.33 = (f32[8,128]{1,0:T(8,128)S(1)}, f32[8,128]{1,0:T(8,128)S(1)}, u32[]{:S(2)}, u32[]{:S(2)}) collective-permute-start(f32[8,128]{1,0:T(8,128)S(1)} %add_add_fusion.1), channel_id=1, source_target_pairs={{0,2},{1,3},{2,0},{3,1},{4,6},{5,7},{6,4},{7,5},{8,10},{9,11},{10,... | collective-permute-start | bytes 12296 | tf_op jit(solution)/shard_map/ppermute | solution.py:582
  124.9 3.6 %collective-permute-start.32 = (f32[8,128]{1,0:T(8,128)S(1)}, f32[8,128]{1,0:T(8,128)S(1)}, u32[]{:S(2)}, u32[]{:S(2)}) collective-permute-start(f32[8,128]{1,0:T(8,128)S(1)} %add_add_fusion.1), channel_id=1, source_target_pairs={{0,3},{1,0},{2,1},{3,2},{4,7},{5,4},{6,5},{7,6},{8,11},{9,8},{10,9... | collective-permute-start | bytes 12296 | tf_op jit(solution)/shard_map/ppermute | solution.py:582
  128.5 4.8 %collective-permute-start.31 = (f32[8,128]{1,0:T(8,128)S(1)}, f32[8,128]{1,0:T(8,128)S(1)}, u32[]{:S(2)}, u32[]{:S(2)}) collective-permute-start(f32[8,128]{1,0:T(8,128)S(1)} %add_add_fusion.1), channel_id=1, source_target_pairs={{0,1},{1,2},{2,3},{3,0},{4,5},{5,6},{6,7},{7,4},{8,9},{9,10},{10,1... | collective-permute-start | bytes 12296 | tf_op jit(solution)/shard_map/ppermute | solution.py:582
  133.3 10.3 %collective-permute-start.36 = (bf16[20,128,128]{2,1,0:T(8,128)(2,1)S(1)}, bf16[20,128,128]{2,1,0:T(8,128)(2,1)S(1)}, u32[]{:S(2)}, u32[]{:S(2)}) collective-permute-start(bf16[20,128,128]{2,1,0:T(8,128)(2,1)S(1)} %pad_maximum_fusion.7), channel_id=1, source_target_pairs={{16,17},{17,18},{18,19},{19,20},{20,21},{21,22},{22,23},{23,24},{2... | collective-permute-start | bytes 1966088 | tf_op jit(solution)/shard_map/ppermute | solution.py:639
  134.0 9.6 %collective-permute-start.39 = (bf16[20,128,128]{2,1,0:T(8,128)(2,1)S(1)}, bf16[20,128,128]{2,1,0:T(8,128)(2,1)S(1)}, u32[]{:S(2)}, u32[]{:S(2)}) collective-permute-start(bf16[20,128,128]{2,1,0:T(8,128)(2,1)S(1)} %pad_maximum_fusion.8), channel_id=1, source_target_pairs={{16,31},{17,16},{18,17},{19,18},{20,19},{21,20},{22,21},{23,22},{2... | collective-permute-start | bytes 1966088 | tf_op jit(solution)/shard_map/ppermute | solution.py:639

commit v7 on v5

--- a/solution.py
+++ b/solution.py
@@ -401,7 +401,7 @@
     def body(p, acc):
         return acc + by[pl.ds(p, 1)] * src[p].astype(jnp.float32)
 
-    acc = lax.fori_loop(0, 3 * PAD, body, jnp.zeros((C, C), jnp.float32), unroll=4)
+    acc = lax.fori_loop(0, 3 * PAD, body, jnp.zeros((C, C), jnp.float32), unroll=8)
     at = at_ref[0]
     for i in range(E):
         acc = acc + c0[pl.ds(PAD + at + i, 1)] * l3[i].astype(jnp.float32)
@@ -444,7 +444,7 @@
         out_ref[j] = lax.dot_general(lhs, rhs, NT, preferred_element_type=jnp.float32)
         return carry
 
-    lax.fori_loop(0, PER, body, 0, unroll=4)
+    lax.fori_loop(0, PER, body, 0, unroll=8)
 
 
 def inner_call(chunk, idx, wv, near):
@@ -481,7 +481,7 @@
             out_ref[t] = got + partial[c][j]
             return carry
 
-        lax.fori_loop(0, PER, body, 0, unroll=4)
+        lax.fori_loop(0, PER, body, 0, unroll=8)
 
 
 def outer_call(idx, wv, parts, partial):

time: 148 us -> 146 us (0.986)
  Pallas kernels: 34.5 us -> 31.7 us
where the time goes in v7:
time: 146 us
  starting transfers between devices  60.9 us (42%)
  waiting for transfers between devices  50.2 us (34%)
  Pallas kernels  31.7 us (22%)
    ppermute x10, waiting for transfers between devices, swap(): return lax.ppermute(v, axis, [(i, to(i)) for i in range(size)])  20.5 us
    ppermute x1, waiting for transfers between devices, usual(): lax.ppermute(qs, 'lon', ring(1))  18.5 us
    ppermute x10, starting transfers between devices, swap(): return lax.ppermute(v, axis, [(i, to(i)) for i in range(size)])  12.8 us
    ppermute x2, starting transfers between devices, usual(): lax.ppermute(jnp.concatenate([x, h], axis=0), both, some(d, POLAR))  9.16 us
    ppermute x2, starting transfers between devices, usual(): lax.ppermute(x, both, some(d, POLAR))  9.15 us
    ppermute x1, waiting for transfers between devices, usual(): cr = lax.ppermute(to_right, 'lon', ring(1))  8.21 us
    pallas_call x4, Pallas kernels, inner_call(): pl.pallas_call(functools.partial(inner_kernel, chunk * PER), in_specs=[pl...  8.05 us
    pallas_call x1, Pallas kernels, sums_call(): pl.pallas_call(sums_kernel, in_specs=[smem, smem, pl.BlockSpec(memory_spa...  7.21 us
  transfers between devices with their start and end apart: 26, of which 8 were waited for; matrix products, arithmetic and copies ran while one was open for 1% of the time, Pallas kernels for 11%

profile of v7, /device:TPU:0, one launch (start us, length us, event | category | flops | bytes accessed | tf_op | source)
XLA Modules:
  0.0 145.7 jit_solution(5369865364642209390)
XLA Ops:
  0.0 2.6 %split.1 = (bf16[32,128,128]{2,1,0:T(8,128)(2,1)S(1)}, bf16[32,128,128]{2,1,0:T(8,128)(2,1)}) custom-call(bf16[64,128,128]{2,1,0:T(8,128)(2,1)} %bitcast.155), custom_call_target="tpu_custom_call" | custom-call | flops 1000 | bytes 2097152 | tf_op jit(solution)/shard_map/split/pallas_call | solution.py:354
  2.6 1.8 %collective-permute-start.16 = (bf16[32,128,128]{2,1,0:T(8,128)(2,1)S(1)}, bf16[32,128,128]{2,1,0:T(8,128)(2,1)S(1)}, u32[]{:S(2)}, u32[]{:S(2)}) collective-permute-start(bf16[32,128,128]{2,1,0:T(8,128)(2,1)S(1)} %get-tuple-element.57.qs), channel_id=1, source_target_pairs={{0,1},{1,2},{2,3},{3,4},{4,5},{5,6},{6,7},{7,8},{8,9},{9,10},{10,1... | collective-permute-start | bytes 3145736 | tf_op jit(solution)/shard_map/ppermute | solution.py:596
  4.3 5.0 %collective-permute-start.18 = (bf16[32,128,128]{2,1,0:T(8,128)(2,1)S(1)}, bf16[32,128,128]{2,1,0:T(8,128)(2,1)S(1)}, u32[]{:S(2)}, u32[]{:S(2)}) collective-permute-start(bf16[32,128,128]{2,1,0:T(8,128)(2,1)S(1)} %get-tuple-element.57.qs), channel_id=1, source_target_pairs={{0,15},{1,0},{2,1},{3,2},{4,3},{5,4},{6,5},{7,6},{8,7},{9,8},{10,9... | collective-permute-start | bytes 3145736 | tf_op jit(solution)/shard_map/ppermute | solution.py:596
  9.3 5.3 %collective-permute-start.19 = (bf16[32,128,128]{2,1,0:T(8,128)(2,1)}, bf16[32,128,128]{2,1,0:T(8,128)(2,1)}, u32[]{:S(2)}, u32[]{:S(2)}) collective-permute-start(bf16[32,128,128]{2,1,0:T(8,128)(2,1)} %get-tuple-element.58.qm), channel_id=1, source_target_pairs={{0,15},{1,0},{2,1},{3,2},{4,3},{5,4},{6,5},{7,6},{8,7},{9,8},{10,9... | collective-permute-start | bytes 3145736 | tf_op jit(solution)/shard_map/ppermute | solution.py:597
  14.8 18.5 %collective-permute-done.16.ls = bf16[32,128,128]{2,1,0:T(8,128)(2,1)S(1)} collective-permute-done((bf16[32,128,128]{2,1,0:T(8,128)(2,1)S(1)}, bf16[32,128,128]{2,1,0:T(8,128)(2,1)S(1)}, u32[]{:S(2)}, u32[]{:S(2)}) %collective-permute-start.16) | collective-permute-done | bytes 1048608 | tf_op jit(solution)/shard_map/ppermute | solution.py:596
  33.3 1.3 collective-permute-start.20
  34.6 1.3 collective-permute-start.21
  36.0 7.2 %sums.1 = (bf16[64,8,128,128]{3,2,1,0:T(8,128)(2,1)S(1)}, f32[144,128]{1,0:T(8,128)S(1)}, f32[144,128]{1,0:T(8,128)S(1)}, f32[216,128]{1,0:T(8,128)S(1)}) custom-call(s32[8,64]{1,0:T(8,128)S(1)} %get-tuple-element.111.idx_ref, f32[64]{0:T(128)S(1)} %add_cosine_fusion.1.area_ref, bf16[64,8,128,128]{3,2,1,0:T(8,128)(2,1)} %bitcast.151), custom_call_target="tpu_custom_call" | custom-call | flops 20000000 | bytes 17825792 | tf_op jit(solution)/shard_map/sums/pallas_call | solution.py:321
  43.2 0.6 convert_reduce_fusion.1
  43.8 0.1 slice_select_fusion.3
  43.9 5.5 %collective-permute-start.14 = (f32[144,128]{1,0:T(8,128)S(1)}, f32[144,128]{1,0:T(8,128)S(1)}, u32[]{:S(2)}, u32[]{:S(2)}) collective-permute-start(f32[144,128]{1,0:T(8,128)S(1)} %get-tuple-element.55), channel_id=1, source_target_pairs={{0,15},{1,0},{2,1},{3,2},{4,3},{5,4},{6,5},{7,6},{8,7},{9,8},{10,9... | collective-permute-start | bytes 221192 | tf_op jit(solution)/shard_map/ppermute | solution.py:604
  49.4 1.9 %collective-permute-start.22 = (bf16[5,128,128]{2,1,0:T(8,128)(2,1)S(1)}, bf16[5,128,128]{2,1,0:T(8,128)(2,1)S(1)}, u32[]{:S(2)}, u32[]{:S(2)}) collective-permute-start(bf16[5,128,128]{2,1,0:T(8,128)(2,1)S(1)} %slice_select_fusion.4), channel_id=1, source_target_pairs={{0,3},{1,4},{2,5},{3,6},{4,7},{5,8},{6,9},{7,10},{8,11},{9,12},{10... | collective-permute-start | bytes 491528 | tf_op jit(solution)/shard_map/ppermute | solution.py:599
  51.3 6.0 %collective-permute-start.23 = (bf16[5,128,128]{2,1,0:T(8,128)(2,1)S(1)}, bf16[5,128,128]{2,1,0:T(8,128)(2,1)S(1)}, u32[]{:S(2)}, u32[]{:S(2)}) collective-permute-start(bf16[5,128,128]{2,1,0:T(8,128)(2,1)S(1)} %slice_select_fusion.4), channel_id=1, source_target_pairs={{0,13},{1,14},{2,15},{3,0},{4,1},{5,2},{6,3},{7,4},{8,5},{9,6},{10... | collective-permute-start | bytes 491528 | tf_op jit(solution)/shard_map/ppermute | solution.py:600
  57.4 0.1 collective-permute-start.15
  57.5 8.2 %collective-permute-done.15.cr = f32[144,128]{1,0:T(8,128)S(1)} collective-permute-done((f32[144,128]{1,0:T(8,128)S(1)}, f32[144,128]{1,0:T(8,128)S(1)}, u32[]{:S(2)}, u32[]{:S(2)}) %collective-permute-start.15) | collective-permute-done | bytes 73760 | tf_op jit(solution)/shard_map/ppermute | solution.py:605
  65.7 4.8 %mass.1 = (f32[8,128]{1,0:T(8,128)S(1)}, bf16[217,128,128]{2,1,0:T(8,128)(2,1)S(1)}) custom-call(f32[64]{0:T(128)S(1)} %add_cosine_fusion.1.area_ref, f32[1]{0:T(128)} %bitcast.24.lost_ref, s32[8]{0:T(128)S(1)} %compare_select_fusion.1.at_ref, f32[216,128]{1,0:T(8,128)S(1)} %get-tuple-element.54.c0, f32[144,128]{1,0:T(8,128)S(1)} %collective-permute-done.14.cl, ...), custom_call_target="tpu_custom_call" | custom-call | flops 9000000 | bytes 3145728 | tf_op jit(solution)/shard_map/mass/pallas_call | solution.py:420
  70.5 0.1 pad_maximum_fusion.7
  70.6 0.7 collective-permute-start.36
  71.3 0.4 collective-permute-done.24
  71.7 3.9 %collective-permute-start.26 = (f32[8,128]{1,0:T(8,128)S(1)}, f32[8,128]{1,0:T(8,128)S(1)}, u32[]{:S(2)}, u32[]{:S(2)}) collective-permute-start(f32[8,128]{1,0:T(8,128)S(1)} %add.234), channel_id=1, source_target_pairs={{0,96},{16,112},{32,0},{48,16},{64,32},{80,48},{96,64},{112,80},{1... | collective-permute-start | bytes 12296 | tf_op jit(solution)/shard_map/ppermute | solution.py:571
  75.6 1.4 collective-permute-start.27
  77.0 0.1 pad_maximum_fusion.5
  77.1 3.6 %collective-permute-done.27 = f32[8,128]{1,0:T(8,128)S(1)} collective-permute-done((f32[8,128]{1,0:T(8,128)S(1)}, f32[8,128]{1,0:T(8,128)S(1)}, u32[]{:S(2)}, u32[]{:S(2)}) %collective-permute-start.27) | collective-permute-done | bytes 4128 | tf_op jit(solution)/shard_map/ppermute | solution.py:571
  80.7 3.2 %collective-permute-start.29 = (f32[8,128]{1,0:T(8,128)S(1)}, f32[8,128]{1,0:T(8,128)S(1)}, u32[]{:S(2)}, u32[]{:S(2)}) collective-permute-start(f32[8,128]{1,0:T(8,128)S(1)} %add_add_fusion.2), channel_id=1, source_target_pairs={{0,12},{1,13},{2,14},{3,15},{4,0},{5,1},{6,2},{7,3},{8,4},{9,5},{1... | collective-permute-start | bytes 12296 | tf_op jit(solution)/shard_map/ppermute | solution.py:571
  83.9 0.1 pad_maximum_fusion.6
  84.0 1.9 %collective-permute-start.34 = (bf16[36,128,128]{2,1,0:T(8,128)(2,1)S(1)}, bf16[36,128,128]{2,1,0:T(8,128)(2,1)S(1)}, u32[]{:S(2)}, u32[]{:S(2)}) collective-permute-start(bf16[36,128,128]{2,1,0:T(8,128)(2,1)S(1)} %pad_maximum_fusion.5), channel_id=1, source_target_pairs={{0,1},{1,2},{2,3},{3,4},{4,5},{5,6},{6,7},{7,8},{8,9},{9,10},{10,1... | collective-permute-start | bytes 3538952 | tf_op jit(solution)/shard_map/ppermute | solution.py:624
  86.0 7.2 %collective-permute-start.37 = (bf16[36,128,128]{2,1,0:T(8,128)(2,1)S(1)}, bf16[36,128,128]{2,1,0:T(8,128)(2,1)S(1)}, u32[]{:S(2)}, u32[]{:S(2)}) collective-permute-start(bf16[36,128,128]{2,1,0:T(8,128)(2,1)S(1)} %pad_maximum_fusion.6), channel_id=1, source_target_pairs={{0,15},{1,0},{2,1},{3,2},{4,3},{5,4},{6,5},{7,6},{8,7},{9,8},{10,9... | collective-permute-start | bytes 3538952 | tf_op jit(solution)/shard_map/ppermute | solution.py:624
  93.3 0.1 collective-permute-start.31
  93.3 3.2 %collective-permute-start.32 = (f32[8,128]{1,0:T(8,128)S(1)}, f32[8,128]{1,0:T(8,128)S(1)}, u32[]{:S(2)}, u32[]{:S(2)}) collective-permute-start(f32[8,128]{1,0:T(8,128)S(1)} %add_add_fusion.1), channel_id=1, source_target_pairs={{0,3},{1,0},{2,1},{3,2},{4,7},{5,4},{6,5},{7,6},{8,11},{9,8},{10,9... | collective-permute-start | bytes 12296 | tf_op jit(solution)/shard_map/ppermute | solution.py:571
  96.6 7.8 %collective-permute-done.31 = f32[8,128]{1,0:T(8,128)S(1)} collective-permute-done((f32[8,128]{1,0:T(8,128)S(1)}, f32[8,128]{1,0:T(8,128)S(1)}, u32[]{:S(2)}, u32[]{:S(2)}) %collective-permute-start.31) | collective-permute-done | bytes 4128 | tf_op jit(solution)/shard_map/ppermute | solution.py:571
  104.3 1.0 collective-permute-start.33
  105.3 8.7 %collective-permute-done.32 = f32[8,128]{1,0:T(8,128)S(1)} collective-permute-done((f32[8,128]{1,0:T(8,128)S(1)}, f32[8,128]{1,0:T(8,128)S(1)}, u32[]{:S(2)}, u32[]{:S(2)}) %collective-permute-start.32) | collective-permute-done | bytes 4128 | tf_op jit(solution)/shard_map/ppermute | solution.py:571
  114.1 2.5 %collective-permute-start.35 = (bf16[32,128,128]{2,1,0:T(8,128)(2,1)}, bf16[32,128,128]{2,1,0:T(8,128)(2,1)S(1)}, u32[]{:S(2)}, u32[]{:S(2)}) collective-permute-start(bf16[32,128,128]{2,1,0:T(8,128)(2,1)} %collective-permute-done.17.lm), channel_id=1, source_target_pairs={{0,1},{1,2},{2,3},{3,4},{4,5},{5,6},{6,7},{7,8},{8,9},{9,10},{10,1... | collective-permute-start | bytes 3145736 | tf_op jit(solution)/shard_map/ppermute | solution.py:633
  116.6 6.7 %collective-permute-start.38 = (bf16[32,128,128]{2,1,0:T(8,128)(2,1)}, bf16[32,128,128]{2,1,0:T(8,128)(2,1)S(1)}, u32[]{:S(2)}, u32[]{:S(2)}) collective-permute-start(bf16[32,128,128]{2,1,0:T(8,128)(2,1)} %collective-permute-done.19.rm), channel_id=1, source_target_pairs={{0,15},{1,0},{2,1},{3,2},{4,3},{5,4},{6,5},{7,6},{8,7},{9,8},{10,9... | collective-permute-start | bytes 3145736 | tf_op jit(solution)/shard_map/ppermute | solution.py:633
  123.2 0.1 slice_select_fusion.2
  123.3 0.1 pad_maximum_fusion.8
  123.4 0.9 collective-permute-start.39
  124.3 2.0 %shard_map.58.refs_3_ = f32[16,128,128]{2,1,0:T(8,128)S(1)} custom-call(s32[8,64]{1,0:T(8,128)S(1)} %get-tuple-element.110.idx_ref, bf16[64,8,128,128]{3,2,1,0:T(8,128)(2,1)S(1)} %get-tuple-element.62.wv, bf16[217,128,128]{2,1,0:T(8,128)(2,1)S(1)} %get-tuple-element.63.src), custom_call_target="tpu_custom_call" | custom-call | flops 536870912 | bytes 1048576 | tf_op jit(solution)/shard_map/pallas_call | solution.py:452
  126.3 2.0 %shard_map.57.refs_2_ = f32[16,128,128]{2,1,0:T(8,128)S(1)} custom-call(s32[8,64]{1,0:T(8,128)S(1)} %get-tuple-element.110.idx_ref, bf16[64,8,128,128]{3,2,1,0:T(8,128)(2,1)S(1)} %get-tuple-element.62.wv, bf16[217,128,128]{2,1,0:T(8,128)(2,1)S(1)} %get-tuple-element.63.src), custom_call_target="tpu_custom_call" | custom-call | flops 536870912 | bytes 1048576 | tf_op jit(solution)/shard_map/pallas_call | solution.py:452
  128.3 2.0 %shard_map.56.refs_1_ = f32[16,128,128]{2,1,0:T(8,128)S(1)} custom-call(s32[8,64]{1,0:T(8,128)S(1)} %get-tuple-element.110.idx_ref, bf16[64,8,128,128]{3,2,1,0:T(8,128)(2,1)S(1)} %get-tuple-element.62.wv, bf16[217,128,128]{2,1,0:T(8,128)(2,1)S(1)} %get-tuple-element.63.src), custom_call_target="tpu_custom_call" | custom-call | flops 536870912 | bytes 1048576 | tf_op jit(solution)/shard_map/pallas_call | solution.py:452
  130.3 2.0 %shard_map.55.refs_0_ = f32[16,128,128]{2,1,0:T(8,128)S(1)} custom-call(s32[8,64]{1,0:T(8,128)S(1)} %get-tuple-element.110.idx_ref, bf16[64,8,128,128]{3,2,1,0:T(8,128)(2,1)S(1)} %get-tuple-element.62.wv, bf16[217,128,128]{2,1,0:T(8,128)(2,1)S(1)} %get-tuple-element.63.src), custom_call_target="tpu_custom_call" | custom-call | flops 536870912 | bytes 1048576 | tf_op jit(solution)/shard_map/pallas_call | solution.py:452
  132.4 0.5 slice.110
  132.9 1.4 collective-permute-done.35.lm
  134.3 1.6 %collective-permute-done.38.rm = bf16[32,128,128]{2,1,0:T(8,128)(2,1)S(1)} collective-permute-done((bf16[32,128,128]{2,1,0:T(8,128)(2,1)}, bf16[32,128,128]{2,1,0:T(8,128)(2,1)S(1)}, u32[]{:S(2)}, u32[]{:S(2)}) %collective-permute-start.38) | collective-permute-done | bytes 1048608 | tf_op jit(solution)/shard_map/ppermute | solution.py:633
  135.9 6.9 %outer.1.in_ref = f32[64,128,128]{2,1,0:T(8,128)S(1)} custom-call(s32[8,64]{1,0:T(8,128)S(1)} %get-tuple-element.112.idx_ref, bf16[64,8,128,128]{3,2,1,0:T(8,128)(2,1)S(1)} %get-tuple-element.62.wv, bf16[36,128,128]{2,1,0:T(8,128)(2,1)S(1)} %collective-permute-done.34.ls, bf16[32,128,128]{2,1,0:T(8,128)(2,1)S(1)} %collective-permute-done.35.lm, ...), custom_call_target="tpu_custom_call" | custom-call | flops 2147483648 | bytes 1048576 | tf_op jit(solution)/shard_map/outer/pallas_call | solution.py:489
  142.8 0.1 broadcast_in_dim.44.corr_ref
  142.9 2.1 %write.1 = f32[64,128,128]{2,1,0:T(8,128)} custom-call(f32[128,128]{1,0:T(8,128)S(1)} %broadcast_in_dim.44.corr_ref, f32[64,128,128]{2,1,0:T(8,128)S(1)} %outer.1.in_ref), custom_call_target="tpu_custom_call" | custom-call | flops 1000000 | bytes 4194304 | tf_op jit(solution)/shard_map/write/pallas_call | solution.py:525
  145.0 0.6 while.9
  (41 shorter events, 0.3 us)
Async XLA Ops:
  0.0 14.7 %copy-start.6 = (s32[64,1]{0,1:T(1,128)S(1)}, s32[64,1]{0,1:T(1,128)}, u32[]{:S(2)}) copy-start(s32[64,1]{0,1:T(1,128)} %param.11) | copy-start | bytes 772
  0.0 14.7 %copy-start.4 = (s32[64,1,8]{0,2,1:T(8,128)S(1)}, s32[64,1,8]{0,2,1:T(8,128)}, u32[]{:S(2)}) copy-start(s32[64,1,8]{0,2,1:T(8,128)} %param.10) | copy-start | bytes 6148
  0.0 14.7 %copy-start.2 = (s32[64,1,8]{0,2,1:T(8,128)S(1)}, s32[64,1,8]{0,2,1:T(8,128)}, u32[]{:S(2)}) copy-start(s32[64,1,8]{0,2,1:T(8,128)} %param.9) | copy-start | bytes 6148
  2.6 30.7 %collective-permute-start.16 = (bf16[32,128,128]{2,1,0:T(8,128)(2,1)S(1)}, bf16[32,128,128]{2,1,0:T(8,128)(2,1)S(1)}, u32[]{:S(2)}, u32[]{:S(2)}) collective-permute-start(bf16[32,128,128]{2,1,0:T(8,128)(2,1)S(1)} %get-tuple-element.57.qs), channel_id=1, source_target_pairs={{0,1},{1,2},{2,3},{3,4},{4,5},{5,6},{6,7},{7,8},{8,9},{9,10},{10,1... | collective-permute-start | bytes 3145736 | tf_op jit(solution)/shard_map/ppermute | solution.py:596
  4.3 28.9 %collective-permute-start.18 = (bf16[32,128,128]{2,1,0:T(8,128)(2,1)S(1)}, bf16[32,128,128]{2,1,0:T(8,128)(2,1)S(1)}, u32[]{:S(2)}, u32[]{:S(2)}) collective-permute-start(bf16[32,128,128]{2,1,0:T(8,128)(2,1)S(1)} %get-tuple-element.57.qs), channel_id=1, source_target_pairs={{0,15},{1,0},{2,1},{3,2},{4,3},{5,4},{6,5},{7,6},{8,7},{9,8},{10,9... | collective-permute-start | bytes 3145736 | tf_op jit(solution)/shard_map/ppermute | solution.py:596
  9.3 56.4 %collective-permute-start.17 = (bf16[32,128,128]{2,1,0:T(8,128)(2,1)}, bf16[32,128,128]{2,1,0:T(8,128)(2,1)}, u32[]{:S(2)}, u32[]{:S(2)}) collective-permute-start(bf16[32,128,128]{2,1,0:T(8,128)(2,1)} %get-tuple-element.58.qm), channel_id=1, source_target_pairs={{0,1},{1,2},{2,3},{3,4},{4,5},{5,6},{6,7},{7,8},{8,9},{9,10},{10,1... | collective-permute-start | bytes 3145736 | tf_op jit(solution)/shard_map/ppermute | solution.py:597
  9.3 56.4 %collective-permute-start.19 = (bf16[32,128,128]{2,1,0:T(8,128)(2,1)}, bf16[32,128,128]{2,1,0:T(8,128)(2,1)}, u32[]{:S(2)}, u32[]{:S(2)}) collective-permute-start(bf16[32,128,128]{2,1,0:T(8,128)(2,1)} %get-tuple-element.58.qm), channel_id=1, source_target_pairs={{0,15},{1,0},{2,1},{3,2},{4,3},{5,4},{6,5},{7,6},{8,7},{9,8},{10,9... | collective-permute-start | bytes 3145736 | tf_op jit(solution)/shard_map/ppermute | solution.py:597
  33.3 16.0 %collective-permute-start.20 = (bf16[12,128,128]{2,1,0:T(8,128)(2,1)S(1)}, bf16[12,128,128]{2,1,0:T(8,128)(2,1)S(1)}, u32[]{:S(2)}, u32[]{:S(2)}) collective-permute-start(bf16[12,128,128]{2,1,0:T(8,128)(2,1)S(1)} %get-tuple-element.59), channel_id=1, source_target_pairs={{0,16},{16,32},{32,48},{48,64},{64,80},{80,96},{96,112},{1,17},{17... | collective-permute-start | bytes 1179656 | tf_op jit(solution)/shard_map/ppermute | solution.py:607
  34.6 16.6 %collective-permute-start.21 = (bf16[12,128,128]{2,1,0:T(8,128)(2,1)S(1)}, bf16[12,128,128]{2,1,0:T(8,128)(2,1)S(1)}, u32[]{:S(2)}, u32[]{:S(2)}) collective-permute-start(bf16[12,128,128]{2,1,0:T(8,128)(2,1)S(1)} %get-tuple-element.60), channel_id=1, source_target_pairs={{16,0},{32,16},{48,32},{64,48},{80,64},{96,80},{112,96},{17,1},{33... | collective-permute-start | bytes 1179656 | tf_op jit(solution)/shard_map/ppermute | solution.py:607
  43.9 13.5 %collective-permute-start.14 = (f32[144,128]{1,0:T(8,128)S(1)}, f32[144,128]{1,0:T(8,128)S(1)}, u32[]{:S(2)}, u32[]{:S(2)}) collective-permute-start(f32[144,128]{1,0:T(8,128)S(1)} %get-tuple-element.55), channel_id=1, source_target_pairs={{0,15},{1,0},{2,1},{3,2},{4,3},{5,4},{6,5},{7,6},{8,7},{9,8},{10,9... | collective-permute-start | bytes 221192 | tf_op jit(solution)/shard_map/ppermute | solution.py:604
  49.4 16.3 %collective-permute-start.22 = (bf16[5,128,128]{2,1,0:T(8,128)(2,1)S(1)}, bf16[5,128,128]{2,1,0:T(8,128)(2,1)S(1)}, u32[]{:S(2)}, u32[]{:S(2)}) collective-permute-start(bf16[5,128,128]{2,1,0:T(8,128)(2,1)S(1)} %slice_select_fusion.4), channel_id=1, source_target_pairs={{0,3},{1,4},{2,5},{3,6},{4,7},{5,8},{6,9},{7,10},{8,11},{9,12},{10... | collective-permute-start | bytes 491528 | tf_op jit(solution)/shard_map/ppermute | solution.py:599
  51.3 14.4 %collective-permute-start.23 = (bf16[5,128,128]{2,1,0:T(8,128)(2,1)S(1)}, bf16[5,128,128]{2,1,0:T(8,128)(2,1)S(1)}, u32[]{:S(2)}, u32[]{:S(2)}) collective-permute-start(bf16[5,128,128]{2,1,0:T(8,128)(2,1)S(1)} %slice_select_fusion.4), channel_id=1, source_target_pairs={{0,13},{1,14},{2,15},{3,0},{4,1},{5,2},{6,3},{7,4},{8,5},{9,6},{10... | collective-permute-start | bytes 491528 | tf_op jit(solution)/shard_map/ppermute | solution.py:600
  57.4 8.3 %collective-permute-start.15 = (f32[144,128]{1,0:T(8,128)S(1)}, f32[144,128]{1,0:T(8,128)S(1)}, u32[]{:S(2)}, u32[]{:S(2)}) collective-permute-start(f32[144,128]{1,0:T(8,128)S(1)} %get-tuple-element.56), channel_id=1, source_target_pairs={{0,1},{1,2},{2,3},{3,4},{4,5},{5,6},{6,7},{7,8},{8,9},{9,10},{10,1... | collective-permute-start | bytes 221192 | tf_op jit(solution)/shard_map/ppermute | solution.py:605
  70.5 1.2 collective-permute-start.24
  70.6 52.8 %collective-permute-start.36 = (bf16[20,128,128]{2,1,0:T(8,128)(2,1)S(1)}, bf16[20,128,128]{2,1,0:T(8,128)(2,1)S(1)}, u32[]{:S(2)}, u32[]{:S(2)}) collective-permute-start(bf16[20,128,128]{2,1,0:T(8,128)(2,1)S(1)} %pad_maximum_fusion.7), channel_id=1, source_target_pairs={{16,17},{17,18},{18,19},{19,20},{20,21},{21,22},{22,23},{23,24},{2... | collective-permute-start | bytes 1966088 | tf_op jit(solution)/shard_map/ppermute | solution.py:627
  71.7 5.4 %collective-permute-start.25 = (f32[8,128]{1,0:T(8,128)S(1)}, f32[8,128]{1,0:T(8,128)S(1)}, u32[]{:S(2)}, u32[]{:S(2)}) collective-permute-start(f32[8,128]{1,0:T(8,128)S(1)} %add.234), channel_id=1, source_target_pairs={{0,32},{16,48},{32,64},{48,80},{64,96},{80,112},{96,0},{112,16},{1... | collective-permute-start | bytes 12296 | tf_op jit(solution)/shard_map/ppermute | solution.py:571
  71.7 5.4 %collective-permute-start.26 = (f32[8,128]{1,0:T(8,128)S(1)}, f32[8,128]{1,0:T(8,128)S(1)}, u32[]{:S(2)}, u32[]{:S(2)}) collective-permute-start(f32[8,128]{1,0:T(8,128)S(1)} %add.234), channel_id=1, source_target_pairs={{0,96},{16,112},{32,0},{48,16},{64,32},{80,48},{96,64},{112,80},{1... | collective-permute-start | bytes 12296 | tf_op jit(solution)/shard_map/ppermute | solution.py:571
  75.6 5.1 %collective-permute-start.27 = (f32[8,128]{1,0:T(8,128)S(1)}, f32[8,128]{1,0:T(8,128)S(1)}, u32[]{:S(2)}, u32[]{:S(2)}) collective-permute-start(f32[8,128]{1,0:T(8,128)S(1)} %add.234), channel_id=1, source_target_pairs={{0,64},{16,80},{32,96},{48,112},{64,0},{80,16},{96,32},{112,48},{1... | collective-permute-start | bytes 12296 | tf_op jit(solution)/shard_map/ppermute | solution.py:571
  80.7 5.3 %collective-permute-start.28 = (f32[8,128]{1,0:T(8,128)S(1)}, f32[8,128]{1,0:T(8,128)S(1)}, u32[]{:S(2)}, u32[]{:S(2)}) collective-permute-start(f32[8,128]{1,0:T(8,128)S(1)} %add_add_fusion.2), channel_id=1, source_target_pairs={{0,4},{1,5},{2,6},{3,7},{4,8},{5,9},{6,10},{7,11},{8,12},{9,13},{1... | collective-permute-start | bytes 12296 | tf_op jit(solution)/shard_map/ppermute | solution.py:571
  80.7 12.5 %collective-permute-start.29 = (f32[8,128]{1,0:T(8,128)S(1)}, f32[8,128]{1,0:T(8,128)S(1)}, u32[]{:S(2)}, u32[]{:S(2)}) collective-permute-start(f32[8,128]{1,0:T(8,128)S(1)} %add_add_fusion.2), channel_id=1, source_target_pairs={{0,12},{1,13},{2,14},{3,15},{4,0},{5,1},{6,2},{7,3},{8,4},{9,5},{1... | collective-permute-start | bytes 12296 | tf_op jit(solution)/shard_map/ppermute | solution.py:571
  83.9 9.3 %collective-permute-start.30 = (f32[8,128]{1,0:T(8,128)S(1)}, f32[8,128]{1,0:T(8,128)S(1)}, u32[]{:S(2)}, u32[]{:S(2)}) collective-permute-start(f32[8,128]{1,0:T(8,128)S(1)} %add_add_fusion.2), channel_id=1, source_target_pairs={{0,8},{1,9},{2,10},{3,11},{4,12},{5,13},{6,14},{7,15},{8,0},{9,1},... | collective-permute-start | bytes 12296 | tf_op jit(solution)/shard_map/ppermute | solution.py:571
  84.0 51.8 %collective-permute-start.34 = (bf16[36,128,128]{2,1,0:T(8,128)(2,1)S(1)}, bf16[36,128,128]{2,1,0:T(8,128)(2,1)S(1)}, u32[]{:S(2)}, u32[]{:S(2)}) collective-permute-start(bf16[36,128,128]{2,1,0:T(8,128)(2,1)S(1)} %pad_maximum_fusion.5), channel_id=1, source_target_pairs={{0,1},{1,2},{2,3},{3,4},{4,5},{5,6},{6,7},{7,8},{8,9},{9,10},{10,1... | collective-permute-start | bytes 3538952 | tf_op jit(solution)/shard_map/ppermute | solution.py:624
  86.0 49.9 %collective-permute-start.37 = (bf16[36,128,128]{2,1,0:T(8,128)(2,1)S(1)}, bf16[36,128,128]{2,1,0:T(8,128)(2,1)S(1)}, u32[]{:S(2)}, u32[]{:S(2)}) collective-permute-start(bf16[36,128,128]{2,1,0:T(8,128)(2,1)S(1)} %pad_maximum_fusion.6), channel_id=1, source_target_pairs={{0,15},{1,0},{2,1},{3,2},{4,3},{5,4},{6,5},{7,6},{8,7},{9,8},{10,9... | collective-permute-start | bytes 3538952 | tf_op jit(solution)/shard_map/ppermute | solution.py:624
  93.3 11.1 %collective-permute-start.31 = (f32[8,128]{1,0:T(8,128)S(1)}, f32[8,128]{1,0:T(8,128)S(1)}, u32[]{:S(2)}, u32[]{:S(2)}) collective-permute-start(f32[8,128]{1,0:T(8,128)S(1)} %add_add_fusion.1), channel_id=1, source_target_pairs={{0,1},{1,2},{2,3},{3,0},{4,5},{5,6},{6,7},{7,4},{8,9},{9,10},{10,1... | collective-permute-start | bytes 12296 | tf_op jit(solution)/shard_map/ppermute | solution.py:571
  93.3 20.7 %collective-permute-start.32 = (f32[8,128]{1,0:T(8,128)S(1)}, f32[8,128]{1,0:T(8,128)S(1)}, u32[]{:S(2)}, u32[]{:S(2)}) collective-permute-start(f32[8,128]{1,0:T(8,128)S(1)} %add_add_fusion.1), channel_id=1, source_target_pairs={{0,3},{1,0},{2,1},{3,2},{4,7},{5,4},{6,5},{7,6},{8,11},{9,8},{10,9... | collective-permute-start | bytes 12296 | tf_op jit(solution)/shard_map/ppermute | solution.py:571
  104.3 12.2 %collective-permute-start.33 = (f32[8,128]{1,0:T(8,128)S(1)}, f32[8,128]{1,0:T(8,128)S(1)}, u32[]{:S(2)}, u32[]{:S(2)}) collective-permute-start(f32[8,128]{1,0:T(8,128)S(1)} %add_add_fusion.1), channel_id=1, source_target_pairs={{0,2},{1,3},{2,0},{3,1},{4,6},{5,7},{6,4},{7,5},{8,10},{9,11},{10,... | collective-permute-start | bytes 12296 | tf_op jit(solution)/shard_map/ppermute | solution.py:571
  114.1 20.2 %collective-permute-start.35 = (bf16[32,128,128]{2,1,0:T(8,128)(2,1)}, bf16[32,128,128]{2,1,0:T(8,128)(2,1)S(1)}, u32[]{:S(2)}, u32[]{:S(2)}) collective-permute-start(bf16[32,128,128]{2,1,0:T(8,128)(2,1)} %collective-permute-done.17.lm), channel_id=1, source_target_pairs={{0,1},{1,2},{2,3},{3,4},{4,5},{5,6},{6,7},{7,8},{8,9},{9,10},{10,1... | collective-permute-start | bytes 3145736 | tf_op jit(solution)/shard_map/ppermute | solution.py:633
  116.6 19.3 %collective-permute-start.38 = (bf16[32,128,128]{2,1,0:T(8,128)(2,1)}, bf16[32,128,128]{2,1,0:T(8,128)(2,1)S(1)}, u32[]{:S(2)}, u32[]{:S(2)}) collective-permute-start(bf16[32,128,128]{2,1,0:T(8,128)(2,1)} %collective-permute-done.19.rm), channel_id=1, source_target_pairs={{0,15},{1,0},{2,1},{3,2},{4,3},{5,4},{6,5},{7,6},{8,7},{9,8},{10,9... | collective-permute-start | bytes 3145736 | tf_op jit(solution)/shard_map/ppermute | solution.py:633
  123.4 9.5 %collective-permute-start.39 = (bf16[20,128,128]{2,1,0:T(8,128)(2,1)S(1)}, bf16[20,128,128]{2,1,0:T(8,128)(2,1)S(1)}, u32[]{:S(2)}, u32[]{:S(2)}) collective-permute-start(bf16[20,128,128]{2,1,0:T(8,128)(2,1)S(1)} %pad_maximum_fusion.8), channel_id=1, source_target_pairs={{16,31},{17,16},{18,17},{19,18},{20,19},{21,20},{22,21},{23,22},{2... | collective-permute-start | bytes 1966088 | tf_op jit(solution)/shard_map/ppermute | solution.py:627
